TPU v7x, 512 devices: a whole 4x4x16 slice. The times are simulated.
512 devices in a mesh: tok: 8 (over x, core), vocab: 64 (over z, y).
Axes of the slice: x: 4, y: 4, z: 16, core: 2. Of those that a mesh axis runs over, the one named last changes fastest.
Arguments:
- hidden: bfloat16 [6144, 4096], P('tok', 'vocab'), as said below
- weight: bfloat16 [4096, 65536], P('tok', 'vocab'), may hold values from -0.09375 to 0.09375
- targets: int32 [6144], P('tok'), may hold values from 0 to 65535
- domains: int32 [6144], P('tok'), may hold values from 0 to 63
- seq_len: int32 [48], P('tok'), may hold values from 1 to 128
Outputs:
- token_loss: float32 [6144], P(('tok', 'vocab'))
- domain_mean: float32 [64], replicated
Inputs may be any that keep to these rules, and one draw needn't show every extreme that they name: hidden states of the eval window.
All inputs are finite; a program needn't handle non-finite values.
Results may differ from a plain program's by a relative error of at most 0.0003.
Values may be sent and summed in bfloat16 or wider, within the bound.
No kernel may reach another device: no remote copies, remote signals or barrier semaphores. Data moves between devices by JAX's collectives and lax.ppermute only.
A program may use at most 64 MiB of HBM per device.

v0:
```python
import jax
import jax.numpy as jnp
from jax import lax
from jax.sharding import Mesh
from jax.sharding import PartitionSpec as P

SEQ_LEN = 128
DOMAINS = 64
VOCAB = ("vocab_0", "vocab_1")
TOK = ("tok_0", "tok_1")
TOK_VOCAB = ("tok_0", "tok_1", "vocab_0", "vocab_1")


def whole_of(array, axes, dim):
    if not axes:
        return array
    nearer = lax.all_gather(array, axes[-1], axis=dim, tiled=True)
    return whole_of(nearer, axes[:-1], dim)


def laid_out(pieces, dim):
    lengths = list(pieces.shape[1:])
    lengths[dim] *= pieces.shape[0]
    return jnp.moveaxis(pieces, 0, dim).reshape(lengths)


def sent_to_all(array, axis):
    devices = lax.axis_size(axis)
    return lax.all_to_all(
        jnp.broadcast_to(array[None], (devices, *array.shape)), axis, 0, 0, tiled=True
    )


def collect(array, axis, dim):
    return laid_out(sent_to_all(array, axis), dim)


def in_one_piece(arrays, axis, split_dim, concat_dim, along):
    widths = [a.shape[along] for a in arrays]
    both = jnp.concatenate(arrays, axis=along)
    filled = lax.all_to_all(both, axis, split_axis=split_dim, concat_axis=concat_dim, tiled=True)
    return tuple(jnp.split(filled, [sum(widths[:k]) for k in range(1, len(widths))], axis=along))


def over_copies(array, axis):
    everything = sent_to_all(array, axis)
    return jnp.sum(everything, axis=0)


def by_axis(array, axes):
    far, near = axes
    nearer = over_copies(array, near)
    return over_copies(nearer, far)


def together(arrays, axis):
    flat, at, finished = (jnp.concatenate([a.reshape(-1) for a in arrays]), 0, [])
    so_far = by_axis(flat, axis)
    for a in arrays:
        finished.append(so_far[at : at + a.size].reshape(a.shape))
        at += a.size
    return tuple(finished)


def body(hidden, weight, targets, domains, seq_len):
    features = whole_of(hidden, VOCAB, 1)
    tok_rows = features.shape[0]
    columns = weight.shape[1]
    logits = jnp.dot(features, collect(weight, TOK, 0), preferred_element_type=jnp.float32)
    first_col = lax.axis_index(VOCAB) * columns
    column_ids = first_col + lax.broadcasted_iota(jnp.int32, (tok_rows, columns), 1)
    picked_loc = jnp.sum(jnp.where(column_ids == targets[:, None], logits, 0.0), axis=1)
    top_loc = jnp.max(logits, axis=1)
    groups = lax.axis_size(VOCAB)
    share_len = tok_rows // groups
    share_start = lax.axis_index(VOCAB) * share_len
    sum_loc = jnp.sum(jnp.exp(logits - top_loc[:, None]), axis=1)
    gathered = in_one_piece(
        (
            top_loc.reshape(groups, share_len),
            sum_loc.reshape(groups, share_len),
            picked_loc.reshape(groups, share_len),
        ),
        VOCAB,
        0,
        0,
        1,
    )
    row_top = jnp.max(gathered[0], axis=0)
    row_total = jnp.sum(gathered[1] * jnp.exp(gathered[0] - row_top[None, :]), axis=0)
    picked = jnp.sum(gathered[2], axis=0)
    loss_raw = jnp.log(row_total) + row_top - picked
    positions = share_start + lax.iota(jnp.int32, share_len)
    seq_ids = positions // SEQ_LEN
    seq_count = seq_len.shape[0]
    lengths = jnp.sum(
        jnp.where(
            seq_ids[:, None] == lax.broadcasted_iota(jnp.int32, (share_len, seq_count), 1),
            seq_len[None, :],
            0,
        ),
        axis=1,
    )
    valid_mask = (positions % SEQ_LEN < lengths).astype(jnp.float32)
    token_loss = loss_raw * valid_mask
    domain_share = lax.dynamic_slice_in_dim(domains, share_start, share_len)
    onehot = (
        domain_share[:, None] == lax.broadcasted_iota(jnp.int32, (share_len, DOMAINS), 1)
    ).astype(jnp.float32)
    domain_sum = jnp.dot(token_loss, onehot, precision=lax.Precision.HIGHEST)
    domain_count = jnp.dot(valid_mask, onehot, precision=lax.Precision.HIGHEST)
    domain_sum, domain_count = together(
        (domain_sum, domain_count), (("tok_0", "tok_1"), ("vocab_0", "vocab_1"))
    )
    domain_mean = domain_sum / jnp.maximum(domain_count, 1.0)
    return (token_loss, domain_mean)


def solution(mesh):
    split = Mesh(mesh.devices.reshape(4, 2, 16, 4), ("tok_0", "tok_1", "vocab_0", "vocab_1"))
    placed = (P(TOK, VOCAB), P(TOK, VOCAB), P(TOK), P(TOK), P(TOK))
    return jax.shard_map(
        body, mesh=split, in_specs=placed, out_specs=(P(TOK_VOCAB), P()), check_vma=False
    )
```

profile of v0, /device:TPU:1, one launch (start us, length us, event | category | flops | bytes accessed | tf_op | source)
XLA Modules:
  0.0 207.3 jit_solution(3366472268311308119)
XLA Ops:
  7.2 0.0 all-gather.2.cloned.1.call-start
  7.2 13.0 %all_gather.6 = bf16[768,256]{0,1:T(8,128)(2,1)} all-gather(bf16[768,64]{0,1:T(8,128)(2,1)} %param.5), channel_id=1, replica_groups=mesh['tok_0'=4,'tok_1'=2,'vocab_0'=16,'vocab_1'=4] {'vocab_1'}, dimensions={1}, use_global_device_ids=true | all-gather | bytes 491520 | tf_op jit(solution)/shard_map/all_gather | solution.py:17
  20.2 0.0 all-gather.2.cloned.1.call-update
  20.2 5.5 %broadcast_in_dim.24 = bf16[8,512,1024]{2,1,0:T(8,128)(2,1)} broadcast(bf16[512,1024]{1,0:T(8,128)(2,1)} %param.6), dimensions={1,2} | broadcast | bytes 9437184 | tf_op jit(solution)/shard_map/broadcast_in_dim | solution.py:30
  25.8 0.0 copy-start.2
  25.8 12.3 %all-to-all-start = ((bf16[8,512,1024]{2,1,0:T(8,128)(2,1)}), bf16[8,512,1024]{2,1,0:T(8,128)(2,1)}, u32[]{:S(2)}, u32[]{:S(2)}) async-start(bf16[8,512,1024]{2,1,0:T(8,128)(2,1)} %broadcast_in_dim.24), calls=%async_computation | async-start | bytes 16777216 | tf_op jit(solution)/shard_map/all_to_all | solution.py:29
  38.0 0.8 dynamic_slice.3
  38.8 0.0 copy-done.2
  38.8 0.1 select_reduce_fusion.1
  38.9 92.9 %all-to-all-done = bf16[8,512,1024]{2,1,0:T(8,128)(2,1)} async-done(((bf16[8,512,1024]{2,1,0:T(8,128)(2,1)}), bf16[8,512,1024]{2,1,0:T(8,128)(2,1)}, u32[]{:S(2)}, u32[]{:S(2)}) %all-to-all-start) | async-done | bytes 8388640 | tf_op jit(solution)/shard_map/all_to_all | solution.py:29
  131.8 0.0 all-gather.2.cloned.1.call-done
  131.8 0.0 copy-start
  131.8 11.1 %fusion.7 = (f32[768]{0:T(1024)S(1)}, f32[768,1024]{1,0:T(8,128)S(1)}) fusion(bf16[768,4096]{0,1:T(8,128)(2,1)} %all-gather.2.cloned.1.call-done, bf16[4096,1024]{1,0:T(8,128)(2,1)} %bitcast), kind=kOutput, calls=%fused_computation.27 | convolution fusion | flops 6443236352 | bytes 17828864 | tf_op jit(solution)/shard_map/dot_general | solution.py:69
  142.9 0.1 reshape.56
  143.0 0.0 copy-done
  143.0 0.9 exponential_reduce_fusion
  143.9 0.1 reshape.57
  144.1 0.1 reshape.58
  144.2 0.7 pad_maximum_fusion
  144.8 12.9 %all-to-all-start.1 = ((f32[64,1,36]{2,1,0:T(1,128)}), f32[64,1,36]{2,1,0:T(1,128)S(1)}, u32[]{:S(2)}, u32[]{:S(2)}) async-start(f32[64,1,36]{2,1,0:T(1,128)} %bitcast.2), calls=%async_computation.1 | async-start | bytes 65536 | tf_op jit(solution)/shard_map/all_to_all | solution.py:41
  157.8 0.2 convolution_bitcast_fusion
  158.0 13.4 %all-to-all-done.1 = f32[64,1,36]{2,1,0:T(1,128)S(1)} async-done(((f32[64,1,36]{2,1,0:T(1,128)}), f32[64,1,36]{2,1,0:T(1,128)S(1)}, u32[]{:S(2)}, u32[]{:S(2)}) %all-to-all-start.1) | async-done | bytes 9248 | tf_op jit(solution)/shard_map/all_to_all | solution.py:41
  171.4 0.1 fusion
  171.5 0.0 copy-start.1
  171.6 0.2 convolution_bitcast_fusion.1
  171.7 0.1 pad_maximum_fusion.1
  171.9 17.4 %all_to_all.29 = f32[64,1,128]{2,1,0:T(1,128)S(1)} all-to-all(f32[64,1,128]{2,1,0:T(1,128)S(1)} %broadcast_in_dim.26), channel_id=1, replica_groups=mesh['tok_0'=4,'tok_1'=2,'vocab_0'=16,'vocab_1'=4] {'vocab_0','vocab_1'}, dimensions={0} | all-to-all | bytes 65536 | tf_op jit(solution)/shard_map/all_to_all | solution.py:29
  189.3 10.5 %all_to_all.30 = f32[8,1,128]{2,1,0:T(1,128)S(1)} all-to-all(f32[8,1,128]{2,1,0:T(1,128)S(1)} %broadcast_in_dim.27), channel_id=1, replica_groups=mesh['tok_0'=4,'tok_1'=2,'vocab_0'=16,'vocab_1'=4] {'tok_0','tok_1'}, dimensions={0} | all-to-all | bytes 8192 | tf_op jit(solution)/shard_map/all_to_all | solution.py:29
  199.8 0.6 maximum_divide_fusion
  200.4 0.0 copy-done.1
  (8 shorter events, 0.1 us)
Async XLA Ops:
  7.2 124.6 %all-gather.2.cloned.1.call-start = ((), (), s32[]{:S(2)}) async-start(), calls=%async_computation.4 | async-start | bytes 6684672 | tf_op jit(solution)/shard_map/all_gather | solution.py:17
  25.8 13.1 %copy-start.2 = (s32[6]{0:T(128)S(1)}, s32[6]{0:T(128)}, u32[]{:S(2)}) copy-start(s32[6]{0:T(128)} %param.9) | copy-start | bytes 76
  25.8 106.0 %all-to-all-start = ((bf16[8,512,1024]{2,1,0:T(8,128)(2,1)}), bf16[8,512,1024]{2,1,0:T(8,128)(2,1)}, u32[]{:S(2)}, u32[]{:S(2)}) async-start(bf16[8,512,1024]{2,1,0:T(8,128)(2,1)} %broadcast_in_dim.24), calls=%async_computation | async-start | bytes 16777216 | tf_op jit(solution)/shard_map/all_to_all | solution.py:29
  131.8 11.2 %copy-start = (s32[768]{0:T(1024)S(1)}, s32[768]{0:T(1024)}, u32[]{:S(2)}) copy-start(s32[768]{0:T(1024)} %param.7) | copy-start | bytes 9220
  144.8 26.6 %all-to-all-start.1 = ((f32[64,1,36]{2,1,0:T(1,128)}), f32[64,1,36]{2,1,0:T(1,128)S(1)}, u32[]{:S(2)}, u32[]{:S(2)}) async-start(f32[64,1,36]{2,1,0:T(1,128)} %bitcast.2), calls=%async_computation.1 | async-start | bytes 65536 | tf_op jit(solution)/shard_map/all_to_all | solution.py:41
  171.5 28.9 %copy-start.1 = (f32[12]{0:T(128)}, f32[12]{0:T(128)S(1)}, u32[]{:S(2)}) copy-start(f32[12]{0:T(128)S(1)} %subtract_select_fusion) | copy-start | bytes 148
Sparse Core Ops, SparseCore 0:
  20.3 88.6 all-gather.1
where the time goes:
time: 208 us; the launch traced here: 207 us
  waiting for transfers between devices  106 us (51%)
  blocking collectives  40.9 us (20%)
  starting transfers between devices  25.2 us (12%)
  between operations  14.1 us (7%)
  matrix products  11.5 us (6%)
  local copies, waits for them, and re-layouts  6.62 us (3%)
  other arithmetic  2.54 us (1%)
    all_to_all x1, waiting for transfers between devices, sent_to_all(): lax.all_to_all(jnp.broadcast_to(array[None], (devices, *array.shape)), ax...  92.9 us
    all_to_all x2, blocking collectives, sent_to_all(): lax.all_to_all(jnp.broadcast_to(array[None], (devices, *array.shape)), ax...  27.9 us
    all_to_all x1, waiting for transfers between devices, in_one_piece(): lax.all_to_all(both, axis, split_axis=split_dim, concat_axis=concat_dim,...  13.4 us
    all_gather x1, blocking collectives, whole_of(): nearer = lax.all_gather(array, axes[-1], axis=dim, tiled=True)  13 us
    all_to_all x1, starting transfers between devices, in_one_piece(): lax.all_to_all(both, axis, split_axis=split_dim, concat_axis=concat_dim,...  12.9 us
    all_to_all x1, starting transfers between devices, sent_to_all(): lax.all_to_all(jnp.broadcast_to(array[None], (devices, *array.shape)), ax...  12.3 us
    dot_general x1, matrix products, body(): jnp.dot(features, collect(weight, TOK, 0), preferred_element_type=jnp.flo...  11.1 us
    broadcast_in_dim x3, local copies, waits for them, and re-layouts, sent_to_all(): jnp.broadcast_to(array[None], (devices, *array.shape))  5.55 us
  transfers between devices with their start and end apart: 3, of which 2 were waited for; matrix products, arithmetic and copies ran while one was open for 3% of the time, Pallas kernels for 0%

commit v1 on v0

v1 whole, which is shorter than its diff:
```python
import jax
import jax.numpy as jnp
from jax import lax
from jax.sharding import Mesh
from jax.sharding import PartitionSpec as P

SEQ_LEN = 128
DOMAINS = 64
TOK = ("x", "c")
VOCAB = ("z", "y")
SWAP = [(0, 1), (1, 0)]


def to_all(array, axis, copies):
    return lax.all_to_all(
        jnp.broadcast_to(array[None], (copies, *array.shape)), axis, 0, 0, tiled=True
    )


def gathered_weight(weight):
    core = lax.axis_index("c")
    half = weight.shape[1] // 2
    keep = lax.dynamic_slice_in_dim(weight, core * half, half, 1)
    give = lax.dynamic_slice_in_dim(weight, (1 - core) * half, half, 1)
    other = lax.ppermute(give, "c", SWAP)
    rows = jnp.where(
        core == 0, jnp.concatenate([keep, other], 0), jnp.concatenate([other, keep], 0)
    )
    chips = lax.axis_size("x")
    own = to_all(rows, "x", chips).reshape(chips * rows.shape[0], half)
    return own, lax.ppermute(own, "c", SWAP)


def tail(lse, picked, domains, seq_len):
    tokens = lse.shape[0]
    zs, ys = lax.axis_size("z"), lax.axis_size("y")
    own = tokens // (zs * ys)
    y = lax.axis_index("y")
    slices = jnp.stack([lse, picked]).reshape(2, zs, ys, own).transpose(2, 0, 1, 3)
    send = jnp.broadcast_to(slices.reshape(1, ys, -1), (zs, ys, 2 * zs * own))
    got = lax.all_to_all(send.reshape(zs * ys, -1), VOCAB, 0, 0, tiled=True)
    got = got.reshape(zs * ys, 2, zs * own)
    top = jnp.max(got[:, 0], axis=0)
    total = jnp.sum(jnp.exp(got[:, 0] - top[None]), axis=0)
    raw = jnp.log(total) + top - jnp.sum(got[:, 1], axis=0)
    index = lax.iota(jnp.int32, zs * own)
    local = (index // own) * (ys * own) + y * own + index % own
    seqs = seq_len.shape[0]
    lengths = jnp.sum(
        jnp.where((local // SEQ_LEN)[:, None] == lax.broadcasted_iota(jnp.int32, (zs * own, seqs), 1), seq_len[None], 0),
        axis=1,
    )
    mask = (local % SEQ_LEN < lengths).astype(jnp.float32)
    loss = raw * mask
    domain = lax.dynamic_index_in_dim(domains.reshape(zs, ys, own), y, 1, False).reshape(-1)
    here = domain[None, :] == lax.broadcasted_iota(jnp.int32, (DOMAINS, zs * own), 0)
    sums = jnp.sum(jnp.where(here, loss[None], 0.0), axis=1)
    counts = jnp.sum(jnp.where(here, mask[None], 0.0), axis=1)
    part = jnp.concatenate([sums, counts])
    axes = ("x", "c", "y")
    whole = jnp.sum(to_all(part, axes, lax.axis_size(axes)), axis=0)
    mean = whole[:DOMAINS] / jnp.maximum(whole[DOMAINS:], 1.0)
    token_loss = lax.dynamic_index_in_dim(loss.reshape(zs, own), lax.axis_index("z"), 0, False)
    return token_loss, mean


def body(hidden, weight, targets, domains, seq_len):
    features = lax.all_gather(hidden, "y", axis=1, tiled=True)
    features = lax.all_gather(features, "z", axis=1, tiled=True)
    core = lax.axis_index("c")
    halves = gathered_weight(weight)
    columns = weight.shape[1]
    half = columns // 2
    first = lax.axis_index(VOCAB) * columns
    logits = [jnp.dot(features, w, preferred_element_type=jnp.float32) for w in halves]
    tops = jnp.maximum(jnp.max(logits[0], axis=1), jnp.max(logits[1], axis=1))
    total, picked = 0.0, 0.0
    for values, start in zip(logits, (core * half, (1 - core) * half)):
        ids = first + start + lax.broadcasted_iota(jnp.int32, values.shape, 1)
        total += jnp.sum(jnp.exp(values - tops[:, None]), axis=1)
        picked += jnp.sum(jnp.where(ids == targets[:, None], values, 0.0), axis=1)
    return tail(jnp.log(total) + tops, picked, domains, seq_len)


def solution(mesh):
    split = Mesh(mesh.devices.reshape(4, 2, 16, 4), ("x", "c", "z", "y"))
    placed = (P(TOK, VOCAB), P(TOK, VOCAB), P(TOK), P(TOK), P(TOK))
    return jax.shard_map(
        body, mesh=split, in_specs=placed, out_specs=(P((*TOK, *VOCAB)), P()), check_vma=False
    )
```

time: 208 us -> 176 us (0.85)
  waiting for transfers between devices: 106 us -> 42.7 us
  blocking collectives: 40.9 us -> 64.9 us
  starting transfers between devices: 25.2 us -> 34.1 us
  local copies, waits for them, and re-layouts: 6.62 us -> 3.85 us
    all_to_all x2, waiting for transfers between devices: 106 us -> 20.4 us  [the longest x1 14.1 us: tail(): got = lax.all_to_all(send.reshape(zs * ys, -1), VOCAB, 0, 0, tiled=True)]
    all_to_all x2 -> x1, blocking collectives: 27.9 us -> 51.9 us  [to_all(): lax.all_to_all(jnp.broadcast_to(array[None], (copies, *array.shape)), axi...]
    all_gather x1, waiting for transfers between devices: 0.01 us -> 20.7 us  [body(): features = lax.all_gather(features, 'z', axis=1, tiled=True)]
    ppermute x0 -> x2, starting transfers between devices: none -> 12.4 us  [the longest x1 9.23 us: gathered_weight(): other = lax.ppermute(give, 'c', SWAP)]
    broadcast_in_dim x3 -> x4, local copies, waits for them, and re-layouts: 5.55 us -> 1.06 us  [the longest x2 0.94 us: to_all(): jnp.broadcast_to(array[None], (copies, *array.shape))]
    all_to_all x2, starting transfers between devices: 25.2 us -> 21.7 us  [the longest x1 13.5 us: tail(): got = lax.all_to_all(send.reshape(zs * ys, -1), VOCAB, 0, 0, tiled=True)]
    dot_general x3 -> x2, matrix products: 11.5 us -> 12.7 us  [body(): jnp.dot(features, w, preferred_element_type=jnp.float32)]
  transfers between devices with their start and end apart: 3 -> 5, of which waited for: 2 -> 4; matrix products, arithmetic and copies ran while one was open for 3% -> 6% of each run, Pallas kernels for 0% -> 0%
where the time goes in v1:
time: 176 us
  blocking collectives  64.9 us (37%)
  waiting for transfers between devices  42.7 us (24%)
  starting transfers between devices  34.1 us (19%)
  between operations  14.3 us (8%)
  matrix products  12.7 us (7%)
  local copies, waits for them, and re-layouts  3.85 us (2%)
  other arithmetic  3.23 us (2%)
    all_to_all x1, blocking collectives, to_all(): lax.all_to_all(jnp.broadcast_to(array[None], (copies, *array.shape)), axi...  51.9 us
    all_gather x1, waiting for transfers between devices, body(): features = lax.all_gather(features, 'z', axis=1, tiled=True)  20.7 us
    all_to_all x1, waiting for transfers between devices, tail(): got = lax.all_to_all(send.reshape(zs * ys, -1), VOCAB, 0, 0, tiled=True)  14.1 us
    all_to_all x1, starting transfers between devices, tail(): got = lax.all_to_all(send.reshape(zs * ys, -1), VOCAB, 0, 0, tiled=True)  13.5 us
    all_gather x1, blocking collectives, body(): features = lax.all_gather(hidden, 'y', axis=1, tiled=True)  13 us
    dot_general x2, matrix products, body(): jnp.dot(features, w, preferred_element_type=jnp.float32)  12.7 us
    ppermute x1, starting transfers between devices, gathered_weight(): other = lax.ppermute(give, 'c', SWAP)  9.23 us
    all_to_all x1, starting transfers between devices, to_all(): lax.all_to_all(jnp.broadcast_to(array[None], (copies, *array.shape)), axi...  8.29 us
  transfers between devices with their start and end apart: 5, of which 4 were waited for; matrix products, arithmetic and copies ran while one was open for 6% of the time, Pallas kernels for 0%

profile of v1, /device:TPU:1, one launch (start us, length us, event | category | flops | bytes accessed | tf_op | source)
XLA Modules:
  0.0 175.8 jit_solution(721808868574512698)
XLA Ops:
  7.2 0.0 all-gather.2.cloned.1.call-start
  7.2 13.0 %all_gather.6 = bf16[768,256]{0,1:T(8,128)(2,1)} all-gather(bf16[768,64]{0,1:T(8,128)(2,1)} %param.5), channel_id=1, replica_groups=mesh['x'=4,'c'=2,'z'=16,'y'=4] {'y'}, dimensions={1}, use_global_device_ids=true | all-gather | bytes 491520 | tf_op jit(solution)/shard_map/all_gather | solution.py:68
  20.2 0.0 all-gather.2.cloned.1.call-update
  20.2 1.3 constant_dynamic-slice_fusion.6
  21.5 9.2 %collective-permute-start = (bf16[512,512]{1,0:T(8,128)(2,1)S(1)}, bf16[512,512]{1,0:T(8,128)(2,1)S(1)}, u32[]{:S(2)}, u32[]{:S(2)}) collective-permute-start(bf16[512,512]{1,0:T(8,128)(2,1)S(1)} %get-tuple-element.17), channel_id=1, source_target_pairs={{0,64},{64,0},{1,65},{65,1},{2,66},{66,2},{3,67},{67,3},{4,68},{68... | collective-permute-start | bytes 1572872 | tf_op jit(solution)/shard_map/ppermute | solution.py:25
  30.7 1.5 collective-permute-done
  32.3 0.5 maximum_select_fusion
  32.7 0.3 broadcast_in_dim.65
  33.1 0.0 copy-start.2
  33.1 51.9 %all_to_all.20 = bf16[4,1024,512]{2,1,0:T(8,128)(2,1)} all-to-all(bf16[4,1024,512]{2,1,0:T(8,128)(2,1)S(1)} %broadcast_in_dim.65), channel_id=1, replica_groups=mesh['x'=4,'c'=2,'z'=16,'y'=4] {'x'}, dimensions={0} | all-to-all | bytes 8388608 | tf_op jit(solution)/shard_map/all_to_all | solution.py:15
  85.0 3.1 %collective-permute-start.1 = (bf16[4096,512]{1,0:T(8,128)(2,1)}, bf16[4096,512]{1,0:T(8,128)(2,1)}, u32[]{:S(2)}, u32[]{:S(2)}) collective-permute-start(bf16[4096,512]{1,0:T(8,128)(2,1)} %bitcast), channel_id=1, source_target_pairs={{0,64},{64,0},{1,65},{65,1},{2,66},{66,2},{3,67},{67,3},{4,68},{68... | collective-permute-start | bytes 12582920 | tf_op jit(solution)/shard_map/ppermute | solution.py:31
  88.2 0.0 copy-done.2
  88.2 0.1 select_reduce_fusion.2
  88.3 20.7 %all-gather.2.cloned.1.call-done = bf16[768,4096]{0,1:T(8,128)(2,1)} async-done(((bf16[768,256]{0,1:T(8,128)(2,1)}), bf16[768,4096]{0,1:T(8,128)(2,1)}) %all-gather.2.cloned.1.call-update) | async-done | bytes 6291472 | tf_op jit(solution)/shard_map/all_gather | solution.py:69
  109.0 0.0 copy-start.3
  109.0 7.4 %fusion.28 = (f32[768]{0:T(1024)S(1)}, f32[512,768]{1,0:T(8,128)S(1)}) fusion(bf16[4096,512]{1,0:T(8,128)(2,1)} %bitcast, bf16[768,4096]{0,1:T(8,128)(2,1)} %all-gather.2.cloned.1.call-done), kind=kOutput, calls=%fused_computation.76 | convolution fusion | flops 3221617920 | bytes 12061696 | tf_op jit(solution)/shard_map/dot_general | solution.py:75
  116.5 0.0 copy-start
  116.5 0.0 collective-permute-done.1
  116.5 0.0 copy-done.3
  116.5 5.3 %fusion.29 = (f32[768]{0:T(1024)S(1)}, f32[512,768]{1,0:T(8,128)S(1)}) fusion(bf16[4096,512]{1,0:T(8,128)(2,1)} %collective-permute-done.1, bf16[768,4096]{0,1:T(8,128)(2,1)S(1)} %copy-done.3), kind=kOutput, calls=%fused_computation.77 | convolution fusion | flops 3221617920 | bytes 12061696 | tf_op jit(solution)/shard_map/dot_general | solution.py:75
  121.8 0.0 copy-start.1
  121.8 0.0 copy-done
  121.8 0.8 fusion.4
  122.6 0.1 add.194
  122.7 0.1 add.203
  122.9 0.1 broadcast_in_dim.67
  123.0 0.7 all_to_all.14
  123.8 13.5 %all-to-all-start.1 = ((f32[64,1,384]{2,1,0:T(1,128)}), f32[64,1,384]{2,1,0:T(1,128)S(1)}, u32[]{:S(2)}, u32[]{:S(2)}) async-start(f32[64,1,384]{2,1,0:T(1,128)} %all_to_all.14), calls=%async_computation.1 | async-start | bytes 196608 | tf_op jit(solution)/shard_map/all_to_all | solution.py:41
  137.2 0.0 copy-done.1
  137.3 0.1 reshape.234
  137.4 0.1 eq.44
  137.5 0.1 reduce_sum.93
  137.6 14.1 %all-to-all-done.1 = f32[64,1,384]{2,1,0:T(1,128)S(1)} async-done(((f32[64,1,384]{2,1,0:T(1,128)}), f32[64,1,384]{2,1,0:T(1,128)S(1)}, u32[]{:S(2)}, u32[]{:S(2)}) %all-to-all-start.1) | async-done | bytes 98336 | tf_op jit(solution)/shard_map/all_to_all | solution.py:41
  151.7 0.2 reduce.5
  152.0 0.1 reshape.233
  152.1 0.2 slice_reduce_fusion.1
  152.3 0.1 select_reduce_fusion.1
  152.4 0.1 pad_maximum_fusion
  152.5 0.6 broadcast_in_dim.72
  153.1 8.3 %all-to-all-start.2 = ((f32[32,1,128]{2,1,0:T(1,128)}), f32[32,1,128]{2,1,0:T(1,128)S(1)}, u32[]{:S(2)}, u32[]{:S(2)}) async-start(f32[32,1,128]{2,1,0:T(1,128)} %broadcast_in_dim.72), calls=%async_computation.2 | async-start | bytes 32768 | tf_op jit(solution)/shard_map/all_to_all | solution.py:15
  161.4 0.1 sub.59
  161.5 0.5 fusion.25
  162.1 6.3 %all-to-all-done.2 = f32[32,1,128]{2,1,0:T(1,128)S(1)} async-done(((f32[32,1,128]{2,1,0:T(1,128)}), f32[32,1,128]{2,1,0:T(1,128)S(1)}, u32[]{:S(2)}, u32[]{:S(2)}) %all-to-all-start.2) | async-done | bytes 16416 | tf_op jit(solution)/shard_map/all_to_all | solution.py:15
  168.4 0.6 maximum_divide_fusion
  (15 shorter events, 0.3 us)
Async XLA Ops:
  7.2 101.9 %all-gather.2.cloned.1.call-start = ((), (), s32[]{:S(2)}) async-start(), calls=%async_computation.3 | async-start | bytes 6684672 | tf_op jit(solution)/shard_map/all_gather | solution.py:69
  21.5 10.7 %collective-permute-start = (bf16[512,512]{1,0:T(8,128)(2,1)S(1)}, bf16[512,512]{1,0:T(8,128)(2,1)S(1)}, u32[]{:S(2)}, u32[]{:S(2)}) collective-permute-start(bf16[512,512]{1,0:T(8,128)(2,1)S(1)} %get-tuple-element.17), channel_id=1, source_target_pairs={{0,64},{64,0},{1,65},{65,1},{2,66},{66,2},{3,67},{67,3},{4,68},{68... | collective-permute-start | bytes 1572872 | tf_op jit(solution)/shard_map/ppermute | solution.py:25
  33.1 55.1 %copy-start.2 = (s32[6]{0:T(128)S(1)}, s32[6]{0:T(128)}, u32[]{:S(2)}) copy-start(s32[6]{0:T(128)} %param.9) | copy-start | bytes 76
  85.0 31.5 %collective-permute-start.1 = (bf16[4096,512]{1,0:T(8,128)(2,1)}, bf16[4096,512]{1,0:T(8,128)(2,1)}, u32[]{:S(2)}, u32[]{:S(2)}) collective-permute-start(bf16[4096,512]{1,0:T(8,128)(2,1)} %bitcast), channel_id=1, source_target_pairs={{0,64},{64,0},{1,65},{65,1},{2,66},{66,2},{3,67},{67,3},{4,68},{68... | collective-permute-start | bytes 12582920 | tf_op jit(solution)/shard_map/ppermute | solution.py:31
  109.0 7.4 %copy-start.3 = (bf16[768,4096]{0,1:T(8,128)(2,1)S(1)}, bf16[768,4096]{0,1:T(8,128)(2,1)}, u32[]{:S(2)}) copy-start(bf16[768,4096]{0,1:T(8,128)(2,1)} %all-gather.2.cloned.1.call-done) | copy-start | bytes 18874372
  116.5 5.4 %copy-start = (s32[768]{0:T(1024)S(1)}, s32[768]{0:T(1024)}, u32[]{:S(2)}) copy-start(s32[768]{0:T(1024)} %param.7) | copy-start | bytes 9220
  121.8 15.5 %copy-start.1 = (s32[768]{0:T(1024)S(1)}, s32[768]{0:T(1024)}, u32[]{:S(2)}) copy-start(s32[768]{0:T(1024)} %param.8) | copy-start | bytes 9220
  123.8 28.0 %all-to-all-start.1 = ((f32[64,1,384]{2,1,0:T(1,128)}), f32[64,1,384]{2,1,0:T(1,128)S(1)}, u32[]{:S(2)}, u32[]{:S(2)}) async-start(f32[64,1,384]{2,1,0:T(1,128)} %all_to_all.14), calls=%async_computation.1 | async-start | bytes 196608 | tf_op jit(solution)/shard_map/all_to_all | solution.py:41
  153.1 15.2 %all-to-all-start.2 = ((f32[32,1,128]{2,1,0:T(1,128)}), f32[32,1,128]{2,1,0:T(1,128)S(1)}, u32[]{:S(2)}, u32[]{:S(2)}) async-start(f32[32,1,128]{2,1,0:T(1,128)} %broadcast_in_dim.72), calls=%async_computation.2 | async-start | bytes 32768 | tf_op jit(solution)/shard_map/all_to_all | solution.py:15
Sparse Core Ops, SparseCore 0:
  20.3 88.6 all-gather.1

commit v2 on v1

--- a/solution.py
+++ b/solution.py
@@ -1,14 +1,21 @@
 import jax
 import jax.numpy as jnp
 from jax import lax
+from jax.experimental import pallas as pl
+from jax.experimental.pallas import tpu as pltpu
 from jax.sharding import Mesh
 from jax.sharding import PartitionSpec as P
+
 
 SEQ_LEN = 128
 DOMAINS = 64
 TOK = ("x", "c")
 VOCAB = ("z", "y")
 SWAP = [(0, 1), (1, 0)]
+BLOCK = 256
+TILE = 256
+BATCHES = ((1, 2, 3), (4, 5, 6), (7,))
+GROUPS = ((range(0, 7), (0,)), ((7, 8), (1, 2)))
 
 
 def to_all(array, axis, copies):
@@ -27,8 +34,10 @@
         core == 0, jnp.concatenate([keep, other], 0), jnp.concatenate([other, keep], 0)
     )
     chips = lax.axis_size("x")
-    own = to_all(rows, "x", chips).reshape(chips * rows.shape[0], half)
-    return own, lax.ppermute(own, "c", SWAP)
+    own = to_all(rows, "x", chips)
+    own = own.reshape(chips * rows.shape[0], half)
+    swapped = lax.ppermute(own, "c", SWAP)
+    return own, swapped
 
 
 def tail(lse, picked, domains, seq_len):
@@ -64,15 +73,101 @@
     return token_loss, mean
 
 
-def body(hidden, weight, targets, domains, seq_len):
-    features = lax.all_gather(hidden, "y", axis=1, tiled=True)
-    features = lax.all_gather(features, "z", axis=1, tiled=True)
-    core = lax.axis_index("c")
+def product_kernel(stacks, first):
+    def kernel(*refs):
+        which, given, rest = refs[0], refs[1 : 1 + len(stacks)], refs[1 + len(stacks) :]
+        blocks = [
+            (ref,) if n is None else (ref, k)
+            for ref, n in zip(given, stacks)
+            for k in range(n or 1)
+        ]
+        count, tokens = len(blocks), given[0].shape[-2]
+        halves, rest = rest[:2], rest[2:]
+        if not first:
+            before, rest = rest[:2], rest[2:]
+        outs, (rows, sems) = rest[:2], rest[2:]
+        copies = []
+        for k in range(count):
+            for h in range(2):
+                copy = pltpu.make_async_copy(
+                    halves[h].at[pl.ds(which[k] * BLOCK, BLOCK)], rows.at[k, h], sems.at[k, h]
+                )
+                copy.start()
+                copies.append(copy)
+        for copy in copies:
+            copy.wait()
+        for at in range(0, tokens, TILE):
+            for h in range(2):
+                total = None if first else before[h][at : at + TILE]
+                for k in range(count):
+                    ref, *at_k = blocks[k]
+                    block = ref[(*at_k, slice(at, at + TILE))]
+                    part = jnp.dot(block, rows[k, h], preferred_element_type=jnp.float32)
+                    total = part if total is None else total + part
+                outs[h][at : at + TILE] = total
+
+    return kernel
+
+
+def product(which, blocks, halves, before=None):
+    tokens, depth = blocks[0].shape[-2:]
+    half, arrays = halves[0].shape[1], len(blocks)
+    stacks = [b.shape[0] if b.ndim == 3 else None for b in blocks]
+    count = sum(n or 1 for n in stacks)
+    vmem = pl.BlockSpec(memory_space=pltpu.VMEM)
+    anywhere = pl.BlockSpec(memory_space=pl.ANY)
+    shape = jax.ShapeDtypeStruct((tokens, half), jnp.float32)
+    return pl.pallas_call(
+        product_kernel(stacks, before is None),
+        in_specs=[pl.BlockSpec(memory_space=pltpu.SMEM)]
+        + [vmem] * arrays
+        + [anywhere] * 2
+        + ([] if before is None else [vmem] * 2),
+        out_specs=[vmem, vmem],
+        out_shape=[shape, shape],
+        scratch_shapes=[
+            pltpu.VMEM((count, 2, depth, half), jnp.bfloat16),
+            pltpu.SemaphoreType.DMA((count, 2)),
+        ],
+        input_output_aliases={} if before is None else {3 + arrays: 0, 4 + arrays: 1},
+        cost_estimate=pl.CostEstimate(
+            flops=2 * count * tokens * depth * half * 2,
+            bytes_accessed=count * depth * (tokens + 2 * half) * 2,
+            transcendentals=0,
+        ),
+    )(which, *blocks, *halves, *(before or ()))
+
+
+def along_z(array):
+    zs = lax.axis_size("z")
+    pairs = [(c * zs + z, c * zs + (z + (1 - 2 * c)) % zs) for c in range(2) for z in range(zs)]
+    return lax.ppermute(array, ("c", "z"), pairs)
+
+
+def loss(hidden, weight, targets, domains, seq_len):
+    core, z = lax.axis_index("c"), lax.axis_index("z")
+    zs, ys = lax.axis_size("z"), lax.axis_size("y")
     halves = gathered_weight(weight)
+    mine = to_all(hidden.T, "y", ys).reshape(BLOCK, -1).T
+    rings = zs // 2
+    own, other = [mine], [lax.ppermute(mine, "c", SWAP)]
+    for r in range(1, rings + 1):
+        own.append(along_z(own[-1]))
+        if r < rings:
+            other.append(along_z(other[-1]))
+    swapped = []
+    for some in BATCHES:
+        swapped.append(lax.ppermute(jnp.stack([other[r] for r in some]), "c", SWAP))
+    step = 2 * core - 1
+    logits = None
+    for rounds, batches in GROUPS:
+        away = [r for r in rounds] + [-r for k in batches for r in BATCHES[k]]
+        which = lax.rem(z + step * jnp.array(away, jnp.int32) + zs, zs)
+        blocks = [own[r] for r in rounds] + [swapped[k] for k in batches]
+        logits = product(which, blocks, halves, logits)
     columns = weight.shape[1]
     half = columns // 2
     first = lax.axis_index(VOCAB) * columns
-    logits = [jnp.dot(features, w, preferred_element_type=jnp.float32) for w in halves]
     tops = jnp.maximum(jnp.max(logits[0], axis=1), jnp.max(logits[1], axis=1))
     total, picked = 0.0, 0.0
     for values, start in zip(logits, (core * half, (1 - core) * half)):
@@ -86,5 +181,5 @@
     split = Mesh(mesh.devices.reshape(4, 2, 16, 4), ("x", "c", "z", "y"))
     placed = (P(TOK, VOCAB), P(TOK, VOCAB), P(TOK), P(TOK), P(TOK))
     return jax.shard_map(
-        body, mesh=split, in_specs=placed, out_specs=(P((*TOK, *VOCAB)), P()), check_vma=False
+        loss, mesh=split, in_specs=placed, out_specs=(P((*TOK, *VOCAB)), P()), check_vma=False
     )

time: 176 us -> 239 us (1.36)
  starting transfers between devices: 34.1 us -> 113 us
  Pallas kernels: 0 us -> 18.6 us
  waiting for transfers between devices: 42.7 us -> 29.7 us
  between operations: 14.3 us -> 1.31 us
  matrix products: 12.7 us -> 0 us
  other arithmetic: 3.23 us -> 6.68 us
  blocking collectives: 64.9 us -> 62.3 us
  local copies, waits for them, and re-layouts: 3.85 us -> 6.25 us
    ppermute x1 -> x20, starting transfers between devices: 3.13 us -> 88 us  [the longest x15 69.1 us: along_z(): return lax.ppermute(array, ('c', 'z'), pairs)]
    all_gather x1 -> x0, waiting for transfers between devices: 20.7 us -> none  [body(): features = lax.all_gather(features, 'z', axis=1, tiled=True)]
    pallas_call x0 -> x2, Pallas kernels: none -> 18.6 us  [product(): pl.pallas_call(product_kernel(stacks, before is None), in_specs=[pl.Block...]
    all_gather x1 -> x0, blocking collectives: 13 us -> none  [body(): features = lax.all_gather(hidden, 'y', axis=1, tiled=True)]
    dot_general x2 -> x0, matrix products: 12.7 us -> none  [body(): jnp.dot(features, w, preferred_element_type=jnp.float32)]
    all_to_all x1 -> x2, blocking collectives: 51.9 us -> 62.3 us  [to_all(): lax.all_to_all(jnp.broadcast_to(array[None], (copies, *array.shape)), axi...]
    ppermute x1 -> x20, waiting for transfers between devices: 0.01 us -> 7.62 us  [the longest x15 6.28 us: along_z(): return lax.ppermute(array, ('c', 'z'), pairs)]
    all_to_all x1, starting transfers between devices: 13.5 us -> 10.2 us  [tail(): got = lax.all_to_all(send.reshape(zs * ys, -1), VOCAB, 0, 0, tiled=True)]
  transfers between devices with their start and end apart: 5 -> 23, of which waited for: 4 -> 11; matrix products, arithmetic and copies ran while one was open for 6% -> 1% of each run, Pallas kernels for 0% -> 4%
where the time goes in v2:
time: 239 us; the launch traced here: 238 us
  starting transfers between devices  113 us (47%)
  blocking collectives  62.3 us (26%)
  waiting for transfers between devices  29.7 us (12%)
  Pallas kernels  18.6 us (8%)
  other arithmetic  6.68 us (3%)
  local copies, waits for them, and re-layouts  6.25 us (3%)
    ppermute x15, starting transfers between devices, along_z(): return lax.ppermute(array, ('c', 'z'), pairs)  69.1 us
    all_to_all x2, blocking collectives, to_all(): lax.all_to_all(jnp.broadcast_to(array[None], (copies, *array.shape)), axi...  62.3 us
    pallas_call x2, Pallas kernels, product(): pl.pallas_call(product_kernel(stacks, before is None), in_specs=[pl.Block...  18.6 us
    all_to_all x1, waiting for transfers between devices, tail(): got = lax.all_to_all(send.reshape(zs * ys, -1), VOCAB, 0, 0, tiled=True)  14.3 us
    ppermute x3, starting transfers between devices, loss(): swapped.append(lax.ppermute(jnp.stack([other[r] for r in some]), 'c', SWAP))  12.6 us
    all_to_all x1, starting transfers between devices, tail(): got = lax.all_to_all(send.reshape(zs * ys, -1), VOCAB, 0, 0, tiled=True)  10.2 us
    ppermute x1, starting transfers between devices, gathered_weight(): other = lax.ppermute(give, 'c', SWAP)  8.75 us
    all_to_all x1, waiting for transfers between devices, to_all(): lax.all_to_all(jnp.broadcast_to(array[None], (copies, *array.shape)), axi...  6.34 us
  transfers between devices with their start and end apart: 23, of which 11 were waited for; matrix products, arithmetic and copies ran while one was open for 1% of the time, Pallas kernels for 4%

profile of v2, /device:TPU:1, one launch (start us, length us, event | category | flops | bytes accessed | tf_op | source)
XLA Modules:
  0.0 237.9 jit_solution(6973737536105745675)
XLA Ops:
  0.6 1.3 constant_dynamic-slice_fusion.6
  1.9 8.7 %collective-permute-start.18 = (bf16[512,512]{1,0:T(8,128)(2,1)S(1)}, bf16[512,512]{1,0:T(8,128)(2,1)S(1)}, u32[]{:S(2)}, u32[]{:S(2)}) collective-permute-start(bf16[512,512]{1,0:T(8,128)(2,1)S(1)} %get-tuple-element.25), channel_id=1, source_target_pairs={{0,64},{64,0},{1,65},{65,1},{2,66},{66,2},{3,67},{67,3},{4,68},{68... | collective-permute-start | bytes 1572872 | tf_op jit(solution)/shard_map/ppermute | solution.py:32
  10.7 1.5 collective-permute-done.18
  12.2 0.5 maximum_select_fusion
  12.6 0.3 broadcast_in_dim.72
  13.0 52.1 %all_to_all.25 = bf16[4,1024,512]{2,1,0:T(8,128)(2,1)} all-to-all(bf16[4,1024,512]{2,1,0:T(8,128)(2,1)S(1)} %broadcast_in_dim.72), channel_id=1, replica_groups=mesh['x'=4,'c'=2,'z'=16,'y'=4] {'x'}, dimensions={0} | all-to-all | bytes 8388608 | tf_op jit(solution)/shard_map/all_to_all | solution.py:22
  65.1 3.1 %collective-permute-start.19 = (bf16[4096,512]{1,0:T(8,128)(2,1)}, bf16[4096,512]{1,0:T(8,128)(2,1)}, u32[]{:S(2)}, u32[]{:S(2)}) collective-permute-start(bf16[4096,512]{1,0:T(8,128)(2,1)} %bitcast.7.refs_9_.refs_5_), channel_id=1, source_target_pairs={{0,64},{64,0},{1,65},{65,1},{2,66},{66,2},{3,67},{67,3},{4,68},{68... | collective-permute-start | bytes 12582920 | tf_op jit(solution)/shard_map/ppermute | solution.py:39
  68.2 10.3 %all_to_all.26 = bf16[4,64,768]{2,1,0:T(8,128)(2,1)S(1)} all-to-all(bf16[4,64,768]{2,1,0:T(8,128)(2,1)S(1)} %broadcast_in_dim.71), channel_id=1, replica_groups=mesh['x'=4,'c'=2,'z'=16,'y'=4] {'y'}, dimensions={0} | all-to-all | bytes 786432 | tf_op jit(solution)/shard_map/all_to_all | solution.py:22
  78.5 0.2 copy.18
  78.7 3.1 %collective-permute-start.8 = (bf16[768,256]{1,0:T(8,128)(2,1)S(1)}, bf16[768,256]{1,0:T(8,128)(2,1)S(1)}, u32[]{:S(2)}, u32[]{:S(2)}) collective-permute-start(bf16[768,256]{1,0:T(8,128)(2,1)S(1)} %bitcast.31), channel_id=1, source_target_pairs={{0,64},{64,0},{1,65},{65,1},{2,66},{66,2},{3,67},{67,3},{4,68},{68... | collective-permute-start | bytes 1179656 | tf_op jit(solution)/shard_map/ppermute | solution.py:153
  81.8 1.3 collective-permute-done.8
  83.1 7.9 %collective-permute-start.9 = (bf16[768,256]{1,0:T(8,128)(2,1)S(1)}, bf16[768,256]{1,0:T(8,128)(2,1)S(1)}, u32[]{:S(2)}, u32[]{:S(2)}) collective-permute-start(bf16[768,256]{1,0:T(8,128)(2,1)S(1)} %collective-permute-done.8), channel_id=1, source_target_pairs={{0,4},{4,8},{8,12},{12,16},{16,20},{20,24},{24,28},{28,32},{32,36}... | collective-permute-start | bytes 1179656 | tf_op jit(solution)/shard_map/ppermute | solution.py:144
  91.0 2.6 %collective-permute-start = (bf16[768,256]{1,0:T(8,128)(2,1)S(1)}, bf16[768,256]{1,0:T(8,128)(2,1)S(1)}, u32[]{:S(2)}, u32[]{:S(2)}) collective-permute-start(bf16[768,256]{1,0:T(8,128)(2,1)S(1)} %bitcast.32), channel_id=1, source_target_pairs={{0,4},{4,8},{8,12},{12,16},{16,20},{20,24},{24,28},{28,32},{32,36}... | collective-permute-start | bytes 1179656 | tf_op jit(solution)/shard_map/ppermute | solution.py:144
  93.6 2.1 collective-permute-done.9
  95.7 5.0 %collective-permute-start.10 = (bf16[768,256]{1,0:T(8,128)(2,1)S(1)}, bf16[768,256]{1,0:T(8,128)(2,1)S(1)}, u32[]{:S(2)}, u32[]{:S(2)}) collective-permute-start(bf16[768,256]{1,0:T(8,128)(2,1)S(1)} %collective-permute-done.9), channel_id=1, source_target_pairs={{0,4},{4,8},{8,12},{12,16},{16,20},{20,24},{24,28},{28,32},{32,36}... | collective-permute-start | bytes 1179656 | tf_op jit(solution)/shard_map/ppermute | solution.py:144
  100.7 4.2 %collective-permute-start.1 = (bf16[768,256]{1,0:T(8,128)(2,1)S(1)}, bf16[768,256]{1,0:T(8,128)(2,1)S(1)}, u32[]{:S(2)}, u32[]{:S(2)}) collective-permute-start(bf16[768,256]{1,0:T(8,128)(2,1)S(1)} %collective-permute-done.refs_2_), channel_id=1, source_target_pairs={{0,4},{4,8},{8,12},{12,16},{16,20},{20,24},{24,28},{28,32},{32,36}... | collective-permute-start | bytes 1179656 | tf_op jit(solution)/shard_map/ppermute | solution.py:144
  104.9 0.5 collective-permute-done.10
  105.4 5.0 %collective-permute-start.11 = (bf16[768,256]{1,0:T(8,128)(2,1)S(1)}, bf16[768,256]{1,0:T(8,128)(2,1)S(1)}, u32[]{:S(2)}, u32[]{:S(2)}) collective-permute-start(bf16[768,256]{1,0:T(8,128)(2,1)S(1)} %collective-permute-done.10), channel_id=1, source_target_pairs={{0,4},{4,8},{8,12},{12,16},{16,20},{20,24},{24,28},{28,32},{32,36}... | collective-permute-start | bytes 1179656 | tf_op jit(solution)/shard_map/ppermute | solution.py:144
  110.4 4.2 %collective-permute-start.2 = (bf16[768,256]{1,0:T(8,128)(2,1)S(1)}, bf16[768,256]{1,0:T(8,128)(2,1)S(1)}, u32[]{:S(2)}, u32[]{:S(2)}) collective-permute-start(bf16[768,256]{1,0:T(8,128)(2,1)S(1)} %collective-permute-done.1.refs_3_), channel_id=1, source_target_pairs={{0,4},{4,8},{8,12},{12,16},{16,20},{20,24},{24,28},{28,32},{32,36}... | collective-permute-start | bytes 1179656 | tf_op jit(solution)/shard_map/ppermute | solution.py:144
  114.6 0.5 collective-permute-done.11
  115.1 5.0 %collective-permute-start.12 = (bf16[768,256]{1,0:T(8,128)(2,1)S(1)}, bf16[768,256]{1,0:T(8,128)(2,1)S(1)}, u32[]{:S(2)}, u32[]{:S(2)}) collective-permute-start(bf16[768,256]{1,0:T(8,128)(2,1)S(1)} %collective-permute-done.11), channel_id=1, source_target_pairs={{0,4},{4,8},{8,12},{12,16},{16,20},{20,24},{24,28},{28,32},{32,36}... | collective-permute-start | bytes 1179656 | tf_op jit(solution)/shard_map/ppermute | solution.py:144
  120.1 4.2 %collective-permute-start.3 = (bf16[768,256]{1,0:T(8,128)(2,1)S(1)}, bf16[768,256]{1,0:T(8,128)(2,1)S(1)}, u32[]{:S(2)}, u32[]{:S(2)}) collective-permute-start(bf16[768,256]{1,0:T(8,128)(2,1)S(1)} %collective-permute-done.2.refs_4_), channel_id=1, source_target_pairs={{0,4},{4,8},{8,12},{12,16},{16,20},{20,24},{24,28},{28,32},{32,36}... | collective-permute-start | bytes 1179656 | tf_op jit(solution)/shard_map/ppermute | solution.py:144
  124.3 0.5 collective-permute-done.12
  124.8 5.0 %collective-permute-start.13 = (bf16[768,256]{1,0:T(8,128)(2,1)S(1)}, bf16[768,256]{1,0:T(8,128)(2,1)S(1)}, u32[]{:S(2)}, u32[]{:S(2)}) collective-permute-start(bf16[768,256]{1,0:T(8,128)(2,1)S(1)} %collective-permute-done.12), channel_id=1, source_target_pairs={{0,4},{4,8},{8,12},{12,16},{16,20},{20,24},{24,28},{28,32},{32,36}... | collective-permute-start | bytes 1179656 | tf_op jit(solution)/shard_map/ppermute | solution.py:144
  129.9 4.2 %collective-permute-start.4 = (bf16[768,256]{1,0:T(8,128)(2,1)S(1)}, bf16[768,256]{1,0:T(8,128)(2,1)}, u32[]{:S(2)}, u32[]{:S(2)}) collective-permute-start(bf16[768,256]{1,0:T(8,128)(2,1)S(1)} %collective-permute-done.3.refs_5_), channel_id=1, source_target_pairs={{0,4},{4,8},{8,12},{12,16},{16,20},{20,24},{24,28},{28,32},{32,36}... | collective-permute-start | bytes 1179656 | tf_op jit(solution)/shard_map/ppermute | solution.py:144
  134.1 0.5 collective-permute-done.13
  134.5 5.0 %collective-permute-start.14 = (bf16[768,256]{1,0:T(8,128)(2,1)S(1)}, bf16[768,256]{1,0:T(8,128)(2,1)S(1)}, u32[]{:S(2)}, u32[]{:S(2)}) collective-permute-start(bf16[768,256]{1,0:T(8,128)(2,1)S(1)} %collective-permute-done.13), channel_id=1, source_target_pairs={{0,4},{4,8},{8,12},{12,16},{16,20},{20,24},{24,28},{28,32},{32,36}... | collective-permute-start | bytes 1179656 | tf_op jit(solution)/shard_map/ppermute | solution.py:144
  139.6 0.1 pad_maximum_fusion.1
  139.8 5.2 %collective-permute-start.20 = (bf16[3,768,256]{2,1,0:T(8,128)(2,1)S(1)}, bf16[3,768,256]{2,1,0:T(8,128)(2,1)}, u32[]{:S(2)}, u32[]{:S(2)}) collective-permute-start(bf16[3,768,256]{2,1,0:T(8,128)(2,1)S(1)} %pad_maximum_fusion.1), channel_id=1, source_target_pairs={{0,64},{64,0},{1,65},{65,1},{2,66},{66,2},{3,67},{67,3},{4,68},{68... | collective-permute-start | bytes 3538952 | tf_op jit(solution)/shard_map/ppermute | solution.py:160
  145.0 4.9 %collective-permute-start.5 = (bf16[768,256]{1,0:T(8,128)(2,1)}, bf16[768,256]{1,0:T(8,128)(2,1)}, u32[]{:S(2)}, u32[]{:S(2)}) collective-permute-start(bf16[768,256]{1,0:T(8,128)(2,1)} %collective-permute-done.4.refs_6_), channel_id=1, source_target_pairs={{0,4},{4,8},{8,12},{12,16},{16,20},{20,24},{24,28},{28,32},{32,36}... | collective-permute-start | bytes 1179656 | tf_op jit(solution)/shard_map/ppermute | solution.py:144
  149.9 0.7 copy-done.3
  150.6 0.1 pad_maximum_fusion
  150.8 3.7 %collective-permute-start.15 = (bf16[3,768,256]{2,1,0:T(8,128)(2,1)S(1)}, bf16[3,768,256]{2,1,0:T(8,128)(2,1)S(1)}, u32[]{:S(2)}, u32[]{:S(2)}) collective-permute-start(bf16[3,768,256]{2,1,0:T(8,128)(2,1)S(1)} %pad_maximum_fusion), channel_id=1, source_target_pairs={{0,64},{64,0},{1,65},{65,1},{2,66},{66,2},{3,67},{67,3},{4,68},{68... | collective-permute-start | bytes 3538952 | tf_op jit(solution)/shard_map/ppermute | solution.py:160
  154.6 0.3 collective-permute-done.5.refs_7_
  154.9 5.0 %collective-permute-start.6 = (bf16[768,256]{1,0:T(8,128)(2,1)}, bf16[768,256]{1,0:T(8,128)(2,1)}, u32[]{:S(2)}, u32[]{:S(2)}) collective-permute-start(bf16[768,256]{1,0:T(8,128)(2,1)} %collective-permute-done.5.refs_7_), channel_id=1, source_target_pairs={{0,4},{4,8},{8,12},{12,16},{16,20},{20,24},{24,28},{28,32},{32,36}... | collective-permute-start | bytes 1179656 | tf_op jit(solution)/shard_map/ppermute | solution.py:144
  159.9 1.9 collective-permute-start.16
  161.9 0.5 compare_select_fusion.refs_0_
  162.4 0.5 compare_select_fusion.2.refs_0_
  162.9 2.0 collective-permute-done.6.refs_1_
  164.9 5.0 %collective-permute-start.7 = (bf16[768,256]{1,0:T(8,128)(2,1)}, bf16[768,256]{1,0:T(8,128)(2,1)}, u32[]{:S(2)}, u32[]{:S(2)}) collective-permute-start(bf16[768,256]{1,0:T(8,128)(2,1)} %collective-permute-done.6.refs_1_), channel_id=1, source_target_pairs={{0,4},{4,8},{8,12},{12,16},{16,20},{20,24},{24,28},{28,32},{32,36}... | collective-permute-start | bytes 1179656 | tf_op jit(solution)/shard_map/ppermute | solution.py:144
  170.0 3.7 %collective-permute-start.17 = (bf16[1,768,256]{2,1,0:T(8,128)(2,1)}, bf16[1,768,256]{2,1,0:T(8,128)(2,1)}, u32[]{:S(2)}, u32[]{:S(2)}) collective-permute-start(bf16[1,768,256]{2,1,0:T(8,128)(2,1)} %bitcast.6), channel_id=1, source_target_pairs={{0,64},{64,0},{1,65},{65,1},{2,66},{66,2},{3,67},{67,3},{4,68},{68... | collective-permute-start | bytes 1179656 | tf_op jit(solution)/shard_map/ppermute | solution.py:160
  173.7 10.1 %shard_map.86 = (f32[768,512]{1,0:T(8,128)}, f32[768,512]{1,0:T(8,128)}) custom-call(s32[10]{0:T(128)} %compare_select_fusion.refs_0_, bf16[768,256]{1,0:T(8,128)(2,1)} %bitcast.33, bf16[768,256]{1,0:T(8,128)(2,1)} %copy-done.11, bf16[768,256]{1,0:T(8,128)(2,1)} %copy-done.12, bf16[768,256]{1,0:T(8,128)(2,1)} %copy-done.13, bf16[768,256]{1,0:T(8,128)(2,1)} %copy-done.14, ...), custom_call_target="tpu_custom_call" | custom-call | flops 4026531840 | bytes 9175040 | tf_op jit(solution)/shard_map/pallas_call | solution.py:120
  183.8 1.0 copy-done.2
  184.9 8.5 %shard_map.87 = (f32[768,512]{1,0:T(8,128)}, f32[768,512]{1,0:T(8,128)}) custom-call(s32[6]{0:T(128)} %compare_select_fusion.2.refs_0_, bf16[768,256]{1,0:T(8,128)(2,1)} %collective-permute-done.6.refs_1_, bf16[768,256]{1,0:T(8,128)(2,1)} %collective-permute-done.7.refs_2_, ...), custom_call_target="tpu_custom_call", output_to_operand_aliasing={{0}: (7, {}), {1}: (8, {})} | custom-call | flops 2415919104 | bytes 5505024 | tf_op jit(solution)/shard_map/pallas_call | solution.py:120
  193.4 1.7 reduce_max.27
  195.1 0.1 copy-done.1
  195.2 0.2 reduce_max.28
  195.4 0.3 copy-done
  195.7 1.0 exponential_reduce_fusion.1
  196.7 0.1 add.219
  196.9 0.1 add.228
  197.2 0.7 all_to_all.18
  197.9 10.2 %all-to-all-start.2 = ((f32[64,1,384]{2,1,0:T(1,128)}), f32[64,1,384]{2,1,0:T(1,128)S(1)}, u32[]{:S(2)}, u32[]{:S(2)}) async-start(f32[64,1,384]{2,1,0:T(1,128)} %all_to_all.18), calls=%async_computation.2 | async-start | bytes 196608 | tf_op jit(solution)/shard_map/all_to_all | solution.py:50
  208.1 0.1 reshape.239
  208.5 14.3 %all-to-all-done.2 = f32[64,1,384]{2,1,0:T(1,128)S(1)} async-done(((f32[64,1,384]{2,1,0:T(1,128)}), f32[64,1,384]{2,1,0:T(1,128)S(1)}, u32[]{:S(2)}, u32[]{:S(2)}) %all-to-all-start.2) | async-done | bytes 98336 | tf_op jit(solution)/shard_map/all_to_all | solution.py:50
  222.8 0.2 reduce.3
  223.0 0.1 reshape.238
  223.2 0.2 slice_reduce_fusion.1
  223.4 0.1 select_reduce_fusion.3
  223.6 0.6 broadcast_in_dim.79
  224.2 6.2 %all-to-all-start.3 = ((f32[32,1,128]{2,1,0:T(1,128)}), f32[32,1,128]{2,1,0:T(1,128)S(1)}, u32[]{:S(2)}, u32[]{:S(2)}) async-start(f32[32,1,128]{2,1,0:T(1,128)} %broadcast_in_dim.79), calls=%async_computation.3 | async-start | bytes 32768 | tf_op jit(solution)/shard_map/all_to_all | solution.py:22
  230.5 0.5 fusion.21
  231.0 6.3 %all-to-all-done.3 = f32[32,1,128]{2,1,0:T(1,128)S(1)} async-done(((f32[32,1,128]{2,1,0:T(1,128)}), f32[32,1,128]{2,1,0:T(1,128)S(1)}, u32[]{:S(2)}, u32[]{:S(2)}) %all-to-all-start.3) | async-done | bytes 16416 | tf_op jit(solution)/shard_map/all_to_all | solution.py:22
  237.3 0.6 maximum_divide_fusion
  (60 shorter events, 0.9 us)
Async XLA Ops:
  1.9 10.3 %collective-permute-start.18 = (bf16[512,512]{1,0:T(8,128)(2,1)S(1)}, bf16[512,512]{1,0:T(8,128)(2,1)S(1)}, u32[]{:S(2)}, u32[]{:S(2)}) collective-permute-start(bf16[512,512]{1,0:T(8,128)(2,1)S(1)} %get-tuple-element.25), channel_id=1, source_target_pairs={{0,64},{64,0},{1,65},{65,1},{2,66},{66,2},{3,67},{67,3},{4,68},{68... | collective-permute-start | bytes 1572872 | tf_op jit(solution)/shard_map/ppermute | solution.py:32
  13.0 55.2 %copy-start.5 = (bf16[768,64]{0,1:T(8,128)(2,1)S(1)}, bf16[768,64]{0,1:T(8,128)(2,1)}, u32[]{:S(2)}) copy-start(bf16[768,64]{0,1:T(8,128)(2,1)} %param.7) | copy-start | bytes 294916
  65.1 108.6 %collective-permute-start.19 = (bf16[4096,512]{1,0:T(8,128)(2,1)}, bf16[4096,512]{1,0:T(8,128)(2,1)}, u32[]{:S(2)}, u32[]{:S(2)}) collective-permute-start(bf16[4096,512]{1,0:T(8,128)(2,1)} %bitcast.7.refs_9_.refs_5_), channel_id=1, source_target_pairs={{0,64},{64,0},{1,65},{65,1},{2,66},{66,2},{3,67},{67,3},{4,68},{68... | collective-permute-start | bytes 12582920 | tf_op jit(solution)/shard_map/ppermute | solution.py:39
  78.7 60.9 %copy-start.4 = (bf16[256,768]{0,1:T(8,128)(2,1)}, bf16[256,768]{0,1:T(8,128)(2,1)S(1)}, u32[]{:S(2)}) copy-start(bf16[256,768]{0,1:T(8,128)(2,1)S(1)} %copy.18) | copy-start | bytes 1179652
  78.7 4.4 %collective-permute-start.8 = (bf16[768,256]{1,0:T(8,128)(2,1)S(1)}, bf16[768,256]{1,0:T(8,128)(2,1)S(1)}, u32[]{:S(2)}, u32[]{:S(2)}) collective-permute-start(bf16[768,256]{1,0:T(8,128)(2,1)S(1)} %bitcast.31), channel_id=1, source_target_pairs={{0,64},{64,0},{1,65},{65,1},{2,66},{66,2},{3,67},{67,3},{4,68},{68... | collective-permute-start | bytes 1179656 | tf_op jit(solution)/shard_map/ppermute | solution.py:153
  83.1 12.6 %collective-permute-start.9 = (bf16[768,256]{1,0:T(8,128)(2,1)S(1)}, bf16[768,256]{1,0:T(8,128)(2,1)S(1)}, u32[]{:S(2)}, u32[]{:S(2)}) collective-permute-start(bf16[768,256]{1,0:T(8,128)(2,1)S(1)} %collective-permute-done.8), channel_id=1, source_target_pairs={{0,4},{4,8},{8,12},{12,16},{16,20},{20,24},{24,28},{28,32},{32,36}... | collective-permute-start | bytes 1179656 | tf_op jit(solution)/shard_map/ppermute | solution.py:144
  91.0 9.7 %collective-permute-start = (bf16[768,256]{1,0:T(8,128)(2,1)S(1)}, bf16[768,256]{1,0:T(8,128)(2,1)S(1)}, u32[]{:S(2)}, u32[]{:S(2)}) collective-permute-start(bf16[768,256]{1,0:T(8,128)(2,1)S(1)} %bitcast.32), channel_id=1, source_target_pairs={{0,4},{4,8},{8,12},{12,16},{16,20},{20,24},{24,28},{28,32},{32,36}... | collective-permute-start | bytes 1179656 | tf_op jit(solution)/shard_map/ppermute | solution.py:144
  95.7 9.7 %collective-permute-start.10 = (bf16[768,256]{1,0:T(8,128)(2,1)S(1)}, bf16[768,256]{1,0:T(8,128)(2,1)S(1)}, u32[]{:S(2)}, u32[]{:S(2)}) collective-permute-start(bf16[768,256]{1,0:T(8,128)(2,1)S(1)} %collective-permute-done.9), channel_id=1, source_target_pairs={{0,4},{4,8},{8,12},{12,16},{16,20},{20,24},{24,28},{28,32},{32,36}... | collective-permute-start | bytes 1179656 | tf_op jit(solution)/shard_map/ppermute | solution.py:144
  100.7 38.9 %copy-start.11 = (bf16[768,256]{1,0:T(8,128)(2,1)}, bf16[768,256]{1,0:T(8,128)(2,1)S(1)}, u32[]{:S(2)}) copy-start(bf16[768,256]{1,0:T(8,128)(2,1)S(1)} %collective-permute-done.refs_2_) | copy-start | bytes 1179652
  100.7 9.7 %collective-permute-start.1 = (bf16[768,256]{1,0:T(8,128)(2,1)S(1)}, bf16[768,256]{1,0:T(8,128)(2,1)S(1)}, u32[]{:S(2)}, u32[]{:S(2)}) collective-permute-start(bf16[768,256]{1,0:T(8,128)(2,1)S(1)} %collective-permute-done.refs_2_), channel_id=1, source_target_pairs={{0,4},{4,8},{8,12},{12,16},{16,20},{20,24},{24,28},{28,32},{32,36}... | collective-permute-start | bytes 1179656 | tf_op jit(solution)/shard_map/ppermute | solution.py:144
  105.4 9.7 %collective-permute-start.11 = (bf16[768,256]{1,0:T(8,128)(2,1)S(1)}, bf16[768,256]{1,0:T(8,128)(2,1)S(1)}, u32[]{:S(2)}, u32[]{:S(2)}) collective-permute-start(bf16[768,256]{1,0:T(8,128)(2,1)S(1)} %collective-permute-done.10), channel_id=1, source_target_pairs={{0,4},{4,8},{8,12},{12,16},{16,20},{20,24},{24,28},{28,32},{32,36}... | collective-permute-start | bytes 1179656 | tf_op jit(solution)/shard_map/ppermute | solution.py:144
  110.4 29.2 %copy-start.12 = (bf16[768,256]{1,0:T(8,128)(2,1)}, bf16[768,256]{1,0:T(8,128)(2,1)S(1)}, u32[]{:S(2)}) copy-start(bf16[768,256]{1,0:T(8,128)(2,1)S(1)} %collective-permute-done.1.refs_3_) | copy-start | bytes 1179652
  110.4 9.7 %collective-permute-start.2 = (bf16[768,256]{1,0:T(8,128)(2,1)S(1)}, bf16[768,256]{1,0:T(8,128)(2,1)S(1)}, u32[]{:S(2)}, u32[]{:S(2)}) collective-permute-start(bf16[768,256]{1,0:T(8,128)(2,1)S(1)} %collective-permute-done.1.refs_3_), channel_id=1, source_target_pairs={{0,4},{4,8},{8,12},{12,16},{16,20},{20,24},{24,28},{28,32},{32,36}... | collective-permute-start | bytes 1179656 | tf_op jit(solution)/shard_map/ppermute | solution.py:144
  115.1 9.7 %collective-permute-start.12 = (bf16[768,256]{1,0:T(8,128)(2,1)S(1)}, bf16[768,256]{1,0:T(8,128)(2,1)S(1)}, u32[]{:S(2)}, u32[]{:S(2)}) collective-permute-start(bf16[768,256]{1,0:T(8,128)(2,1)S(1)} %collective-permute-done.11), channel_id=1, source_target_pairs={{0,4},{4,8},{8,12},{12,16},{16,20},{20,24},{24,28},{28,32},{32,36}... | collective-permute-start | bytes 1179656 | tf_op jit(solution)/shard_map/ppermute | solution.py:144
  120.1 13.9 %copy-start.13 = (bf16[768,256]{1,0:T(8,128)(2,1)}, bf16[768,256]{1,0:T(8,128)(2,1)S(1)}, u32[]{:S(2)}) copy-start(bf16[768,256]{1,0:T(8,128)(2,1)S(1)} %collective-permute-done.2.refs_4_) | copy-start | bytes 1179652
  120.1 9.7 %collective-permute-start.3 = (bf16[768,256]{1,0:T(8,128)(2,1)S(1)}, bf16[768,256]{1,0:T(8,128)(2,1)S(1)}, u32[]{:S(2)}, u32[]{:S(2)}) collective-permute-start(bf16[768,256]{1,0:T(8,128)(2,1)S(1)} %collective-permute-done.2.refs_4_), channel_id=1, source_target_pairs={{0,4},{4,8},{8,12},{12,16},{16,20},{20,24},{24,28},{28,32},{32,36}... | collective-permute-start | bytes 1179656 | tf_op jit(solution)/shard_map/ppermute | solution.py:144
  124.8 9.7 %collective-permute-start.13 = (bf16[768,256]{1,0:T(8,128)(2,1)S(1)}, bf16[768,256]{1,0:T(8,128)(2,1)S(1)}, u32[]{:S(2)}, u32[]{:S(2)}) collective-permute-start(bf16[768,256]{1,0:T(8,128)(2,1)S(1)} %collective-permute-done.12), channel_id=1, source_target_pairs={{0,4},{4,8},{8,12},{12,16},{16,20},{20,24},{24,28},{28,32},{32,36}... | collective-permute-start | bytes 1179656 | tf_op jit(solution)/shard_map/ppermute | solution.py:144
  129.9 20.0 %copy-start.14 = (bf16[768,256]{1,0:T(8,128)(2,1)}, bf16[768,256]{1,0:T(8,128)(2,1)S(1)}, u32[]{:S(2)}) copy-start(bf16[768,256]{1,0:T(8,128)(2,1)S(1)} %collective-permute-done.3.refs_5_) | copy-start | bytes 1179652
  129.9 15.1 %collective-permute-start.4 = (bf16[768,256]{1,0:T(8,128)(2,1)S(1)}, bf16[768,256]{1,0:T(8,128)(2,1)}, u32[]{:S(2)}, u32[]{:S(2)}) collective-permute-start(bf16[768,256]{1,0:T(8,128)(2,1)S(1)} %collective-permute-done.3.refs_5_), channel_id=1, source_target_pairs={{0,4},{4,8},{8,12},{12,16},{16,20},{20,24},{24,28},{28,32},{32,36}... | collective-permute-start | bytes 1179656 | tf_op jit(solution)/shard_map/ppermute | solution.py:144
  134.5 15.3 %collective-permute-start.14 = (bf16[768,256]{1,0:T(8,128)(2,1)S(1)}, bf16[768,256]{1,0:T(8,128)(2,1)S(1)}, u32[]{:S(2)}, u32[]{:S(2)}) collective-permute-start(bf16[768,256]{1,0:T(8,128)(2,1)S(1)} %collective-permute-done.13), channel_id=1, source_target_pairs={{0,4},{4,8},{8,12},{12,16},{16,20},{20,24},{24,28},{28,32},{32,36}... | collective-permute-start | bytes 1179656 | tf_op jit(solution)/shard_map/ppermute | solution.py:144
  139.7 14.8 %copy-start.8 = (s32[6]{0:T(128)S(1)}, s32[6]{0:T(128)}, u32[]{:S(2)}) copy-start(s32[6]{0:T(128)} %param.11) | copy-start | bytes 76
  139.7 22.1 %copy-start.10 = (s32[10]{0:T(128)S(1)}, s32[10]{0:T(128)}, u32[]{:S(2)}) copy-start(s32[10]{0:T(128)} %constant.101.clone) | copy-start | bytes 124
  139.8 22.6 %copy-start.9 = (s32[6]{0:T(128)S(1)}, s32[6]{0:T(128)}, u32[]{:S(2)}) copy-start(s32[6]{0:T(128)} %constant.102.clone) | copy-start | bytes 76
  139.8 33.9 %collective-permute-start.20 = (bf16[3,768,256]{2,1,0:T(8,128)(2,1)S(1)}, bf16[3,768,256]{2,1,0:T(8,128)(2,1)}, u32[]{:S(2)}, u32[]{:S(2)}) collective-permute-start(bf16[3,768,256]{2,1,0:T(8,128)(2,1)S(1)} %pad_maximum_fusion.1), channel_id=1, source_target_pairs={{0,64},{64,0},{1,65},{65,1},{2,66},{66,2},{3,67},{67,3},{4,68},{68... | collective-permute-start | bytes 3538952 | tf_op jit(solution)/shard_map/ppermute | solution.py:160
  145.0 9.9 %collective-permute-start.5 = (bf16[768,256]{1,0:T(8,128)(2,1)}, bf16[768,256]{1,0:T(8,128)(2,1)}, u32[]{:S(2)}, u32[]{:S(2)}) collective-permute-start(bf16[768,256]{1,0:T(8,128)(2,1)} %collective-permute-done.4.refs_6_), channel_id=1, source_target_pairs={{0,4},{4,8},{8,12},{12,16},{16,20},{20,24},{24,28},{28,32},{32,36}... | collective-permute-start | bytes 1179656 | tf_op jit(solution)/shard_map/ppermute | solution.py:144
  149.9 0.7 copy-start.3
  150.8 33.1 %collective-permute-start.15 = (bf16[3,768,256]{2,1,0:T(8,128)(2,1)S(1)}, bf16[3,768,256]{2,1,0:T(8,128)(2,1)S(1)}, u32[]{:S(2)}, u32[]{:S(2)}) collective-permute-start(bf16[3,768,256]{2,1,0:T(8,128)(2,1)S(1)} %pad_maximum_fusion), channel_id=1, source_target_pairs={{0,64},{64,0},{1,65},{65,1},{2,66},{66,2},{3,67},{67,3},{4,68},{68... | collective-permute-start | bytes 3538952 | tf_op jit(solution)/shard_map/ppermute | solution.py:160
  154.9 10.0 %collective-permute-start.6 = (bf16[768,256]{1,0:T(8,128)(2,1)}, bf16[768,256]{1,0:T(8,128)(2,1)}, u32[]{:S(2)}, u32[]{:S(2)}) collective-permute-start(bf16[768,256]{1,0:T(8,128)(2,1)} %collective-permute-done.5.refs_7_), channel_id=1, source_target_pairs={{0,4},{4,8},{8,12},{12,16},{16,20},{20,24},{24,28},{28,32},{32,36}... | collective-permute-start | bytes 1179656 | tf_op jit(solution)/shard_map/ppermute | solution.py:144
  159.9 10.0 %collective-permute-start.16 = (bf16[768,256]{1,0:T(8,128)(2,1)}, bf16[768,256]{1,0:T(8,128)(2,1)}, u32[]{:S(2)}, u32[]{:S(2)}) collective-permute-start(bf16[768,256]{1,0:T(8,128)(2,1)} %copy-done.3), channel_id=1, source_target_pairs={{0,4},{4,8},{8,12},{12,16},{16,20},{20,24},{24,28},{28,32},{32,36}... | collective-permute-start | bytes 1179656 | tf_op jit(solution)/shard_map/ppermute | solution.py:144
  164.9 18.9 %collective-permute-start.7 = (bf16[768,256]{1,0:T(8,128)(2,1)}, bf16[768,256]{1,0:T(8,128)(2,1)}, u32[]{:S(2)}, u32[]{:S(2)}) collective-permute-start(bf16[768,256]{1,0:T(8,128)(2,1)} %collective-permute-done.6.refs_1_), channel_id=1, source_target_pairs={{0,4},{4,8},{8,12},{12,16},{16,20},{20,24},{24,28},{28,32},{32,36}... | collective-permute-start | bytes 1179656 | tf_op jit(solution)/shard_map/ppermute | solution.py:144
  170.0 13.8 %collective-permute-start.17 = (bf16[1,768,256]{2,1,0:T(8,128)(2,1)}, bf16[1,768,256]{2,1,0:T(8,128)(2,1)}, u32[]{:S(2)}, u32[]{:S(2)}) collective-permute-start(bf16[1,768,256]{2,1,0:T(8,128)(2,1)} %bitcast.6), channel_id=1, source_target_pairs={{0,64},{64,0},{1,65},{65,1},{2,66},{66,2},{3,67},{67,3},{4,68},{68... | collective-permute-start | bytes 1179656 | tf_op jit(solution)/shard_map/ppermute | solution.py:160
  183.8 1.0 copy-start.2
  193.4 1.9 copy-start.1
  193.4 2.3 copy-start
  193.4 2.3 copy-start.6
  195.7 12.4 %copy-start.7 = (s32[768]{0:T(1024)S(1)}, s32[768]{0:T(1024)}, u32[]{:S(2)}) copy-start(s32[768]{0:T(1024)} %param.10) | copy-start | bytes 9220
  197.9 24.9 %all-to-all-start.2 = ((f32[64,1,384]{2,1,0:T(1,128)}), f32[64,1,384]{2,1,0:T(1,128)S(1)}, u32[]{:S(2)}, u32[]{:S(2)}) async-start(f32[64,1,384]{2,1,0:T(1,128)} %all_to_all.18), calls=%async_computation.2 | async-start | bytes 196608 | tf_op jit(solution)/shard_map/all_to_all | solution.py:50
  224.2 13.1 %all-to-all-start.3 = ((f32[32,1,128]{2,1,0:T(1,128)}), f32[32,1,128]{2,1,0:T(1,128)S(1)}, u32[]{:S(2)}, u32[]{:S(2)}) async-start(f32[32,1,128]{2,1,0:T(1,128)} %broadcast_in_dim.79), calls=%async_computation.3 | async-start | bytes 32768 | tf_op jit(solution)/shard_map/all_to_all | solution.py:22

commit v3 on v2

--- a/solution.py
+++ b/solution.py
@@ -14,8 +14,13 @@
 SWAP = [(0, 1), (1, 0)]
 BLOCK = 256
 TILE = 256
+LIMIT = 24 << 20
 BATCHES = ((1, 2, 3), (4, 5, 6), (7,))
-GROUPS = ((range(0, 7), (0,)), ((7, 8), (1, 2)))
+GROUPS = (
+    ("early", range(0, 5), ()),
+    ("middle", (5, 6, 7), (0,)),
+    ("late", (8,), (1, 2)),
+)
 
 
 def to_all(array, axis, copies):
@@ -40,12 +45,12 @@
     return own, swapped
 
 
-def tail(lse, picked, domains, seq_len):
-    tokens = lse.shape[0]
+def tail(stats, domains, seq_len):
+    tokens = stats.shape[1]
     zs, ys = lax.axis_size("z"), lax.axis_size("y")
     own = tokens // (zs * ys)
     y = lax.axis_index("y")
-    slices = jnp.stack([lse, picked]).reshape(2, zs, ys, own).transpose(2, 0, 1, 3)
+    slices = stats.reshape(2, zs, ys, own).transpose(2, 0, 1, 3)
     send = jnp.broadcast_to(slices.reshape(1, ys, -1), (zs, ys, 2 * zs * own))
     got = lax.all_to_all(send.reshape(zs * ys, -1), VOCAB, 0, 0, tiled=True)
     got = got.reshape(zs * ys, 2, zs * own)
@@ -73,7 +78,7 @@
     return token_loss, mean
 
 
-def product_kernel(stacks, first):
+def product_kernel(stacks, first, last):
     def kernel(*refs):
         which, given, rest = refs[0], refs[1 : 1 + len(stacks)], refs[1 + len(stacks) :]
         blocks = [
@@ -85,7 +90,9 @@
         halves, rest = rest[:2], rest[2:]
         if not first:
             before, rest = rest[:2], rest[2:]
-        outs, (rows, sems) = rest[:2], rest[2:]
+        if last:
+            wanted, rest = rest[0], rest[1:]
+        *outs, rows, sems = rest
         copies = []
         for k in range(count):
             for h in range(2):
@@ -97,45 +104,66 @@
         for copy in copies:
             copy.wait()
         for at in range(0, tokens, TILE):
+            part = slice(at, at + TILE)
+            totals = []
             for h in range(2):
-                total = None if first else before[h][at : at + TILE]
+                total = None if first else before[h][part]
                 for k in range(count):
                     ref, *at_k = blocks[k]
-                    block = ref[(*at_k, slice(at, at + TILE))]
-                    part = jnp.dot(block, rows[k, h], preferred_element_type=jnp.float32)
-                    total = part if total is None else total + part
-                outs[h][at : at + TILE] = total
+                    more = jnp.dot(
+                        ref[(*at_k, part)], rows[k, h], preferred_element_type=jnp.float32
+                    )
+                    total = more if total is None else total + more
+                totals.append(total)
+            if not last:
+                outs[0][part], outs[1][part] = totals
+                continue
+            tops = [jnp.max(values, axis=1, keepdims=True) for values in totals]
+            top = jnp.maximum(*tops)
+            lane = lax.broadcasted_iota(jnp.int32, totals[0].shape, 1)
+            total, picked = 0.0, 0.0
+            for h, values in enumerate(totals):
+                total += jnp.sum(jnp.exp(values - top), axis=1, keepdims=True)
+                here = lane == wanted[part] - which[count + h]
+                picked += jnp.sum(jnp.where(here, values, 0.0), axis=1, keepdims=True)
+            lse = jnp.log(total) + top
+            side = lax.broadcasted_iota(jnp.int32, (TILE, 128), 1)
+            both = jnp.where(side == 0, lse, picked)
+            outs[0][:, part] = both.T[:8]
 
     return kernel
 
 
-def product(which, blocks, halves, before=None):
+def product(which, blocks, halves, before=None, wanted=None):
     tokens, depth = blocks[0].shape[-2:]
     half, arrays = halves[0].shape[1], len(blocks)
     stacks = [b.shape[0] if b.ndim == 3 else None for b in blocks]
     count = sum(n or 1 for n in stacks)
+    last = wanted is not None
     vmem = pl.BlockSpec(memory_space=pltpu.VMEM)
-    anywhere = pl.BlockSpec(memory_space=pl.ANY)
     shape = jax.ShapeDtypeStruct((tokens, half), jnp.float32)
+    extra = (before or ()) + ((wanted,) if last else ())
+    aliases = {} if before is None or last else {3 + arrays: 0, 4 + arrays: 1}
     return pl.pallas_call(
-        product_kernel(stacks, before is None),
+        product_kernel(stacks, before is None, last),
         in_specs=[pl.BlockSpec(memory_space=pltpu.SMEM)]
         + [vmem] * arrays
-        + [anywhere] * 2
-        + ([] if before is None else [vmem] * 2),
-        out_specs=[vmem, vmem],
-        out_shape=[shape, shape],
+        + [pl.BlockSpec(memory_space=pltpu.HBM)] * 2
+        + [vmem] * len(extra),
+        out_specs=vmem if last else [vmem, vmem],
+        out_shape=jax.ShapeDtypeStruct((8, tokens), jnp.float32) if last else [shape, shape],
         scratch_shapes=[
             pltpu.VMEM((count, 2, depth, half), jnp.bfloat16),
             pltpu.SemaphoreType.DMA((count, 2)),
         ],
-        input_output_aliases={} if before is None else {3 + arrays: 0, 4 + arrays: 1},
+        input_output_aliases=aliases,
+        compiler_params=pltpu.CompilerParams(vmem_limit_bytes=LIMIT),
         cost_estimate=pl.CostEstimate(
             flops=2 * count * tokens * depth * half * 2,
             bytes_accessed=count * depth * (tokens + 2 * half) * 2,
             transcendentals=0,
         ),
-    )(which, *blocks, *halves, *(before or ()))
+    )(which, *blocks, *halves, *extra)
 
 
 def along_z(array):
@@ -150,7 +178,8 @@
     halves = gathered_weight(weight)
     mine = to_all(hidden.T, "y", ys).reshape(BLOCK, -1).T
     rings = zs // 2
-    own, other = [mine], [lax.ppermute(mine, "c", SWAP)]
+    own = [mine]
+    other = [lax.ppermute(mine, "c", SWAP)]
     for r in range(1, rings + 1):
         own.append(along_z(own[-1]))
         if r < rings:
@@ -159,22 +188,21 @@
     for some in BATCHES:
         swapped.append(lax.ppermute(jnp.stack([other[r] for r in some]), "c", SWAP))
     step = 2 * core - 1
+    columns = weight.shape[1]
+    half = columns // 2
+    starts = jnp.stack([core * half, (1 - core) * half])
+    wanted = (targets - lax.axis_index(VOCAB) * columns)[:, None]
     logits = None
-    for rounds, batches in GROUPS:
+    for name, rounds, batches in GROUPS:
         away = [r for r in rounds] + [-r for k in batches for r in BATCHES[k]]
         which = lax.rem(z + step * jnp.array(away, jnp.int32) + zs, zs)
         blocks = [own[r] for r in rounds] + [swapped[k] for k in batches]
-        logits = product(which, blocks, halves, logits)
-    columns = weight.shape[1]
-    half = columns // 2
-    first = lax.axis_index(VOCAB) * columns
-    tops = jnp.maximum(jnp.max(logits[0], axis=1), jnp.max(logits[1], axis=1))
-    total, picked = 0.0, 0.0
-    for values, start in zip(logits, (core * half, (1 - core) * half)):
-        ids = first + start + lax.broadcasted_iota(jnp.int32, values.shape, 1)
-        total += jnp.sum(jnp.exp(values - tops[:, None]), axis=1)
-        picked += jnp.sum(jnp.where(ids == targets[:, None], values, 0.0), axis=1)
-    return tail(jnp.log(total) + tops, picked, domains, seq_len)
+        if name == "late":
+            which = jnp.concatenate([which, starts])
+            stats = product(which, blocks, halves, tuple(logits), wanted)
+        else:
+            logits = product(which, blocks, halves, logits and tuple(logits))
+    return tail(stats[:2], domains, seq_len)
 
 
 def solution(mesh):

time: 239 us -> 230 us (0.962)
  Pallas kernels: 18.6 us -> 14.7 us
  other arithmetic: 6.68 us -> 3.81 us
    pallas_call x2 -> x3, Pallas kernels: 18.6 us -> 14.7 us  [product(): pl.pallas_call(product_kernel(stacks, before is None, last), in_specs=[pl...]
  transfers between devices with their start and end apart: 23 -> 23, of which waited for: 11 -> 10; matrix products, arithmetic and copies ran while one was open for 1% -> 1% of each run, Pallas kernels for 4% -> 4%
where the time goes in v3:
time: 230 us; the launch traced here: 229 us
  starting transfers between devices  113 us (49%)
  blocking collectives  62.3 us (27%)
  waiting for transfers between devices  30 us (13%)
  Pallas kernels  14.7 us (6%)
  local copies, waits for them, and re-layouts  4.13 us (2%)
  other arithmetic  3.81 us (2%)
    ppermute x15, starting transfers between devices, along_z(): return lax.ppermute(array, ('c', 'z'), pairs)  68.6 us
    all_to_all x2, blocking collectives, to_all(): lax.all_to_all(jnp.broadcast_to(array[None], (copies, *array.shape)), axi...  62.3 us
    pallas_call x3, Pallas kernels, product(): pl.pallas_call(product_kernel(stacks, before is None, last), in_specs=[pl...  14.7 us
    all_to_all x1, waiting for transfers between devices, tail(): got = lax.all_to_all(send.reshape(zs * ys, -1), VOCAB, 0, 0, tiled=True)  14.3 us
    ppermute x3, starting transfers between devices, loss(): swapped.append(lax.ppermute(jnp.stack([other[r] for r in some]), 'c', SWAP))  13.1 us
    all_to_all x1, starting transfers between devices, tail(): got = lax.all_to_all(send.reshape(zs * ys, -1), VOCAB, 0, 0, tiled=True)  10.2 us
    ppermute x1, starting transfers between devices, gathered_weight(): other = lax.ppermute(give, 'c', SWAP)  8.75 us
    ppermute x15, waiting for transfers between devices, along_z(): return lax.ppermute(array, ('c', 'z'), pairs)  6.43 us
  transfers between devices with their start and end apart: 23, of which 10 were waited for; matrix products, arithmetic and copies ran while one was open for 1% of the time, Pallas kernels for 4%

profile of v3, /device:TPU:1, one launch (start us, length us, event | category | flops | bytes accessed | tf_op | source)
XLA Modules:
  0.0 229.2 jit_solution(7631987899606995452)
XLA Ops:
  0.6 1.3 constant_dynamic-slice_fusion.6
  1.9 8.7 %collective-permute-start.18 = (bf16[512,512]{1,0:T(8,128)(2,1)S(1)}, bf16[512,512]{1,0:T(8,128)(2,1)S(1)}, u32[]{:S(2)}, u32[]{:S(2)}) collective-permute-start(bf16[512,512]{1,0:T(8,128)(2,1)S(1)} %get-tuple-element.19), channel_id=1, source_target_pairs={{0,64},{64,0},{1,65},{65,1},{2,66},{66,2},{3,67},{67,3},{4,68},{68... | collective-permute-start | bytes 1572872 | tf_op jit(solution)/shard_map/ppermute | solution.py:37
  10.7 1.5 collective-permute-done.18
  12.2 0.5 maximum_select_fusion
  12.6 0.3 broadcast_in_dim.66
  13.0 52.1 %all_to_all.25 = bf16[4,1024,512]{2,1,0:T(8,128)(2,1)} all-to-all(bf16[4,1024,512]{2,1,0:T(8,128)(2,1)S(1)} %broadcast_in_dim.66), channel_id=1, replica_groups=mesh['x'=4,'c'=2,'z'=16,'y'=4] {'x'}, dimensions={0} | all-to-all | bytes 8388608 | tf_op jit(solution)/shard_map/all_to_all | solution.py:27
  65.1 3.3 %collective-permute-start.19 = (bf16[4096,512]{1,0:T(8,128)(2,1)}, bf16[4096,512]{1,0:T(8,128)(2,1)}, u32[]{:S(2)}, u32[]{:S(2)}) collective-permute-start(bf16[4096,512]{1,0:T(8,128)(2,1)} %bitcast.9.refs_6_.refs_5_.refs_4_), channel_id=1, source_target_pairs={{0,64},{64,0},{1,65},{65,1},{2,66},{66,2},{3,67},{67,3},{4,68},{68... | collective-permute-start | bytes 12582920 | tf_op jit(solution)/shard_map/ppermute | solution.py:44
  68.4 10.3 %all_to_all.26 = bf16[4,64,768]{2,1,0:T(8,128)(2,1)S(1)} all-to-all(bf16[4,64,768]{2,1,0:T(8,128)(2,1)S(1)} %broadcast_in_dim.65), channel_id=1, replica_groups=mesh['x'=4,'c'=2,'z'=16,'y'=4] {'y'}, dimensions={0} | all-to-all | bytes 786432 | tf_op jit(solution)/shard_map/all_to_all | solution.py:27
  78.6 0.2 copy.22
  78.8 3.1 %collective-permute-start.8 = (bf16[768,256]{1,0:T(8,128)(2,1)S(1)}, bf16[768,256]{1,0:T(8,128)(2,1)S(1)}, u32[]{:S(2)}, u32[]{:S(2)}) collective-permute-start(bf16[768,256]{1,0:T(8,128)(2,1)S(1)} %bitcast.25), channel_id=1, source_target_pairs={{0,64},{64,0},{1,65},{65,1},{2,66},{66,2},{3,67},{67,3},{4,68},{68... | collective-permute-start | bytes 1179656 | tf_op jit(solution)/shard_map/ppermute | solution.py:182
  81.9 1.3 collective-permute-done.8
  83.2 7.9 %collective-permute-start.9 = (bf16[768,256]{1,0:T(8,128)(2,1)S(1)}, bf16[768,256]{1,0:T(8,128)(2,1)S(1)}, u32[]{:S(2)}, u32[]{:S(2)}) collective-permute-start(bf16[768,256]{1,0:T(8,128)(2,1)S(1)} %collective-permute-done.8), channel_id=1, source_target_pairs={{0,4},{4,8},{8,12},{12,16},{16,20},{20,24},{24,28},{28,32},{32,36}... | collective-permute-start | bytes 1179656 | tf_op jit(solution)/shard_map/ppermute | solution.py:172
  91.1 2.6 %collective-permute-start = (bf16[768,256]{1,0:T(8,128)(2,1)S(1)}, bf16[768,256]{1,0:T(8,128)(2,1)S(1)}, u32[]{:S(2)}, u32[]{:S(2)}) collective-permute-start(bf16[768,256]{1,0:T(8,128)(2,1)S(1)} %bitcast.26), channel_id=1, source_target_pairs={{0,4},{4,8},{8,12},{12,16},{16,20},{20,24},{24,28},{28,32},{32,36}... | collective-permute-start | bytes 1179656 | tf_op jit(solution)/shard_map/ppermute | solution.py:172
  93.7 2.1 collective-permute-done.9
  95.8 5.0 %collective-permute-start.10 = (bf16[768,256]{1,0:T(8,128)(2,1)S(1)}, bf16[768,256]{1,0:T(8,128)(2,1)S(1)}, u32[]{:S(2)}, u32[]{:S(2)}) collective-permute-start(bf16[768,256]{1,0:T(8,128)(2,1)S(1)} %collective-permute-done.9), channel_id=1, source_target_pairs={{0,4},{4,8},{8,12},{12,16},{16,20},{20,24},{24,28},{28,32},{32,36}... | collective-permute-start | bytes 1179656 | tf_op jit(solution)/shard_map/ppermute | solution.py:172
  100.8 4.2 %collective-permute-start.1 = (bf16[768,256]{1,0:T(8,128)(2,1)S(1)}, bf16[768,256]{1,0:T(8,128)(2,1)S(1)}, u32[]{:S(2)}, u32[]{:S(2)}) collective-permute-start(bf16[768,256]{1,0:T(8,128)(2,1)S(1)} %collective-permute-done.refs_2_), channel_id=1, source_target_pairs={{0,4},{4,8},{8,12},{12,16},{16,20},{20,24},{24,28},{28,32},{32,36}... | collective-permute-start | bytes 1179656 | tf_op jit(solution)/shard_map/ppermute | solution.py:172
  105.0 0.5 collective-permute-done.10
  105.5 5.0 %collective-permute-start.11 = (bf16[768,256]{1,0:T(8,128)(2,1)S(1)}, bf16[768,256]{1,0:T(8,128)(2,1)S(1)}, u32[]{:S(2)}, u32[]{:S(2)}) collective-permute-start(bf16[768,256]{1,0:T(8,128)(2,1)S(1)} %collective-permute-done.10), channel_id=1, source_target_pairs={{0,4},{4,8},{8,12},{12,16},{16,20},{20,24},{24,28},{28,32},{32,36}... | collective-permute-start | bytes 1179656 | tf_op jit(solution)/shard_map/ppermute | solution.py:172
  110.5 4.2 %collective-permute-start.2 = (bf16[768,256]{1,0:T(8,128)(2,1)S(1)}, bf16[768,256]{1,0:T(8,128)(2,1)S(1)}, u32[]{:S(2)}, u32[]{:S(2)}) collective-permute-start(bf16[768,256]{1,0:T(8,128)(2,1)S(1)} %collective-permute-done.1.refs_3_), channel_id=1, source_target_pairs={{0,4},{4,8},{8,12},{12,16},{16,20},{20,24},{24,28},{28,32},{32,36}... | collective-permute-start | bytes 1179656 | tf_op jit(solution)/shard_map/ppermute | solution.py:172
  114.7 0.5 collective-permute-done.11
  115.2 5.0 %collective-permute-start.12 = (bf16[768,256]{1,0:T(8,128)(2,1)S(1)}, bf16[768,256]{1,0:T(8,128)(2,1)S(1)}, u32[]{:S(2)}, u32[]{:S(2)}) collective-permute-start(bf16[768,256]{1,0:T(8,128)(2,1)S(1)} %collective-permute-done.11), channel_id=1, source_target_pairs={{0,4},{4,8},{8,12},{12,16},{16,20},{20,24},{24,28},{28,32},{32,36}... | collective-permute-start | bytes 1179656 | tf_op jit(solution)/shard_map/ppermute | solution.py:172
  120.3 4.2 %collective-permute-start.3 = (bf16[768,256]{1,0:T(8,128)(2,1)S(1)}, bf16[768,256]{1,0:T(8,128)(2,1)S(1)}, u32[]{:S(2)}, u32[]{:S(2)}) collective-permute-start(bf16[768,256]{1,0:T(8,128)(2,1)S(1)} %collective-permute-done.2.refs_4_), channel_id=1, source_target_pairs={{0,4},{4,8},{8,12},{12,16},{16,20},{20,24},{24,28},{28,32},{32,36}... | collective-permute-start | bytes 1179656 | tf_op jit(solution)/shard_map/ppermute | solution.py:172
  124.5 0.5 collective-permute-done.12
  124.9 5.0 %collective-permute-start.13 = (bf16[768,256]{1,0:T(8,128)(2,1)S(1)}, bf16[768,256]{1,0:T(8,128)(2,1)}, u32[]{:S(2)}, u32[]{:S(2)}) collective-permute-start(bf16[768,256]{1,0:T(8,128)(2,1)S(1)} %collective-permute-done.12), channel_id=1, source_target_pairs={{0,4},{4,8},{8,12},{12,16},{16,20},{20,24},{24,28},{28,32},{32,36}... | collective-permute-start | bytes 1179656 | tf_op jit(solution)/shard_map/ppermute | solution.py:172
  130.0 4.2 %collective-permute-start.4 = (bf16[768,256]{1,0:T(8,128)(2,1)S(1)}, bf16[768,256]{1,0:T(8,128)(2,1)S(1)}, u32[]{:S(2)}, u32[]{:S(2)}) collective-permute-start(bf16[768,256]{1,0:T(8,128)(2,1)S(1)} %collective-permute-done.3.refs_5_), channel_id=1, source_target_pairs={{0,4},{4,8},{8,12},{12,16},{16,20},{20,24},{24,28},{28,32},{32,36}... | collective-permute-start | bytes 1179656 | tf_op jit(solution)/shard_map/ppermute | solution.py:172
  134.2 0.5 collective-permute-done.13
  134.7 5.1 %collective-permute-start.14 = (bf16[768,256]{1,0:T(8,128)(2,1)}, bf16[768,256]{1,0:T(8,128)(2,1)S(1)}, u32[]{:S(2)}, u32[]{:S(2)}) collective-permute-start(bf16[768,256]{1,0:T(8,128)(2,1)} %collective-permute-done.13), channel_id=1, source_target_pairs={{0,4},{4,8},{8,12},{12,16},{16,20},{20,24},{24,28},{28,32},{32,36}... | collective-permute-start | bytes 1179656 | tf_op jit(solution)/shard_map/ppermute | solution.py:172
  139.8 0.1 pad_maximum_fusion.1
  140.0 5.1 %collective-permute-start.20 = (bf16[3,768,256]{2,1,0:T(8,128)(2,1)S(1)}, bf16[3,768,256]{2,1,0:T(8,128)(2,1)S(1)}, u32[]{:S(2)}, u32[]{:S(2)}) collective-permute-start(bf16[3,768,256]{2,1,0:T(8,128)(2,1)S(1)} %pad_maximum_fusion.1), channel_id=1, source_target_pairs={{0,64},{64,0},{1,65},{65,1},{2,66},{66,2},{3,67},{67,3},{4,68},{68... | collective-permute-start | bytes 3538952 | tf_op jit(solution)/shard_map/ppermute | solution.py:189
  145.1 4.9 %collective-permute-start.5 = (bf16[768,256]{1,0:T(8,128)(2,1)S(1)}, bf16[768,256]{1,0:T(8,128)(2,1)S(1)}, u32[]{:S(2)}, u32[]{:S(2)}) collective-permute-start(bf16[768,256]{1,0:T(8,128)(2,1)S(1)} %collective-permute-done.4.refs_1_), channel_id=1, source_target_pairs={{0,4},{4,8},{8,12},{12,16},{16,20},{20,24},{24,28},{28,32},{32,36}... | collective-permute-start | bytes 1179656 | tf_op jit(solution)/shard_map/ppermute | solution.py:172
  150.0 0.0 copy-start.2
  150.0 0.0 copy-start.4
  150.0 1.1 pad_maximum_fusion
  151.1 4.1 %collective-permute-start.15 = (bf16[3,768,256]{2,1,0:T(8,128)(2,1)S(1)}, bf16[3,768,256]{2,1,0:T(8,128)(2,1)S(1)}, u32[]{:S(2)}, u32[]{:S(2)}) collective-permute-start(bf16[3,768,256]{2,1,0:T(8,128)(2,1)S(1)} %pad_maximum_fusion), channel_id=1, source_target_pairs={{0,64},{64,0},{1,65},{65,1},{2,66},{66,2},{3,67},{67,3},{4,68},{68... | collective-permute-start | bytes 3538952 | tf_op jit(solution)/shard_map/ppermute | solution.py:189
  155.3 4.4 %collective-permute-start.6 = (bf16[768,256]{1,0:T(8,128)(2,1)S(1)}, bf16[768,256]{1,0:T(8,128)(2,1)S(1)}, u32[]{:S(2)}, u32[]{:S(2)}) collective-permute-start(bf16[768,256]{1,0:T(8,128)(2,1)S(1)} %collective-permute-done.5.refs_2_), channel_id=1, source_target_pairs={{0,4},{4,8},{8,12},{12,16},{16,20},{20,24},{24,28},{28,32},{32,36}... | collective-permute-start | bytes 1179656 | tf_op jit(solution)/shard_map/ppermute | solution.py:172
  159.7 1.9 collective-permute-start.16
  161.6 0.1 pad_add_fusion.refs_0_
  161.7 0.2 broadcast_in_dim.74.refs_8_
  161.9 0.1 select_reduce_fusion.2
  162.0 2.4 %collective-permute-done.6.refs_3_ = bf16[768,256]{1,0:T(8,128)(2,1)S(1)} collective-permute-done((bf16[768,256]{1,0:T(8,128)(2,1)S(1)}, bf16[768,256]{1,0:T(8,128)(2,1)S(1)}, u32[]{:S(2)}, u32[]{:S(2)}) %collective-permute-start.6) | collective-permute-done | bytes 393248 | tf_op jit(solution)/shard_map/ppermute | solution.py:172
  164.4 5.0 %collective-permute-start.7 = (bf16[768,256]{1,0:T(8,128)(2,1)S(1)}, bf16[768,256]{1,0:T(8,128)(2,1)S(1)}, u32[]{:S(2)}, u32[]{:S(2)}) collective-permute-start(bf16[768,256]{1,0:T(8,128)(2,1)S(1)} %collective-permute-done.6.refs_3_), channel_id=1, source_target_pairs={{0,4},{4,8},{8,12},{12,16},{16,20},{20,24},{24,28},{28,32},{32,36}... | collective-permute-start | bytes 1179656 | tf_op jit(solution)/shard_map/ppermute | solution.py:172
  169.4 3.9 %collective-permute-start.17 = (bf16[1,768,256]{2,1,0:T(8,128)(2,1)S(1)}, bf16[1,768,256]{2,1,0:T(8,128)(2,1)S(1)}, u32[]{:S(2)}, u32[]{:S(2)}) collective-permute-start(bf16[1,768,256]{2,1,0:T(8,128)(2,1)S(1)} %bitcast.37), channel_id=1, source_target_pairs={{0,64},{64,0},{1,65},{65,1},{2,66},{66,2},{3,67},{67,3},{4,68},{68... | collective-permute-start | bytes 1179656 | tf_op jit(solution)/shard_map/ppermute | solution.py:189
  173.4 4.5 %shard_map.95 = (f32[768,512]{1,0:T(8,128)S(1)}, f32[768,512]{1,0:T(8,128)S(1)}) custom-call(s32[5]{0:T(128)S(1)} %compare_select_fusion.refs_0_, bf16[768,256]{1,0:T(8,128)(2,1)S(1)} %bitcast.27, bf16[768,256]{1,0:T(8,128)(2,1)S(1)} %collective-permute-done.refs_2_, bf16[768,256]{1,0:T(8,128)(2,1)S(1)} %collective-permute-done.1.refs_3_, ...), custom_call_target="tpu_custom_call" | custom-call | flops 2013265920 | bytes 4587520 | tf_op jit(solution)/shard_map/pallas_call | solution.py:147
  177.9 5.2 %shard_map.96 = (f32[768,512]{1,0:T(8,128)S(1)}, f32[768,512]{1,0:T(8,128)S(1)}) custom-call(s32[6]{0:T(128)S(1)} %compare_select_fusion.2.refs_0_, bf16[768,256]{1,0:T(8,128)(2,1)S(1)} %collective-permute-done.4.refs_1_, bf16[768,256]{1,0:T(8,128)(2,1)S(1)} %collective-permute-done.5.refs_2_, ...), custom_call_target="tpu_custom_call", output_to_operand_aliasing={{0}: (7, {}), {1}: (8, {})} | custom-call | flops 2415919104 | bytes 5505024 | tf_op jit(solution)/shard_map/pallas_call | solution.py:147
  183.2 5.0 %shard_map.97 = f32[8,768]{1,0:T(8,128)S(1)} custom-call(s32[7]{0:T(128)S(1)} %pad_add_fusion.refs_0_, bf16[768,256]{1,0:T(8,128)(2,1)S(1)} %collective-permute-done.7.refs_1_, bf16[3,768,256]{2,1,0:T(8,128)(2,1)S(1)} %collective-permute-done.15.refs_2_, bf16[1,768,256]{2,1,0:T(8,128)(2,1)S(1)} %collective-permute-done.17.refs_3_, ...), custom_call_target="tpu_custom_call" | custom-call | flops 2013265920 | bytes 4587520 | tf_op jit(solution)/shard_map/pallas_call | solution.py:147
  188.2 0.1 reshape.164
  188.3 0.1 broadcast_in_dim.68
  188.5 0.7 all_to_all.18
  189.2 10.2 %all-to-all-start.2 = ((f32[64,1,384]{2,1,0:T(1,128)}), f32[64,1,384]{2,1,0:T(1,128)S(1)}, u32[]{:S(2)}, u32[]{:S(2)}) async-start(f32[64,1,384]{2,1,0:T(1,128)} %all_to_all.18), calls=%async_computation.2 | async-start | bytes 196608 | tf_op jit(solution)/shard_map/all_to_all | solution.py:55
  199.4 0.1 reshape.166
  199.6 0.1 eq.27
  199.7 0.1 reduce_sum.57
  199.8 14.3 %all-to-all-done.2 = f32[64,1,384]{2,1,0:T(1,128)S(1)} async-done(((f32[64,1,384]{2,1,0:T(1,128)}), f32[64,1,384]{2,1,0:T(1,128)S(1)}, u32[]{:S(2)}, u32[]{:S(2)}) %all-to-all-start.2) | async-done | bytes 98336 | tf_op jit(solution)/shard_map/all_to_all | solution.py:55
  214.1 0.2 reduce.3
  214.4 0.1 reshape.165
  214.5 0.2 slice_reduce_fusion.1
  214.7 0.1 select_reduce_fusion.1
  214.9 0.1 pad_maximum_fusion.2
  214.9 0.6 broadcast_in_dim.73
  215.6 6.1 %all-to-all-start.3 = ((f32[32,1,128]{2,1,0:T(1,128)}), f32[32,1,128]{2,1,0:T(1,128)S(1)}, u32[]{:S(2)}, u32[]{:S(2)}) async-start(f32[32,1,128]{2,1,0:T(1,128)} %broadcast_in_dim.73), calls=%async_computation.3 | async-start | bytes 32768 | tf_op jit(solution)/shard_map/all_to_all | solution.py:27
  221.7 0.1 sub.54
  221.8 0.5 fusion.22
  222.3 6.3 %all-to-all-done.3 = f32[32,1,128]{2,1,0:T(1,128)S(1)} async-done(((f32[32,1,128]{2,1,0:T(1,128)}), f32[32,1,128]{2,1,0:T(1,128)S(1)}, u32[]{:S(2)}, u32[]{:S(2)}) %all-to-all-start.3) | async-done | bytes 16416 | tf_op jit(solution)/shard_map/all_to_all | solution.py:27
  228.7 0.6 maximum_divide_fusion
  (39 shorter events, 0.4 us)
Async XLA Ops:
  1.9 10.3 %collective-permute-start.18 = (bf16[512,512]{1,0:T(8,128)(2,1)S(1)}, bf16[512,512]{1,0:T(8,128)(2,1)S(1)}, u32[]{:S(2)}, u32[]{:S(2)}) collective-permute-start(bf16[512,512]{1,0:T(8,128)(2,1)S(1)} %get-tuple-element.19), channel_id=1, source_target_pairs={{0,64},{64,0},{1,65},{65,1},{2,66},{66,2},{3,67},{67,3},{4,68},{68... | collective-permute-start | bytes 1572872 | tf_op jit(solution)/shard_map/ppermute | solution.py:37
  13.0 55.4 %copy-start = (bf16[768,64]{0,1:T(8,128)(2,1)S(1)}, bf16[768,64]{0,1:T(8,128)(2,1)}, u32[]{:S(2)}) copy-start(bf16[768,64]{0,1:T(8,128)(2,1)} %param.8) | copy-start | bytes 294916
  65.1 74.7 %copy-start.5 = (s32[5]{0:T(128)S(1)}, s32[5]{0:T(128)}, u32[]{:S(2)}) copy-start(s32[5]{0:T(128)} %constant.106.clone) | copy-start | bytes 64
  65.1 108.3 %collective-permute-start.19 = (bf16[4096,512]{1,0:T(8,128)(2,1)}, bf16[4096,512]{1,0:T(8,128)(2,1)}, u32[]{:S(2)}, u32[]{:S(2)}) collective-permute-start(bf16[4096,512]{1,0:T(8,128)(2,1)} %bitcast.9.refs_6_.refs_5_.refs_4_), channel_id=1, source_target_pairs={{0,64},{64,0},{1,65},{65,1},{2,66},{66,2},{3,67},{67,3},{4,68},{68... | collective-permute-start | bytes 12582920 | tf_op jit(solution)/shard_map/ppermute | solution.py:44
  78.8 4.4 %collective-permute-start.8 = (bf16[768,256]{1,0:T(8,128)(2,1)S(1)}, bf16[768,256]{1,0:T(8,128)(2,1)S(1)}, u32[]{:S(2)}, u32[]{:S(2)}) collective-permute-start(bf16[768,256]{1,0:T(8,128)(2,1)S(1)} %bitcast.25), channel_id=1, source_target_pairs={{0,64},{64,0},{1,65},{65,1},{2,66},{66,2},{3,67},{67,3},{4,68},{68... | collective-permute-start | bytes 1179656 | tf_op jit(solution)/shard_map/ppermute | solution.py:182
  83.2 12.6 %collective-permute-start.9 = (bf16[768,256]{1,0:T(8,128)(2,1)S(1)}, bf16[768,256]{1,0:T(8,128)(2,1)S(1)}, u32[]{:S(2)}, u32[]{:S(2)}) collective-permute-start(bf16[768,256]{1,0:T(8,128)(2,1)S(1)} %collective-permute-done.8), channel_id=1, source_target_pairs={{0,4},{4,8},{8,12},{12,16},{16,20},{20,24},{24,28},{28,32},{32,36}... | collective-permute-start | bytes 1179656 | tf_op jit(solution)/shard_map/ppermute | solution.py:172
  91.1 9.7 %collective-permute-start = (bf16[768,256]{1,0:T(8,128)(2,1)S(1)}, bf16[768,256]{1,0:T(8,128)(2,1)S(1)}, u32[]{:S(2)}, u32[]{:S(2)}) collective-permute-start(bf16[768,256]{1,0:T(8,128)(2,1)S(1)} %bitcast.26), channel_id=1, source_target_pairs={{0,4},{4,8},{8,12},{12,16},{16,20},{20,24},{24,28},{28,32},{32,36}... | collective-permute-start | bytes 1179656 | tf_op jit(solution)/shard_map/ppermute | solution.py:172
  95.8 9.7 %collective-permute-start.10 = (bf16[768,256]{1,0:T(8,128)(2,1)S(1)}, bf16[768,256]{1,0:T(8,128)(2,1)S(1)}, u32[]{:S(2)}, u32[]{:S(2)}) collective-permute-start(bf16[768,256]{1,0:T(8,128)(2,1)S(1)} %collective-permute-done.9), channel_id=1, source_target_pairs={{0,4},{4,8},{8,12},{12,16},{16,20},{20,24},{24,28},{28,32},{32,36}... | collective-permute-start | bytes 1179656 | tf_op jit(solution)/shard_map/ppermute | solution.py:172
  100.8 9.7 %collective-permute-start.1 = (bf16[768,256]{1,0:T(8,128)(2,1)S(1)}, bf16[768,256]{1,0:T(8,128)(2,1)S(1)}, u32[]{:S(2)}, u32[]{:S(2)}) collective-permute-start(bf16[768,256]{1,0:T(8,128)(2,1)S(1)} %collective-permute-done.refs_2_), channel_id=1, source_target_pairs={{0,4},{4,8},{8,12},{12,16},{16,20},{20,24},{24,28},{28,32},{32,36}... | collective-permute-start | bytes 1179656 | tf_op jit(solution)/shard_map/ppermute | solution.py:172
  105.5 9.7 %collective-permute-start.11 = (bf16[768,256]{1,0:T(8,128)(2,1)S(1)}, bf16[768,256]{1,0:T(8,128)(2,1)S(1)}, u32[]{:S(2)}, u32[]{:S(2)}) collective-permute-start(bf16[768,256]{1,0:T(8,128)(2,1)S(1)} %collective-permute-done.10), channel_id=1, source_target_pairs={{0,4},{4,8},{8,12},{12,16},{16,20},{20,24},{24,28},{28,32},{32,36}... | collective-permute-start | bytes 1179656 | tf_op jit(solution)/shard_map/ppermute | solution.py:172
  110.5 9.7 %collective-permute-start.2 = (bf16[768,256]{1,0:T(8,128)(2,1)S(1)}, bf16[768,256]{1,0:T(8,128)(2,1)S(1)}, u32[]{:S(2)}, u32[]{:S(2)}) collective-permute-start(bf16[768,256]{1,0:T(8,128)(2,1)S(1)} %collective-permute-done.1.refs_3_), channel_id=1, source_target_pairs={{0,4},{4,8},{8,12},{12,16},{16,20},{20,24},{24,28},{28,32},{32,36}... | collective-permute-start | bytes 1179656 | tf_op jit(solution)/shard_map/ppermute | solution.py:172
  115.2 9.7 %collective-permute-start.12 = (bf16[768,256]{1,0:T(8,128)(2,1)S(1)}, bf16[768,256]{1,0:T(8,128)(2,1)S(1)}, u32[]{:S(2)}, u32[]{:S(2)}) collective-permute-start(bf16[768,256]{1,0:T(8,128)(2,1)S(1)} %collective-permute-done.11), channel_id=1, source_target_pairs={{0,4},{4,8},{8,12},{12,16},{16,20},{20,24},{24,28},{28,32},{32,36}... | collective-permute-start | bytes 1179656 | tf_op jit(solution)/shard_map/ppermute | solution.py:172
  120.3 9.7 %collective-permute-start.3 = (bf16[768,256]{1,0:T(8,128)(2,1)S(1)}, bf16[768,256]{1,0:T(8,128)(2,1)S(1)}, u32[]{:S(2)}, u32[]{:S(2)}) collective-permute-start(bf16[768,256]{1,0:T(8,128)(2,1)S(1)} %collective-permute-done.2.refs_4_), channel_id=1, source_target_pairs={{0,4},{4,8},{8,12},{12,16},{16,20},{20,24},{24,28},{28,32},{32,36}... | collective-permute-start | bytes 1179656 | tf_op jit(solution)/shard_map/ppermute | solution.py:172
  124.9 9.7 %collective-permute-start.13 = (bf16[768,256]{1,0:T(8,128)(2,1)S(1)}, bf16[768,256]{1,0:T(8,128)(2,1)}, u32[]{:S(2)}, u32[]{:S(2)}) collective-permute-start(bf16[768,256]{1,0:T(8,128)(2,1)S(1)} %collective-permute-done.12), channel_id=1, source_target_pairs={{0,4},{4,8},{8,12},{12,16},{16,20},{20,24},{24,28},{28,32},{32,36}... | collective-permute-start | bytes 1179656 | tf_op jit(solution)/shard_map/ppermute | solution.py:172
  130.0 15.1 %collective-permute-start.4 = (bf16[768,256]{1,0:T(8,128)(2,1)S(1)}, bf16[768,256]{1,0:T(8,128)(2,1)S(1)}, u32[]{:S(2)}, u32[]{:S(2)}) collective-permute-start(bf16[768,256]{1,0:T(8,128)(2,1)S(1)} %collective-permute-done.3.refs_5_), channel_id=1, source_target_pairs={{0,4},{4,8},{8,12},{12,16},{16,20},{20,24},{24,28},{28,32},{32,36}... | collective-permute-start | bytes 1179656 | tf_op jit(solution)/shard_map/ppermute | solution.py:172
  134.7 15.3 %collective-permute-start.14 = (bf16[768,256]{1,0:T(8,128)(2,1)}, bf16[768,256]{1,0:T(8,128)(2,1)S(1)}, u32[]{:S(2)}, u32[]{:S(2)}) collective-permute-start(bf16[768,256]{1,0:T(8,128)(2,1)} %collective-permute-done.13), channel_id=1, source_target_pairs={{0,4},{4,8},{8,12},{12,16},{16,20},{20,24},{24,28},{28,32},{32,36}... | collective-permute-start | bytes 1179656 | tf_op jit(solution)/shard_map/ppermute | solution.py:172
  140.0 37.9 %collective-permute-start.20 = (bf16[3,768,256]{2,1,0:T(8,128)(2,1)S(1)}, bf16[3,768,256]{2,1,0:T(8,128)(2,1)S(1)}, u32[]{:S(2)}, u32[]{:S(2)}) collective-permute-start(bf16[3,768,256]{2,1,0:T(8,128)(2,1)S(1)} %pad_maximum_fusion.1), channel_id=1, source_target_pairs={{0,64},{64,0},{1,65},{65,1},{2,66},{66,2},{3,67},{67,3},{4,68},{68... | collective-permute-start | bytes 3538952 | tf_op jit(solution)/shard_map/ppermute | solution.py:189
  145.1 10.2 %collective-permute-start.5 = (bf16[768,256]{1,0:T(8,128)(2,1)S(1)}, bf16[768,256]{1,0:T(8,128)(2,1)S(1)}, u32[]{:S(2)}, u32[]{:S(2)}) collective-permute-start(bf16[768,256]{1,0:T(8,128)(2,1)S(1)} %collective-permute-done.4.refs_1_), channel_id=1, source_target_pairs={{0,4},{4,8},{8,12},{12,16},{16,20},{20,24},{24,28},{28,32},{32,36}... | collective-permute-start | bytes 1179656 | tf_op jit(solution)/shard_map/ppermute | solution.py:172
  150.0 5.3 %copy-start.2 = (s32[768]{0:T(1024)S(1)}, s32[768]{0:T(1024)}, u32[]{:S(2)}) copy-start(s32[768]{0:T(1024)} %param.10) | copy-start | bytes 9220
  150.0 11.9 %copy-start.3 = (s32[6]{0:T(128)S(1)}, s32[6]{0:T(128)}, u32[]{:S(2)}) copy-start(s32[6]{0:T(128)} %param.12) | copy-start | bytes 76
  150.0 12.0 %copy-start.4 = (s32[6]{0:T(128)S(1)}, s32[6]{0:T(128)}, u32[]{:S(2)}) copy-start(s32[6]{0:T(128)} %constant.105.clone) | copy-start | bytes 76
  151.1 32.0 %collective-permute-start.15 = (bf16[3,768,256]{2,1,0:T(8,128)(2,1)S(1)}, bf16[3,768,256]{2,1,0:T(8,128)(2,1)S(1)}, u32[]{:S(2)}, u32[]{:S(2)}) collective-permute-start(bf16[3,768,256]{2,1,0:T(8,128)(2,1)S(1)} %pad_maximum_fusion), channel_id=1, source_target_pairs={{0,64},{64,0},{1,65},{65,1},{2,66},{66,2},{3,67},{67,3},{4,68},{68... | collective-permute-start | bytes 3538952 | tf_op jit(solution)/shard_map/ppermute | solution.py:189
  155.3 9.1 %collective-permute-start.6 = (bf16[768,256]{1,0:T(8,128)(2,1)S(1)}, bf16[768,256]{1,0:T(8,128)(2,1)S(1)}, u32[]{:S(2)}, u32[]{:S(2)}) collective-permute-start(bf16[768,256]{1,0:T(8,128)(2,1)S(1)} %collective-permute-done.5.refs_2_), channel_id=1, source_target_pairs={{0,4},{4,8},{8,12},{12,16},{16,20},{20,24},{24,28},{28,32},{32,36}... | collective-permute-start | bytes 1179656 | tf_op jit(solution)/shard_map/ppermute | solution.py:172
  159.7 9.7 %collective-permute-start.16 = (bf16[768,256]{1,0:T(8,128)(2,1)S(1)}, bf16[768,256]{1,0:T(8,128)(2,1)S(1)}, u32[]{:S(2)}, u32[]{:S(2)}) collective-permute-start(bf16[768,256]{1,0:T(8,128)(2,1)S(1)} %collective-permute-done.14), channel_id=1, source_target_pairs={{0,4},{4,8},{8,12},{12,16},{16,20},{20,24},{24,28},{28,32},{32,36}... | collective-permute-start | bytes 1179656 | tf_op jit(solution)/shard_map/ppermute | solution.py:172
  164.4 18.7 %collective-permute-start.7 = (bf16[768,256]{1,0:T(8,128)(2,1)S(1)}, bf16[768,256]{1,0:T(8,128)(2,1)S(1)}, u32[]{:S(2)}, u32[]{:S(2)}) collective-permute-start(bf16[768,256]{1,0:T(8,128)(2,1)S(1)} %collective-permute-done.6.refs_3_), channel_id=1, source_target_pairs={{0,4},{4,8},{8,12},{12,16},{16,20},{20,24},{24,28},{28,32},{32,36}... | collective-permute-start | bytes 1179656 | tf_op jit(solution)/shard_map/ppermute | solution.py:172
  169.4 13.7 %collective-permute-start.17 = (bf16[1,768,256]{2,1,0:T(8,128)(2,1)S(1)}, bf16[1,768,256]{2,1,0:T(8,128)(2,1)S(1)}, u32[]{:S(2)}, u32[]{:S(2)}) collective-permute-start(bf16[1,768,256]{2,1,0:T(8,128)(2,1)S(1)} %bitcast.37), channel_id=1, source_target_pairs={{0,64},{64,0},{1,65},{65,1},{2,66},{66,2},{3,67},{67,3},{4,68},{68... | collective-permute-start | bytes 1179656 | tf_op jit(solution)/shard_map/ppermute | solution.py:189
  183.2 16.3 %copy-start.1 = (s32[768]{0:T(1024)S(1)}, s32[768]{0:T(1024)}, u32[]{:S(2)}) copy-start(s32[768]{0:T(1024)} %param.11) | copy-start | bytes 9220
  189.2 24.9 %all-to-all-start.2 = ((f32[64,1,384]{2,1,0:T(1,128)}), f32[64,1,384]{2,1,0:T(1,128)S(1)}, u32[]{:S(2)}, u32[]{:S(2)}) async-start(f32[64,1,384]{2,1,0:T(1,128)} %all_to_all.18), calls=%async_computation.2 | async-start | bytes 196608 | tf_op jit(solution)/shard_map/all_to_all | solution.py:55
  215.6 13.1 %all-to-all-start.3 = ((f32[32,1,128]{2,1,0:T(1,128)}), f32[32,1,128]{2,1,0:T(1,128)S(1)}, u32[]{:S(2)}, u32[]{:S(2)}) async-start(f32[32,1,128]{2,1,0:T(1,128)} %broadcast_in_dim.73), calls=%async_computation.3 | async-start | bytes 32768 | tf_op jit(solution)/shard_map/all_to_all | solution.py:27

commit v4 on v1

v4 whole, which is shorter than its diff:
```python
import jax
import jax.numpy as jnp
from jax import lax
from jax.experimental import pallas as pl
from jax.experimental.pallas import tpu as pltpu
from jax.sharding import Mesh
from jax.sharding import PartitionSpec as P


SEQ_LEN = 128
DOMAINS = 64
TOK = ("x", "c")
VOCAB = ("z", "y")
SWAP = [(0, 1), (1, 0)]
BLOCK = 256
TILE = 256
LONG = 512
LIMIT = 24 << 20
ROUNDS = 8
BATCHES = ((1, 2, 3), (4, 5, 6), (7,))
GROUPS = (
    ("early", range(0, 7), (0,)),
    ("middle", (7,), (1,)),
    ("late", (8,), (2,)),
)


def to_all(array, axis, copies):
    return lax.all_to_all(
        jnp.broadcast_to(array[None], (copies, *array.shape)), axis, 0, 0, tiled=True
    )


def gathered_weight(weight):
    own = to_all(weight, "x", lax.axis_size("x"))
    return own, lax.ppermute(own, "c", SWAP)


def tail(stats, domains, seq_len):
    tokens = stats.shape[1]
    zs, ys = lax.axis_size("z"), lax.axis_size("y")
    own = tokens // (zs * ys)
    y = lax.axis_index("y")
    slices = stats.reshape(2, zs, ys, own).transpose(2, 0, 1, 3)
    send = jnp.broadcast_to(slices.reshape(1, ys, -1), (zs, ys, 2 * zs * own))
    got = lax.all_to_all(send.reshape(zs * ys, -1), VOCAB, 0, 0, tiled=True)
    got = got.reshape(zs * ys, 2, zs * own)
    top = jnp.max(got[:, 0], axis=0)
    total = jnp.sum(jnp.exp(got[:, 0] - top[None]), axis=0)
    raw = jnp.log(total) + top - jnp.sum(got[:, 1], axis=0)
    index = lax.iota(jnp.int32, zs * own)
    local = (index // own) * (ys * own) + y * own + index % own
    seqs = seq_len.shape[0]
    lengths = jnp.sum(
        jnp.where((local // SEQ_LEN)[:, None] == lax.broadcasted_iota(jnp.int32, (zs * own, seqs), 1), seq_len[None], 0),
        axis=1,
    )
    mask = (local % SEQ_LEN < lengths).astype(jnp.float32)
    loss = raw * mask
    domain = lax.dynamic_index_in_dim(domains.reshape(zs, ys, own), y, 1, False).reshape(-1)
    here = domain[None, :] == lax.broadcasted_iota(jnp.int32, (DOMAINS, zs * own), 0)
    sums = jnp.sum(jnp.where(here, loss[None], 0.0), axis=1)
    counts = jnp.sum(jnp.where(here, mask[None], 0.0), axis=1)
    part = jnp.concatenate([sums, counts])
    axes = ("x", "c", "y")
    whole = jnp.sum(to_all(part, axes, lax.axis_size(axes)), axis=0)
    mean = whole[:DOMAINS] / jnp.maximum(whole[DOMAINS:], 1.0)
    token_loss = lax.dynamic_index_in_dim(loss.reshape(zs, own), lax.axis_index("z"), 0, False)
    return token_loss, mean


def product_kernel(kinds, first, last):
    def kernel(which, *refs):
        refs = list(refs)
        blocks = []
        for kind in kinds:
            if kind == "parts":
                blocks.append((refs.pop(0), refs.pop(0)))
            else:
                ref = refs.pop(0)
                blocks += [(ref.at[k],) for k in range(kind)] if kind else [(ref,)]
        count, weights = len(blocks), (refs.pop(0), refs.pop(0))
        before = None if first else refs.pop(0)
        wanted = refs.pop(0) if last else None
        out, rows, sems, *more = refs
        acc = more[0] if last else out

        def fetch(k, source):
            z = which[k]
            return pltpu.make_async_copy(
                source.at[z // 4, pl.ds((z % 2) * BLOCK, BLOCK)],
                rows.at[pl.ds(k * BLOCK, BLOCK)],
                sems.at[k],
            )

        for k in range(count):
            mine = (which[k] // 2) % 2 == which[count]
            pl.when(mine)(fetch(k, weights[0]).start)
            pl.when(jnp.logical_not(mine))(fetch(k, weights[1]).start)

        def tile(block, at):
            ref, at = (block[0], at) if len(block) == 1 or at < LONG else (block[1], at - LONG)
            return ref[at : at + TILE]

        tokens, columns = acc.shape
        steps = [range(0, min(2, count)), range(2, count)]
        steps = [ks for ks in steps if len(ks)]
        for n, ks in enumerate(steps):
            for k in ks:
                fetch(k, weights[0]).wait()
            deep = slice(ks[0] * BLOCK, (ks[-1] + 1) * BLOCK)
            for at in range(0, tokens, TILE):
                part = slice(at, at + TILE)
                left = jnp.concatenate([tile(blocks[k], at) for k in ks], axis=1)
                for low in range(0, columns, LONG):
                    side = slice(low, low + LONG)
                    total = jnp.dot(left, rows[deep, side], preferred_element_type=jnp.float32)
                    if n:
                        total += acc[part, side]
                    elif not first:
                        total += before[part, side]
                    acc[part, side] = total
                if last and n == len(steps) - 1:
                    values = acc[part]
                    top = jnp.max(values, axis=1, keepdims=True)
                    total = jnp.sum(jnp.exp(values - top), axis=1, keepdims=True)
                    lane = lax.broadcasted_iota(jnp.int32, values.shape, 1)
                    picked = jnp.where(lane == wanted[part], values, 0.0)
                    picked = jnp.sum(picked, axis=1, keepdims=True)
                    lse = jnp.log(total) + top
                    lane = lax.broadcasted_iota(jnp.int32, (TILE, 128), 1)
                    out[:, part] = jnp.where(lane == 0, lse, picked).T[:8]

    return kernel


def product(which, blocks, weights, before=None, wanted=None):
    kinds = ["parts" if isinstance(b, tuple) else b.shape[0] if b.ndim == 3 else 0 for b in blocks]
    count = sum(1 if kind == "parts" else kind or 1 for kind in kinds)
    arrays = [array for b in blocks for array in (b if isinstance(b, tuple) else (b,))]
    columns, tokens, last = weights[0].shape[2], 768, wanted is not None
    vmem = pl.BlockSpec(memory_space=pltpu.VMEM)
    extra = [array for array in (before, wanted) if array is not None]
    shape = (8, tokens) if last else (tokens, columns)
    return pl.pallas_call(
        product_kernel(kinds, before is None, last),
        in_specs=[pl.BlockSpec(memory_space=pltpu.SMEM)]
        + [vmem] * len(arrays)
        + [pl.BlockSpec(memory_space=pltpu.HBM)] * 2
        + [vmem] * len(extra),
        out_specs=vmem,
        out_shape=jax.ShapeDtypeStruct(shape, jnp.float32),
        scratch_shapes=[
            pltpu.VMEM((count * BLOCK, columns), jnp.bfloat16),
            pltpu.SemaphoreType.DMA((count,)),
        ]
        + ([pltpu.VMEM((tokens, columns), jnp.float32)] if last else []),
        input_output_aliases={} if before is None or last else {3 + len(arrays): 0},
        compiler_params=pltpu.CompilerParams(vmem_limit_bytes=LIMIT),
        cost_estimate=pl.CostEstimate(
            flops=2 * count * tokens * BLOCK * columns,
            bytes_accessed=count * BLOCK * (tokens + columns) * 2,
            transcendentals=0,
        ),
    )(which, *arrays, *weights, *extra)


def along_z(array):
    zs = lax.axis_size("z")
    pairs = [(c * zs + z, c * zs + (z + (1 - 2 * c)) % zs) for c in range(2) for z in range(zs)]
    return lax.ppermute(array, ("c", "z"), pairs)


def loss(hidden, weight, targets, domains, seq_len):
    core, z = lax.axis_index("c"), lax.axis_index("z")
    zs, ys = lax.axis_size("z"), lax.axis_size("y")
    weights = gathered_weight(weight)
    mine = to_all(hidden.T, "y", ys).reshape(BLOCK, -1).T
    theirs = lax.ppermute(mine, "c", SWAP)
    a, b = [mine[:LONG]], [jnp.concatenate([mine[LONG:], theirs[LONG:]], 0)]
    c = [theirs[:LONG]]
    for r in range(1, ROUNDS + 1):
        a.append(along_z(a[-1]))
        b.append(along_z(b[-1] if r < ROUNDS else b[-1][: mine.shape[0] - LONG]))
        if r < ROUNDS:
            c.append(along_z(c[-1]))
    swapped = []
    for some in BATCHES:
        give = [jnp.concatenate([c[r], b[r][mine.shape[0] - LONG :]], 0) for r in some]
        swapped.append(lax.ppermute(jnp.stack(give), "c", SWAP))
    step = 2 * core - 1
    wanted = (targets - lax.axis_index(VOCAB) * weight.shape[1])[:, None]
    logits = None
    for name, rounds, batches in GROUPS:
        away = [r for r in rounds] + [-r for k in batches for r in BATCHES[k]]
        which = lax.rem(z + step * jnp.array(away, jnp.int32) + zs, zs)
        which = jnp.concatenate([which, core[None]])
        blocks = [(a[r], b[r]) if r else mine for r in rounds] + [swapped[k] for k in batches]
        logits = product(which, blocks, weights, logits, wanted if name == "late" else None)
    return tail(logits[:2], domains, seq_len)


def solution(mesh):
    split = Mesh(mesh.devices.reshape(4, 2, 16, 4), ("x", "c", "z", "y"))
    placed = (P(TOK, VOCAB), P(TOK, VOCAB), P(TOK), P(TOK), P(TOK))
    return jax.shard_map(loss, mesh=split, in_specs=placed, out_specs=(P((*TOK, *VOCAB)), P()), check_vma=False)
```

time: 176 us -> 219 us (1.24)
  starting transfers between devices: 34.1 us -> 111 us
  waiting for transfers between devices: 42.7 us -> 23.7 us
  Pallas kernels: 0 us -> 14.1 us
  between operations: 14.3 us -> 1.53 us
  matrix products: 12.7 us -> 0 us
  blocking collectives: 64.9 us -> 59.8 us
    ppermute x1 -> x27, starting transfers between devices: 9.23 us -> 91.5 us  [the longest x23 75.2 us: along_z(): return lax.ppermute(array, ('c', 'z'), pairs)]
    all_gather x1 -> x0, waiting for transfers between devices: 20.7 us -> none  [body(): features = lax.all_gather(features, 'z', axis=1, tiled=True)]
    pallas_call x0 -> x3, Pallas kernels: none -> 14.1 us  [product(): pl.pallas_call(product_kernel(kinds, before is None, last), in_specs=[pl....]
    all_gather x1 -> x0, blocking collectives: 13 us -> none  [body(): features = lax.all_gather(hidden, 'y', axis=1, tiled=True)]
    dot_general x2 -> x0, matrix products: 12.7 us -> none  [body(): jnp.dot(features, w, preferred_element_type=jnp.float32)]
    all_to_all x1 -> x2, blocking collectives: 51.9 us -> 59.8 us  [to_all(): lax.all_to_all(jnp.broadcast_to(array[None], (copies, *array.shape)), axi...]
    all_to_all x1, starting transfers between devices: 13.5 us -> 7.43 us  [tail(): got = lax.all_to_all(send.reshape(zs * ys, -1), VOCAB, 0, 0, tiled=True)]
    ppermute x1, starting transfers between devices: 3.13 us -> 8.56 us  [gathered_weight(): return (own, lax.ppermute(own, 'c', SWAP))]
  transfers between devices with their start and end apart: 5 -> 30, of which waited for: 4 -> 3; matrix products, arithmetic and copies ran while one was open for 6% -> 1% of each run, Pallas kernels for 0% -> 5%
where the time goes in v4:
time: 219 us; the launch traced here: 218 us
  starting transfers between devices  111 us (51%)
  blocking collectives  59.8 us (27%)
  waiting for transfers between devices  23.7 us (11%)
  Pallas kernels  14.1 us (6%)
  local copies, waits for them, and re-layouts  4.44 us (2%)
  other arithmetic  3.21 us (1%)
    ppermute x23, starting transfers between devices, along_z(): return lax.ppermute(array, ('c', 'z'), pairs)  75.2 us
    all_to_all x2, blocking collectives, to_all(): lax.all_to_all(jnp.broadcast_to(array[None], (copies, *array.shape)), axi...  59.8 us
    all_to_all x1, waiting for transfers between devices, tail(): got = lax.all_to_all(send.reshape(zs * ys, -1), VOCAB, 0, 0, tiled=True)  15.7 us
    pallas_call x3, Pallas kernels, product(): pl.pallas_call(product_kernel(kinds, before is None, last), in_specs=[pl....  14.1 us
    ppermute x3, starting transfers between devices, loss(): swapped.append(lax.ppermute(jnp.stack(give), 'c', SWAP))  13.1 us
    ppermute x1, starting transfers between devices, gathered_weight(): return (own, lax.ppermute(own, 'c', SWAP))  8.56 us
    all_to_all x1, starting transfers between devices, tail(): got = lax.all_to_all(send.reshape(zs * ys, -1), VOCAB, 0, 0, tiled=True)  7.43 us
    all_to_all x1, waiting for transfers between devices, to_all(): lax.all_to_all(jnp.broadcast_to(array[None], (copies, *array.shape)), axi...  6.33 us
  transfers between devices with their start and end apart: 30, of which 3 were waited for; matrix products, arithmetic and copies ran while one was open for 1% of the time, Pallas kernels for 5%

profile of v4, /device:TPU:1, one launch (start us, length us, event | category | flops | bytes accessed | tf_op | source)
XLA Modules:
  0.0 218.0 jit_solution(384918321223559465)
XLA Ops:
  0.6 1.7 broadcast_in_dim.72
  2.4 48.0 %all_to_all.25.refs_14_.refs_3_ = bf16[4,512,1024]{2,1,0:T(8,128)(2,1)} all-to-all(bf16[4,512,1024]{2,1,0:T(8,128)(2,1)S(1)} %broadcast_in_dim.72), channel_id=1, replica_groups=mesh['x'=4,'c'=2,'z'=16,'y'=4] {'x'}, dimensions={0} | all-to-all | bytes 8388608 | tf_op jit(solution)/shard_map/all_to_all | solution.py:29
  50.4 8.6 %collective-permute-start.25 = (bf16[4,512,1024]{2,1,0:T(8,128)(2,1)}, bf16[4,512,1024]{2,1,0:T(8,128)(2,1)}, u32[]{:S(2)}, u32[]{:S(2)}) collective-permute-start(bf16[4,512,1024]{2,1,0:T(8,128)(2,1)} %all_to_all.25.refs_14_.refs_3_), channel_id=1, source_target_pairs={{0,64},{64,0},{1,65},{65,1},{2,66},{66,2},{3,67},{67,3},{4,68},{68... | collective-permute-start | bytes 12582920 | tf_op jit(solution)/shard_map/ppermute | solution.py:36
  59.0 11.9 %all_to_all.26 = bf16[4,64,768]{2,1,0:T(8,128)(2,1)S(1)} all-to-all(bf16[4,64,768]{2,1,0:T(8,128)(2,1)S(1)} %broadcast_in_dim.71), channel_id=1, replica_groups=mesh['x'=4,'c'=2,'z'=16,'y'=4] {'y'}, dimensions={0} | all-to-all | bytes 786432 | tf_op jit(solution)/shard_map/all_to_all | solution.py:29
  70.8 0.2 copy.21
  71.0 0.0 copy-start.7
  71.1 3.2 %collective-permute-start.8 = (bf16[768,256]{1,0:T(8,128)(2,1)S(1)}, bf16[768,256]{1,0:T(8,128)(2,1)S(1)}, u32[]{:S(2)}, u32[]{:S(2)}) collective-permute-start(bf16[768,256]{1,0:T(8,128)(2,1)S(1)} %bitcast.30), channel_id=1, source_target_pairs={{0,64},{64,0},{1,65},{65,1},{2,66},{66,2},{3,67},{67,3},{4,68},{68... | collective-permute-start | bytes 1179656 | tf_op jit(solution)/shard_map/ppermute | solution.py:179
  74.3 11.1 %collective-permute-start = (bf16[512,256]{1,0:T(8,128)(2,1)S(1)}, bf16[512,256]{1,0:T(8,128)(2,1)S(1)}, u32[]{:S(2)}, u32[]{:S(2)}) collective-permute-start(bf16[512,256]{1,0:T(8,128)(2,1)S(1)} %slice.69), channel_id=1, source_target_pairs={{0,4},{4,8},{8,12},{12,16},{16,20},{20,24},{24,28},{28,32},{32,36}... | collective-permute-start | bytes 786440 | tf_op jit(solution)/shard_map/ppermute | solution.py:171
  85.5 2.6 %collective-permute-start.9 = (bf16[512,256]{1,0:T(8,128)(2,1)S(1)}, bf16[512,256]{1,0:T(8,128)(2,1)S(1)}, u32[]{:S(2)}, u32[]{:S(2)}) collective-permute-start(bf16[512,256]{1,0:T(8,128)(2,1)S(1)} %pad_maximum_fusion.2), channel_id=1, source_target_pairs={{0,4},{4,8},{8,12},{12,16},{16,20},{20,24},{24,28},{28,32},{32,36}... | collective-permute-start | bytes 786440 | tf_op jit(solution)/shard_map/ppermute | solution.py:171
  88.2 2.6 %collective-permute-start.17 = (bf16[512,256]{1,0:T(8,128)(2,1)S(1)}, bf16[512,256]{1,0:T(8,128)(2,1)S(1)}, u32[]{:S(2)}, u32[]{:S(2)}) collective-permute-start(bf16[512,256]{1,0:T(8,128)(2,1)S(1)} %slice.73), channel_id=1, source_target_pairs={{0,4},{4,8},{8,12},{12,16},{16,20},{20,24},{24,28},{28,32},{32,36}... | collective-permute-start | bytes 786440 | tf_op jit(solution)/shard_map/ppermute | solution.py:171
  90.8 2.9 %collective-permute-start.1 = (bf16[512,256]{1,0:T(8,128)(2,1)S(1)}, bf16[512,256]{1,0:T(8,128)(2,1)S(1)}, u32[]{:S(2)}, u32[]{:S(2)}) collective-permute-start(bf16[512,256]{1,0:T(8,128)(2,1)S(1)} %collective-permute-done.refs_1_), channel_id=1, source_target_pairs={{0,4},{4,8},{8,12},{12,16},{16,20},{20,24},{24,28},{28,32},{32,36}... | collective-permute-start | bytes 786440 | tf_op jit(solution)/shard_map/ppermute | solution.py:171
  93.8 3.6 %collective-permute-start.10 = (bf16[512,256]{1,0:T(8,128)(2,1)S(1)}, bf16[512,256]{1,0:T(8,128)(2,1)S(1)}, u32[]{:S(2)}, u32[]{:S(2)}) collective-permute-start(bf16[512,256]{1,0:T(8,128)(2,1)S(1)} %collective-permute-done.9.refs_2_), channel_id=1, source_target_pairs={{0,4},{4,8},{8,12},{12,16},{16,20},{20,24},{24,28},{28,32},{32,36}... | collective-permute-start | bytes 786440 | tf_op jit(solution)/shard_map/ppermute | solution.py:171
  97.3 2.6 %collective-permute-start.18 = (bf16[512,256]{1,0:T(8,128)(2,1)S(1)}, bf16[512,256]{1,0:T(8,128)(2,1)S(1)}, u32[]{:S(2)}, u32[]{:S(2)}) collective-permute-start(bf16[512,256]{1,0:T(8,128)(2,1)S(1)} %collective-permute-done.17), channel_id=1, source_target_pairs={{0,4},{4,8},{8,12},{12,16},{16,20},{20,24},{24,28},{28,32},{32,36}... | collective-permute-start | bytes 786440 | tf_op jit(solution)/shard_map/ppermute | solution.py:171
  100.0 2.6 %collective-permute-start.2 = (bf16[512,256]{1,0:T(8,128)(2,1)S(1)}, bf16[512,256]{1,0:T(8,128)(2,1)S(1)}, u32[]{:S(2)}, u32[]{:S(2)}) collective-permute-start(bf16[512,256]{1,0:T(8,128)(2,1)S(1)} %collective-permute-done.1.refs_3_), channel_id=1, source_target_pairs={{0,4},{4,8},{8,12},{12,16},{16,20},{20,24},{24,28},{28,32},{32,36}... | collective-permute-start | bytes 786440 | tf_op jit(solution)/shard_map/ppermute | solution.py:171
  102.7 3.0 %collective-permute-start.11 = (bf16[512,256]{1,0:T(8,128)(2,1)S(1)}, bf16[512,256]{1,0:T(8,128)(2,1)S(1)}, u32[]{:S(2)}, u32[]{:S(2)}) collective-permute-start(bf16[512,256]{1,0:T(8,128)(2,1)S(1)} %collective-permute-done.10.refs_4_), channel_id=1, source_target_pairs={{0,4},{4,8},{8,12},{12,16},{16,20},{20,24},{24,28},{28,32},{32,36}... | collective-permute-start | bytes 786440 | tf_op jit(solution)/shard_map/ppermute | solution.py:171
  105.6 2.8 %collective-permute-start.19 = (bf16[512,256]{1,0:T(8,128)(2,1)S(1)}, bf16[512,256]{1,0:T(8,128)(2,1)S(1)}, u32[]{:S(2)}, u32[]{:S(2)}) collective-permute-start(bf16[512,256]{1,0:T(8,128)(2,1)S(1)} %collective-permute-done.18), channel_id=1, source_target_pairs={{0,4},{4,8},{8,12},{12,16},{16,20},{20,24},{24,28},{28,32},{32,36}... | collective-permute-start | bytes 786440 | tf_op jit(solution)/shard_map/ppermute | solution.py:171
  108.5 0.5 compare_select_fusion.2
  109.0 2.8 %collective-permute-start.3 = (bf16[512,256]{1,0:T(8,128)(2,1)S(1)}, bf16[512,256]{1,0:T(8,128)(2,1)S(1)}, u32[]{:S(2)}, u32[]{:S(2)}) collective-permute-start(bf16[512,256]{1,0:T(8,128)(2,1)S(1)} %collective-permute-done.2.refs_5_), channel_id=1, source_target_pairs={{0,4},{4,8},{8,12},{12,16},{16,20},{20,24},{24,28},{28,32},{32,36}... | collective-permute-start | bytes 786440 | tf_op jit(solution)/shard_map/ppermute | solution.py:171
  111.8 2.8 %collective-permute-start.12 = (bf16[512,256]{1,0:T(8,128)(2,1)S(1)}, bf16[512,256]{1,0:T(8,128)(2,1)S(1)}, u32[]{:S(2)}, u32[]{:S(2)}) collective-permute-start(bf16[512,256]{1,0:T(8,128)(2,1)S(1)} %collective-permute-done.11.refs_6_), channel_id=1, source_target_pairs={{0,4},{4,8},{8,12},{12,16},{16,20},{20,24},{24,28},{28,32},{32,36}... | collective-permute-start | bytes 786440 | tf_op jit(solution)/shard_map/ppermute | solution.py:171
  114.6 2.8 %collective-permute-start.20 = (bf16[512,256]{1,0:T(8,128)(2,1)S(1)}, bf16[512,256]{1,0:T(8,128)(2,1)S(1)}, u32[]{:S(2)}, u32[]{:S(2)}) collective-permute-start(bf16[512,256]{1,0:T(8,128)(2,1)S(1)} %collective-permute-done.19), channel_id=1, source_target_pairs={{0,4},{4,8},{8,12},{12,16},{16,20},{20,24},{24,28},{28,32},{32,36}... | collective-permute-start | bytes 786440 | tf_op jit(solution)/shard_map/ppermute | solution.py:171
  117.4 2.8 %collective-permute-start.4 = (bf16[512,256]{1,0:T(8,128)(2,1)S(1)}, bf16[512,256]{1,0:T(8,128)(2,1)S(1)}, u32[]{:S(2)}, u32[]{:S(2)}) collective-permute-start(bf16[512,256]{1,0:T(8,128)(2,1)S(1)} %collective-permute-done.3.refs_7_), channel_id=1, source_target_pairs={{0,4},{4,8},{8,12},{12,16},{16,20},{20,24},{24,28},{28,32},{32,36}... | collective-permute-start | bytes 786440 | tf_op jit(solution)/shard_map/ppermute | solution.py:171
  120.2 2.6 %collective-permute-start.13 = (bf16[512,256]{1,0:T(8,128)(2,1)S(1)}, bf16[512,256]{1,0:T(8,128)(2,1)S(1)}, u32[]{:S(2)}, u32[]{:S(2)}) collective-permute-start(bf16[512,256]{1,0:T(8,128)(2,1)S(1)} %collective-permute-done.12.refs_8_), channel_id=1, source_target_pairs={{0,4},{4,8},{8,12},{12,16},{16,20},{20,24},{24,28},{28,32},{32,36}... | collective-permute-start | bytes 786440 | tf_op jit(solution)/shard_map/ppermute | solution.py:171
  122.9 2.8 %collective-permute-start.21 = (bf16[512,256]{1,0:T(8,128)(2,1)S(1)}, bf16[512,256]{1,0:T(8,128)(2,1)S(1)}, u32[]{:S(2)}, u32[]{:S(2)}) collective-permute-start(bf16[512,256]{1,0:T(8,128)(2,1)S(1)} %collective-permute-done.20), channel_id=1, source_target_pairs={{0,4},{4,8},{8,12},{12,16},{16,20},{20,24},{24,28},{28,32},{32,36}... | collective-permute-start | bytes 786440 | tf_op jit(solution)/shard_map/ppermute | solution.py:171
  125.9 2.7 %collective-permute-start.5 = (bf16[512,256]{1,0:T(8,128)(2,1)S(1)}, bf16[512,256]{1,0:T(8,128)(2,1)S(1)}, u32[]{:S(2)}, u32[]{:S(2)}) collective-permute-start(bf16[512,256]{1,0:T(8,128)(2,1)S(1)} %collective-permute-done.4.refs_9_), channel_id=1, source_target_pairs={{0,4},{4,8},{8,12},{12,16},{16,20},{20,24},{24,28},{28,32},{32,36}... | collective-permute-start | bytes 786440 | tf_op jit(solution)/shard_map/ppermute | solution.py:171
  128.6 2.8 %collective-permute-start.14 = (bf16[512,256]{1,0:T(8,128)(2,1)S(1)}, bf16[512,256]{1,0:T(8,128)(2,1)S(1)}, u32[]{:S(2)}, u32[]{:S(2)}) collective-permute-start(bf16[512,256]{1,0:T(8,128)(2,1)S(1)} %collective-permute-done.13.refs_10_), channel_id=1, source_target_pairs={{0,4},{4,8},{8,12},{12,16},{16,20},{20,24},{24,28},{28,32},{32,36}... | collective-permute-start | bytes 786440 | tf_op jit(solution)/shard_map/ppermute | solution.py:171
  131.4 2.8 %collective-permute-start.22 = (bf16[512,256]{1,0:T(8,128)(2,1)S(1)}, bf16[512,256]{1,0:T(8,128)(2,1)S(1)}, u32[]{:S(2)}, u32[]{:S(2)}) collective-permute-start(bf16[512,256]{1,0:T(8,128)(2,1)S(1)} %collective-permute-done.21), channel_id=1, source_target_pairs={{0,4},{4,8},{8,12},{12,16},{16,20},{20,24},{24,28},{28,32},{32,36}... | collective-permute-start | bytes 786440 | tf_op jit(solution)/shard_map/ppermute | solution.py:171
  134.2 0.1 pad_maximum_fusion.1
  134.3 7.3 %collective-permute-start.27 = (bf16[3,768,256]{2,1,0:T(8,128)(2,1)S(1)}, bf16[3,768,256]{2,1,0:T(8,128)(2,1)S(1)}, u32[]{:S(2)}, u32[]{:S(2)}) collective-permute-start(bf16[3,768,256]{2,1,0:T(8,128)(2,1)S(1)} %pad_maximum_fusion.1), channel_id=1, source_target_pairs={{0,64},{64,0},{1,65},{65,1},{2,66},{66,2},{3,67},{67,3},{4,68},{68... | collective-permute-start | bytes 3538952 | tf_op jit(solution)/shard_map/ppermute | solution.py:190
  141.7 3.8 %collective-permute-start.6 = (bf16[512,256]{1,0:T(8,128)(2,1)S(1)}, bf16[512,256]{1,0:T(8,128)(2,1)S(1)}, u32[]{:S(2)}, u32[]{:S(2)}) collective-permute-start(bf16[512,256]{1,0:T(8,128)(2,1)S(1)} %collective-permute-done.5.refs_11_), channel_id=1, source_target_pairs={{0,4},{4,8},{8,12},{12,16},{16,20},{20,24},{24,28},{28,32},{32,36}... | collective-permute-start | bytes 786440 | tf_op jit(solution)/shard_map/ppermute | solution.py:171
  145.6 0.1 pad_maximum_fusion
  145.8 2.4 %collective-permute-start.26 = (bf16[3,768,256]{2,1,0:T(8,128)(2,1)S(1)}, bf16[3,768,256]{2,1,0:T(8,128)(2,1)S(1)}, u32[]{:S(2)}, u32[]{:S(2)}) collective-permute-start(bf16[3,768,256]{2,1,0:T(8,128)(2,1)S(1)} %pad_maximum_fusion), channel_id=1, source_target_pairs={{0,64},{64,0},{1,65},{65,1},{2,66},{66,2},{3,67},{67,3},{4,68},{68... | collective-permute-start | bytes 3538952 | tf_op jit(solution)/shard_map/ppermute | solution.py:190
  148.2 0.1 pad_add_fusion.2.which
  148.2 2.5 %collective-permute-start.15 = (bf16[512,256]{1,0:T(8,128)(2,1)S(1)}, bf16[512,256]{1,0:T(8,128)(2,1)S(1)}, u32[]{:S(2)}, u32[]{:S(2)}) collective-permute-start(bf16[512,256]{1,0:T(8,128)(2,1)S(1)} %collective-permute-done.14.refs_12_), channel_id=1, source_target_pairs={{0,4},{4,8},{8,12},{12,16},{16,20},{20,24},{24,28},{28,32},{32,36}... | collective-permute-start | bytes 786440 | tf_op jit(solution)/shard_map/ppermute | solution.py:171
  150.8 0.1 pad_add_fusion.1.which
  150.8 0.1 select_reduce_fusion.2
  150.9 2.9 %collective-permute-start.23 = (bf16[512,256]{1,0:T(8,128)(2,1)S(1)}, bf16[512,256]{1,0:T(8,128)(2,1)S(1)}, u32[]{:S(2)}, u32[]{:S(2)}) collective-permute-start(bf16[512,256]{1,0:T(8,128)(2,1)S(1)} %collective-permute-done.22), channel_id=1, source_target_pairs={{0,4},{4,8},{8,12},{12,16},{16,20},{20,24},{24,28},{28,32},{32,36}... | collective-permute-start | bytes 786440 | tf_op jit(solution)/shard_map/ppermute | solution.py:171
  153.8 0.1 pad_add_fusion.which
  153.9 0.2 broadcast_in_dim.80.refs_6_
  154.0 1.6 collective-permute-done.15.refs_1_
  155.6 3.4 %collective-permute-start.7 = (bf16[512,256]{1,0:T(8,128)(2,1)S(1)}, bf16[512,256]{1,0:T(8,128)(2,1)S(1)}, u32[]{:S(2)}, u32[]{:S(2)}) collective-permute-start(bf16[512,256]{1,0:T(8,128)(2,1)S(1)} %collective-permute-done.6.refs_0_), channel_id=1, source_target_pairs={{0,4},{4,8},{8,12},{12,16},{16,20},{20,24},{24,28},{28,32},{32,36}... | collective-permute-start | bytes 786440 | tf_op jit(solution)/shard_map/ppermute | solution.py:171
  159.1 3.4 %collective-permute-start.24 = (bf16[1,768,256]{2,1,0:T(8,128)(2,1)S(1)}, bf16[1,768,256]{2,1,0:T(8,128)(2,1)S(1)}, u32[]{:S(2)}, u32[]{:S(2)}) collective-permute-start(bf16[1,768,256]{2,1,0:T(8,128)(2,1)S(1)} %maximum_bitcast_fusion), channel_id=1, source_target_pairs={{0,64},{64,0},{1,65},{65,1},{2,66},{66,2},{3,67},{67,3},{4,68},{68... | collective-permute-start | bytes 1179656 | tf_op jit(solution)/shard_map/ppermute | solution.py:190
  162.6 3.9 %collective-permute-start.16 = (bf16[256,256]{1,0:T(8,128)(2,1)S(1)}, bf16[256,256]{1,0:T(8,128)(2,1)S(1)}, u32[]{:S(2)}, u32[]{:S(2)}) collective-permute-start(bf16[256,256]{1,0:T(8,128)(2,1)S(1)} %get-tuple-element.11), channel_id=1, source_target_pairs={{0,4},{4,8},{8,12},{12,16},{16,20},{20,24},{24,28},{28,32},{32,36}... | collective-permute-start | bytes 393224 | tf_op jit(solution)/shard_map/ppermute | solution.py:171
  166.5 6.6 %shard_map.95.refs_5_ = f32[768,1024]{1,0:T(8,128)S(1)} custom-call(s32[11]{0:T(128)S(1)} %pad_add_fusion.2.which, bf16[768,256]{1,0:T(8,128)(2,1)S(1)} %bitcast.33, bf16[512,256]{1,0:T(8,128)(2,1)S(1)} %collective-permute-done.refs_1_, bf16[512,256]{1,0:T(8,128)(2,1)S(1)} %collective-permute-done.9.refs_2_, ...), custom_call_target="tpu_custom_call" | custom-call | flops 4026531840 | bytes 9175040 | tf_op jit(solution)/shard_map/pallas_call | solution.py:145
  173.2 3.9 %shard_map.96.refs_5_ = f32[768,1024]{1,0:T(8,128)S(1)} custom-call(s32[5]{0:T(128)S(1)} %pad_add_fusion.1.which, bf16[512,256]{1,0:T(8,128)(2,1)S(1)} %collective-permute-done.6.refs_0_, bf16[512,256]{1,0:T(8,128)(2,1)S(1)} %collective-permute-done.15.refs_1_, ...), custom_call_target="tpu_custom_call", output_to_operand_aliasing={{}: (6, {})} | custom-call | flops 1610612736 | bytes 3670016 | tf_op jit(solution)/shard_map/pallas_call | solution.py:145
  177.1 3.5 %shard_map.97 = f32[8,768]{1,0:T(8,128)S(1)} custom-call(s32[3]{0:T(128)S(1)} %pad_add_fusion.which, bf16[512,256]{1,0:T(8,128)(2,1)S(1)} %collective-permute-done.7.refs_0_, bf16[256,256]{1,0:T(8,128)(2,1)S(1)} %collective-permute-done.16.refs_1_, bf16[1,768,256]{2,1,0:T(8,128)(2,1)S(1)} %collective-permute-done.24.refs_2_, ...), custom_call_target="tpu_custom_call" | custom-call | flops 805306368 | bytes 1835008 | tf_op jit(solution)/shard_map/pallas_call | solution.py:145
  180.7 0.1 reshape.132
  180.8 0.1 broadcast_in_dim.74
  181.0 0.8 all_to_all.18
  181.7 7.4 %all-to-all-start.2 = ((f32[64,1,384]{2,1,0:T(1,128)}), f32[64,1,384]{2,1,0:T(1,128)S(1)}, u32[]{:S(2)}, u32[]{:S(2)}) async-start(f32[64,1,384]{2,1,0:T(1,128)} %all_to_all.18), calls=%async_computation.2 | async-start | bytes 196608 | tf_op jit(solution)/shard_map/all_to_all | solution.py:46
  189.2 0.1 reshape.134
  189.3 0.1 eq.23
  189.4 0.1 reduce_sum.57
  189.6 15.7 %all-to-all-done.2 = f32[64,1,384]{2,1,0:T(1,128)S(1)} async-done(((f32[64,1,384]{2,1,0:T(1,128)}), f32[64,1,384]{2,1,0:T(1,128)S(1)}, u32[]{:S(2)}, u32[]{:S(2)}) %all-to-all-start.2) | async-done | bytes 98336 | tf_op jit(solution)/shard_map/all_to_all | solution.py:46
  205.3 0.2 reduce.3
  205.5 0.1 reshape.133
  205.7 0.2 slice_reduce_fusion.1
  205.9 0.1 select_reduce_fusion.1
  206.0 0.1 pad_maximum_fusion.3
  206.1 0.6 broadcast_in_dim.79
  206.7 3.7 %all-to-all-start.3 = ((f32[32,1,128]{2,1,0:T(1,128)}), f32[32,1,128]{2,1,0:T(1,128)S(1)}, u32[]{:S(2)}, u32[]{:S(2)}) async-start(f32[32,1,128]{2,1,0:T(1,128)} %broadcast_in_dim.79), calls=%async_computation.3 | async-start | bytes 32768 | tf_op jit(solution)/shard_map/all_to_all | solution.py:29
  210.5 0.1 sub.49
  210.6 0.5 fusion.21
  211.1 6.3 %all-to-all-done.3 = f32[32,1,128]{2,1,0:T(1,128)S(1)} async-done(((f32[32,1,128]{2,1,0:T(1,128)}), f32[32,1,128]{2,1,0:T(1,128)S(1)}, u32[]{:S(2)}, u32[]{:S(2)}) %all-to-all-start.3) | async-done | bytes 16416 | tf_op jit(solution)/shard_map/all_to_all | solution.py:29
  217.4 0.6 maximum_divide_fusion
  (76 shorter events, 0.8 us)
Async XLA Ops:
  2.4 56.5 %copy-start = (bf16[768,64]{0,1:T(8,128)(2,1)S(1)}, bf16[768,64]{0,1:T(8,128)(2,1)}, u32[]{:S(2)}) copy-start(bf16[768,64]{0,1:T(8,128)(2,1)} %param.8) | copy-start | bytes 294916
  50.4 116.2 %collective-permute-start.25 = (bf16[4,512,1024]{2,1,0:T(8,128)(2,1)}, bf16[4,512,1024]{2,1,0:T(8,128)(2,1)}, u32[]{:S(2)}, u32[]{:S(2)}) collective-permute-start(bf16[4,512,1024]{2,1,0:T(8,128)(2,1)} %all_to_all.25.refs_14_.refs_3_), channel_id=1, source_target_pairs={{0,64},{64,0},{1,65},{65,1},{2,66},{66,2},{3,67},{67,3},{4,68},{68... | collective-permute-start | bytes 12582920 | tf_op jit(solution)/shard_map/ppermute | solution.py:36
  71.0 29.0 %copy-start.7 = (s32[10]{0:T(128)S(1)}, s32[10]{0:T(128)}, u32[]{:S(2)}) copy-start(s32[10]{0:T(128)} %constant.104.clone) | copy-start | bytes 124
  71.0 37.4 %copy-start.6 = (s32[4]{0:T(128)S(1)}, s32[4]{0:T(128)}, u32[]{:S(2)}) copy-start(s32[4]{0:T(128)} %constant.105.clone) | copy-start | bytes 52
  71.0 37.9 %copy-start.5 = (s32[2]{0:T(128)S(1)}, s32[2]{0:T(128)}, u32[]{:S(2)}) copy-start(s32[2]{0:T(128)} %constant.106.clone) | copy-start | bytes 28
  71.0 46.3 %copy-start.2 = (s32[768]{0:T(1024)S(1)}, s32[768]{0:T(1024)}, u32[]{:S(2)}) copy-start(s32[768]{0:T(1024)} %param.10) | copy-start | bytes 9220
  71.1 14.4 %collective-permute-start.8 = (bf16[768,256]{1,0:T(8,128)(2,1)S(1)}, bf16[768,256]{1,0:T(8,128)(2,1)S(1)}, u32[]{:S(2)}, u32[]{:S(2)}) collective-permute-start(bf16[768,256]{1,0:T(8,128)(2,1)S(1)} %bitcast.30), channel_id=1, source_target_pairs={{0,64},{64,0},{1,65},{65,1},{2,66},{66,2},{3,67},{67,3},{4,68},{68... | collective-permute-start | bytes 1179656 | tf_op jit(solution)/shard_map/ppermute | solution.py:179
  74.3 16.5 %collective-permute-start = (bf16[512,256]{1,0:T(8,128)(2,1)S(1)}, bf16[512,256]{1,0:T(8,128)(2,1)S(1)}, u32[]{:S(2)}, u32[]{:S(2)}) collective-permute-start(bf16[512,256]{1,0:T(8,128)(2,1)S(1)} %slice.69), channel_id=1, source_target_pairs={{0,4},{4,8},{8,12},{12,16},{16,20},{20,24},{24,28},{28,32},{32,36}... | collective-permute-start | bytes 786440 | tf_op jit(solution)/shard_map/ppermute | solution.py:171
  85.5 8.3 %collective-permute-start.9 = (bf16[512,256]{1,0:T(8,128)(2,1)S(1)}, bf16[512,256]{1,0:T(8,128)(2,1)S(1)}, u32[]{:S(2)}, u32[]{:S(2)}) collective-permute-start(bf16[512,256]{1,0:T(8,128)(2,1)S(1)} %pad_maximum_fusion.2), channel_id=1, source_target_pairs={{0,4},{4,8},{8,12},{12,16},{16,20},{20,24},{24,28},{28,32},{32,36}... | collective-permute-start | bytes 786440 | tf_op jit(solution)/shard_map/ppermute | solution.py:171
  88.2 9.2 %collective-permute-start.17 = (bf16[512,256]{1,0:T(8,128)(2,1)S(1)}, bf16[512,256]{1,0:T(8,128)(2,1)S(1)}, u32[]{:S(2)}, u32[]{:S(2)}) collective-permute-start(bf16[512,256]{1,0:T(8,128)(2,1)S(1)} %slice.73), channel_id=1, source_target_pairs={{0,4},{4,8},{8,12},{12,16},{16,20},{20,24},{24,28},{28,32},{32,36}... | collective-permute-start | bytes 786440 | tf_op jit(solution)/shard_map/ppermute | solution.py:171
  90.8 9.2 %collective-permute-start.1 = (bf16[512,256]{1,0:T(8,128)(2,1)S(1)}, bf16[512,256]{1,0:T(8,128)(2,1)S(1)}, u32[]{:S(2)}, u32[]{:S(2)}) collective-permute-start(bf16[512,256]{1,0:T(8,128)(2,1)S(1)} %collective-permute-done.refs_1_), channel_id=1, source_target_pairs={{0,4},{4,8},{8,12},{12,16},{16,20},{20,24},{24,28},{28,32},{32,36}... | collective-permute-start | bytes 786440 | tf_op jit(solution)/shard_map/ppermute | solution.py:171
  93.8 8.9 %collective-permute-start.10 = (bf16[512,256]{1,0:T(8,128)(2,1)S(1)}, bf16[512,256]{1,0:T(8,128)(2,1)S(1)}, u32[]{:S(2)}, u32[]{:S(2)}) collective-permute-start(bf16[512,256]{1,0:T(8,128)(2,1)S(1)} %collective-permute-done.9.refs_2_), channel_id=1, source_target_pairs={{0,4},{4,8},{8,12},{12,16},{16,20},{20,24},{24,28},{28,32},{32,36}... | collective-permute-start | bytes 786440 | tf_op jit(solution)/shard_map/ppermute | solution.py:171
  97.3 8.3 %collective-permute-start.18 = (bf16[512,256]{1,0:T(8,128)(2,1)S(1)}, bf16[512,256]{1,0:T(8,128)(2,1)S(1)}, u32[]{:S(2)}, u32[]{:S(2)}) collective-permute-start(bf16[512,256]{1,0:T(8,128)(2,1)S(1)} %collective-permute-done.17), channel_id=1, source_target_pairs={{0,4},{4,8},{8,12},{12,16},{16,20},{20,24},{24,28},{28,32},{32,36}... | collective-permute-start | bytes 786440 | tf_op jit(solution)/shard_map/ppermute | solution.py:171
  100.0 9.0 %collective-permute-start.2 = (bf16[512,256]{1,0:T(8,128)(2,1)S(1)}, bf16[512,256]{1,0:T(8,128)(2,1)S(1)}, u32[]{:S(2)}, u32[]{:S(2)}) collective-permute-start(bf16[512,256]{1,0:T(8,128)(2,1)S(1)} %collective-permute-done.1.refs_3_), channel_id=1, source_target_pairs={{0,4},{4,8},{8,12},{12,16},{16,20},{20,24},{24,28},{28,32},{32,36}... | collective-permute-start | bytes 786440 | tf_op jit(solution)/shard_map/ppermute | solution.py:171
  102.7 9.1 %collective-permute-start.11 = (bf16[512,256]{1,0:T(8,128)(2,1)S(1)}, bf16[512,256]{1,0:T(8,128)(2,1)S(1)}, u32[]{:S(2)}, u32[]{:S(2)}) collective-permute-start(bf16[512,256]{1,0:T(8,128)(2,1)S(1)} %collective-permute-done.10.refs_4_), channel_id=1, source_target_pairs={{0,4},{4,8},{8,12},{12,16},{16,20},{20,24},{24,28},{28,32},{32,36}... | collective-permute-start | bytes 786440 | tf_op jit(solution)/shard_map/ppermute | solution.py:171
  105.6 8.9 %collective-permute-start.19 = (bf16[512,256]{1,0:T(8,128)(2,1)S(1)}, bf16[512,256]{1,0:T(8,128)(2,1)S(1)}, u32[]{:S(2)}, u32[]{:S(2)}) collective-permute-start(bf16[512,256]{1,0:T(8,128)(2,1)S(1)} %collective-permute-done.18), channel_id=1, source_target_pairs={{0,4},{4,8},{8,12},{12,16},{16,20},{20,24},{24,28},{28,32},{32,36}... | collective-permute-start | bytes 786440 | tf_op jit(solution)/shard_map/ppermute | solution.py:171
  109.0 8.4 %collective-permute-start.3 = (bf16[512,256]{1,0:T(8,128)(2,1)S(1)}, bf16[512,256]{1,0:T(8,128)(2,1)S(1)}, u32[]{:S(2)}, u32[]{:S(2)}) collective-permute-start(bf16[512,256]{1,0:T(8,128)(2,1)S(1)} %collective-permute-done.2.refs_5_), channel_id=1, source_target_pairs={{0,4},{4,8},{8,12},{12,16},{16,20},{20,24},{24,28},{28,32},{32,36}... | collective-permute-start | bytes 786440 | tf_op jit(solution)/shard_map/ppermute | solution.py:171
  111.8 8.5 %collective-permute-start.12 = (bf16[512,256]{1,0:T(8,128)(2,1)S(1)}, bf16[512,256]{1,0:T(8,128)(2,1)S(1)}, u32[]{:S(2)}, u32[]{:S(2)}) collective-permute-start(bf16[512,256]{1,0:T(8,128)(2,1)S(1)} %collective-permute-done.11.refs_6_), channel_id=1, source_target_pairs={{0,4},{4,8},{8,12},{12,16},{16,20},{20,24},{24,28},{28,32},{32,36}... | collective-permute-start | bytes 786440 | tf_op jit(solution)/shard_map/ppermute | solution.py:171
  114.6 8.3 %collective-permute-start.20 = (bf16[512,256]{1,0:T(8,128)(2,1)S(1)}, bf16[512,256]{1,0:T(8,128)(2,1)S(1)}, u32[]{:S(2)}, u32[]{:S(2)}) collective-permute-start(bf16[512,256]{1,0:T(8,128)(2,1)S(1)} %collective-permute-done.19), channel_id=1, source_target_pairs={{0,4},{4,8},{8,12},{12,16},{16,20},{20,24},{24,28},{28,32},{32,36}... | collective-permute-start | bytes 786440 | tf_op jit(solution)/shard_map/ppermute | solution.py:171
  117.4 8.4 %collective-permute-start.4 = (bf16[512,256]{1,0:T(8,128)(2,1)S(1)}, bf16[512,256]{1,0:T(8,128)(2,1)S(1)}, u32[]{:S(2)}, u32[]{:S(2)}) collective-permute-start(bf16[512,256]{1,0:T(8,128)(2,1)S(1)} %collective-permute-done.3.refs_7_), channel_id=1, source_target_pairs={{0,4},{4,8},{8,12},{12,16},{16,20},{20,24},{24,28},{28,32},{32,36}... | collective-permute-start | bytes 786440 | tf_op jit(solution)/shard_map/ppermute | solution.py:171
  120.2 8.3 %collective-permute-start.13 = (bf16[512,256]{1,0:T(8,128)(2,1)S(1)}, bf16[512,256]{1,0:T(8,128)(2,1)S(1)}, u32[]{:S(2)}, u32[]{:S(2)}) collective-permute-start(bf16[512,256]{1,0:T(8,128)(2,1)S(1)} %collective-permute-done.12.refs_8_), channel_id=1, source_target_pairs={{0,4},{4,8},{8,12},{12,16},{16,20},{20,24},{24,28},{28,32},{32,36}... | collective-permute-start | bytes 786440 | tf_op jit(solution)/shard_map/ppermute | solution.py:171
  122.9 8.5 %collective-permute-start.21 = (bf16[512,256]{1,0:T(8,128)(2,1)S(1)}, bf16[512,256]{1,0:T(8,128)(2,1)S(1)}, u32[]{:S(2)}, u32[]{:S(2)}) collective-permute-start(bf16[512,256]{1,0:T(8,128)(2,1)S(1)} %collective-permute-done.20), channel_id=1, source_target_pairs={{0,4},{4,8},{8,12},{12,16},{16,20},{20,24},{24,28},{28,32},{32,36}... | collective-permute-start | bytes 786440 | tf_op jit(solution)/shard_map/ppermute | solution.py:171
  125.9 15.8 %collective-permute-start.5 = (bf16[512,256]{1,0:T(8,128)(2,1)S(1)}, bf16[512,256]{1,0:T(8,128)(2,1)S(1)}, u32[]{:S(2)}, u32[]{:S(2)}) collective-permute-start(bf16[512,256]{1,0:T(8,128)(2,1)S(1)} %collective-permute-done.4.refs_9_), channel_id=1, source_target_pairs={{0,4},{4,8},{8,12},{12,16},{16,20},{20,24},{24,28},{28,32},{32,36}... | collective-permute-start | bytes 786440 | tf_op jit(solution)/shard_map/ppermute | solution.py:171
  128.6 17.0 %collective-permute-start.14 = (bf16[512,256]{1,0:T(8,128)(2,1)S(1)}, bf16[512,256]{1,0:T(8,128)(2,1)S(1)}, u32[]{:S(2)}, u32[]{:S(2)}) collective-permute-start(bf16[512,256]{1,0:T(8,128)(2,1)S(1)} %collective-permute-done.13.refs_10_), channel_id=1, source_target_pairs={{0,4},{4,8},{8,12},{12,16},{16,20},{20,24},{24,28},{28,32},{32,36}... | collective-permute-start | bytes 786440 | tf_op jit(solution)/shard_map/ppermute | solution.py:171
  131.4 14.2 %collective-permute-start.22 = (bf16[512,256]{1,0:T(8,128)(2,1)S(1)}, bf16[512,256]{1,0:T(8,128)(2,1)S(1)}, u32[]{:S(2)}, u32[]{:S(2)}) collective-permute-start(bf16[512,256]{1,0:T(8,128)(2,1)S(1)} %collective-permute-done.21), channel_id=1, source_target_pairs={{0,4},{4,8},{8,12},{12,16},{16,20},{20,24},{24,28},{28,32},{32,36}... | collective-permute-start | bytes 786440 | tf_op jit(solution)/shard_map/ppermute | solution.py:171
  134.3 28.3 %collective-permute-start.27 = (bf16[3,768,256]{2,1,0:T(8,128)(2,1)S(1)}, bf16[3,768,256]{2,1,0:T(8,128)(2,1)S(1)}, u32[]{:S(2)}, u32[]{:S(2)}) collective-permute-start(bf16[3,768,256]{2,1,0:T(8,128)(2,1)S(1)} %pad_maximum_fusion.1), channel_id=1, source_target_pairs={{0,64},{64,0},{1,65},{65,1},{2,66},{66,2},{3,67},{67,3},{4,68},{68... | collective-permute-start | bytes 3538952 | tf_op jit(solution)/shard_map/ppermute | solution.py:190
  141.7 9.3 %collective-permute-start.6 = (bf16[512,256]{1,0:T(8,128)(2,1)S(1)}, bf16[512,256]{1,0:T(8,128)(2,1)S(1)}, u32[]{:S(2)}, u32[]{:S(2)}) collective-permute-start(bf16[512,256]{1,0:T(8,128)(2,1)S(1)} %collective-permute-done.5.refs_11_), channel_id=1, source_target_pairs={{0,4},{4,8},{8,12},{12,16},{16,20},{20,24},{24,28},{28,32},{32,36}... | collective-permute-start | bytes 786440 | tf_op jit(solution)/shard_map/ppermute | solution.py:171
  145.6 5.1 %copy-start.4 = (s32[4]{0:T(128)S(1)}, s32[4]{0:T(128)}, u32[]{:S(2)}) copy-start(s32[4]{0:T(128)} %compare_select_fusion.2) | copy-start | bytes 52
  145.6 5.2 %copy-start.3 = (s32[6]{0:T(128)S(1)}, s32[6]{0:T(128)}, u32[]{:S(2)}) copy-start(s32[6]{0:T(128)} %param.12) | copy-start | bytes 76
  145.8 27.4 %collective-permute-start.26 = (bf16[3,768,256]{2,1,0:T(8,128)(2,1)S(1)}, bf16[3,768,256]{2,1,0:T(8,128)(2,1)S(1)}, u32[]{:S(2)}, u32[]{:S(2)}) collective-permute-start(bf16[3,768,256]{2,1,0:T(8,128)(2,1)S(1)} %pad_maximum_fusion), channel_id=1, source_target_pairs={{0,64},{64,0},{1,65},{65,1},{2,66},{66,2},{3,67},{67,3},{4,68},{68... | collective-permute-start | bytes 3538952 | tf_op jit(solution)/shard_map/ppermute | solution.py:190
  148.2 7.4 %collective-permute-start.15 = (bf16[512,256]{1,0:T(8,128)(2,1)S(1)}, bf16[512,256]{1,0:T(8,128)(2,1)S(1)}, u32[]{:S(2)}, u32[]{:S(2)}) collective-permute-start(bf16[512,256]{1,0:T(8,128)(2,1)S(1)} %collective-permute-done.14.refs_12_), channel_id=1, source_target_pairs={{0,4},{4,8},{8,12},{12,16},{16,20},{20,24},{24,28},{28,32},{32,36}... | collective-permute-start | bytes 786440 | tf_op jit(solution)/shard_map/ppermute | solution.py:171
  150.9 8.2 %collective-permute-start.23 = (bf16[512,256]{1,0:T(8,128)(2,1)S(1)}, bf16[512,256]{1,0:T(8,128)(2,1)S(1)}, u32[]{:S(2)}, u32[]{:S(2)}) collective-permute-start(bf16[512,256]{1,0:T(8,128)(2,1)S(1)} %collective-permute-done.22), channel_id=1, source_target_pairs={{0,4},{4,8},{8,12},{12,16},{16,20},{20,24},{24,28},{28,32},{32,36}... | collective-permute-start | bytes 786440 | tf_op jit(solution)/shard_map/ppermute | solution.py:171
  155.6 21.5 %collective-permute-start.7 = (bf16[512,256]{1,0:T(8,128)(2,1)S(1)}, bf16[512,256]{1,0:T(8,128)(2,1)S(1)}, u32[]{:S(2)}, u32[]{:S(2)}) collective-permute-start(bf16[512,256]{1,0:T(8,128)(2,1)S(1)} %collective-permute-done.6.refs_0_), channel_id=1, source_target_pairs={{0,4},{4,8},{8,12},{12,16},{16,20},{20,24},{24,28},{28,32},{32,36}... | collective-permute-start | bytes 786440 | tf_op jit(solution)/shard_map/ppermute | solution.py:171
  159.1 18.0 %collective-permute-start.24 = (bf16[1,768,256]{2,1,0:T(8,128)(2,1)S(1)}, bf16[1,768,256]{2,1,0:T(8,128)(2,1)S(1)}, u32[]{:S(2)}, u32[]{:S(2)}) collective-permute-start(bf16[1,768,256]{2,1,0:T(8,128)(2,1)S(1)} %maximum_bitcast_fusion), channel_id=1, source_target_pairs={{0,64},{64,0},{1,65},{65,1},{2,66},{66,2},{3,67},{67,3},{4,68},{68... | collective-permute-start | bytes 1179656 | tf_op jit(solution)/shard_map/ppermute | solution.py:190
  162.6 14.5 %collective-permute-start.16 = (bf16[256,256]{1,0:T(8,128)(2,1)S(1)}, bf16[256,256]{1,0:T(8,128)(2,1)S(1)}, u32[]{:S(2)}, u32[]{:S(2)}) collective-permute-start(bf16[256,256]{1,0:T(8,128)(2,1)S(1)} %get-tuple-element.11), channel_id=1, source_target_pairs={{0,4},{4,8},{8,12},{12,16},{16,20},{20,24},{24,28},{28,32},{32,36}... | collective-permute-start | bytes 393224 | tf_op jit(solution)/shard_map/ppermute | solution.py:171
  177.1 12.1 %copy-start.1 = (s32[768]{0:T(1024)S(1)}, s32[768]{0:T(1024)}, u32[]{:S(2)}) copy-start(s32[768]{0:T(1024)} %param.11) | copy-start | bytes 9220
  181.7 23.6 %all-to-all-start.2 = ((f32[64,1,384]{2,1,0:T(1,128)}), f32[64,1,384]{2,1,0:T(1,128)S(1)}, u32[]{:S(2)}, u32[]{:S(2)}) async-start(f32[64,1,384]{2,1,0:T(1,128)} %all_to_all.18), calls=%async_computation.2 | async-start | bytes 196608 | tf_op jit(solution)/shard_map/all_to_all | solution.py:46
  206.7 10.7 %all-to-all-start.3 = ((f32[32,1,128]{2,1,0:T(1,128)}), f32[32,1,128]{2,1,0:T(1,128)S(1)}, u32[]{:S(2)}, u32[]{:S(2)}) async-start(f32[32,1,128]{2,1,0:T(1,128)} %broadcast_in_dim.79), calls=%async_computation.3 | async-start | bytes 32768 | tf_op jit(solution)/shard_map/all_to_all | solution.py:29

commit v5 on v4

--- a/solution.py
+++ b/solution.py
@@ -19,8 +19,8 @@
 ROUNDS = 8
 BATCHES = ((1, 2, 3), (4, 5, 6), (7,))
 GROUPS = (
-    ("early", range(0, 7), (0,)),
-    ("middle", (7,), (1,)),
+    ("early", range(0, 6), (0,)),
+    ("middle", (6, 7), (1,)),
     ("late", (8,), (2,)),
 )
 
@@ -177,17 +177,14 @@
     weights = gathered_weight(weight)
     mine = to_all(hidden.T, "y", ys).reshape(BLOCK, -1).T
     theirs = lax.ppermute(mine, "c", SWAP)
-    a, b = [mine[:LONG]], [jnp.concatenate([mine[LONG:], theirs[LONG:]], 0)]
-    c = [theirs[:LONG]]
+    own, other = [mine], [theirs]
     for r in range(1, ROUNDS + 1):
-        a.append(along_z(a[-1]))
-        b.append(along_z(b[-1] if r < ROUNDS else b[-1][: mine.shape[0] - LONG]))
+        own.append(along_z(own[-1]))
         if r < ROUNDS:
-            c.append(along_z(c[-1]))
+            other.append(along_z(other[-1]))
     swapped = []
     for some in BATCHES:
-        give = [jnp.concatenate([c[r], b[r][mine.shape[0] - LONG :]], 0) for r in some]
-        swapped.append(lax.ppermute(jnp.stack(give), "c", SWAP))
+        swapped.append(lax.ppermute(jnp.stack([other[r] for r in some]), "c", SWAP))
     step = 2 * core - 1
     wanted = (targets - lax.axis_index(VOCAB) * weight.shape[1])[:, None]
     logits = None
@@ -195,7 +192,7 @@
         away = [r for r in rounds] + [-r for k in batches for r in BATCHES[k]]
         which = lax.rem(z + step * jnp.array(away, jnp.int32) + zs, zs)
         which = jnp.concatenate([which, core[None]])
-        blocks = [(a[r], b[r]) if r else mine for r in rounds] + [swapped[k] for k in batches]
+        blocks = [own[r] for r in rounds] + [swapped[k] for k in batches]
         logits = product(which, blocks, weights, logits, wanted if name == "late" else None)
     return tail(logits[:2], domains, seq_len)
 

time: 219 us -> 230 us (1.050)
  blocking collectives: 59.8 us -> 48 us
  starting transfers between devices: 111 us -> 118 us
  local copies, waits for them, and re-layouts: 4.44 us -> 11 us
  waiting for transfers between devices: 23.7 us -> 30 us
  other arithmetic: 3.21 us -> 6.96 us
    all_to_all x2 -> x1, blocking collectives: 59.8 us -> 48 us  [to_all(): lax.all_to_all(jnp.broadcast_to(array[None], (copies, *array.shape)), axi...]
    all_to_all x1 -> x2, starting transfers between devices: 3.75 us -> 15.3 us  [to_all(): lax.all_to_all(jnp.broadcast_to(array[None], (copies, *array.shape)), axi...]
    unnamed x16 -> x28, local copies, waits for them, and re-layouts: 0.05 us -> 5.98 us
    ppermute x1, starting transfers between devices: 8.56 us -> 3.99 us  [gathered_weight(): return (own, lax.ppermute(own, 'c', SWAP))]
    ppermute x23 -> x15, starting transfers between devices: 75.2 us -> 70.8 us  [along_z(): return lax.ppermute(array, ('c', 'z'), pairs)]
    ppermute x23 -> x15, waiting for transfers between devices: 1.66 us -> 5.78 us  [along_z(): return lax.ppermute(array, ('c', 'z'), pairs)]
    all_to_all x1, starting transfers between devices: 7.43 us -> 11.2 us  [tail(): got = lax.all_to_all(send.reshape(zs * ys, -1), VOCAB, 0, 0, tiled=True)]
    another operation x9 -> x2, other arithmetic: 0.46 us -> 3.56 us  [loss(): swapped.append(lax.ppermute(jnp.stack([other[r] for r in some]), 'c', SWAP))]
  transfers between devices with their start and end apart: 30 -> 23, of which waited for: 3 -> 9; matrix products, arithmetic and copies ran while one was open for 1% -> 3% of each run, Pallas kernels for 5% -> 4%
where the time goes in v5:
time: 230 us; the launch traced here: 229 us
  starting transfers between devices  118 us (51%)
  blocking collectives  48 us (21%)
  waiting for transfers between devices  30 us (13%)
  Pallas kernels  13.8 us (6%)
  local copies, waits for them, and re-layouts  11 us (5%)
  other arithmetic  6.96 us (3%)
    ppermute x15, starting transfers between devices, along_z(): return lax.ppermute(array, ('c', 'z'), pairs)  70.8 us
    all_to_all x1, blocking collectives, to_all(): lax.all_to_all(jnp.broadcast_to(array[None], (copies, *array.shape)), axi...  48 us
    all_to_all x2, starting transfers between devices, to_all(): lax.all_to_all(jnp.broadcast_to(array[None], (copies, *array.shape)), axi...  15.3 us
    all_to_all x1, waiting for transfers between devices, tail(): got = lax.all_to_all(send.reshape(zs * ys, -1), VOCAB, 0, 0, tiled=True)  14.3 us
    pallas_call x3, Pallas kernels, product(): pl.pallas_call(product_kernel(kinds, before is None, last), in_specs=[pl....  13.8 us
    ppermute x3, starting transfers between devices, loss(): swapped.append(lax.ppermute(jnp.stack([other[r] for r in some]), 'c', SWAP))  11.8 us
    all_to_all x1, starting transfers between devices, tail(): got = lax.all_to_all(send.reshape(zs * ys, -1), VOCAB, 0, 0, tiled=True)  11.2 us
    all_to_all x2, waiting for transfers between devices, to_all(): lax.all_to_all(jnp.broadcast_to(array[None], (copies, *array.shape)), axi...  8.56 us
  transfers between devices with their start and end apart: 23, of which 9 were waited for; matrix products, arithmetic and copies ran while one was open for 3% of the time, Pallas kernels for 4%

profile of v5, /device:TPU:1, one launch (start us, length us, event | category | flops | bytes accessed | tf_op | source)
XLA Modules:
  0.0 229.0 jit_solution(4297262154549098467)
XLA Ops:
  0.6 1.7 broadcast_in_dim.72
  2.4 48.0 %all_to_all.25.refs_7_.refs_3_.refs_2_ = bf16[4,512,1024]{2,1,0:T(8,128)(2,1)} all-to-all(bf16[4,512,1024]{2,1,0:T(8,128)(2,1)S(1)} %broadcast_in_dim.72), channel_id=1, replica_groups=mesh['x'=4,'c'=2,'z'=16,'y'=4] {'x'}, dimensions={0} | all-to-all | bytes 8388608 | tf_op jit(solution)/shard_map/all_to_all | solution.py:29
  50.4 0.8 broadcast_in_dim.71
  51.2 9.0 %all-to-all-start = ((bf16[4,64,768]{2,1,0:T(8,128)(2,1)}), bf16[4,64,768]{2,1,0:T(8,128)(2,1)S(1)}, u32[]{:S(2)}, u32[]{:S(2)}) async-start(bf16[4,64,768]{2,1,0:T(8,128)(2,1)} %broadcast_in_dim.71), calls=%async_computation | async-start | bytes 786432 | tf_op jit(solution)/shard_map/all_to_all | solution.py:29
  60.2 4.0 %collective-permute-start.17 = (bf16[4,512,1024]{2,1,0:T(8,128)(2,1)}, bf16[4,512,1024]{2,1,0:T(8,128)(2,1)}, u32[]{:S(2)}, u32[]{:S(2)}) collective-permute-start(bf16[4,512,1024]{2,1,0:T(8,128)(2,1)} %all_to_all.25.refs_7_.refs_3_.refs_2_), channel_id=1, source_target_pairs={{0,64},{64,0},{1,65},{65,1},{2,66},{66,2},{3,67},{67,3},{4,68},{68... | collective-permute-start | bytes 12582920 | tf_op jit(solution)/shard_map/ppermute | solution.py:36
  64.2 2.2 all-to-all-done
  66.4 0.2 copy.21
  66.6 5.1 %collective-permute-start.8 = (bf16[768,256]{1,0:T(8,128)(2,1)S(1)}, bf16[768,256]{1,0:T(8,128)(2,1)S(1)}, u32[]{:S(2)}, u32[]{:S(2)}) collective-permute-start(bf16[768,256]{1,0:T(8,128)(2,1)S(1)} %bitcast.23), channel_id=1, source_target_pairs={{0,64},{64,0},{1,65},{65,1},{2,66},{66,2},{3,67},{67,3},{4,68},{68... | collective-permute-start | bytes 1179656 | tf_op jit(solution)/shard_map/ppermute | solution.py:179
  71.8 1.3 collective-permute-done.8
  73.1 11.1 %collective-permute-start.9 = (bf16[768,256]{1,0:T(8,128)(2,1)S(1)}, bf16[768,256]{1,0:T(8,128)(2,1)S(1)}, u32[]{:S(2)}, u32[]{:S(2)}) collective-permute-start(bf16[768,256]{1,0:T(8,128)(2,1)S(1)} %collective-permute-done.8), channel_id=1, source_target_pairs={{0,4},{4,8},{8,12},{12,16},{16,20},{20,24},{24,28},{28,32},{32,36}... | collective-permute-start | bytes 1179656 | tf_op jit(solution)/shard_map/ppermute | solution.py:171
  84.2 2.6 %collective-permute-start = (bf16[768,256]{1,0:T(8,128)(2,1)S(1)}, bf16[768,256]{1,0:T(8,128)(2,1)S(1)}, u32[]{:S(2)}, u32[]{:S(2)}) collective-permute-start(bf16[768,256]{1,0:T(8,128)(2,1)S(1)} %bitcast.24), channel_id=1, source_target_pairs={{0,4},{4,8},{8,12},{12,16},{16,20},{20,24},{24,28},{28,32},{32,36}... | collective-permute-start | bytes 1179656 | tf_op jit(solution)/shard_map/ppermute | solution.py:171
  86.8 2.1 collective-permute-done.9
  88.9 5.0 %collective-permute-start.10 = (bf16[768,256]{1,0:T(8,128)(2,1)S(1)}, bf16[768,256]{1,0:T(8,128)(2,1)S(1)}, u32[]{:S(2)}, u32[]{:S(2)}) collective-permute-start(bf16[768,256]{1,0:T(8,128)(2,1)S(1)} %collective-permute-done.9), channel_id=1, source_target_pairs={{0,4},{4,8},{8,12},{12,16},{16,20},{20,24},{24,28},{28,32},{32,36}... | collective-permute-start | bytes 1179656 | tf_op jit(solution)/shard_map/ppermute | solution.py:171
  93.9 4.2 %collective-permute-start.1 = (bf16[768,256]{1,0:T(8,128)(2,1)S(1)}, bf16[768,256]{1,0:T(8,128)(2,1)S(1)}, u32[]{:S(2)}, u32[]{:S(2)}) collective-permute-start(bf16[768,256]{1,0:T(8,128)(2,1)S(1)} %collective-permute-done.refs_1_), channel_id=1, source_target_pairs={{0,4},{4,8},{8,12},{12,16},{16,20},{20,24},{24,28},{28,32},{32,36}... | collective-permute-start | bytes 1179656 | tf_op jit(solution)/shard_map/ppermute | solution.py:171
  98.1 0.5 collective-permute-done.10
  98.6 5.0 %collective-permute-start.11 = (bf16[768,256]{1,0:T(8,128)(2,1)S(1)}, bf16[768,256]{1,0:T(8,128)(2,1)S(1)}, u32[]{:S(2)}, u32[]{:S(2)}) collective-permute-start(bf16[768,256]{1,0:T(8,128)(2,1)S(1)} %collective-permute-done.10), channel_id=1, source_target_pairs={{0,4},{4,8},{8,12},{12,16},{16,20},{20,24},{24,28},{28,32},{32,36}... | collective-permute-start | bytes 1179656 | tf_op jit(solution)/shard_map/ppermute | solution.py:171
  103.6 4.2 %collective-permute-start.2 = (bf16[768,256]{1,0:T(8,128)(2,1)S(1)}, bf16[768,256]{1,0:T(8,128)(2,1)S(1)}, u32[]{:S(2)}, u32[]{:S(2)}) collective-permute-start(bf16[768,256]{1,0:T(8,128)(2,1)S(1)} %collective-permute-done.1.refs_2_), channel_id=1, source_target_pairs={{0,4},{4,8},{8,12},{12,16},{16,20},{20,24},{24,28},{28,32},{32,36}... | collective-permute-start | bytes 1179656 | tf_op jit(solution)/shard_map/ppermute | solution.py:171
  107.9 0.8 copy-done.1
  108.6 4.7 %collective-permute-start.12 = (bf16[768,256]{1,0:T(8,128)(2,1)S(1)}, bf16[768,256]{1,0:T(8,128)(2,1)S(1)}, u32[]{:S(2)}, u32[]{:S(2)}) collective-permute-start(bf16[768,256]{1,0:T(8,128)(2,1)S(1)} %collective-permute-done.11), channel_id=1, source_target_pairs={{0,4},{4,8},{8,12},{12,16},{16,20},{20,24},{24,28},{28,32},{32,36}... | collective-permute-start | bytes 1179656 | tf_op jit(solution)/shard_map/ppermute | solution.py:171
  113.4 4.2 %collective-permute-start.3 = (bf16[768,256]{1,0:T(8,128)(2,1)S(1)}, bf16[768,256]{1,0:T(8,128)(2,1)S(1)}, u32[]{:S(2)}, u32[]{:S(2)}) collective-permute-start(bf16[768,256]{1,0:T(8,128)(2,1)S(1)} %collective-permute-done.2.refs_3_), channel_id=1, source_target_pairs={{0,4},{4,8},{8,12},{12,16},{16,20},{20,24},{24,28},{28,32},{32,36}... | collective-permute-start | bytes 1179656 | tf_op jit(solution)/shard_map/ppermute | solution.py:171
  117.6 0.5 collective-permute-done.12
  118.1 5.0 %collective-permute-start.13 = (bf16[768,256]{1,0:T(8,128)(2,1)S(1)}, bf16[768,256]{1,0:T(8,128)(2,1)}, u32[]{:S(2)}, u32[]{:S(2)}) collective-permute-start(bf16[768,256]{1,0:T(8,128)(2,1)S(1)} %collective-permute-done.12), channel_id=1, source_target_pairs={{0,4},{4,8},{8,12},{12,16},{16,20},{20,24},{24,28},{28,32},{32,36}... | collective-permute-start | bytes 1179656 | tf_op jit(solution)/shard_map/ppermute | solution.py:171
  123.1 4.2 %collective-permute-start.4 = (bf16[768,256]{1,0:T(8,128)(2,1)S(1)}, bf16[768,256]{1,0:T(8,128)(2,1)}, u32[]{:S(2)}, u32[]{:S(2)}) collective-permute-start(bf16[768,256]{1,0:T(8,128)(2,1)S(1)} %collective-permute-done.3.refs_4_), channel_id=1, source_target_pairs={{0,4},{4,8},{8,12},{12,16},{16,20},{20,24},{24,28},{28,32},{32,36}... | collective-permute-start | bytes 1179656 | tf_op jit(solution)/shard_map/ppermute | solution.py:171
  127.3 0.5 collective-permute-done.13
  127.8 5.1 %collective-permute-start.14 = (bf16[768,256]{1,0:T(8,128)(2,1)}, bf16[768,256]{1,0:T(8,128)(2,1)}, u32[]{:S(2)}, u32[]{:S(2)}) collective-permute-start(bf16[768,256]{1,0:T(8,128)(2,1)} %collective-permute-done.13), channel_id=1, source_target_pairs={{0,4},{4,8},{8,12},{12,16},{16,20},{20,24},{24,28},{28,32},{32,36}... | collective-permute-start | bytes 1179656 | tf_op jit(solution)/shard_map/ppermute | solution.py:171
  132.9 1.2 pad_maximum_fusion.1
  134.1 5.1 %collective-permute-start.19 = (bf16[3,768,256]{2,1,0:T(8,128)(2,1)}, bf16[3,768,256]{2,1,0:T(8,128)(2,1)S(1)}, u32[]{:S(2)}, u32[]{:S(2)}) collective-permute-start(bf16[3,768,256]{2,1,0:T(8,128)(2,1)} %pad_maximum_fusion.1), channel_id=1, source_target_pairs={{0,64},{64,0},{1,65},{65,1},{2,66},{66,2},{3,67},{67,3},{4,68},{68... | collective-permute-start | bytes 3538952 | tf_op jit(solution)/shard_map/ppermute | solution.py:187
  139.3 4.9 %collective-permute-start.5 = (bf16[768,256]{1,0:T(8,128)(2,1)}, bf16[768,256]{1,0:T(8,128)(2,1)}, u32[]{:S(2)}, u32[]{:S(2)}) collective-permute-start(bf16[768,256]{1,0:T(8,128)(2,1)} %collective-permute-done.4.refs_5_), channel_id=1, source_target_pairs={{0,4},{4,8},{8,12},{12,16},{16,20},{20,24},{24,28},{28,32},{32,36}... | collective-permute-start | bytes 1179656 | tf_op jit(solution)/shard_map/ppermute | solution.py:171
  144.2 2.4 %pad_maximum_fusion = bf16[3,768,256]{2,1,0:T(8,128)(2,1)} fusion(bf16[1,768,256]{2,1,0:T(8,128)(2,1)} %bitcast.7, bf16[1,768,256]{2,1,0:T(8,128)(2,1)} %bitcast.6, bf16[1,768,256]{2,1,0:T(8,128)(2,1)S(1)} %bitcast.29), kind=kLoop, calls=%fused_computation | loop fusion | flops 1179648 | bytes 2359296 | tf_op jit(solution)/shard_map/stack | solution.py:187
  146.5 3.1 %collective-permute-start.18 = (bf16[3,768,256]{2,1,0:T(8,128)(2,1)}, bf16[3,768,256]{2,1,0:T(8,128)(2,1)S(1)}, u32[]{:S(2)}, u32[]{:S(2)}) collective-permute-start(bf16[3,768,256]{2,1,0:T(8,128)(2,1)} %pad_maximum_fusion), channel_id=1, source_target_pairs={{0,64},{64,0},{1,65},{65,1},{2,66},{66,2},{3,67},{67,3},{4,68},{68... | collective-permute-start | bytes 3538952 | tf_op jit(solution)/shard_map/ppermute | solution.py:187
  149.7 0.5 compare_select_fusion.4
  150.3 3.9 %collective-permute-start.6 = (bf16[768,256]{1,0:T(8,128)(2,1)}, bf16[768,256]{1,0:T(8,128)(2,1)}, u32[]{:S(2)}, u32[]{:S(2)}) collective-permute-start(bf16[768,256]{1,0:T(8,128)(2,1)} %collective-permute-done.5.refs_0_), channel_id=1, source_target_pairs={{0,4},{4,8},{8,12},{12,16},{16,20},{20,24},{24,28},{28,32},{32,36}... | collective-permute-start | bytes 1179656 | tf_op jit(solution)/shard_map/ppermute | solution.py:171
  154.2 1.9 collective-permute-start.15
  156.2 0.2 broadcast_in_dim.80.refs_5_
  156.3 0.7 pad_add_fusion.which
  157.1 0.1 select_reduce_fusion.2
  157.2 2.2 collective-permute-done.6.refs_1_
  159.4 4.8 %collective-permute-start.7 = (bf16[768,256]{1,0:T(8,128)(2,1)}, bf16[768,256]{1,0:T(8,128)(2,1)S(1)}, u32[]{:S(2)}, u32[]{:S(2)}) collective-permute-start(bf16[768,256]{1,0:T(8,128)(2,1)} %collective-permute-done.6.refs_1_), channel_id=1, source_target_pairs={{0,4},{4,8},{8,12},{12,16},{16,20},{20,24},{24,28},{28,32},{32,36}... | collective-permute-start | bytes 1179656 | tf_op jit(solution)/shard_map/ppermute | solution.py:171
  164.2 3.6 %collective-permute-start.16 = (bf16[1,768,256]{2,1,0:T(8,128)(2,1)}, bf16[1,768,256]{2,1,0:T(8,128)(2,1)S(1)}, u32[]{:S(2)}, u32[]{:S(2)}) collective-permute-start(bf16[1,768,256]{2,1,0:T(8,128)(2,1)} %bitcast.4), channel_id=1, source_target_pairs={{0,64},{64,0},{1,65},{65,1},{2,66},{66,2},{3,67},{67,3},{4,68},{68... | collective-permute-start | bytes 1179656 | tf_op jit(solution)/shard_map/ppermute | solution.py:187
  167.8 2.2 copy-done
  170.0 1.0 copy-done.2
  171.0 1.0 copy-done.4
  172.0 1.0 copy-done.6
  173.0 6.3 %shard_map.95.refs_5_ = f32[768,1024]{1,0:T(8,128)S(1)} custom-call(s32[10]{0:T(128)S(1)} %pad_add_fusion.2.which, bf16[768,256]{1,0:T(8,128)(2,1)S(1)} %bitcast.25, bf16[768,256]{1,0:T(8,128)(2,1)S(1)} %collective-permute-done.refs_1_, bf16[768,256]{1,0:T(8,128)(2,1)S(1)} %copy-done.2, bf16[768,256]{1,0:T(8,128)(2,1)S(1)} %copy-done.4, ...), custom_call_target="tpu_custom_call" | custom-call | flops 3623878656 | bytes 8257536 | tf_op jit(solution)/shard_map/pallas_call | solution.py:145
  179.3 4.0 %shard_map.96.refs_4_ = f32[768,1024]{1,0:T(8,128)S(1)} custom-call(s32[6]{0:T(128)S(1)} %pad_add_fusion.1.which, bf16[768,256]{1,0:T(8,128)(2,1)} %collective-permute-done.5.refs_0_, bf16[768,256]{1,0:T(8,128)(2,1)} %collective-permute-done.6.refs_1_, bf16[3,768,256]{2,1,0:T(8,128)(2,1)S(1)} %collective-permute-done.18.refs_2_, ...), custom_call_target="tpu_custom_call", output_to_operand_aliasing={{}: (6, {})} | custom-call | flops 2013265920 | bytes 4587520 | tf_op jit(solution)/shard_map/pallas_call | solution.py:145
  183.3 3.5 %shard_map.97 = f32[8,768]{1,0:T(8,128)S(1)} custom-call(s32[3]{0:T(128)S(1)} %pad_add_fusion.which, bf16[768,256]{1,0:T(8,128)(2,1)S(1)} %collective-permute-done.7.refs_0_, bf16[1,768,256]{2,1,0:T(8,128)(2,1)S(1)} %collective-permute-done.16.refs_1_, bf16[4,512,1024]{2,1,0:T(8,128)(2,1)S(1)} %copy-done, ...), custom_call_target="tpu_custom_call" | custom-call | flops 805306368 | bytes 1835008 | tf_op jit(solution)/shard_map/pallas_call | solution.py:145
  186.8 0.1 reshape.132
  187.0 0.1 broadcast_in_dim.74
  187.1 0.8 all_to_all.18
  187.9 11.2 %all-to-all-start.2 = ((f32[64,1,384]{2,1,0:T(1,128)}), f32[64,1,384]{2,1,0:T(1,128)S(1)}, u32[]{:S(2)}, u32[]{:S(2)}) async-start(f32[64,1,384]{2,1,0:T(1,128)} %all_to_all.18), calls=%async_computation.2 | async-start | bytes 196608 | tf_op jit(solution)/shard_map/all_to_all | solution.py:46
  199.1 0.1 reshape.134
  199.2 0.1 eq.23
  199.3 0.1 reduce_sum.57
  199.5 14.3 %all-to-all-done.2 = f32[64,1,384]{2,1,0:T(1,128)S(1)} async-done(((f32[64,1,384]{2,1,0:T(1,128)}), f32[64,1,384]{2,1,0:T(1,128)S(1)}, u32[]{:S(2)}, u32[]{:S(2)}) %all-to-all-start.2) | async-done | bytes 98336 | tf_op jit(solution)/shard_map/all_to_all | solution.py:46
  213.8 0.2 reduce.3
  214.0 0.1 reshape.133
  214.2 0.2 slice_reduce_fusion.1
  214.4 0.1 select_reduce_fusion.1
  214.6 0.6 broadcast_in_dim.79
  215.2 6.2 %all-to-all-start.3 = ((f32[32,1,128]{2,1,0:T(1,128)}), f32[32,1,128]{2,1,0:T(1,128)S(1)}, u32[]{:S(2)}, u32[]{:S(2)}) async-start(f32[32,1,128]{2,1,0:T(1,128)} %broadcast_in_dim.79), calls=%async_computation.3 | async-start | bytes 32768 | tf_op jit(solution)/shard_map/all_to_all | solution.py:29
  221.4 0.1 sub.49
  221.5 0.5 fusion.21
  222.1 6.3 %all-to-all-done.3 = f32[32,1,128]{2,1,0:T(1,128)S(1)} async-done(((f32[32,1,128]{2,1,0:T(1,128)}), f32[32,1,128]{2,1,0:T(1,128)S(1)}, u32[]{:S(2)}, u32[]{:S(2)}) %all-to-all-start.3) | async-done | bytes 16416 | tf_op jit(solution)/shard_map/all_to_all | solution.py:29
  228.4 0.6 maximum_divide_fusion
  (54 shorter events, 0.6 us)
Async XLA Ops:
  2.4 48.0 %copy-start.7 = (bf16[768,64]{0,1:T(8,128)(2,1)S(1)}, bf16[768,64]{0,1:T(8,128)(2,1)}, u32[]{:S(2)}) copy-start(bf16[768,64]{0,1:T(8,128)(2,1)} %param.8) | copy-start | bytes 294916
  50.4 82.6 %copy-start.13 = (s32[9]{0:T(128)S(1)}, s32[9]{0:T(128)}, u32[]{:S(2)}) copy-start(s32[9]{0:T(128)} %constant.104.clone) | copy-start | bytes 112
  51.2 15.3 %all-to-all-start = ((bf16[4,64,768]{2,1,0:T(8,128)(2,1)}), bf16[4,64,768]{2,1,0:T(8,128)(2,1)S(1)}, u32[]{:S(2)}, u32[]{:S(2)}) async-start(bf16[4,64,768]{2,1,0:T(8,128)(2,1)} %broadcast_in_dim.71), calls=%async_computation | async-start | bytes 786432 | tf_op jit(solution)/shard_map/all_to_all | solution.py:29
  60.2 107.6 %collective-permute-start.17 = (bf16[4,512,1024]{2,1,0:T(8,128)(2,1)}, bf16[4,512,1024]{2,1,0:T(8,128)(2,1)}, u32[]{:S(2)}, u32[]{:S(2)}) collective-permute-start(bf16[4,512,1024]{2,1,0:T(8,128)(2,1)} %all_to_all.25.refs_7_.refs_3_.refs_2_), channel_id=1, source_target_pairs={{0,64},{64,0},{1,65},{65,1},{2,66},{66,2},{3,67},{67,3},{4,68},{68... | collective-permute-start | bytes 12582920 | tf_op jit(solution)/shard_map/ppermute | solution.py:36
  66.6 6.5 %collective-permute-start.8 = (bf16[768,256]{1,0:T(8,128)(2,1)S(1)}, bf16[768,256]{1,0:T(8,128)(2,1)S(1)}, u32[]{:S(2)}, u32[]{:S(2)}) collective-permute-start(bf16[768,256]{1,0:T(8,128)(2,1)S(1)} %bitcast.23), channel_id=1, source_target_pairs={{0,64},{64,0},{1,65},{65,1},{2,66},{66,2},{3,67},{67,3},{4,68},{68... | collective-permute-start | bytes 1179656 | tf_op jit(solution)/shard_map/ppermute | solution.py:179
  73.1 15.8 %collective-permute-start.9 = (bf16[768,256]{1,0:T(8,128)(2,1)S(1)}, bf16[768,256]{1,0:T(8,128)(2,1)S(1)}, u32[]{:S(2)}, u32[]{:S(2)}) collective-permute-start(bf16[768,256]{1,0:T(8,128)(2,1)S(1)} %collective-permute-done.8), channel_id=1, source_target_pairs={{0,4},{4,8},{8,12},{12,16},{16,20},{20,24},{24,28},{28,32},{32,36}... | collective-permute-start | bytes 1179656 | tf_op jit(solution)/shard_map/ppermute | solution.py:171
  84.2 9.7 %collective-permute-start = (bf16[768,256]{1,0:T(8,128)(2,1)S(1)}, bf16[768,256]{1,0:T(8,128)(2,1)S(1)}, u32[]{:S(2)}, u32[]{:S(2)}) collective-permute-start(bf16[768,256]{1,0:T(8,128)(2,1)S(1)} %bitcast.24), channel_id=1, source_target_pairs={{0,4},{4,8},{8,12},{12,16},{16,20},{20,24},{24,28},{28,32},{32,36}... | collective-permute-start | bytes 1179656 | tf_op jit(solution)/shard_map/ppermute | solution.py:171
  88.9 9.7 %collective-permute-start.10 = (bf16[768,256]{1,0:T(8,128)(2,1)S(1)}, bf16[768,256]{1,0:T(8,128)(2,1)S(1)}, u32[]{:S(2)}, u32[]{:S(2)}) collective-permute-start(bf16[768,256]{1,0:T(8,128)(2,1)S(1)} %collective-permute-done.9), channel_id=1, source_target_pairs={{0,4},{4,8},{8,12},{12,16},{16,20},{20,24},{24,28},{28,32},{32,36}... | collective-permute-start | bytes 1179656 | tf_op jit(solution)/shard_map/ppermute | solution.py:171
  93.9 9.7 %collective-permute-start.1 = (bf16[768,256]{1,0:T(8,128)(2,1)S(1)}, bf16[768,256]{1,0:T(8,128)(2,1)S(1)}, u32[]{:S(2)}, u32[]{:S(2)}) collective-permute-start(bf16[768,256]{1,0:T(8,128)(2,1)S(1)} %collective-permute-done.refs_1_), channel_id=1, source_target_pairs={{0,4},{4,8},{8,12},{12,16},{16,20},{20,24},{24,28},{28,32},{32,36}... | collective-permute-start | bytes 1179656 | tf_op jit(solution)/shard_map/ppermute | solution.py:171
  98.6 10.0 %collective-permute-start.11 = (bf16[768,256]{1,0:T(8,128)(2,1)S(1)}, bf16[768,256]{1,0:T(8,128)(2,1)S(1)}, u32[]{:S(2)}, u32[]{:S(2)}) collective-permute-start(bf16[768,256]{1,0:T(8,128)(2,1)S(1)} %collective-permute-done.10), channel_id=1, source_target_pairs={{0,4},{4,8},{8,12},{12,16},{16,20},{20,24},{24,28},{28,32},{32,36}... | collective-permute-start | bytes 1179656 | tf_op jit(solution)/shard_map/ppermute | solution.py:171
  103.6 9.7 %collective-permute-start.2 = (bf16[768,256]{1,0:T(8,128)(2,1)S(1)}, bf16[768,256]{1,0:T(8,128)(2,1)S(1)}, u32[]{:S(2)}, u32[]{:S(2)}) collective-permute-start(bf16[768,256]{1,0:T(8,128)(2,1)S(1)} %collective-permute-done.1.refs_2_), channel_id=1, source_target_pairs={{0,4},{4,8},{8,12},{12,16},{16,20},{20,24},{24,28},{28,32},{32,36}... | collective-permute-start | bytes 1179656 | tf_op jit(solution)/shard_map/ppermute | solution.py:171
  107.9 0.8 copy-start.1
  108.6 9.4 %collective-permute-start.12 = (bf16[768,256]{1,0:T(8,128)(2,1)S(1)}, bf16[768,256]{1,0:T(8,128)(2,1)S(1)}, u32[]{:S(2)}, u32[]{:S(2)}) collective-permute-start(bf16[768,256]{1,0:T(8,128)(2,1)S(1)} %collective-permute-done.11), channel_id=1, source_target_pairs={{0,4},{4,8},{8,12},{12,16},{16,20},{20,24},{24,28},{28,32},{32,36}... | collective-permute-start | bytes 1179656 | tf_op jit(solution)/shard_map/ppermute | solution.py:171
  113.4 20.8 %copy-start.3 = (bf16[768,256]{1,0:T(8,128)(2,1)}, bf16[768,256]{1,0:T(8,128)(2,1)S(1)}, u32[]{:S(2)}) copy-start(bf16[768,256]{1,0:T(8,128)(2,1)S(1)} %collective-permute-done.2.refs_3_) | copy-start | bytes 1179652
  113.4 9.7 %collective-permute-start.3 = (bf16[768,256]{1,0:T(8,128)(2,1)S(1)}, bf16[768,256]{1,0:T(8,128)(2,1)S(1)}, u32[]{:S(2)}, u32[]{:S(2)}) collective-permute-start(bf16[768,256]{1,0:T(8,128)(2,1)S(1)} %collective-permute-done.2.refs_3_), channel_id=1, source_target_pairs={{0,4},{4,8},{8,12},{12,16},{16,20},{20,24},{24,28},{28,32},{32,36}... | collective-permute-start | bytes 1179656 | tf_op jit(solution)/shard_map/ppermute | solution.py:171
  118.1 9.7 %collective-permute-start.13 = (bf16[768,256]{1,0:T(8,128)(2,1)S(1)}, bf16[768,256]{1,0:T(8,128)(2,1)}, u32[]{:S(2)}, u32[]{:S(2)}) collective-permute-start(bf16[768,256]{1,0:T(8,128)(2,1)S(1)} %collective-permute-done.12), channel_id=1, source_target_pairs={{0,4},{4,8},{8,12},{12,16},{16,20},{20,24},{24,28},{28,32},{32,36}... | collective-permute-start | bytes 1179656 | tf_op jit(solution)/shard_map/ppermute | solution.py:171
  123.1 11.0 %copy-start.5 = (bf16[768,256]{1,0:T(8,128)(2,1)}, bf16[768,256]{1,0:T(8,128)(2,1)S(1)}, u32[]{:S(2)}) copy-start(bf16[768,256]{1,0:T(8,128)(2,1)S(1)} %collective-permute-done.3.refs_4_) | copy-start | bytes 1179652
  123.1 16.1 %collective-permute-start.4 = (bf16[768,256]{1,0:T(8,128)(2,1)S(1)}, bf16[768,256]{1,0:T(8,128)(2,1)}, u32[]{:S(2)}, u32[]{:S(2)}) collective-permute-start(bf16[768,256]{1,0:T(8,128)(2,1)S(1)} %collective-permute-done.3.refs_4_), channel_id=1, source_target_pairs={{0,4},{4,8},{8,12},{12,16},{16,20},{20,24},{24,28},{28,32},{32,36}... | collective-permute-start | bytes 1179656 | tf_op jit(solution)/shard_map/ppermute | solution.py:171
  127.8 16.3 %collective-permute-start.14 = (bf16[768,256]{1,0:T(8,128)(2,1)}, bf16[768,256]{1,0:T(8,128)(2,1)}, u32[]{:S(2)}, u32[]{:S(2)}) collective-permute-start(bf16[768,256]{1,0:T(8,128)(2,1)} %collective-permute-done.13), channel_id=1, source_target_pairs={{0,4},{4,8},{8,12},{12,16},{16,20},{20,24},{24,28},{28,32},{32,36}... | collective-permute-start | bytes 1179656 | tf_op jit(solution)/shard_map/ppermute | solution.py:171
  132.9 6.3 %copy-start.12 = (s32[5]{0:T(128)S(1)}, s32[5]{0:T(128)}, u32[]{:S(2)}) copy-start(s32[5]{0:T(128)} %constant.105.clone) | copy-start | bytes 64
  134.1 33.6 %collective-permute-start.19 = (bf16[3,768,256]{2,1,0:T(8,128)(2,1)}, bf16[3,768,256]{2,1,0:T(8,128)(2,1)S(1)}, u32[]{:S(2)}, u32[]{:S(2)}) collective-permute-start(bf16[3,768,256]{2,1,0:T(8,128)(2,1)} %pad_maximum_fusion.1), channel_id=1, source_target_pairs={{0,64},{64,0},{1,65},{65,1},{2,66},{66,2},{3,67},{67,3},{4,68},{68... | collective-permute-start | bytes 3538952 | tf_op jit(solution)/shard_map/ppermute | solution.py:187
  139.3 11.0 %collective-permute-start.5 = (bf16[768,256]{1,0:T(8,128)(2,1)}, bf16[768,256]{1,0:T(8,128)(2,1)}, u32[]{:S(2)}, u32[]{:S(2)}) collective-permute-start(bf16[768,256]{1,0:T(8,128)(2,1)} %collective-permute-done.4.refs_5_), channel_id=1, source_target_pairs={{0,4},{4,8},{8,12},{12,16},{16,20},{20,24},{24,28},{28,32},{32,36}... | collective-permute-start | bytes 1179656 | tf_op jit(solution)/shard_map/ppermute | solution.py:171
  144.1 5.5 %copy-start.11 = (s32[2]{0:T(128)S(1)}, s32[2]{0:T(128)}, u32[]{:S(2)}) copy-start(s32[2]{0:T(128)} %constant.106.clone) | copy-start | bytes 28
  144.1 6.1 %copy-start.9 = (s32[768]{0:T(1024)S(1)}, s32[768]{0:T(1024)}, u32[]{:S(2)}) copy-start(s32[768]{0:T(1024)} %param.10) | copy-start | bytes 9220
  144.2 12.9 %copy-start.10 = (s32[6]{0:T(128)S(1)}, s32[6]{0:T(128)}, u32[]{:S(2)}) copy-start(s32[6]{0:T(128)} %param.12) | copy-start | bytes 76
  146.5 32.7 %collective-permute-start.18 = (bf16[3,768,256]{2,1,0:T(8,128)(2,1)}, bf16[3,768,256]{2,1,0:T(8,128)(2,1)S(1)}, u32[]{:S(2)}, u32[]{:S(2)}) collective-permute-start(bf16[3,768,256]{2,1,0:T(8,128)(2,1)} %pad_maximum_fusion), channel_id=1, source_target_pairs={{0,64},{64,0},{1,65},{65,1},{2,66},{66,2},{3,67},{67,3},{4,68},{68... | collective-permute-start | bytes 3538952 | tf_op jit(solution)/shard_map/ppermute | solution.py:187
  150.3 9.1 %collective-permute-start.6 = (bf16[768,256]{1,0:T(8,128)(2,1)}, bf16[768,256]{1,0:T(8,128)(2,1)}, u32[]{:S(2)}, u32[]{:S(2)}) collective-permute-start(bf16[768,256]{1,0:T(8,128)(2,1)} %collective-permute-done.5.refs_0_), channel_id=1, source_target_pairs={{0,4},{4,8},{8,12},{12,16},{16,20},{20,24},{24,28},{28,32},{32,36}... | collective-permute-start | bytes 1179656 | tf_op jit(solution)/shard_map/ppermute | solution.py:171
  154.2 10.0 %collective-permute-start.15 = (bf16[768,256]{1,0:T(8,128)(2,1)}, bf16[768,256]{1,0:T(8,128)(2,1)}, u32[]{:S(2)}, u32[]{:S(2)}) collective-permute-start(bf16[768,256]{1,0:T(8,128)(2,1)} %collective-permute-done.14), channel_id=1, source_target_pairs={{0,4},{4,8},{8,12},{12,16},{16,20},{20,24},{24,28},{28,32},{32,36}... | collective-permute-start | bytes 1179656 | tf_op jit(solution)/shard_map/ppermute | solution.py:171
  159.4 23.8 %collective-permute-start.7 = (bf16[768,256]{1,0:T(8,128)(2,1)}, bf16[768,256]{1,0:T(8,128)(2,1)S(1)}, u32[]{:S(2)}, u32[]{:S(2)}) collective-permute-start(bf16[768,256]{1,0:T(8,128)(2,1)} %collective-permute-done.6.refs_1_), channel_id=1, source_target_pairs={{0,4},{4,8},{8,12},{12,16},{16,20},{20,24},{24,28},{28,32},{32,36}... | collective-permute-start | bytes 1179656 | tf_op jit(solution)/shard_map/ppermute | solution.py:171
  164.2 19.1 %collective-permute-start.16 = (bf16[1,768,256]{2,1,0:T(8,128)(2,1)}, bf16[1,768,256]{2,1,0:T(8,128)(2,1)S(1)}, u32[]{:S(2)}, u32[]{:S(2)}) collective-permute-start(bf16[1,768,256]{2,1,0:T(8,128)(2,1)} %bitcast.4), channel_id=1, source_target_pairs={{0,64},{64,0},{1,65},{65,1},{2,66},{66,2},{3,67},{67,3},{4,68},{68... | collective-permute-start | bytes 1179656 | tf_op jit(solution)/shard_map/ppermute | solution.py:187
  167.8 2.2 copy-start
  170.0 1.0 copy-start.2
  171.0 1.0 copy-start.4
  172.0 1.0 copy-start.6
  183.2 15.8 %copy-start.8 = (s32[768]{0:T(1024)S(1)}, s32[768]{0:T(1024)}, u32[]{:S(2)}) copy-start(s32[768]{0:T(1024)} %param.11) | copy-start | bytes 9220
  187.9 25.9 %all-to-all-start.2 = ((f32[64,1,384]{2,1,0:T(1,128)}), f32[64,1,384]{2,1,0:T(1,128)S(1)}, u32[]{:S(2)}, u32[]{:S(2)}) async-start(f32[64,1,384]{2,1,0:T(1,128)} %all_to_all.18), calls=%async_computation.2 | async-start | bytes 196608 | tf_op jit(solution)/shard_map/all_to_all | solution.py:46
  215.2 13.2 %all-to-all-start.3 = ((f32[32,1,128]{2,1,0:T(1,128)}), f32[32,1,128]{2,1,0:T(1,128)S(1)}, u32[]{:S(2)}, u32[]{:S(2)}) async-start(f32[32,1,128]{2,1,0:T(1,128)} %broadcast_in_dim.79), calls=%async_computation.3 | async-start | bytes 32768 | tf_op jit(solution)/shard_map/all_to_all | solution.py:29

commit v6 on v5

--- a/solution.py
+++ b/solution.py
@@ -15,12 +15,12 @@
 BLOCK = 256
 TILE = 256
 LONG = 512
-LIMIT = 24 << 20
+LIMIT = 60 << 20
 ROUNDS = 8
-BATCHES = ((1, 2, 3), (4, 5, 6), (7,))
+BATCHES = ((1, 2, 3), (4, 5), (6, 7))
 GROUPS = (
-    ("early", range(0, 6), (0,)),
-    ("middle", (6, 7), (1,)),
+    ("early", range(0, 5), ()),
+    ("middle", (5, 6, 7), (0, 1)),
     ("late", (8,), (2,)),
 )
 
@@ -74,53 +74,58 @@
         refs = list(refs)
         blocks = []
         for kind in kinds:
-            if kind == "parts":
-                blocks.append((refs.pop(0), refs.pop(0)))
-            else:
-                ref = refs.pop(0)
-                blocks += [(ref.at[k],) for k in range(kind)] if kind else [(ref,)]
+            ref = refs.pop(0)
+            blocks += [ref.at[k] for k in range(kind)] if kind else [ref]
         count, weights = len(blocks), (refs.pop(0), refs.pop(0))
         before = None if first else refs.pop(0)
         wanted = refs.pop(0) if last else None
-        out, rows, sems, *more = refs
-        acc = more[0] if last else out
+        out, acc, rows, lefts, sems, ends = refs
 
         def fetch(k, source):
             z = which[k]
             return pltpu.make_async_copy(
                 source.at[z // 4, pl.ds((z % 2) * BLOCK, BLOCK)],
                 rows.at[pl.ds(k * BLOCK, BLOCK)],
-                sems.at[k],
+                sems.at[0, k],
             )
 
+        def fetch_block(k):
+            return pltpu.make_async_copy(blocks[k], lefts.at[k], sems.at[1, k])
+
+        def whole(part, source, target, n):
+            return pltpu.make_async_copy(source.at[part], target.at[part], ends.at[n])
+
+        tokens, columns = acc.shape
+        parts = [slice(at, at + TILE) for at in range(0, tokens, TILE)]
         for k in range(count):
+            fetch_block(k).start()
             mine = (which[k] // 2) % 2 == which[count]
             pl.when(mine)(fetch(k, weights[0]).start)
             pl.when(jnp.logical_not(mine))(fetch(k, weights[1]).start)
 
-        def tile(block, at):
-            ref, at = (block[0], at) if len(block) == 1 or at < LONG else (block[1], at - LONG)
-            return ref[at : at + TILE]
-
-        tokens, columns = acc.shape
+        if not first:
+            for n, part in enumerate(parts):
+                whole(part, before, acc, n).start()
         steps = [range(0, min(2, count)), range(2, count)]
         steps = [ks for ks in steps if len(ks)]
         for n, ks in enumerate(steps):
             for k in ks:
+                fetch_block(k).wait()
                 fetch(k, weights[0]).wait()
             deep = slice(ks[0] * BLOCK, (ks[-1] + 1) * BLOCK)
-            for at in range(0, tokens, TILE):
-                part = slice(at, at + TILE)
-                left = jnp.concatenate([tile(blocks[k], at) for k in ks], axis=1)
+            for place, part in enumerate(parts):
+                left = jnp.concatenate([lefts[k, part] for k in ks], axis=1)
+                if n == 0 and not first:
+                    whole(part, before, acc, place).wait()
                 for low in range(0, columns, LONG):
                     side = slice(low, low + LONG)
                     total = jnp.dot(left, rows[deep, side], preferred_element_type=jnp.float32)
-                    if n:
-                        total += acc[part, side]
-                    elif not first:
-                        total += before[part, side]
-                    acc[part, side] = total
-                if last and n == len(steps) - 1:
+                    acc[part, side] = total if n == 0 and first else total + acc[part, side]
+                if n < len(steps) - 1:
+                    continue
+                if not last:
+                    whole(part, acc, out, place).start()
+                else:
                     values = acc[part]
                     top = jnp.max(values, axis=1, keepdims=True)
                     total = jnp.sum(jnp.exp(values - top), axis=1, keepdims=True)
@@ -130,39 +135,42 @@
                     lse = jnp.log(total) + top
                     lane = lax.broadcasted_iota(jnp.int32, (TILE, 128), 1)
                     out[:, part] = jnp.where(lane == 0, lse, picked).T[:8]
+        if not last:
+            for place, part in enumerate(parts):
+                whole(part, acc, out, place).wait()
 
     return kernel
 
 
 def product(which, blocks, weights, before=None, wanted=None):
-    kinds = ["parts" if isinstance(b, tuple) else b.shape[0] if b.ndim == 3 else 0 for b in blocks]
-    count = sum(1 if kind == "parts" else kind or 1 for kind in kinds)
-    arrays = [array for b in blocks for array in (b if isinstance(b, tuple) else (b,))]
+    kinds = [b.shape[0] if b.ndim == 3 else 0 for b in blocks]
+    count = sum(kind or 1 for kind in kinds)
     columns, tokens, last = weights[0].shape[2], 768, wanted is not None
     vmem = pl.BlockSpec(memory_space=pltpu.VMEM)
-    extra = [array for array in (before, wanted) if array is not None]
+    hbm = pl.BlockSpec(memory_space=pltpu.HBM)
     shape = (8, tokens) if last else (tokens, columns)
     return pl.pallas_call(
         product_kernel(kinds, before is None, last),
         in_specs=[pl.BlockSpec(memory_space=pltpu.SMEM)]
-        + [vmem] * len(arrays)
-        + [pl.BlockSpec(memory_space=pltpu.HBM)] * 2
-        + [vmem] * len(extra),
-        out_specs=vmem,
+        + [hbm] * (len(blocks) + 2)
+        + [hbm] * (before is not None)
+        + [vmem] * last,
+        out_specs=vmem if last else hbm,
         out_shape=jax.ShapeDtypeStruct(shape, jnp.float32),
         scratch_shapes=[
+            pltpu.VMEM((tokens, columns), jnp.float32),
             pltpu.VMEM((count * BLOCK, columns), jnp.bfloat16),
-            pltpu.SemaphoreType.DMA((count,)),
-        ]
-        + ([pltpu.VMEM((tokens, columns), jnp.float32)] if last else []),
-        input_output_aliases={} if before is None or last else {3 + len(arrays): 0},
+            pltpu.VMEM((count, tokens, BLOCK), jnp.bfloat16),
+            pltpu.SemaphoreType.DMA((2, count)),
+            pltpu.SemaphoreType.DMA((tokens // TILE,)),
+        ],
         compiler_params=pltpu.CompilerParams(vmem_limit_bytes=LIMIT),
         cost_estimate=pl.CostEstimate(
             flops=2 * count * tokens * BLOCK * columns,
             bytes_accessed=count * BLOCK * (tokens + columns) * 2,
             transcendentals=0,
         ),
-    )(which, *arrays, *weights, *extra)
+    )(which, *blocks, *weights, *(array for array in (before, wanted) if array is not None))
 
 
 def along_z(array):

time: 230 us -> 236 us (1.026)
  blocking collectives: 48 us -> 59.8 us
  starting transfers between devices: 118 us -> 109 us
  Pallas kernels: 13.8 us -> 20.7 us
  local copies, waits for them, and re-layouts: 11 us -> 8.45 us
  waiting for transfers between devices: 30 us -> 27.6 us
    all_to_all x1 -> x2, blocking collectives: 48 us -> 59.8 us  [to_all(): lax.all_to_all(jnp.broadcast_to(array[None], (copies, *array.shape)), axi...]
    all_to_all x2 -> x1, starting transfers between devices: 15.3 us -> 3.76 us  [to_all(): lax.all_to_all(jnp.broadcast_to(array[None], (copies, *array.shape)), axi...]
    pallas_call x3, Pallas kernels: 13.8 us -> 20.7 us  [product(): pl.pallas_call(product_kernel(kinds, before is None, last), in_specs=[pl....]
    ppermute x1, starting transfers between devices: 3.99 us -> 8.7 us  [gathered_weight(): return (own, lax.ppermute(own, 'c', SWAP))]
    unnamed x28, local copies, waits for them, and re-layouts: 5.98 us -> 2.71 us
    all_to_all x2 -> x1, waiting for transfers between devices: 8.56 us -> 6.34 us  [to_all(): lax.all_to_all(jnp.broadcast_to(array[None], (copies, *array.shape)), axi...]
  transfers between devices with their start and end apart: 23 -> 22, of which waited for: 9 -> 9; matrix products, arithmetic and copies ran while one was open for 3% -> 3% of each run, Pallas kernels for 4% -> 6%
where the time goes in v6:
time: 236 us; the launch traced here: 235 us
  starting transfers between devices  109 us (46%)
  blocking collectives  59.8 us (25%)
  waiting for transfers between devices  27.6 us (12%)
  Pallas kernels  20.7 us (9%)
  local copies, waits for them, and re-layouts  8.45 us (4%)
  other arithmetic  7.92 us (3%)
    ppermute x15, starting transfers between devices, along_z(): return lax.ppermute(array, ('c', 'z'), pairs)  72.3 us
    all_to_all x2, blocking collectives, to_all(): lax.all_to_all(jnp.broadcast_to(array[None], (copies, *array.shape)), axi...  59.8 us
    pallas_call x3, Pallas kernels, product(): pl.pallas_call(product_kernel(kinds, before is None, last), in_specs=[pl....  20.7 us
    all_to_all x1, waiting for transfers between devices, tail(): got = lax.all_to_all(send.reshape(zs * ys, -1), VOCAB, 0, 0, tiled=True)  15.7 us
    ppermute x3, starting transfers between devices, loss(): swapped.append(lax.ppermute(jnp.stack([other[r] for r in some]), 'c', SWAP))  11.3 us
    all_to_all x1, starting transfers between devices, tail(): got = lax.all_to_all(send.reshape(zs * ys, -1), VOCAB, 0, 0, tiled=True)  10.2 us
    ppermute x1, starting transfers between devices, gathered_weight(): return (own, lax.ppermute(own, 'c', SWAP))  8.7 us
    all_to_all x1, waiting for transfers between devices, to_all(): lax.all_to_all(jnp.broadcast_to(array[None], (copies, *array.shape)), axi...  6.34 us
  transfers between devices with their start and end apart: 22, of which 9 were waited for; matrix products, arithmetic and copies ran while one was open for 3% of the time, Pallas kernels for 6%

profile of v6, /device:TPU:1, one launch (start us, length us, event | category | flops | bytes accessed | tf_op | source)
XLA Modules:
  0.0 234.9 jit_solution(14306375960951857548)
XLA Ops:
  0.6 1.7 broadcast_in_dim.72
  2.4 48.0 %all_to_all.25.refs_5_.refs_2_ = bf16[4,512,1024]{2,1,0:T(8,128)(2,1)} all-to-all(bf16[4,512,1024]{2,1,0:T(8,128)(2,1)S(1)} %broadcast_in_dim.72), channel_id=1, replica_groups=mesh['x'=4,'c'=2,'z'=16,'y'=4] {'x'}, dimensions={0} | all-to-all | bytes 8388608 | tf_op jit(solution)/shard_map/all_to_all | solution.py:29
  50.4 8.7 %collective-permute-start.17 = (bf16[4,512,1024]{2,1,0:T(8,128)(2,1)}, bf16[4,512,1024]{2,1,0:T(8,128)(2,1)}, u32[]{:S(2)}, u32[]{:S(2)}) collective-permute-start(bf16[4,512,1024]{2,1,0:T(8,128)(2,1)} %all_to_all.25.refs_5_.refs_2_), channel_id=1, source_target_pairs={{0,64},{64,0},{1,65},{65,1},{2,66},{66,2},{3,67},{67,3},{4,68},{68... | collective-permute-start | bytes 12582920 | tf_op jit(solution)/shard_map/ppermute | solution.py:36
  59.1 11.9 %all_to_all.26 = bf16[4,64,768]{2,1,0:T(8,128)(2,1)S(1)} all-to-all(bf16[4,64,768]{2,1,0:T(8,128)(2,1)S(1)} %broadcast_in_dim.71), channel_id=1, replica_groups=mesh['x'=4,'c'=2,'z'=16,'y'=4] {'y'}, dimensions={0} | all-to-all | bytes 786432 | tf_op jit(solution)/shard_map/all_to_all | solution.py:29
  71.0 0.2 copy.20
  71.1 3.1 %collective-permute-start.8 = (bf16[768,256]{1,0:T(8,128)(2,1)S(1)}, bf16[768,256]{1,0:T(8,128)(2,1)S(1)}, u32[]{:S(2)}, u32[]{:S(2)}) collective-permute-start(bf16[768,256]{1,0:T(8,128)(2,1)S(1)} %bitcast.24), channel_id=1, source_target_pairs={{0,64},{64,0},{1,65},{65,1},{2,66},{66,2},{3,67},{67,3},{4,68},{68... | collective-permute-start | bytes 1179656 | tf_op jit(solution)/shard_map/ppermute | solution.py:187
  74.2 1.3 collective-permute-done.8
  75.5 11.1 %collective-permute-start.9 = (bf16[768,256]{1,0:T(8,128)(2,1)S(1)}, bf16[768,256]{1,0:T(8,128)(2,1)S(1)}, u32[]{:S(2)}, u32[]{:S(2)}) collective-permute-start(bf16[768,256]{1,0:T(8,128)(2,1)S(1)} %collective-permute-done.8), channel_id=1, source_target_pairs={{0,4},{4,8},{8,12},{12,16},{16,20},{20,24},{24,28},{28,32},{32,36}... | collective-permute-start | bytes 1179656 | tf_op jit(solution)/shard_map/ppermute | solution.py:179
  86.7 2.6 %collective-permute-start = (bf16[768,256]{1,0:T(8,128)(2,1)S(1)}, bf16[768,256]{1,0:T(8,128)(2,1)S(1)}, u32[]{:S(2)}, u32[]{:S(2)}) collective-permute-start(bf16[768,256]{1,0:T(8,128)(2,1)S(1)} %bitcast.25), channel_id=1, source_target_pairs={{0,4},{4,8},{8,12},{12,16},{16,20},{20,24},{24,28},{28,32},{32,36}... | collective-permute-start | bytes 1179656 | tf_op jit(solution)/shard_map/ppermute | solution.py:179
  89.3 2.1 collective-permute-done.9
  91.4 5.0 %collective-permute-start.10 = (bf16[768,256]{1,0:T(8,128)(2,1)S(1)}, bf16[768,256]{1,0:T(8,128)(2,1)S(1)}, u32[]{:S(2)}, u32[]{:S(2)}) collective-permute-start(bf16[768,256]{1,0:T(8,128)(2,1)S(1)} %collective-permute-done.9), channel_id=1, source_target_pairs={{0,4},{4,8},{8,12},{12,16},{16,20},{20,24},{24,28},{28,32},{32,36}... | collective-permute-start | bytes 1179656 | tf_op jit(solution)/shard_map/ppermute | solution.py:179
  96.4 4.2 %collective-permute-start.1 = (bf16[768,256]{1,0:T(8,128)(2,1)S(1)}, bf16[768,256]{1,0:T(8,128)(2,1)S(1)}, u32[]{:S(2)}, u32[]{:S(2)}) collective-permute-start(bf16[768,256]{1,0:T(8,128)(2,1)S(1)} %collective-permute-done.refs_1_), channel_id=1, source_target_pairs={{0,4},{4,8},{8,12},{12,16},{16,20},{20,24},{24,28},{28,32},{32,36}... | collective-permute-start | bytes 1179656 | tf_op jit(solution)/shard_map/ppermute | solution.py:179
  100.6 0.5 collective-permute-done.10
  101.1 5.0 %collective-permute-start.11 = (bf16[768,256]{1,0:T(8,128)(2,1)S(1)}, bf16[768,256]{1,0:T(8,128)(2,1)S(1)}, u32[]{:S(2)}, u32[]{:S(2)}) collective-permute-start(bf16[768,256]{1,0:T(8,128)(2,1)S(1)} %collective-permute-done.10), channel_id=1, source_target_pairs={{0,4},{4,8},{8,12},{12,16},{16,20},{20,24},{24,28},{28,32},{32,36}... | collective-permute-start | bytes 1179656 | tf_op jit(solution)/shard_map/ppermute | solution.py:179
  106.1 4.2 %collective-permute-start.2 = (bf16[768,256]{1,0:T(8,128)(2,1)S(1)}, bf16[768,256]{1,0:T(8,128)(2,1)S(1)}, u32[]{:S(2)}, u32[]{:S(2)}) collective-permute-start(bf16[768,256]{1,0:T(8,128)(2,1)S(1)} %collective-permute-done.1.refs_2_), channel_id=1, source_target_pairs={{0,4},{4,8},{8,12},{12,16},{16,20},{20,24},{24,28},{28,32},{32,36}... | collective-permute-start | bytes 1179656 | tf_op jit(solution)/shard_map/ppermute | solution.py:179
  110.3 0.5 collective-permute-done.11
  110.8 5.0 %collective-permute-start.12 = (bf16[768,256]{1,0:T(8,128)(2,1)S(1)}, bf16[768,256]{1,0:T(8,128)(2,1)S(1)}, u32[]{:S(2)}, u32[]{:S(2)}) collective-permute-start(bf16[768,256]{1,0:T(8,128)(2,1)S(1)} %collective-permute-done.11), channel_id=1, source_target_pairs={{0,4},{4,8},{8,12},{12,16},{16,20},{20,24},{24,28},{28,32},{32,36}... | collective-permute-start | bytes 1179656 | tf_op jit(solution)/shard_map/ppermute | solution.py:179
  115.8 4.2 %collective-permute-start.3 = (bf16[768,256]{1,0:T(8,128)(2,1)S(1)}, bf16[768,256]{1,0:T(8,128)(2,1)}, u32[]{:S(2)}, u32[]{:S(2)}) collective-permute-start(bf16[768,256]{1,0:T(8,128)(2,1)S(1)} %collective-permute-done.2.refs_3_), channel_id=1, source_target_pairs={{0,4},{4,8},{8,12},{12,16},{16,20},{20,24},{24,28},{28,32},{32,36}... | collective-permute-start | bytes 1179656 | tf_op jit(solution)/shard_map/ppermute | solution.py:179
  120.0 0.5 collective-permute-done.12
  120.5 5.0 %collective-permute-start.13 = (bf16[768,256]{1,0:T(8,128)(2,1)S(1)}, bf16[768,256]{1,0:T(8,128)(2,1)}, u32[]{:S(2)}, u32[]{:S(2)}) collective-permute-start(bf16[768,256]{1,0:T(8,128)(2,1)S(1)} %collective-permute-done.12), channel_id=1, source_target_pairs={{0,4},{4,8},{8,12},{12,16},{16,20},{20,24},{24,28},{28,32},{32,36}... | collective-permute-start | bytes 1179656 | tf_op jit(solution)/shard_map/ppermute | solution.py:179
  125.6 4.3 %collective-permute-start.4 = (bf16[768,256]{1,0:T(8,128)(2,1)}, bf16[768,256]{1,0:T(8,128)(2,1)}, u32[]{:S(2)}, u32[]{:S(2)}) collective-permute-start(bf16[768,256]{1,0:T(8,128)(2,1)} %collective-permute-done.3.refs_4_), channel_id=1, source_target_pairs={{0,4},{4,8},{8,12},{12,16},{16,20},{20,24},{24,28},{28,32},{32,36}... | collective-permute-start | bytes 1179656 | tf_op jit(solution)/shard_map/ppermute | solution.py:179
  129.9 0.4 collective-permute-done.13
  130.2 5.1 %collective-permute-start.14 = (bf16[768,256]{1,0:T(8,128)(2,1)}, bf16[768,256]{1,0:T(8,128)(2,1)}, u32[]{:S(2)}, u32[]{:S(2)}) collective-permute-start(bf16[768,256]{1,0:T(8,128)(2,1)} %collective-permute-done.13), channel_id=1, source_target_pairs={{0,4},{4,8},{8,12},{12,16},{16,20},{20,24},{24,28},{28,32},{32,36}... | collective-permute-start | bytes 1179656 | tf_op jit(solution)/shard_map/ppermute | solution.py:179
  135.4 0.1 pad_maximum_fusion
  135.6 5.1 %collective-permute-start.18 = (bf16[3,768,256]{2,1,0:T(8,128)(2,1)S(1)}, bf16[3,768,256]{2,1,0:T(8,128)(2,1)S(1)}, u32[]{:S(2)}, u32[]{:S(2)}) collective-permute-start(bf16[3,768,256]{2,1,0:T(8,128)(2,1)S(1)} %pad_maximum_fusion), channel_id=1, source_target_pairs={{0,64},{64,0},{1,65},{65,1},{2,66},{66,2},{3,67},{67,3},{4,68},{68... | collective-permute-start | bytes 3538952 | tf_op jit(solution)/shard_map/ppermute | solution.py:195
  140.7 4.9 %collective-permute-start.5 = (bf16[768,256]{1,0:T(8,128)(2,1)}, bf16[768,256]{1,0:T(8,128)(2,1)}, u32[]{:S(2)}, u32[]{:S(2)}) collective-permute-start(bf16[768,256]{1,0:T(8,128)(2,1)} %collective-permute-done.4.refs_0_), channel_id=1, source_target_pairs={{0,4},{4,8},{8,12},{12,16},{16,20},{20,24},{24,28},{28,32},{32,36}... | collective-permute-start | bytes 1179656 | tf_op jit(solution)/shard_map/ppermute | solution.py:179
  145.6 1.9 collective-permute-start.15
  147.5 2.0 pad_maximum_fusion.2
  149.5 4.3 %collective-permute-start.19 = (bf16[2,768,256]{2,1,0:T(8,128)(2,1)}, bf16[2,768,256]{2,1,0:T(8,128)(2,1)S(1)}, u32[]{:S(2)}, u32[]{:S(2)}) collective-permute-start(bf16[2,768,256]{2,1,0:T(8,128)(2,1)} %pad_maximum_fusion.2), channel_id=1, source_target_pairs={{0,64},{64,0},{1,65},{65,1},{2,66},{66,2},{3,67},{67,3},{4,68},{68... | collective-permute-start | bytes 2359304 | tf_op jit(solution)/shard_map/ppermute | solution.py:195
  153.8 0.6 pad_add_fusion.2.which
  154.4 0.9 broadcast_in_dim.80.refs_5_
  155.3 0.6 pad_add_fusion.1.which
  155.9 4.8 %collective-permute-start.6 = (bf16[768,256]{1,0:T(8,128)(2,1)}, bf16[768,256]{1,0:T(8,128)(2,1)S(1)}, u32[]{:S(2)}, u32[]{:S(2)}) collective-permute-start(bf16[768,256]{1,0:T(8,128)(2,1)} %collective-permute-done.5.refs_1_), channel_id=1, source_target_pairs={{0,4},{4,8},{8,12},{12,16},{16,20},{20,24},{24,28},{28,32},{32,36}... | collective-permute-start | bytes 1179656 | tf_op jit(solution)/shard_map/ppermute | solution.py:179
  160.7 2.1 pad_maximum_fusion.1
  162.8 1.9 collective-permute-start.16
  164.7 0.6 pad_add_fusion.which
  165.3 0.1 select_reduce_fusion.2
  165.4 0.3 collective-permute-done.6.refs_2_
  165.7 4.9 %collective-permute-start.7 = (bf16[768,256]{1,0:T(8,128)(2,1)S(1)}, bf16[768,256]{1,0:T(8,128)(2,1)S(1)}, u32[]{:S(2)}, u32[]{:S(2)}) collective-permute-start(bf16[768,256]{1,0:T(8,128)(2,1)S(1)} %collective-permute-done.6.refs_2_), channel_id=1, source_target_pairs={{0,4},{4,8},{8,12},{12,16},{16,20},{20,24},{24,28},{28,32},{32,36}... | collective-permute-start | bytes 1179656 | tf_op jit(solution)/shard_map/ppermute | solution.py:179
  170.7 5.6 %shard_map.95.refs_7_ = f32[768,1024]{1,0:T(8,128)} custom-call(s32[6]{0:T(128)} %pad_add_fusion.2.which, bf16[768,256]{1,0:T(8,128)(2,1)} %bitcast.26, bf16[768,256]{1,0:T(8,128)(2,1)} %copy-done.4, bf16[768,256]{1,0:T(8,128)(2,1)} %copy-done.5, bf16[768,256]{1,0:T(8,128)(2,1)} %copy-done.6, bf16[768,256]{1,0:T(8,128)(2,1)} %collective-permute-done.3.refs_4_, ...), custom_call_target="tpu_custom_call" | custom-call | flops 2013265920 | bytes 4587520 | tf_op jit(solution)/shard_map/pallas_call | solution.py:152
  176.3 1.0 copy-done.1
  177.3 0.9 copy-done.2
  178.2 9.0 %shard_map.96.refs_4_ = f32[768,1024]{1,0:T(8,128)} custom-call(s32[9]{0:T(128)} %pad_add_fusion.1.which, bf16[768,256]{1,0:T(8,128)(2,1)} %collective-permute-done.4.refs_0_, bf16[768,256]{1,0:T(8,128)(2,1)} %collective-permute-done.5.refs_1_, bf16[768,256]{1,0:T(8,128)(2,1)} %copy-done.7, bf16[3,768,256]{2,1,0:T(8,128)(2,1)} %copy-done.1, ...), custom_call_target="tpu_custom_call" | custom-call | flops 3221225472 | bytes 7340032 | tf_op jit(solution)/shard_map/pallas_call | solution.py:152
  187.2 0.7 copy-done.3
  188.0 6.2 %shard_map.97 = f32[8,768]{1,0:T(8,128)} custom-call(s32[4]{0:T(128)} %pad_add_fusion.which, bf16[768,256]{1,0:T(8,128)(2,1)} %copy-done.3, bf16[2,768,256]{2,1,0:T(8,128)(2,1)} %collective-permute-done.16.refs_1_, bf16[4,512,1024]{2,1,0:T(8,128)(2,1)} %all_to_all.25.refs_5_.refs_2_, bf16[4,512,1024]{2,1,0:T(8,128)(2,1)} %collective-permute-done.17.refs_6_.refs_3_, ...), custom_call_target="tpu_custom_call" | custom-call | flops 1207959552 | bytes 2752512 | tf_op jit(solution)/shard_map/pallas_call | solution.py:152
  194.2 0.7 slice.21
  194.9 0.1 reshape.132
  195.0 0.1 broadcast_in_dim.74
  195.2 0.8 all_to_all.18
  195.9 10.2 %all-to-all-start.2 = ((f32[64,1,384]{2,1,0:T(1,128)}), f32[64,1,384]{2,1,0:T(1,128)S(1)}, u32[]{:S(2)}, u32[]{:S(2)}) async-start(f32[64,1,384]{2,1,0:T(1,128)} %all_to_all.18), calls=%async_computation.2 | async-start | bytes 196608 | tf_op jit(solution)/shard_map/all_to_all | solution.py:46
  206.1 0.1 reshape.134
  206.3 0.1 eq.23
  206.4 0.1 reduce_sum.57
  206.5 15.7 %all-to-all-done.2 = f32[64,1,384]{2,1,0:T(1,128)S(1)} async-done(((f32[64,1,384]{2,1,0:T(1,128)}), f32[64,1,384]{2,1,0:T(1,128)S(1)}, u32[]{:S(2)}, u32[]{:S(2)}) %all-to-all-start.2) | async-done | bytes 98336 | tf_op jit(solution)/shard_map/all_to_all | solution.py:46
  222.2 0.2 reduce.3
  222.4 0.1 reshape.133
  222.6 0.2 slice_reduce_fusion.1
  222.8 0.1 select_reduce_fusion.1
  223.0 0.6 broadcast_in_dim.79
  223.6 3.8 %all-to-all-start.3 = ((f32[32,1,128]{2,1,0:T(1,128)}), f32[32,1,128]{2,1,0:T(1,128)S(1)}, u32[]{:S(2)}, u32[]{:S(2)}) async-start(f32[32,1,128]{2,1,0:T(1,128)} %broadcast_in_dim.79), calls=%async_computation.3 | async-start | bytes 32768 | tf_op jit(solution)/shard_map/all_to_all | solution.py:29
  227.4 0.1 sub.49
  227.4 0.5 fusion.21
  228.0 6.3 %all-to-all-done.3 = f32[32,1,128]{2,1,0:T(1,128)S(1)} async-done(((f32[32,1,128]{2,1,0:T(1,128)}), f32[32,1,128]{2,1,0:T(1,128)S(1)}, u32[]{:S(2)}, u32[]{:S(2)}) %all-to-all-start.3) | async-done | bytes 16416 | tf_op jit(solution)/shard_map/all_to_all | solution.py:29
  234.3 0.6 maximum_divide_fusion
  (54 shorter events, 0.5 us)
Async XLA Ops:
  2.4 56.7 %copy-start.8 = (bf16[768,64]{0,1:T(8,128)(2,1)S(1)}, bf16[768,64]{0,1:T(8,128)(2,1)}, u32[]{:S(2)}) copy-start(bf16[768,64]{0,1:T(8,128)(2,1)} %param.8) | copy-start | bytes 294916
  50.4 75.2 %copy-start.10 = (s32[768]{0:T(1024)S(1)}, s32[768]{0:T(1024)}, u32[]{:S(2)}) copy-start(s32[768]{0:T(1024)} %param.10) | copy-start | bytes 9220
  50.4 85.0 %copy-start.13 = (s32[8]{0:T(128)S(1)}, s32[8]{0:T(128)}, u32[]{:S(2)}) copy-start(s32[8]{0:T(128)} %constant.104.clone) | copy-start | bytes 100
  50.4 120.3 %collective-permute-start.17 = (bf16[4,512,1024]{2,1,0:T(8,128)(2,1)}, bf16[4,512,1024]{2,1,0:T(8,128)(2,1)}, u32[]{:S(2)}, u32[]{:S(2)}) collective-permute-start(bf16[4,512,1024]{2,1,0:T(8,128)(2,1)} %all_to_all.25.refs_5_.refs_2_), channel_id=1, source_target_pairs={{0,64},{64,0},{1,65},{65,1},{2,66},{66,2},{3,67},{67,3},{4,68},{68... | collective-permute-start | bytes 12582920 | tf_op jit(solution)/shard_map/ppermute | solution.py:36
  71.1 64.4 %copy-start = (bf16[256,768]{0,1:T(8,128)(2,1)}, bf16[256,768]{0,1:T(8,128)(2,1)S(1)}, u32[]{:S(2)}) copy-start(bf16[256,768]{0,1:T(8,128)(2,1)S(1)} %copy.20) | copy-start | bytes 1179652
  71.1 4.4 %collective-permute-start.8 = (bf16[768,256]{1,0:T(8,128)(2,1)S(1)}, bf16[768,256]{1,0:T(8,128)(2,1)S(1)}, u32[]{:S(2)}, u32[]{:S(2)}) collective-permute-start(bf16[768,256]{1,0:T(8,128)(2,1)S(1)} %bitcast.24), channel_id=1, source_target_pairs={{0,64},{64,0},{1,65},{65,1},{2,66},{66,2},{3,67},{67,3},{4,68},{68... | collective-permute-start | bytes 1179656 | tf_op jit(solution)/shard_map/ppermute | solution.py:187
  75.5 15.8 %collective-permute-start.9 = (bf16[768,256]{1,0:T(8,128)(2,1)S(1)}, bf16[768,256]{1,0:T(8,128)(2,1)S(1)}, u32[]{:S(2)}, u32[]{:S(2)}) collective-permute-start(bf16[768,256]{1,0:T(8,128)(2,1)S(1)} %collective-permute-done.8), channel_id=1, source_target_pairs={{0,4},{4,8},{8,12},{12,16},{16,20},{20,24},{24,28},{28,32},{32,36}... | collective-permute-start | bytes 1179656 | tf_op jit(solution)/shard_map/ppermute | solution.py:179
  86.7 9.7 %collective-permute-start = (bf16[768,256]{1,0:T(8,128)(2,1)S(1)}, bf16[768,256]{1,0:T(8,128)(2,1)S(1)}, u32[]{:S(2)}, u32[]{:S(2)}) collective-permute-start(bf16[768,256]{1,0:T(8,128)(2,1)S(1)} %bitcast.25), channel_id=1, source_target_pairs={{0,4},{4,8},{8,12},{12,16},{16,20},{20,24},{24,28},{28,32},{32,36}... | collective-permute-start | bytes 1179656 | tf_op jit(solution)/shard_map/ppermute | solution.py:179
  91.4 9.7 %collective-permute-start.10 = (bf16[768,256]{1,0:T(8,128)(2,1)S(1)}, bf16[768,256]{1,0:T(8,128)(2,1)S(1)}, u32[]{:S(2)}, u32[]{:S(2)}) collective-permute-start(bf16[768,256]{1,0:T(8,128)(2,1)S(1)} %collective-permute-done.9), channel_id=1, source_target_pairs={{0,4},{4,8},{8,12},{12,16},{16,20},{20,24},{24,28},{28,32},{32,36}... | collective-permute-start | bytes 1179656 | tf_op jit(solution)/shard_map/ppermute | solution.py:179
  96.4 24.1 %copy-start.4 = (bf16[768,256]{1,0:T(8,128)(2,1)}, bf16[768,256]{1,0:T(8,128)(2,1)S(1)}, u32[]{:S(2)}) copy-start(bf16[768,256]{1,0:T(8,128)(2,1)S(1)} %collective-permute-done.refs_1_) | copy-start | bytes 1179652
  96.4 9.7 %collective-permute-start.1 = (bf16[768,256]{1,0:T(8,128)(2,1)S(1)}, bf16[768,256]{1,0:T(8,128)(2,1)S(1)}, u32[]{:S(2)}, u32[]{:S(2)}) collective-permute-start(bf16[768,256]{1,0:T(8,128)(2,1)S(1)} %collective-permute-done.refs_1_), channel_id=1, source_target_pairs={{0,4},{4,8},{8,12},{12,16},{16,20},{20,24},{24,28},{28,32},{32,36}... | collective-permute-start | bytes 1179656 | tf_op jit(solution)/shard_map/ppermute | solution.py:179
  101.1 9.7 %collective-permute-start.11 = (bf16[768,256]{1,0:T(8,128)(2,1)S(1)}, bf16[768,256]{1,0:T(8,128)(2,1)S(1)}, u32[]{:S(2)}, u32[]{:S(2)}) collective-permute-start(bf16[768,256]{1,0:T(8,128)(2,1)S(1)} %collective-permute-done.10), channel_id=1, source_target_pairs={{0,4},{4,8},{8,12},{12,16},{16,20},{20,24},{24,28},{28,32},{32,36}... | collective-permute-start | bytes 1179656 | tf_op jit(solution)/shard_map/ppermute | solution.py:179
  106.1 29.3 %copy-start.5 = (bf16[768,256]{1,0:T(8,128)(2,1)}, bf16[768,256]{1,0:T(8,128)(2,1)S(1)}, u32[]{:S(2)}) copy-start(bf16[768,256]{1,0:T(8,128)(2,1)S(1)} %collective-permute-done.1.refs_2_) | copy-start | bytes 1179652
  106.1 9.7 %collective-permute-start.2 = (bf16[768,256]{1,0:T(8,128)(2,1)S(1)}, bf16[768,256]{1,0:T(8,128)(2,1)S(1)}, u32[]{:S(2)}, u32[]{:S(2)}) collective-permute-start(bf16[768,256]{1,0:T(8,128)(2,1)S(1)} %collective-permute-done.1.refs_2_), channel_id=1, source_target_pairs={{0,4},{4,8},{8,12},{12,16},{16,20},{20,24},{24,28},{28,32},{32,36}... | collective-permute-start | bytes 1179656 | tf_op jit(solution)/shard_map/ppermute | solution.py:179
  110.8 9.7 %collective-permute-start.12 = (bf16[768,256]{1,0:T(8,128)(2,1)S(1)}, bf16[768,256]{1,0:T(8,128)(2,1)S(1)}, u32[]{:S(2)}, u32[]{:S(2)}) collective-permute-start(bf16[768,256]{1,0:T(8,128)(2,1)S(1)} %collective-permute-done.11), channel_id=1, source_target_pairs={{0,4},{4,8},{8,12},{12,16},{16,20},{20,24},{24,28},{28,32},{32,36}... | collective-permute-start | bytes 1179656 | tf_op jit(solution)/shard_map/ppermute | solution.py:179
  115.8 19.6 %copy-start.6 = (bf16[768,256]{1,0:T(8,128)(2,1)}, bf16[768,256]{1,0:T(8,128)(2,1)S(1)}, u32[]{:S(2)}) copy-start(bf16[768,256]{1,0:T(8,128)(2,1)S(1)} %collective-permute-done.2.refs_3_) | copy-start | bytes 1179652
  115.8 9.7 %collective-permute-start.3 = (bf16[768,256]{1,0:T(8,128)(2,1)S(1)}, bf16[768,256]{1,0:T(8,128)(2,1)}, u32[]{:S(2)}, u32[]{:S(2)}) collective-permute-start(bf16[768,256]{1,0:T(8,128)(2,1)S(1)} %collective-permute-done.2.refs_3_), channel_id=1, source_target_pairs={{0,4},{4,8},{8,12},{12,16},{16,20},{20,24},{24,28},{28,32},{32,36}... | collective-permute-start | bytes 1179656 | tf_op jit(solution)/shard_map/ppermute | solution.py:179
  120.5 9.7 %collective-permute-start.13 = (bf16[768,256]{1,0:T(8,128)(2,1)S(1)}, bf16[768,256]{1,0:T(8,128)(2,1)}, u32[]{:S(2)}, u32[]{:S(2)}) collective-permute-start(bf16[768,256]{1,0:T(8,128)(2,1)S(1)} %collective-permute-done.12), channel_id=1, source_target_pairs={{0,4},{4,8},{8,12},{12,16},{16,20},{20,24},{24,28},{28,32},{32,36}... | collective-permute-start | bytes 1179656 | tf_op jit(solution)/shard_map/ppermute | solution.py:179
  125.6 15.1 %collective-permute-start.4 = (bf16[768,256]{1,0:T(8,128)(2,1)}, bf16[768,256]{1,0:T(8,128)(2,1)}, u32[]{:S(2)}, u32[]{:S(2)}) collective-permute-start(bf16[768,256]{1,0:T(8,128)(2,1)} %collective-permute-done.3.refs_4_), channel_id=1, source_target_pairs={{0,4},{4,8},{8,12},{12,16},{16,20},{20,24},{24,28},{28,32},{32,36}... | collective-permute-start | bytes 1179656 | tf_op jit(solution)/shard_map/ppermute | solution.py:179
  130.2 15.3 %collective-permute-start.14 = (bf16[768,256]{1,0:T(8,128)(2,1)}, bf16[768,256]{1,0:T(8,128)(2,1)}, u32[]{:S(2)}, u32[]{:S(2)}) collective-permute-start(bf16[768,256]{1,0:T(8,128)(2,1)} %collective-permute-done.13), channel_id=1, source_target_pairs={{0,4},{4,8},{8,12},{12,16},{16,20},{20,24},{24,28},{28,32},{32,36}... | collective-permute-start | bytes 1179656 | tf_op jit(solution)/shard_map/ppermute | solution.py:179
  135.4 5.3 %copy-start.12 = (s32[3]{0:T(128)S(1)}, s32[3]{0:T(128)}, u32[]{:S(2)}) copy-start(s32[3]{0:T(128)} %constant.105.clone) | copy-start | bytes 40
  135.6 40.7 %collective-permute-start.18 = (bf16[3,768,256]{2,1,0:T(8,128)(2,1)S(1)}, bf16[3,768,256]{2,1,0:T(8,128)(2,1)S(1)}, u32[]{:S(2)}, u32[]{:S(2)}) collective-permute-start(bf16[3,768,256]{2,1,0:T(8,128)(2,1)S(1)} %pad_maximum_fusion), channel_id=1, source_target_pairs={{0,64},{64,0},{1,65},{65,1},{2,66},{66,2},{3,67},{67,3},{4,68},{68... | collective-permute-start | bytes 3538952 | tf_op jit(solution)/shard_map/ppermute | solution.py:195
  140.7 15.1 %collective-permute-start.5 = (bf16[768,256]{1,0:T(8,128)(2,1)}, bf16[768,256]{1,0:T(8,128)(2,1)}, u32[]{:S(2)}, u32[]{:S(2)}) collective-permute-start(bf16[768,256]{1,0:T(8,128)(2,1)} %collective-permute-done.4.refs_0_), channel_id=1, source_target_pairs={{0,4},{4,8},{8,12},{12,16},{16,20},{20,24},{24,28},{28,32},{32,36}... | collective-permute-start | bytes 1179656 | tf_op jit(solution)/shard_map/ppermute | solution.py:179
  145.6 15.1 %collective-permute-start.15 = (bf16[768,256]{1,0:T(8,128)(2,1)}, bf16[768,256]{1,0:T(8,128)(2,1)}, u32[]{:S(2)}, u32[]{:S(2)}) collective-permute-start(bf16[768,256]{1,0:T(8,128)(2,1)} %collective-permute-done.14), channel_id=1, source_target_pairs={{0,4},{4,8},{8,12},{12,16},{16,20},{20,24},{24,28},{28,32},{32,36}... | collective-permute-start | bytes 1179656 | tf_op jit(solution)/shard_map/ppermute | solution.py:179
  149.5 15.8 %copy-start.11 = (s32[6]{0:T(128)S(1)}, s32[6]{0:T(128)}, u32[]{:S(2)}) copy-start(s32[6]{0:T(128)} %param.12) | copy-start | bytes 76
  149.5 26.8 %collective-permute-start.19 = (bf16[2,768,256]{2,1,0:T(8,128)(2,1)}, bf16[2,768,256]{2,1,0:T(8,128)(2,1)S(1)}, u32[]{:S(2)}, u32[]{:S(2)}) collective-permute-start(bf16[2,768,256]{2,1,0:T(8,128)(2,1)} %pad_maximum_fusion.2), channel_id=1, source_target_pairs={{0,64},{64,0},{1,65},{65,1},{2,66},{66,2},{3,67},{67,3},{4,68},{68... | collective-permute-start | bytes 2359304 | tf_op jit(solution)/shard_map/ppermute | solution.py:195
  155.9 9.9 %collective-permute-start.6 = (bf16[768,256]{1,0:T(8,128)(2,1)}, bf16[768,256]{1,0:T(8,128)(2,1)S(1)}, u32[]{:S(2)}, u32[]{:S(2)}) collective-permute-start(bf16[768,256]{1,0:T(8,128)(2,1)} %collective-permute-done.5.refs_1_), channel_id=1, source_target_pairs={{0,4},{4,8},{8,12},{12,16},{16,20},{20,24},{24,28},{28,32},{32,36}... | collective-permute-start | bytes 1179656 | tf_op jit(solution)/shard_map/ppermute | solution.py:179
  162.8 24.4 %collective-permute-start.16 = (bf16[2,768,256]{2,1,0:T(8,128)(2,1)}, bf16[2,768,256]{2,1,0:T(8,128)(2,1)}, u32[]{:S(2)}, u32[]{:S(2)}) collective-permute-start(bf16[2,768,256]{2,1,0:T(8,128)(2,1)} %pad_maximum_fusion.1), channel_id=1, source_target_pairs={{0,64},{64,0},{1,65},{65,1},{2,66},{66,2},{3,67},{67,3},{4,68},{68... | collective-permute-start | bytes 2359304 | tf_op jit(solution)/shard_map/ppermute | solution.py:195
  165.7 10.5 %copy-start.7 = (bf16[768,256]{1,0:T(8,128)(2,1)}, bf16[768,256]{1,0:T(8,128)(2,1)S(1)}, u32[]{:S(2)}) copy-start(bf16[768,256]{1,0:T(8,128)(2,1)S(1)} %collective-permute-done.6.refs_2_) | copy-start | bytes 1179652
  165.7 21.5 %collective-permute-start.7 = (bf16[768,256]{1,0:T(8,128)(2,1)S(1)}, bf16[768,256]{1,0:T(8,128)(2,1)S(1)}, u32[]{:S(2)}, u32[]{:S(2)}) collective-permute-start(bf16[768,256]{1,0:T(8,128)(2,1)S(1)} %collective-permute-done.6.refs_2_), channel_id=1, source_target_pairs={{0,4},{4,8},{8,12},{12,16},{16,20},{20,24},{24,28},{28,32},{32,36}... | collective-permute-start | bytes 1179656 | tf_op jit(solution)/shard_map/ppermute | solution.py:179
  176.3 1.0 copy-start.1
  177.3 0.9 copy-start.2
  187.2 18.9 %copy-start.9 = (s32[768]{0:T(1024)S(1)}, s32[768]{0:T(1024)}, u32[]{:S(2)}) copy-start(s32[768]{0:T(1024)} %param.11) | copy-start | bytes 9220
  187.2 0.8 copy-start.3
  195.9 26.3 %all-to-all-start.2 = ((f32[64,1,384]{2,1,0:T(1,128)}), f32[64,1,384]{2,1,0:T(1,128)S(1)}, u32[]{:S(2)}, u32[]{:S(2)}) async-start(f32[64,1,384]{2,1,0:T(1,128)} %all_to_all.18), calls=%async_computation.2 | async-start | bytes 196608 | tf_op jit(solution)/shard_map/all_to_all | solution.py:46
  223.6 10.7 %all-to-all-start.3 = ((f32[32,1,128]{2,1,0:T(1,128)}), f32[32,1,128]{2,1,0:T(1,128)S(1)}, u32[]{:S(2)}, u32[]{:S(2)}) async-start(f32[32,1,128]{2,1,0:T(1,128)} %broadcast_in_dim.79), calls=%async_computation.3 | async-start | bytes 32768 | tf_op jit(solution)/shard_map/all_to_all | solution.py:29

commit v7 on v1

v7 whole, which is shorter than its diff:
```python
import jax
import jax.numpy as jnp
from jax import lax
from jax.experimental import pallas as pl
from jax.experimental.pallas import tpu as pltpu
from jax.sharding import Mesh
from jax.sharding import PartitionSpec as P


SEQ_LEN = 128
DOMAINS = 64
TOK = ("x", "c")
VOCAB = ("z", "y")
SWAP = [(0, 1), (1, 0)]
BLOCK = 256
TILE = 256
LONG = 512
LIMIT = 60 << 20
ROUNDS = 8
BATCHES = ((1, 2, 3), (4, 5, 6), (7,))
DEPTHS = (0, 2, 6, 11, 16)


def to_all(array, axis, copies):
    return lax.all_to_all(
        jnp.broadcast_to(array[None], (copies, *array.shape)), axis, 0, 0, tiled=True
    )


def along_z(array):
    zs = lax.axis_size("z")
    pairs = [(c * zs + z, c * zs + (z + (1 - 2 * c)) % zs) for c in range(2) for z in range(zs)]
    return lax.ppermute(array, ("c", "z"), pairs)


def gathered_weight(weight):
    own = to_all(weight, "x", lax.axis_size("x"))
    return own, lax.ppermute(own, "c", SWAP)


def before_tail(tokens, z, y, domains, seq_len):
    zs, ys = lax.axis_size("z"), lax.axis_size("y")
    own = tokens // (zs * ys)
    index = lax.iota(jnp.int32, zs * own)
    local = (index // own) * (ys * own) + y * own + index % own
    sequence = lax.broadcasted_iota(jnp.int32, (zs * own, seq_len.shape[0]), 1)
    of_token = (local // SEQ_LEN)[:, None] == sequence
    lengths = jnp.sum(jnp.where(of_token, seq_len[None], 0), axis=1)
    mask = (local % SEQ_LEN < lengths).astype(jnp.float32)
    place = lax.broadcasted_iota(jnp.int32, (zs, ys, own), 1)
    domain = jnp.sum(jnp.where(place == y, domains.reshape(zs, ys, own), 0), axis=1).reshape(-1)
    here = domain[None, :] == lax.broadcasted_iota(jnp.int32, (DOMAINS, zs * own), 0)
    here = here.astype(jnp.float32)
    outputs = (lax.broadcasted_iota(jnp.int32, (zs, own), 0) == z).astype(jnp.float32)
    return mask, here, outputs, jnp.sum(here * mask[None], axis=1)


def tail(stats, mask, here, outputs, counts):
    zs, ys = lax.axis_size("z"), lax.axis_size("y")
    own = stats.shape[1] // (zs * ys)
    slices = stats.reshape(2, zs, ys, own).transpose(2, 0, 1, 3)
    send = jnp.broadcast_to(slices.reshape(1, ys, -1), (zs, ys, 2 * zs * own))
    got = lax.all_to_all(send.reshape(zs * ys, -1), VOCAB, 0, 0, tiled=True)
    got = got.reshape(zs * ys, 2, zs * own)
    top = jnp.max(got[:, 0], axis=0)
    total = jnp.sum(jnp.exp(got[:, 0] - top[None]), axis=0)
    loss = (jnp.log(total) + top - jnp.sum(got[:, 1], axis=0)) * mask
    sums = jnp.sum(jnp.where(here > 0, loss[None], 0.0), axis=1)
    token_loss = jnp.sum(jnp.where(outputs > 0, loss.reshape(zs, own), 0.0), axis=0)
    part, token_loss = lax.optimization_barrier((jnp.concatenate([sums, counts]), token_loss))
    axes = ("x", "c", "y")
    whole = jnp.sum(to_all(part, axes, lax.axis_size(axes)), axis=0)
    mean = whole[:DOMAINS] / jnp.maximum(whole[DOMAINS:], 1.0)
    return token_loss, mean


def product_kernel(kinds, away):
    def kernel(where, *refs):
        refs = list(refs)
        blocks = []
        for kind in kinds:
            ref = refs.pop(0)
            blocks += [ref.at[k] for k in range(kind)] if kind else [ref]
        own, theirs, wanted, out, acc, rows, lefts, sems = refs
        core, z = where[0], where[1]

        def fetch(k, weights, source):
            return pltpu.make_async_copy(
                weights.at[source // 4, pl.ds(lax.rem(source, 2) * BLOCK, BLOCK)],
                rows.at[pl.ds(k * BLOCK, BLOCK)],
                sems.at[0, k],
            )

        def fetch_block(k):
            return pltpu.make_async_copy(blocks[k], lefts.at[k], sems.at[1, k])

        for k, far in enumerate(away):
            source = lax.rem(z + far * (2 * core - 1) + 16, 16)
            fetch_block(k).start()
            mine = lax.rem(source // 2, 2) == core
            pl.when(mine)(fetch(k, own, source).start)
            pl.when(jnp.logical_not(mine))(fetch(k, theirs, source).start)

        tokens, columns = acc.shape
        for first, end in zip(DEPTHS, DEPTHS[1:]):
            for k in range(first, end):
                fetch_block(k).wait()
                fetch(k, own, 0).wait()
            deep = slice(first * BLOCK, end * BLOCK)
            for at in range(0, tokens, TILE):
                part = slice(at, at + TILE)
                left = jnp.concatenate([lefts[k, part] for k in range(first, end)], axis=1)
                for begin in range(0, columns, LONG):
                    side = slice(begin, begin + LONG)
                    total = jnp.dot(left, rows[deep, side], preferred_element_type=jnp.float32)
                    acc[part, side] = total + acc[part, side] if first else total
                if end < len(away):
                    continue
                values = acc[part]
                top = jnp.max(values, axis=1, keepdims=True)
                total = jnp.sum(jnp.exp(values - top), axis=1, keepdims=True)
                lane = lax.broadcasted_iota(jnp.int32, values.shape, 1)
                picked = jnp.where(lane == wanted[part], values, 0.0)
                picked = jnp.sum(picked, axis=1, keepdims=True)
                lse = jnp.log(total) + top
                lane = lax.broadcasted_iota(jnp.int32, (TILE, 128), 1)
                out[:, part] = jnp.where(lane == 0, lse, picked).T[:8]

    return kernel


def product(where, away, blocks, weights, wanted):
    kinds = [b.shape[0] if b.ndim == 3 else 0 for b in blocks]
    count, tokens, columns = len(away), blocks[0].shape[-2], weights[0].shape[2]
    vmem = pl.BlockSpec(memory_space=pltpu.VMEM)
    hbm = pl.BlockSpec(memory_space=pltpu.HBM)
    return pl.pallas_call(
        product_kernel(kinds, away),
        in_specs=[pl.BlockSpec(memory_space=pltpu.SMEM)] + [hbm] * (len(blocks) + 2) + [vmem],
        out_specs=vmem,
        out_shape=jax.ShapeDtypeStruct((8, tokens), jnp.float32),
        scratch_shapes=[
            pltpu.VMEM((tokens, columns), jnp.float32),
            pltpu.VMEM((count * BLOCK, columns), jnp.bfloat16),
            pltpu.VMEM((count, tokens, BLOCK), jnp.bfloat16),
            pltpu.SemaphoreType.DMA((2, count)),
        ],
        compiler_params=pltpu.CompilerParams(vmem_limit_bytes=LIMIT),
        cost_estimate=pl.CostEstimate(
            flops=2 * count * tokens * BLOCK * columns,
            bytes_accessed=count * BLOCK * (tokens + columns) * 2,
            transcendentals=tokens * columns,
        ),
    )(where, *blocks, *weights, wanted)


def loss(hidden, weight, targets, domains, seq_len):
    ys = lax.axis_size("y")
    core, z, y = (lax.axis_index(name) for name in ("c", "z", "y"))
    low = lax.axis_index(VOCAB) * weight.shape[1]
    hidden, where, z, y, low = lax.optimization_barrier((hidden, jnp.stack([core, z]), z, y, low))
    mine = to_all(hidden.T, "y", ys).reshape(BLOCK, -1).T
    theirs = lax.ppermute(mine, "c", SWAP)
    weights = gathered_weight(weight)
    own, other = [mine], [theirs]
    for r in range(1, ROUNDS + 1):
        own.append(along_z(own[-1]))
        if r == 2:
            domains, seq_len, targets, own[2] = lax.optimization_barrier(
                (domains, seq_len, targets, own[2])
            )
            ready = before_tail(targets.shape[0], z, y, domains, seq_len)
            wanted = (targets - low)[:, None]
        if r == 4:
            own[4], ready, wanted = lax.optimization_barrier((own[4], ready, wanted))
        if r < ROUNDS:
            other.append(along_z(other[-1]))
    swapped = []
    for some in BATCHES:
        swapped.append(lax.ppermute(jnp.stack([other[r] for r in some]), "c", SWAP))
    away = [*range(7), *(-r for some in BATCHES[:2] for r in some), 7, 8, *(-r for r in BATCHES[2])]
    blocks = [*own[:7], *swapped[:2], own[7], own[8], swapped[2]]
    stats = product(where, away, blocks, weights, wanted)
    return tail(stats[:2], *ready)


def solution(mesh):
    split = Mesh(mesh.devices.reshape(4, 2, 16, 4), ("x", "c", "z", "y"))
    placed = (P(TOK, VOCAB), P(TOK, VOCAB), P(TOK), P(TOK), P(TOK))
    return jax.shard_map(loss, mesh=split, in_specs=placed, out_specs=(P((*TOK, *VOCAB)), P()), check_vma=False)
```

time: 176 us -> 224 us (1.27)
  starting transfers between devices: 34.1 us -> 104 us
  blocking collectives: 64.9 us -> 51 us
  between operations: 14.3 us -> 1.16 us
  matrix products: 12.7 us -> 0 us
  Pallas kernels: 0 us -> 11.3 us
  local copies, waits for them, and re-layouts: 3.85 us -> 6.3 us
    ppermute x1 -> x19, starting transfers between devices: 9.23 us -> 91.7 us  [the longest x15 71.4 us: along_z(): return lax.ppermute(array, ('c', 'z'), pairs)]
    all_to_all x1, waiting for transfers between devices: 6.33 us -> 37.3 us  [to_all(): lax.all_to_all(jnp.broadcast_to(array[None], (copies, *array.shape)), axi...]
    all_to_all x1 -> x2, blocking collectives: 51.9 us -> 26.5 us  [to_all(): lax.all_to_all(jnp.broadcast_to(array[None], (copies, *array.shape)), axi...]
    all_to_all x0 -> x1, blocking collectives: none -> 24.5 us  [tail(): got = lax.all_to_all(send.reshape(zs * ys, -1), VOCAB, 0, 0, tiled=True)]
    all_gather x1 -> x0, waiting for transfers between devices: 20.7 us -> none  [body(): features = lax.all_gather(features, 'z', axis=1, tiled=True)]
    all_to_all x1 -> x0, waiting for transfers between devices: 14.1 us -> none  [tail(): got = lax.all_to_all(send.reshape(zs * ys, -1), VOCAB, 0, 0, tiled=True)]
    all_to_all x1 -> x0, starting transfers between devices: 13.5 us -> none  [tail(): got = lax.all_to_all(send.reshape(zs * ys, -1), VOCAB, 0, 0, tiled=True)]
    all_gather x1 -> x0, blocking collectives: 13 us -> none  [body(): features = lax.all_gather(hidden, 'y', axis=1, tiled=True)]
  transfers between devices with their start and end apart: 5 -> 21, of which waited for: 4 -> 9; matrix products, arithmetic and copies ran while one was open for 6% -> 1% of each run, Pallas kernels for 0% -> 0%
where the time goes in v7:
time: 224 us; the launch traced here: 223 us
  starting transfers between devices  104 us (46%)
  blocking collectives  51 us (23%)
  waiting for transfers between devices  44.7 us (20%)
  Pallas kernels  11.3 us (5%)
  local copies, waits for them, and re-layouts  6.3 us (3%)
  other arithmetic  4.13 us (2%)
    ppermute x15, starting transfers between devices, along_z(): return lax.ppermute(array, ('c', 'z'), pairs)  71.4 us
    all_to_all x1, waiting for transfers between devices, to_all(): lax.all_to_all(jnp.broadcast_to(array[None], (copies, *array.shape)), axi...  37.3 us
    all_to_all x2, blocking collectives, to_all(): lax.all_to_all(jnp.broadcast_to(array[None], (copies, *array.shape)), axi...  26.5 us
    all_to_all x1, blocking collectives, tail(): got = lax.all_to_all(send.reshape(zs * ys, -1), VOCAB, 0, 0, tiled=True)  24.5 us
    ppermute x3, starting transfers between devices, loss(): swapped.append(lax.ppermute(jnp.stack([other[r] for r in some]), 'c', SWAP))  13 us
    pallas_call x1, Pallas kernels, product(): pl.pallas_call(product_kernel(kinds, away), in_specs=[pl.BlockSpec(memory...  11.3 us
    ppermute x1, starting transfers between devices, gathered_weight(): return (own, lax.ppermute(own, 'c', SWAP))  7.55 us
    ppermute x1, starting transfers between devices, loss(): theirs = lax.ppermute(mine, 'c', SWAP)  7.33 us
  transfers between devices with their start and end apart: 21, of which 9 were waited for; matrix products, arithmetic and copies ran while one was open for 1% of the time, Pallas kernels for 0%

profile of v7, /device:TPU:1, one launch (start us, length us, event | category | flops | bytes accessed | tf_op | source)
XLA Modules:
  0.0 223.1 jit_solution(17361175152330184121)
XLA Ops:
  0.7 0.6 pad_add_fusion.where
  1.2 0.9 broadcast_in_dim.40
  2.1 11.0 %all_to_all.25 = bf16[4,64,768]{2,1,0:T(8,128)(2,1)S(1)} all-to-all(bf16[4,64,768]{2,1,0:T(8,128)(2,1)S(1)} %broadcast_in_dim.40), channel_id=1, replica_groups=mesh['x'=4,'c'=2,'z'=16,'y'=4] {'y'}, dimensions={0} | all-to-all | bytes 786432 | tf_op jit(solution)/shard_map/all_to_all | solution.py:25
  13.2 2.5 %broadcast_in_dim.66 = bf16[4,512,1024]{2,1,0:T(8,128)(2,1)} broadcast(bf16[512,1024]{1,0:T(8,128)(2,1)S(1)} %copy-done), dimensions={1,2} | broadcast | bytes 5242880 | tf_op jit(solution)/shard_map/broadcast_in_dim | solution.py:26
  15.7 5.1 %all-to-all-start.1 = ((bf16[4,512,1024]{2,1,0:T(8,128)(2,1)}), bf16[4,512,1024]{2,1,0:T(8,128)(2,1)}, u32[]{:S(2)}, u32[]{:S(2)}) async-start(bf16[4,512,1024]{2,1,0:T(8,128)(2,1)} %broadcast_in_dim.66), calls=%async_computation.1 | async-start | bytes 8388608 | tf_op jit(solution)/shard_map/all_to_all | solution.py:25
  20.9 0.2 copy.17
  21.0 7.3 %collective-permute-start.6 = (bf16[768,256]{1,0:T(8,128)(2,1)S(1)}, bf16[768,256]{1,0:T(8,128)(2,1)S(1)}, u32[]{:S(2)}, u32[]{:S(2)}) collective-permute-start(bf16[768,256]{1,0:T(8,128)(2,1)S(1)} %bitcast.29), channel_id=1, source_target_pairs={{0,64},{64,0},{1,65},{65,1},{2,66},{66,2},{3,67},{67,3},{4,68},{68... | collective-permute-start | bytes 1179656 | tf_op jit(solution)/shard_map/ppermute | solution.py:163
  28.4 37.3 %all-to-all-done.1.refs_12_ = bf16[4,512,1024]{2,1,0:T(8,128)(2,1)} async-done(((bf16[4,512,1024]{2,1,0:T(8,128)(2,1)}), bf16[4,512,1024]{2,1,0:T(8,128)(2,1)}, u32[]{:S(2)}, u32[]{:S(2)}) %all-to-all-start.1) | async-done | bytes 4194336 | tf_op jit(solution)/shard_map/all_to_all | solution.py:25
  65.7 7.5 %collective-permute-start.19 = (bf16[4,512,1024]{2,1,0:T(8,128)(2,1)}, bf16[4,512,1024]{2,1,0:T(8,128)(2,1)}, u32[]{:S(2)}, u32[]{:S(2)}) collective-permute-start(bf16[4,512,1024]{2,1,0:T(8,128)(2,1)} %all-to-all-done.1.refs_12_), channel_id=1, source_target_pairs={{0,64},{64,0},{1,65},{65,1},{2,66},{66,2},{3,67},{67,3},{4,68},{68... | collective-permute-start | bytes 12582920 | tf_op jit(solution)/shard_map/ppermute | solution.py:38
  73.2 11.3 %collective-permute-start.7 = (bf16[768,256]{1,0:T(8,128)(2,1)S(1)}, bf16[768,256]{1,0:T(8,128)(2,1)S(1)}, u32[]{:S(2)}, u32[]{:S(2)}) collective-permute-start(bf16[768,256]{1,0:T(8,128)(2,1)S(1)} %collective-permute-done.6), channel_id=1, source_target_pairs={{0,4},{4,8},{8,12},{12,16},{16,20},{20,24},{24,28},{28,32},{32,36}... | collective-permute-start | bytes 1179656 | tf_op jit(solution)/shard_map/ppermute | solution.py:33
  84.5 2.6 %collective-permute-start = (bf16[768,256]{1,0:T(8,128)(2,1)S(1)}, bf16[768,256]{1,0:T(8,128)(2,1)S(1)}, u32[]{:S(2)}, u32[]{:S(2)}) collective-permute-start(bf16[768,256]{1,0:T(8,128)(2,1)S(1)} %bitcast.30), channel_id=1, source_target_pairs={{0,4},{4,8},{8,12},{12,16},{16,20},{20,24},{24,28},{28,32},{32,36}... | collective-permute-start | bytes 1179656 | tf_op jit(solution)/shard_map/ppermute | solution.py:33
  87.2 2.1 collective-permute-done.7
  89.2 5.0 %collective-permute-start.8 = (bf16[768,256]{1,0:T(8,128)(2,1)S(1)}, bf16[768,256]{1,0:T(8,128)(2,1)S(1)}, u32[]{:S(2)}, u32[]{:S(2)}) collective-permute-start(bf16[768,256]{1,0:T(8,128)(2,1)S(1)} %collective-permute-done.7), channel_id=1, source_target_pairs={{0,4},{4,8},{8,12},{12,16},{16,20},{20,24},{24,28},{28,32},{32,36}... | collective-permute-start | bytes 1179656 | tf_op jit(solution)/shard_map/ppermute | solution.py:33
  94.3 4.2 %collective-permute-start.1 = (bf16[768,256]{1,0:T(8,128)(2,1)S(1)}, bf16[768,256]{1,0:T(8,128)(2,1)S(1)}, u32[]{:S(2)}, u32[]{:S(2)}) collective-permute-start(bf16[768,256]{1,0:T(8,128)(2,1)S(1)} %collective-permute-done.refs_1_), channel_id=1, source_target_pairs={{0,4},{4,8},{8,12},{12,16},{16,20},{20,24},{24,28},{28,32},{32,36}... | collective-permute-start | bytes 1179656 | tf_op jit(solution)/shard_map/ppermute | solution.py:33
  98.5 0.5 collective-permute-done.8
  99.0 5.0 %collective-permute-start.9 = (bf16[768,256]{1,0:T(8,128)(2,1)S(1)}, bf16[768,256]{1,0:T(8,128)(2,1)S(1)}, u32[]{:S(2)}, u32[]{:S(2)}) collective-permute-start(bf16[768,256]{1,0:T(8,128)(2,1)S(1)} %collective-permute-done.8), channel_id=1, source_target_pairs={{0,4},{4,8},{8,12},{12,16},{16,20},{20,24},{24,28},{28,32},{32,36}... | collective-permute-start | bytes 1179656 | tf_op jit(solution)/shard_map/ppermute | solution.py:33
  104.0 0.0 collective-permute-done.1.refs_2_
  104.1 0.1 reshape.109
  104.2 4.1 %collective-permute-start.2 = (bf16[768,256]{1,0:T(8,128)(2,1)S(1)}, bf16[768,256]{1,0:T(8,128)(2,1)S(1)}, u32[]{:S(2)}, u32[]{:S(2)}) collective-permute-start(bf16[768,256]{1,0:T(8,128)(2,1)S(1)} %collective-permute-done.1.refs_2_), channel_id=1, source_target_pairs={{0,4},{4,8},{8,12},{12,16},{16,20},{20,24},{24,28},{28,32},{32,36}... | collective-permute-start | bytes 1179656 | tf_op jit(solution)/shard_map/ppermute | solution.py:33
  108.3 0.1 select_reduce_fusion.4
  108.4 0.2 collective-permute-done.9
  108.7 5.0 %collective-permute-start.11 = (bf16[768,256]{1,0:T(8,128)(2,1)S(1)}, bf16[768,256]{1,0:T(8,128)(2,1)S(1)}, u32[]{:S(2)}, u32[]{:S(2)}) collective-permute-start(bf16[768,256]{1,0:T(8,128)(2,1)S(1)} %collective-permute-done.9), channel_id=1, source_target_pairs={{0,4},{4,8},{8,12},{12,16},{16,20},{20,24},{24,28},{28,32},{32,36}... | collective-permute-start | bytes 1179656 | tf_op jit(solution)/shard_map/ppermute | solution.py:33
  113.8 4.3 %collective-permute-start.3 = (bf16[768,256]{1,0:T(8,128)(2,1)S(1)}, bf16[768,256]{1,0:T(8,128)(2,1)}, u32[]{:S(2)}, u32[]{:S(2)}) collective-permute-start(bf16[768,256]{1,0:T(8,128)(2,1)S(1)} %collective-permute-done.2.refs_3_), channel_id=1, source_target_pairs={{0,4},{4,8},{8,12},{12,16},{16,20},{20,24},{24,28},{28,32},{32,36}... | collective-permute-start | bytes 1179656 | tf_op jit(solution)/shard_map/ppermute | solution.py:33
  118.1 0.4 collective-permute-done.11
  118.4 5.0 %collective-permute-start.12 = (bf16[768,256]{1,0:T(8,128)(2,1)S(1)}, bf16[768,256]{1,0:T(8,128)(2,1)S(1)}, u32[]{:S(2)}, u32[]{:S(2)}) collective-permute-start(bf16[768,256]{1,0:T(8,128)(2,1)S(1)} %collective-permute-done.11), channel_id=1, source_target_pairs={{0,4},{4,8},{8,12},{12,16},{16,20},{20,24},{24,28},{28,32},{32,36}... | collective-permute-start | bytes 1179656 | tf_op jit(solution)/shard_map/ppermute | solution.py:33
  123.4 0.1 select_reduce_fusion.2
  123.5 0.1 eq.39
  123.6 0.6 select_reduce_fusion.1
  124.3 0.6 fusion.2
  124.9 0.1 iota.37
  125.0 3.0 %collective-permute-start.4 = (bf16[768,256]{1,0:T(8,128)(2,1)}, bf16[768,256]{1,0:T(8,128)(2,1)S(1)}, u32[]{:S(2)}, u32[]{:S(2)}) collective-permute-start(bf16[768,256]{1,0:T(8,128)(2,1)} %collective-permute-done.3.refs_4_), channel_id=1, source_target_pairs={{0,4},{4,8},{8,12},{12,16},{16,20},{20,24},{24,28},{28,32},{32,36}... | collective-permute-start | bytes 1179656 | tf_op jit(solution)/shard_map/ppermute | solution.py:33
  128.0 0.2 collective-permute-done.12
  128.1 5.0 %collective-permute-start.13 = (bf16[768,256]{1,0:T(8,128)(2,1)S(1)}, bf16[768,256]{1,0:T(8,128)(2,1)S(1)}, u32[]{:S(2)}, u32[]{:S(2)}) collective-permute-start(bf16[768,256]{1,0:T(8,128)(2,1)S(1)} %collective-permute-done.12), channel_id=1, source_target_pairs={{0,4},{4,8},{8,12},{12,16},{16,20},{20,24},{24,28},{28,32},{32,36}... | collective-permute-start | bytes 1179656 | tf_op jit(solution)/shard_map/ppermute | solution.py:33
  133.2 0.1 pad_maximum_fusion
  133.3 4.7 %collective-permute-start.10 = (bf16[3,768,256]{2,1,0:T(8,128)(2,1)S(1)}, bf16[3,768,256]{2,1,0:T(8,128)(2,1)}, u32[]{:S(2)}, u32[]{:S(2)}) collective-permute-start(bf16[3,768,256]{2,1,0:T(8,128)(2,1)S(1)} %pad_maximum_fusion), channel_id=1, source_target_pairs={{0,64},{64,0},{1,65},{65,1},{2,66},{66,2},{3,67},{67,3},{4,68},{68... | collective-permute-start | bytes 3538952 | tf_op jit(solution)/shard_map/ppermute | solution.py:180
  138.1 4.9 %collective-permute-start.5 = (bf16[768,256]{1,0:T(8,128)(2,1)S(1)}, bf16[768,256]{1,0:T(8,128)(2,1)S(1)}, u32[]{:S(2)}, u32[]{:S(2)}) collective-permute-start(bf16[768,256]{1,0:T(8,128)(2,1)S(1)} %collective-permute-done.4.refs_5_), channel_id=1, source_target_pairs={{0,4},{4,8},{8,12},{12,16},{16,20},{20,24},{24,28},{28,32},{32,36}... | collective-permute-start | bytes 1179656 | tf_op jit(solution)/shard_map/ppermute | solution.py:33
  143.0 0.1 pad_maximum_fusion.1
  143.1 3.9 %collective-permute-start.14 = (bf16[3,768,256]{2,1,0:T(8,128)(2,1)S(1)}, bf16[3,768,256]{2,1,0:T(8,128)(2,1)}, u32[]{:S(2)}, u32[]{:S(2)}) collective-permute-start(bf16[3,768,256]{2,1,0:T(8,128)(2,1)S(1)} %pad_maximum_fusion.1), channel_id=1, source_target_pairs={{0,64},{64,0},{1,65},{65,1},{2,66},{66,2},{3,67},{67,3},{4,68},{68... | collective-permute-start | bytes 3538952 | tf_op jit(solution)/shard_map/ppermute | solution.py:180
  147.0 0.7 collective-permute-done.5.refs_6_
  147.6 5.0 %collective-permute-start.15 = (bf16[768,256]{1,0:T(8,128)(2,1)S(1)}, bf16[768,256]{1,0:T(8,128)(2,1)S(1)}, u32[]{:S(2)}, u32[]{:S(2)}) collective-permute-start(bf16[768,256]{1,0:T(8,128)(2,1)S(1)} %collective-permute-done.5.refs_6_), channel_id=1, source_target_pairs={{0,4},{4,8},{8,12},{12,16},{16,20},{20,24},{24,28},{28,32},{32,36}... | collective-permute-start | bytes 1179656 | tf_op jit(solution)/shard_map/ppermute | solution.py:33
  152.7 1.9 collective-permute-start.17
  154.6 2.8 %collective-permute-done.15.refs_9_ = bf16[768,256]{1,0:T(8,128)(2,1)S(1)} collective-permute-done((bf16[768,256]{1,0:T(8,128)(2,1)S(1)}, bf16[768,256]{1,0:T(8,128)(2,1)S(1)}, u32[]{:S(2)}, u32[]{:S(2)}) %collective-permute-start.15) | collective-permute-done | bytes 393248 | tf_op jit(solution)/shard_map/ppermute | solution.py:33
  157.4 5.0 %collective-permute-start.16 = (bf16[768,256]{1,0:T(8,128)(2,1)S(1)}, bf16[768,256]{1,0:T(8,128)(2,1)S(1)}, u32[]{:S(2)}, u32[]{:S(2)}) collective-permute-start(bf16[768,256]{1,0:T(8,128)(2,1)S(1)} %collective-permute-done.15.refs_9_), channel_id=1, source_target_pairs={{0,4},{4,8},{8,12},{12,16},{16,20},{20,24},{24,28},{28,32},{32,36}... | collective-permute-start | bytes 1179656 | tf_op jit(solution)/shard_map/ppermute | solution.py:33
  162.4 4.4 %collective-permute-start.18 = (bf16[1,768,256]{2,1,0:T(8,128)(2,1)}, bf16[1,768,256]{2,1,0:T(8,128)(2,1)}, u32[]{:S(2)}, u32[]{:S(2)}) collective-permute-start(bf16[1,768,256]{2,1,0:T(8,128)(2,1)} %bitcast.11), channel_id=1, source_target_pairs={{0,64},{64,0},{1,65},{65,1},{2,66},{66,2},{3,67},{67,3},{4,68},{68... | collective-permute-start | bytes 1179656 | tf_op jit(solution)/shard_map/ppermute | solution.py:180
  166.8 1.0 copy.18.refs_14_
  167.7 0.7 collective-permute-done.18.refs_11_
  168.5 0.0 copy-done.13
  168.5 11.3 %shard_map.68 = f32[8,768]{1,0:T(8,128)} custom-call(s32[2]{0:T(128)} %pad_add_fusion.where, bf16[768,256]{1,0:T(8,128)(2,1)} %bitcast.31, bf16[768,256]{1,0:T(8,128)(2,1)} %copy-done.7, bf16[768,256]{1,0:T(8,128)(2,1)} %copy-done.8, bf16[768,256]{1,0:T(8,128)(2,1)} %copy-done.9, bf16[768,256]{1,0:T(8,128)(2,1)} %collective-permute-done.3.refs_4_, ...), custom_call_target="tpu_custom_call" | custom-call | flops 6442450944 | bytes 14680064 | tf_op jit(solution)/shard_map/pallas_call | solution.py:137
  179.8 0.0 copy-start.6
  179.8 0.8 slice.21
  180.6 0.1 reshape.110
  180.8 0.1 broadcast_in_dim.67
  180.9 0.1 all_to_all.18
  181.0 24.5 %all_to_all.26 = f32[64,1,384]{2,1,0:T(1,128)S(1)} all-to-all(f32[64,1,384]{2,1,0:T(1,128)S(1)} %all_to_all.18), channel_id=1, replica_groups=mesh['x'=4,'c'=2,'z'=16,'y'=4] {'z','y'}, dimensions={0} | all-to-all | bytes 196608 | tf_op jit(solution)/shard_map/all_to_all | solution.py:63
  205.6 0.2 reduce.3
  205.8 0.1 reshape.111
  206.0 0.2 slice_reduce_fusion.1
  206.2 0.1 reshape.112
  206.3 0.0 copy-done.2
  206.3 0.1 select_reduce_fusion
  206.4 0.1 pad_maximum_fusion.2
  206.5 0.5 select_reduce_fusion.3
  207.0 15.5 %all_to_all.27 = f32[32,1,128]{2,1,0:T(1,128)S(1)} all-to-all(f32[32,1,128]{2,1,0:T(1,128)S(1)} %broadcast_in_dim.70), channel_id=1, replica_groups=mesh['x'=4,'c'=2,'z'=16,'y'=4] {'x','c','y'}, dimensions={0} | all-to-all | bytes 32768 | tf_op jit(solution)/shard_map/all_to_all | solution.py:25
  222.5 0.6 maximum_divide_fusion
  (48 shorter events, 0.2 us)
Async XLA Ops:
  0.6 12.6 %copy-start = (bf16[512,1024]{1,0:T(8,128)(2,1)S(1)}, bf16[512,1024]{1,0:T(8,128)(2,1)}, u32[]{:S(2)}) copy-start(bf16[512,1024]{1,0:T(8,128)(2,1)} %param.6) | copy-start | bytes 3145732
  15.7 88.3 %copy-start.3 = (s32[768]{0:T(1024)S(1)}, s32[768]{0:T(1024)}, u32[]{:S(2)}) copy-start(s32[768]{0:T(1024)} %param.8) | copy-start | bytes 9220
  15.7 92.6 %copy-start.5 = (s32[6]{0:T(128)S(1)}, s32[6]{0:T(128)}, u32[]{:S(2)}) copy-start(s32[6]{0:T(128)} %param.9) | copy-start | bytes 76
  15.7 98.0 %copy-start.4 = (s32[768]{0:T(1024)S(1)}, s32[768]{0:T(1024)}, u32[]{:S(2)}) copy-start(s32[768]{0:T(1024)} %param.7) | copy-start | bytes 9220
  15.7 49.9 %all-to-all-start.1 = ((bf16[4,512,1024]{2,1,0:T(8,128)(2,1)}), bf16[4,512,1024]{2,1,0:T(8,128)(2,1)}, u32[]{:S(2)}, u32[]{:S(2)}) async-start(bf16[4,512,1024]{2,1,0:T(8,128)(2,1)} %broadcast_in_dim.66), calls=%async_computation.1 | async-start | bytes 8388608 | tf_op jit(solution)/shard_map/all_to_all | solution.py:25
  21.0 112.3 %copy-start.1 = (bf16[256,768]{0,1:T(8,128)(2,1)}, bf16[256,768]{0,1:T(8,128)(2,1)S(1)}, u32[]{:S(2)}) copy-start(bf16[256,768]{0,1:T(8,128)(2,1)S(1)} %copy.17) | copy-start | bytes 1179652
  21.0 52.2 %collective-permute-start.6 = (bf16[768,256]{1,0:T(8,128)(2,1)S(1)}, bf16[768,256]{1,0:T(8,128)(2,1)S(1)}, u32[]{:S(2)}, u32[]{:S(2)}) collective-permute-start(bf16[768,256]{1,0:T(8,128)(2,1)S(1)} %bitcast.29), channel_id=1, source_target_pairs={{0,64},{64,0},{1,65},{65,1},{2,66},{66,2},{3,67},{67,3},{4,68},{68... | collective-permute-start | bytes 1179656 | tf_op jit(solution)/shard_map/ppermute | solution.py:163
  65.7 102.8 %collective-permute-start.19 = (bf16[4,512,1024]{2,1,0:T(8,128)(2,1)}, bf16[4,512,1024]{2,1,0:T(8,128)(2,1)}, u32[]{:S(2)}, u32[]{:S(2)}) collective-permute-start(bf16[4,512,1024]{2,1,0:T(8,128)(2,1)} %all-to-all-done.1.refs_12_), channel_id=1, source_target_pairs={{0,64},{64,0},{1,65},{65,1},{2,66},{66,2},{3,67},{67,3},{4,68},{68... | collective-permute-start | bytes 12582920 | tf_op jit(solution)/shard_map/ppermute | solution.py:38
  73.2 16.0 %collective-permute-start.7 = (bf16[768,256]{1,0:T(8,128)(2,1)S(1)}, bf16[768,256]{1,0:T(8,128)(2,1)S(1)}, u32[]{:S(2)}, u32[]{:S(2)}) collective-permute-start(bf16[768,256]{1,0:T(8,128)(2,1)S(1)} %collective-permute-done.6), channel_id=1, source_target_pairs={{0,4},{4,8},{8,12},{12,16},{16,20},{20,24},{24,28},{28,32},{32,36}... | collective-permute-start | bytes 1179656 | tf_op jit(solution)/shard_map/ppermute | solution.py:33
  84.5 9.7 %collective-permute-start = (bf16[768,256]{1,0:T(8,128)(2,1)S(1)}, bf16[768,256]{1,0:T(8,128)(2,1)S(1)}, u32[]{:S(2)}, u32[]{:S(2)}) collective-permute-start(bf16[768,256]{1,0:T(8,128)(2,1)S(1)} %bitcast.30), channel_id=1, source_target_pairs={{0,4},{4,8},{8,12},{12,16},{16,20},{20,24},{24,28},{28,32},{32,36}... | collective-permute-start | bytes 1179656 | tf_op jit(solution)/shard_map/ppermute | solution.py:33
  89.2 9.7 %collective-permute-start.8 = (bf16[768,256]{1,0:T(8,128)(2,1)S(1)}, bf16[768,256]{1,0:T(8,128)(2,1)S(1)}, u32[]{:S(2)}, u32[]{:S(2)}) collective-permute-start(bf16[768,256]{1,0:T(8,128)(2,1)S(1)} %collective-permute-done.7), channel_id=1, source_target_pairs={{0,4},{4,8},{8,12},{12,16},{16,20},{20,24},{24,28},{28,32},{32,36}... | collective-permute-start | bytes 1179656 | tf_op jit(solution)/shard_map/ppermute | solution.py:33
  94.3 14.2 %copy-start.7 = (bf16[768,256]{1,0:T(8,128)(2,1)}, bf16[768,256]{1,0:T(8,128)(2,1)S(1)}, u32[]{:S(2)}) copy-start(bf16[768,256]{1,0:T(8,128)(2,1)S(1)} %collective-permute-done.refs_1_) | copy-start | bytes 1179652
  94.3 9.8 %collective-permute-start.1 = (bf16[768,256]{1,0:T(8,128)(2,1)S(1)}, bf16[768,256]{1,0:T(8,128)(2,1)S(1)}, u32[]{:S(2)}, u32[]{:S(2)}) collective-permute-start(bf16[768,256]{1,0:T(8,128)(2,1)S(1)} %collective-permute-done.refs_1_), channel_id=1, source_target_pairs={{0,4},{4,8},{8,12},{12,16},{16,20},{20,24},{24,28},{28,32},{32,36}... | collective-permute-start | bytes 1179656 | tf_op jit(solution)/shard_map/ppermute | solution.py:33
  99.0 9.7 %collective-permute-start.9 = (bf16[768,256]{1,0:T(8,128)(2,1)S(1)}, bf16[768,256]{1,0:T(8,128)(2,1)S(1)}, u32[]{:S(2)}, u32[]{:S(2)}) collective-permute-start(bf16[768,256]{1,0:T(8,128)(2,1)S(1)} %collective-permute-done.8), channel_id=1, source_target_pairs={{0,4},{4,8},{8,12},{12,16},{16,20},{20,24},{24,28},{28,32},{32,36}... | collective-permute-start | bytes 1179656 | tf_op jit(solution)/shard_map/ppermute | solution.py:33
  104.1 29.1 %copy-start.8 = (bf16[768,256]{1,0:T(8,128)(2,1)}, bf16[768,256]{1,0:T(8,128)(2,1)S(1)}, u32[]{:S(2)}) copy-start(bf16[768,256]{1,0:T(8,128)(2,1)S(1)} %collective-permute-done.1.refs_2_) | copy-start | bytes 1179652
  104.2 9.6 %collective-permute-start.2 = (bf16[768,256]{1,0:T(8,128)(2,1)S(1)}, bf16[768,256]{1,0:T(8,128)(2,1)S(1)}, u32[]{:S(2)}, u32[]{:S(2)}) collective-permute-start(bf16[768,256]{1,0:T(8,128)(2,1)S(1)} %collective-permute-done.1.refs_2_), channel_id=1, source_target_pairs={{0,4},{4,8},{8,12},{12,16},{16,20},{20,24},{24,28},{28,32},{32,36}... | collective-permute-start | bytes 1179656 | tf_op jit(solution)/shard_map/ppermute | solution.py:33
  108.7 9.7 %collective-permute-start.11 = (bf16[768,256]{1,0:T(8,128)(2,1)S(1)}, bf16[768,256]{1,0:T(8,128)(2,1)S(1)}, u32[]{:S(2)}, u32[]{:S(2)}) collective-permute-start(bf16[768,256]{1,0:T(8,128)(2,1)S(1)} %collective-permute-done.9), channel_id=1, source_target_pairs={{0,4},{4,8},{8,12},{12,16},{16,20},{20,24},{24,28},{28,32},{32,36}... | collective-permute-start | bytes 1179656 | tf_op jit(solution)/shard_map/ppermute | solution.py:33
  113.8 19.4 %copy-start.9 = (bf16[768,256]{1,0:T(8,128)(2,1)}, bf16[768,256]{1,0:T(8,128)(2,1)S(1)}, u32[]{:S(2)}) copy-start(bf16[768,256]{1,0:T(8,128)(2,1)S(1)} %collective-permute-done.2.refs_3_) | copy-start | bytes 1179652
  113.8 11.1 %collective-permute-start.3 = (bf16[768,256]{1,0:T(8,128)(2,1)S(1)}, bf16[768,256]{1,0:T(8,128)(2,1)}, u32[]{:S(2)}, u32[]{:S(2)}) collective-permute-start(bf16[768,256]{1,0:T(8,128)(2,1)S(1)} %collective-permute-done.2.refs_3_), channel_id=1, source_target_pairs={{0,4},{4,8},{8,12},{12,16},{16,20},{20,24},{24,28},{28,32},{32,36}... | collective-permute-start | bytes 1179656 | tf_op jit(solution)/shard_map/ppermute | solution.py:33
  118.4 9.7 %collective-permute-start.12 = (bf16[768,256]{1,0:T(8,128)(2,1)S(1)}, bf16[768,256]{1,0:T(8,128)(2,1)S(1)}, u32[]{:S(2)}, u32[]{:S(2)}) collective-permute-start(bf16[768,256]{1,0:T(8,128)(2,1)S(1)} %collective-permute-done.11), channel_id=1, source_target_pairs={{0,4},{4,8},{8,12},{12,16},{16,20},{20,24},{24,28},{28,32},{32,36}... | collective-permute-start | bytes 1179656 | tf_op jit(solution)/shard_map/ppermute | solution.py:33
  125.0 13.1 %collective-permute-start.4 = (bf16[768,256]{1,0:T(8,128)(2,1)}, bf16[768,256]{1,0:T(8,128)(2,1)S(1)}, u32[]{:S(2)}, u32[]{:S(2)}) collective-permute-start(bf16[768,256]{1,0:T(8,128)(2,1)} %collective-permute-done.3.refs_4_), channel_id=1, source_target_pairs={{0,4},{4,8},{8,12},{12,16},{16,20},{20,24},{24,28},{28,32},{32,36}... | collective-permute-start | bytes 1179656 | tf_op jit(solution)/shard_map/ppermute | solution.py:33
  128.1 14.8 %collective-permute-start.13 = (bf16[768,256]{1,0:T(8,128)(2,1)S(1)}, bf16[768,256]{1,0:T(8,128)(2,1)S(1)}, u32[]{:S(2)}, u32[]{:S(2)}) collective-permute-start(bf16[768,256]{1,0:T(8,128)(2,1)S(1)} %collective-permute-done.12), channel_id=1, source_target_pairs={{0,4},{4,8},{8,12},{12,16},{16,20},{20,24},{24,28},{28,32},{32,36}... | collective-permute-start | bytes 1179656 | tf_op jit(solution)/shard_map/ppermute | solution.py:33
  133.3 34.4 %collective-permute-start.10 = (bf16[3,768,256]{2,1,0:T(8,128)(2,1)S(1)}, bf16[3,768,256]{2,1,0:T(8,128)(2,1)}, u32[]{:S(2)}, u32[]{:S(2)}) collective-permute-start(bf16[3,768,256]{2,1,0:T(8,128)(2,1)S(1)} %pad_maximum_fusion), channel_id=1, source_target_pairs={{0,64},{64,0},{1,65},{65,1},{2,66},{66,2},{3,67},{67,3},{4,68},{68... | collective-permute-start | bytes 3538952 | tf_op jit(solution)/shard_map/ppermute | solution.py:180
  138.1 5.0 %copy-start.10 = (bf16[768,256]{1,0:T(8,128)(2,1)}, bf16[768,256]{1,0:T(8,128)(2,1)S(1)}, u32[]{:S(2)}) copy-start(bf16[768,256]{1,0:T(8,128)(2,1)S(1)} %collective-permute-done.4.refs_5_) | copy-start | bytes 1179652
  138.1 9.6 %collective-permute-start.5 = (bf16[768,256]{1,0:T(8,128)(2,1)S(1)}, bf16[768,256]{1,0:T(8,128)(2,1)S(1)}, u32[]{:S(2)}, u32[]{:S(2)}) collective-permute-start(bf16[768,256]{1,0:T(8,128)(2,1)S(1)} %collective-permute-done.4.refs_5_), channel_id=1, source_target_pairs={{0,4},{4,8},{8,12},{12,16},{16,20},{20,24},{24,28},{28,32},{32,36}... | collective-permute-start | bytes 1179656 | tf_op jit(solution)/shard_map/ppermute | solution.py:33
  143.1 25.3 %collective-permute-start.14 = (bf16[3,768,256]{2,1,0:T(8,128)(2,1)S(1)}, bf16[3,768,256]{2,1,0:T(8,128)(2,1)}, u32[]{:S(2)}, u32[]{:S(2)}) collective-permute-start(bf16[3,768,256]{2,1,0:T(8,128)(2,1)S(1)} %pad_maximum_fusion.1), channel_id=1, source_target_pairs={{0,64},{64,0},{1,65},{65,1},{2,66},{66,2},{3,67},{67,3},{4,68},{68... | collective-permute-start | bytes 3538952 | tf_op jit(solution)/shard_map/ppermute | solution.py:180
  147.6 20.8 %copy-start.11 = (bf16[768,256]{1,0:T(8,128)(2,1)}, bf16[768,256]{1,0:T(8,128)(2,1)S(1)}, u32[]{:S(2)}) copy-start(bf16[768,256]{1,0:T(8,128)(2,1)S(1)} %collective-permute-done.5.refs_6_) | copy-start | bytes 1179652
  147.6 9.7 %collective-permute-start.15 = (bf16[768,256]{1,0:T(8,128)(2,1)S(1)}, bf16[768,256]{1,0:T(8,128)(2,1)S(1)}, u32[]{:S(2)}, u32[]{:S(2)}) collective-permute-start(bf16[768,256]{1,0:T(8,128)(2,1)S(1)} %collective-permute-done.5.refs_6_), channel_id=1, source_target_pairs={{0,4},{4,8},{8,12},{12,16},{16,20},{20,24},{24,28},{28,32},{32,36}... | collective-permute-start | bytes 1179656 | tf_op jit(solution)/shard_map/ppermute | solution.py:33
  152.7 9.7 %collective-permute-start.17 = (bf16[768,256]{1,0:T(8,128)(2,1)S(1)}, bf16[768,256]{1,0:T(8,128)(2,1)}, u32[]{:S(2)}, u32[]{:S(2)}) collective-permute-start(bf16[768,256]{1,0:T(8,128)(2,1)S(1)} %collective-permute-done.13), channel_id=1, source_target_pairs={{0,4},{4,8},{8,12},{12,16},{16,20},{20,24},{24,28},{28,32},{32,36}... | collective-permute-start | bytes 1179656 | tf_op jit(solution)/shard_map/ppermute | solution.py:33
  157.4 11.1 %copy-start.12 = (bf16[768,256]{1,0:T(8,128)(2,1)}, bf16[768,256]{1,0:T(8,128)(2,1)S(1)}, u32[]{:S(2)}) copy-start(bf16[768,256]{1,0:T(8,128)(2,1)S(1)} %collective-permute-done.15.refs_9_) | copy-start | bytes 1179652
  157.4 10.4 %collective-permute-start.16 = (bf16[768,256]{1,0:T(8,128)(2,1)S(1)}, bf16[768,256]{1,0:T(8,128)(2,1)S(1)}, u32[]{:S(2)}, u32[]{:S(2)}) collective-permute-start(bf16[768,256]{1,0:T(8,128)(2,1)S(1)} %collective-permute-done.15.refs_9_), channel_id=1, source_target_pairs={{0,4},{4,8},{8,12},{12,16},{16,20},{20,24},{24,28},{28,32},{32,36}... | collective-permute-start | bytes 1179656 | tf_op jit(solution)/shard_map/ppermute | solution.py:33
  162.4 6.0 %collective-permute-start.18 = (bf16[1,768,256]{2,1,0:T(8,128)(2,1)}, bf16[1,768,256]{2,1,0:T(8,128)(2,1)}, u32[]{:S(2)}, u32[]{:S(2)}) collective-permute-start(bf16[1,768,256]{2,1,0:T(8,128)(2,1)} %bitcast.11), channel_id=1, source_target_pairs={{0,64},{64,0},{1,65},{65,1},{2,66},{66,2},{3,67},{67,3},{4,68},{68... | collective-permute-start | bytes 1179656 | tf_op jit(solution)/shard_map/ppermute | solution.py:180
  167.7 0.8 copy-start.13
  179.8 26.4 %copy-start.2 = (f32[64,192]{1,0:T(8,128)S(1)}, f32[64,192]{1,0:T(8,128)}, u32[]{:S(2)}) copy-start(f32[64,192]{1,0:T(8,128)} %fusion.2) | copy-start | bytes 147460
  179.8 26.5 %copy-start.6 = (f32[64]{0:T(128)S(1)}, f32[64]{0:T(128)}, u32[]{:S(2)}) copy-start(f32[64]{0:T(128)} %select_reduce_fusion.1) | copy-start | bytes 772

commit v8 on v7

--- a/solution.py
+++ b/solution.py
@@ -27,15 +27,29 @@
     )
 
 
+def along(array, axis, step, core_step=0):
+    size = lax.axis_size(axis)
+    way = [step + core_step * c for c in range(2)]
+    if axis == "z":
+        pairs = [(c * size + i, c * size + (i + way[c]) % size) for c in range(2) for i in range(size)]
+        return lax.ppermute(array, ("c", "z"), pairs)
+    pairs = [(2 * i + c, 2 * ((i + way[c]) % size) + c) for c in range(2) for i in range(size)]
+    return lax.ppermute(array, TOK, pairs)
+
+
 def along_z(array):
-    zs = lax.axis_size("z")
-    pairs = [(c * zs + z, c * zs + (z + (1 - 2 * c)) % zs) for c in range(2) for z in range(zs)]
-    return lax.ppermute(array, ("c", "z"), pairs)
-
-
-def gathered_weight(weight):
-    own = to_all(weight, "x", lax.axis_size("x"))
-    return own, lax.ppermute(own, "c", SWAP)
+    return along(array, "z", 1, -2)
+
+
+def gathered_weight(weight, core):
+    third = along(weight, "x", 1)
+    first = along(weight, "x", -1)
+    second = along(jnp.where(core == 0, third, first), "x", 1, -2)
+    own = [weight, first, second, third]
+    theirs = []
+    for shard in own:
+        theirs.append(lax.ppermute(shard, "c", SWAP))
+    return own + theirs
 
 
 def before_tail(tokens, z, y, domains, seq_len):
@@ -81,14 +95,12 @@
         for kind in kinds:
             ref = refs.pop(0)
             blocks += [ref.at[k] for k in range(kind)] if kind else [ref]
-        own, theirs, wanted, out, acc, rows, lefts, sems = refs
-        core, z = where[0], where[1]
-
-        def fetch(k, weights, source):
+        *weights, wanted, out, acc, rows, lefts, sems = refs
+        x, core, z = where[0], where[1], where[2]
+
+        def fetch(k, weight, low):
             return pltpu.make_async_copy(
-                weights.at[source // 4, pl.ds(lax.rem(source, 2) * BLOCK, BLOCK)],
-                rows.at[pl.ds(k * BLOCK, BLOCK)],
-                sems.at[0, k],
+                weight.at[pl.ds(low, BLOCK)], rows.at[pl.ds(k * BLOCK, BLOCK)], sems.at[0, k]
             )
 
         def fetch_block(k):
@@ -97,15 +109,17 @@
         for k, far in enumerate(away):
             source = lax.rem(z + far * (2 * core - 1) + 16, 16)
             fetch_block(k).start()
-            mine = lax.rem(source // 2, 2) == core
-            pl.when(mine)(fetch(k, own, source).start)
-            pl.when(jnp.logical_not(mine))(fetch(k, theirs, source).start)
+            shard = lax.rem(source // 4 - x + 4, 4)
+            shard += 4 * (lax.rem(source // 2, 2) != core).astype(jnp.int32)
+            low = pl.multiple_of(lax.rem(source, 2) * BLOCK, BLOCK)
+            for n, weight in enumerate(weights):
+                pl.when(shard == n)(fetch(k, weight, low).start)
 
         tokens, columns = acc.shape
         for first, end in zip(DEPTHS, DEPTHS[1:]):
             for k in range(first, end):
                 fetch_block(k).wait()
-                fetch(k, own, 0).wait()
+                fetch(k, weights[0], 0).wait()
             deep = slice(first * BLOCK, end * BLOCK)
             for at in range(0, tokens, TILE):
                 part = slice(at, at + TILE)
@@ -131,12 +145,12 @@
 
 def product(where, away, blocks, weights, wanted):
     kinds = [b.shape[0] if b.ndim == 3 else 0 for b in blocks]
-    count, tokens, columns = len(away), blocks[0].shape[-2], weights[0].shape[2]
+    count, tokens, columns = len(away), blocks[0].shape[-2], weights[0].shape[1]
     vmem = pl.BlockSpec(memory_space=pltpu.VMEM)
     hbm = pl.BlockSpec(memory_space=pltpu.HBM)
     return pl.pallas_call(
         product_kernel(kinds, away),
-        in_specs=[pl.BlockSpec(memory_space=pltpu.SMEM)] + [hbm] * (len(blocks) + 2) + [vmem],
+        in_specs=[pl.BlockSpec(memory_space=pltpu.SMEM)] + [hbm] * (len(blocks) + len(weights)) + [vmem],
         out_specs=vmem,
         out_shape=jax.ShapeDtypeStruct((8, tokens), jnp.float32),
         scratch_shapes=[
@@ -156,12 +170,14 @@
 
 def loss(hidden, weight, targets, domains, seq_len):
     ys = lax.axis_size("y")
-    core, z, y = (lax.axis_index(name) for name in ("c", "z", "y"))
+    x, core, z, y = (lax.axis_index(name) for name in ("x", "c", "z", "y"))
     low = lax.axis_index(VOCAB) * weight.shape[1]
-    hidden, where, z, y, low = lax.optimization_barrier((hidden, jnp.stack([core, z]), z, y, low))
+    hidden, where, core, z, y, low = lax.optimization_barrier(
+        (hidden, jnp.stack([x, core, z]), core, z, y, low)
+    )
     mine = to_all(hidden.T, "y", ys).reshape(BLOCK, -1).T
     theirs = lax.ppermute(mine, "c", SWAP)
-    weights = gathered_weight(weight)
+    weights = gathered_weight(weight, core)
     own, other = [mine], [theirs]
     for r in range(1, ROUNDS + 1):
         own.append(along_z(own[-1]))

time: 224 us -> 191 us (0.85)
  waiting for transfers between devices: 44.7 us -> 15.1 us
  local copies, waits for them, and re-layouts: 6.3 us -> 3.99 us
    all_to_all x1 -> x0, waiting for transfers between devices: 37.3 us -> none  [to_all(): lax.all_to_all(jnp.broadcast_to(array[None], (copies, *array.shape)), axi...]
    ppermute x16 -> x22, waiting for transfers between devices: 6.76 us -> 14.4 us  [the longest x15 14.4 us: along(): return lax.ppermute(array, ('c', 'z'), pairs)]
    all_to_all x1 -> x0, starting transfers between devices: 5.13 us -> none  [to_all(): lax.all_to_all(jnp.broadcast_to(array[None], (copies, *array.shape)), axi...]
    ppermute x16 -> x22, starting transfers between devices: 78.9 us -> 81.5 us  [the longest x15 64.5 us: along(): return lax.ppermute(array, ('c', 'z'), pairs)]
    broadcast_in_dim x3 -> x2, local copies, waits for them, and re-layouts: 3.46 us -> 0.93 us  [to_all(): jnp.broadcast_to(array[None], (copies, *array.shape))]
    all_to_all x2, blocking collectives: 26.5 us -> 28.8 us  [to_all(): lax.all_to_all(jnp.broadcast_to(array[None], (copies, *array.shape)), axi...]
  transfers between devices with their start and end apart: 21 -> 26, of which waited for: 9 -> 6; matrix products, arithmetic and copies ran while one was open for 1% -> 2% of each run, Pallas kernels for 0% -> 0%
where the time goes in v8:
time: 191 us; the launch traced here: 190 us
  starting transfers between devices  103 us (54%)
  blocking collectives  51.6 us (27%)
  waiting for transfers between devices  15.1 us (8%)
  Pallas kernels  11.4 us (6%)
  other arithmetic  4.31 us (2%)
  local copies, waits for them, and re-layouts  3.99 us (2%)
    ppermute x15, starting transfers between devices, along(): return lax.ppermute(array, ('c', 'z'), pairs)  64.5 us
    all_to_all x2, blocking collectives, to_all(): lax.all_to_all(jnp.broadcast_to(array[None], (copies, *array.shape)), axi...  28.8 us
    all_to_all x1, blocking collectives, tail(): got = lax.all_to_all(send.reshape(zs * ys, -1), VOCAB, 0, 0, tiled=True)  22.9 us
    ppermute x15, waiting for transfers between devices, along(): return lax.ppermute(array, ('c', 'z'), pairs)  14.4 us
    ppermute x3, starting transfers between devices, loss(): swapped.append(lax.ppermute(jnp.stack([other[r] for r in some]), 'c', SWAP))  13.7 us
    pallas_call x1, Pallas kernels, product(): pl.pallas_call(product_kernel(kinds, away), in_specs=[pl.BlockSpec(memory...  11.4 us
    ppermute x3, starting transfers between devices, along(): return lax.ppermute(array, TOK, pairs)  9.35 us
    ppermute x4, starting transfers between devices, gathered_weight(): theirs.append(lax.ppermute(shard, 'c', SWAP))  7.69 us
  transfers between devices with their start and end apart: 26, of which 6 were waited for; matrix products, arithmetic and copies ran while one was open for 2% of the time, Pallas kernels for 0%

profile of v8, /device:TPU:1, one launch (start us, length us, event | category | flops | bytes accessed | tf_op | source)
XLA Modules:
  0.0 190.3 jit_solution(17176650825228902453)
XLA Ops:
  0.6 0.7 pad_add_fusion.where
  1.3 0.9 broadcast_in_dim.55
  2.2 11.0 %all_to_all.20 = bf16[4,64,768]{2,1,0:T(8,128)(2,1)S(1)} all-to-all(bf16[4,64,768]{2,1,0:T(8,128)(2,1)S(1)} %broadcast_in_dim.55), channel_id=1, replica_groups=mesh['x'=4,'c'=2,'z'=16,'y'=4] {'y'}, dimensions={0} | all-to-all | bytes 786432 | tf_op jit(solution)/shard_map/all_to_all | solution.py:25
  13.3 0.2 copy.17
  13.4 7.5 %collective-permute-start.6 = (bf16[768,256]{1,0:T(8,128)(2,1)S(1)}, bf16[768,256]{1,0:T(8,128)(2,1)S(1)}, u32[]{:S(2)}, u32[]{:S(2)}) collective-permute-start(bf16[768,256]{1,0:T(8,128)(2,1)S(1)} %bitcast.30), channel_id=1, source_target_pairs={{0,64},{64,0},{1,65},{65,1},{2,66},{66,2},{3,67},{67,3},{4,68},{68... | collective-permute-start | bytes 1179656 | tf_op jit(solution)/shard_map/ppermute | solution.py:179
  20.9 1.9 %collective-permute-start.19 = (bf16[512,1024]{1,0:T(8,128)(2,1)}, bf16[512,1024]{1,0:T(8,128)(2,1)S(1)}, u32[]{:S(2)}, u32[]{:S(2)}) collective-permute-start(bf16[512,1024]{1,0:T(8,128)(2,1)} %refs_12_.1), channel_id=1, source_target_pairs={{0,384},{128,0},{256,128},{384,256},{64,448},{192,64},{320,192},{4... | collective-permute-start | bytes 3145736 | tf_op jit(solution)/shard_map/ppermute | solution.py:37
  22.9 3.4 %collective-permute-start.20 = (bf16[512,1024]{1,0:T(8,128)(2,1)}, bf16[512,1024]{1,0:T(8,128)(2,1)}, u32[]{:S(2)}, u32[]{:S(2)}) collective-permute-start(bf16[512,1024]{1,0:T(8,128)(2,1)} %refs_12_.1), channel_id=1, source_target_pairs={{0,128},{128,256},{256,384},{384,0},{64,192},{192,320},{320,448},{... | collective-permute-start | bytes 3145736 | tf_op jit(solution)/shard_map/ppermute | solution.py:37
  26.2 9.4 %collective-permute-start = (bf16[768,256]{1,0:T(8,128)(2,1)S(1)}, bf16[768,256]{1,0:T(8,128)(2,1)S(1)}, u32[]{:S(2)}, u32[]{:S(2)}) collective-permute-start(bf16[768,256]{1,0:T(8,128)(2,1)S(1)} %bitcast.31), channel_id=1, source_target_pairs={{0,4},{4,8},{8,12},{12,16},{16,20},{20,24},{24,28},{28,32},{32,36}... | collective-permute-start | bytes 1179656 | tf_op jit(solution)/shard_map/ppermute | solution.py:35
  35.6 2.6 %collective-permute-start.7 = (bf16[768,256]{1,0:T(8,128)(2,1)S(1)}, bf16[768,256]{1,0:T(8,128)(2,1)S(1)}, u32[]{:S(2)}, u32[]{:S(2)}) collective-permute-start(bf16[768,256]{1,0:T(8,128)(2,1)S(1)} %collective-permute-done.6), channel_id=1, source_target_pairs={{0,4},{4,8},{8,12},{12,16},{16,20},{20,24},{24,28},{28,32},{32,36}... | collective-permute-start | bytes 1179656 | tf_op jit(solution)/shard_map/ppermute | solution.py:35
  38.3 2.0 %collective-permute-done.refs_1_ = bf16[768,256]{1,0:T(8,128)(2,1)S(1)} collective-permute-done((bf16[768,256]{1,0:T(8,128)(2,1)S(1)}, bf16[768,256]{1,0:T(8,128)(2,1)S(1)}, u32[]{:S(2)}, u32[]{:S(2)}) %collective-permute-start) | collective-permute-done | bytes 393248 | tf_op jit(solution)/shard_map/ppermute | solution.py:35
  40.3 5.4 %collective-permute-start.1 = (bf16[768,256]{1,0:T(8,128)(2,1)S(1)}, bf16[768,256]{1,0:T(8,128)(2,1)}, u32[]{:S(2)}, u32[]{:S(2)}) collective-permute-start(bf16[768,256]{1,0:T(8,128)(2,1)S(1)} %collective-permute-done.refs_1_), channel_id=1, source_target_pairs={{0,4},{4,8},{8,12},{12,16},{16,20},{20,24},{24,28},{28,32},{32,36}... | collective-permute-start | bytes 1179656 | tf_op jit(solution)/shard_map/ppermute | solution.py:35
  45.8 4.2 %collective-permute-start.8 = (bf16[768,256]{1,0:T(8,128)(2,1)S(1)}, bf16[768,256]{1,0:T(8,128)(2,1)S(1)}, u32[]{:S(2)}, u32[]{:S(2)}) collective-permute-start(bf16[768,256]{1,0:T(8,128)(2,1)S(1)} %collective-permute-done.7), channel_id=1, source_target_pairs={{0,4},{4,8},{8,12},{12,16},{16,20},{20,24},{24,28},{28,32},{32,36}... | collective-permute-start | bytes 1179656 | tf_op jit(solution)/shard_map/ppermute | solution.py:35
  50.0 1.9 %collective-permute-start.22 = (bf16[512,1024]{1,0:T(8,128)(2,1)}, bf16[512,1024]{1,0:T(8,128)(2,1)}, u32[]{:S(2)}, u32[]{:S(2)}) collective-permute-start(bf16[512,1024]{1,0:T(8,128)(2,1)} %refs_12_.1), channel_id=1, source_target_pairs={{0,64},{64,0},{1,65},{65,1},{2,66},{66,2},{3,67},{67,3},{4,68},{68... | collective-permute-start | bytes 3145736 | tf_op jit(solution)/shard_map/ppermute | solution.py:51
  51.9 0.0 copy-start.2
  52.0 0.0 copy-start.3
  52.0 3.9 %collective-permute-start.2 = (bf16[768,256]{1,0:T(8,128)(2,1)}, bf16[768,256]{1,0:T(8,128)(2,1)}, u32[]{:S(2)}, u32[]{:S(2)}) collective-permute-start(bf16[768,256]{1,0:T(8,128)(2,1)} %collective-permute-done.1.refs_2_), channel_id=1, source_target_pairs={{0,4},{4,8},{8,12},{12,16},{16,20},{20,24},{24,28},{28,32},{32,36}... | collective-permute-start | bytes 1179656 | tf_op jit(solution)/shard_map/ppermute | solution.py:35
  55.9 4.2 %collective-permute-start.9 = (bf16[768,256]{1,0:T(8,128)(2,1)S(1)}, bf16[768,256]{1,0:T(8,128)(2,1)S(1)}, u32[]{:S(2)}, u32[]{:S(2)}) collective-permute-start(bf16[768,256]{1,0:T(8,128)(2,1)S(1)} %collective-permute-done.8), channel_id=1, source_target_pairs={{0,4},{4,8},{8,12},{12,16},{16,20},{20,24},{24,28},{28,32},{32,36}... | collective-permute-start | bytes 1179656 | tf_op jit(solution)/shard_map/ppermute | solution.py:35
  60.1 1.2 broadcast_select_fusion
  61.4 4.1 %collective-permute-start.21 = (bf16[512,1024]{1,0:T(8,128)(2,1)}, bf16[512,1024]{1,0:T(8,128)(2,1)}, u32[]{:S(2)}, u32[]{:S(2)}) collective-permute-start(bf16[512,1024]{1,0:T(8,128)(2,1)} %broadcast_select_fusion), channel_id=1, source_target_pairs={{0,128},{128,256},{256,384},{384,0},{64,448},{192,64},{320,192},{4... | collective-permute-start | bytes 3145736 | tf_op jit(solution)/shard_map/ppermute | solution.py:37
  65.4 1.9 %collective-permute-start.23 = (bf16[512,1024]{1,0:T(8,128)(2,1)S(1)}, bf16[512,1024]{1,0:T(8,128)(2,1)}, u32[]{:S(2)}, u32[]{:S(2)}) collective-permute-start(bf16[512,1024]{1,0:T(8,128)(2,1)S(1)} %collective-permute-done.19.refs_13_), channel_id=1, source_target_pairs={{0,64},{64,0},{1,65},{65,1},{2,66},{66,2},{3,67},{67,3},{4,68},{68... | collective-permute-start | bytes 3145736 | tf_op jit(solution)/shard_map/ppermute | solution.py:51
  67.4 0.1 reshape.108
  67.5 0.1 select_reduce_fusion.2
  67.6 0.1 eq.42
  67.7 3.8 %collective-permute-start.3 = (bf16[768,256]{1,0:T(8,128)(2,1)}, bf16[768,256]{1,0:T(8,128)(2,1)S(1)}, u32[]{:S(2)}, u32[]{:S(2)}) collective-permute-start(bf16[768,256]{1,0:T(8,128)(2,1)} %collective-permute-done.2.refs_3_), channel_id=1, source_target_pairs={{0,4},{4,8},{8,12},{12,16},{16,20},{20,24},{24,28},{28,32},{32,36}... | collective-permute-start | bytes 1179656 | tf_op jit(solution)/shard_map/ppermute | solution.py:35
  71.4 1.9 %collective-permute-start.11 = (bf16[768,256]{1,0:T(8,128)(2,1)S(1)}, bf16[768,256]{1,0:T(8,128)(2,1)S(1)}, u32[]{:S(2)}, u32[]{:S(2)}) collective-permute-start(bf16[768,256]{1,0:T(8,128)(2,1)S(1)} %collective-permute-done.9), channel_id=1, source_target_pairs={{0,4},{4,8},{8,12},{12,16},{16,20},{20,24},{24,28},{28,32},{32,36}... | collective-permute-start | bytes 1179656 | tf_op jit(solution)/shard_map/ppermute | solution.py:35
  73.4 7.5 %collective-permute-done.11 = bf16[768,256]{1,0:T(8,128)(2,1)S(1)} collective-permute-done((bf16[768,256]{1,0:T(8,128)(2,1)S(1)}, bf16[768,256]{1,0:T(8,128)(2,1)S(1)}, u32[]{:S(2)}, u32[]{:S(2)}) %collective-permute-start.11) | collective-permute-done | bytes 393248 | tf_op jit(solution)/shard_map/ppermute | solution.py:35
  80.9 4.7 %collective-permute-start.12 = (bf16[768,256]{1,0:T(8,128)(2,1)S(1)}, bf16[768,256]{1,0:T(8,128)(2,1)S(1)}, u32[]{:S(2)}, u32[]{:S(2)}) collective-permute-start(bf16[768,256]{1,0:T(8,128)(2,1)S(1)} %collective-permute-done.11), channel_id=1, source_target_pairs={{0,4},{4,8},{8,12},{12,16},{16,20},{20,24},{24,28},{28,32},{32,36}... | collective-permute-start | bytes 1179656 | tf_op jit(solution)/shard_map/ppermute | solution.py:35
  85.6 0.1 select_reduce_fusion.4
  85.7 1.9 %collective-permute-start.25 = (bf16[512,1024]{1,0:T(8,128)(2,1)}, bf16[512,1024]{1,0:T(8,128)(2,1)S(1)}, u32[]{:S(2)}, u32[]{:S(2)}) collective-permute-start(bf16[512,1024]{1,0:T(8,128)(2,1)} %collective-permute-done.20.refs_15_), channel_id=1, source_target_pairs={{0,64},{64,0},{1,65},{65,1},{2,66},{66,2},{3,67},{67,3},{4,68},{68... | collective-permute-start | bytes 3145736 | tf_op jit(solution)/shard_map/ppermute | solution.py:51
  87.7 0.1 select_reduce_fusion.1
  87.8 0.1 iota.37
  87.8 4.7 %collective-permute-start.4 = (bf16[768,256]{1,0:T(8,128)(2,1)S(1)}, bf16[768,256]{1,0:T(8,128)(2,1)S(1)}, u32[]{:S(2)}, u32[]{:S(2)}) collective-permute-start(bf16[768,256]{1,0:T(8,128)(2,1)S(1)} %collective-permute-done.3.refs_4_), channel_id=1, source_target_pairs={{0,4},{4,8},{8,12},{12,16},{16,20},{20,24},{24,28},{28,32},{32,36}... | collective-permute-start | bytes 1179656 | tf_op jit(solution)/shard_map/ppermute | solution.py:35
  92.5 2.8 %collective-permute-start.13 = (bf16[768,256]{1,0:T(8,128)(2,1)S(1)}, bf16[768,256]{1,0:T(8,128)(2,1)S(1)}, u32[]{:S(2)}, u32[]{:S(2)}) collective-permute-start(bf16[768,256]{1,0:T(8,128)(2,1)S(1)} %collective-permute-done.12), channel_id=1, source_target_pairs={{0,4},{4,8},{8,12},{12,16},{16,20},{20,24},{24,28},{28,32},{32,36}... | collective-permute-start | bytes 1179656 | tf_op jit(solution)/shard_map/ppermute | solution.py:35
  95.3 0.1 pad_maximum_fusion
  95.4 1.8 collective-permute-done.4.refs_5_
  97.2 3.9 %collective-permute-start.10 = (bf16[3,768,256]{2,1,0:T(8,128)(2,1)S(1)}, bf16[3,768,256]{2,1,0:T(8,128)(2,1)}, u32[]{:S(2)}, u32[]{:S(2)}) collective-permute-start(bf16[3,768,256]{2,1,0:T(8,128)(2,1)S(1)} %pad_maximum_fusion), channel_id=1, source_target_pairs={{0,64},{64,0},{1,65},{65,1},{2,66},{66,2},{3,67},{67,3},{4,68},{68... | collective-permute-start | bytes 3538952 | tf_op jit(solution)/shard_map/ppermute | solution.py:196
  101.1 0.3 collective-permute-done.13
  101.4 5.0 %collective-permute-start.5 = (bf16[768,256]{1,0:T(8,128)(2,1)S(1)}, bf16[768,256]{1,0:T(8,128)(2,1)S(1)}, u32[]{:S(2)}, u32[]{:S(2)}) collective-permute-start(bf16[768,256]{1,0:T(8,128)(2,1)S(1)} %collective-permute-done.4.refs_5_), channel_id=1, source_target_pairs={{0,4},{4,8},{8,12},{12,16},{16,20},{20,24},{24,28},{28,32},{32,36}... | collective-permute-start | bytes 1179656 | tf_op jit(solution)/shard_map/ppermute | solution.py:35
  106.4 0.1 pad_maximum_fusion.1
  106.6 2.6 %collective-permute-start.14 = (bf16[3,768,256]{2,1,0:T(8,128)(2,1)S(1)}, bf16[3,768,256]{2,1,0:T(8,128)(2,1)}, u32[]{:S(2)}, u32[]{:S(2)}) collective-permute-start(bf16[3,768,256]{2,1,0:T(8,128)(2,1)S(1)} %pad_maximum_fusion.1), channel_id=1, source_target_pairs={{0,64},{64,0},{1,65},{65,1},{2,66},{66,2},{3,67},{67,3},{4,68},{68... | collective-permute-start | bytes 3538952 | tf_op jit(solution)/shard_map/ppermute | solution.py:196
  109.2 1.9 %collective-permute-start.24 = (bf16[512,1024]{1,0:T(8,128)(2,1)}, bf16[512,1024]{1,0:T(8,128)(2,1)S(1)}, u32[]{:S(2)}, u32[]{:S(2)}) collective-permute-start(bf16[512,1024]{1,0:T(8,128)(2,1)} %collective-permute-done.21.refs_14_), channel_id=1, source_target_pairs={{0,64},{64,0},{1,65},{65,1},{2,66},{66,2},{3,67},{67,3},{4,68},{68... | collective-permute-start | bytes 3145736 | tf_op jit(solution)/shard_map/ppermute | solution.py:51
  111.2 5.0 %collective-permute-start.15 = (bf16[768,256]{1,0:T(8,128)(2,1)S(1)}, bf16[768,256]{1,0:T(8,128)(2,1)}, u32[]{:S(2)}, u32[]{:S(2)}) collective-permute-start(bf16[768,256]{1,0:T(8,128)(2,1)S(1)} %collective-permute-done.5.refs_6_), channel_id=1, source_target_pairs={{0,4},{4,8},{8,12},{12,16},{16,20},{20,24},{24,28},{28,32},{32,36}... | collective-permute-start | bytes 1179656 | tf_op jit(solution)/shard_map/ppermute | solution.py:35
  116.2 1.9 %collective-permute-start.17 = (bf16[768,256]{1,0:T(8,128)(2,1)S(1)}, bf16[768,256]{1,0:T(8,128)(2,1)}, u32[]{:S(2)}, u32[]{:S(2)}) collective-permute-start(bf16[768,256]{1,0:T(8,128)(2,1)S(1)} %collective-permute-done.13), channel_id=1, source_target_pairs={{0,4},{4,8},{8,12},{12,16},{16,20},{20,24},{24,28},{28,32},{32,36}... | collective-permute-start | bytes 1179656 | tf_op jit(solution)/shard_map/ppermute | solution.py:35
  118.1 2.7 %collective-permute-done.15.refs_9_ = bf16[768,256]{1,0:T(8,128)(2,1)} collective-permute-done((bf16[768,256]{1,0:T(8,128)(2,1)S(1)}, bf16[768,256]{1,0:T(8,128)(2,1)}, u32[]{:S(2)}, u32[]{:S(2)}) %collective-permute-start.15) | collective-permute-done | bytes 393248 | tf_op jit(solution)/shard_map/ppermute | solution.py:35
  120.9 5.1 %collective-permute-start.16 = (bf16[768,256]{1,0:T(8,128)(2,1)}, bf16[768,256]{1,0:T(8,128)(2,1)}, u32[]{:S(2)}, u32[]{:S(2)}) collective-permute-start(bf16[768,256]{1,0:T(8,128)(2,1)} %collective-permute-done.15.refs_9_), channel_id=1, source_target_pairs={{0,4},{4,8},{8,12},{12,16},{16,20},{20,24},{24,28},{28,32},{32,36}... | collective-permute-start | bytes 1179656 | tf_op jit(solution)/shard_map/ppermute | solution.py:35
  126.0 7.2 %collective-permute-start.18 = (bf16[1,768,256]{2,1,0:T(8,128)(2,1)}, bf16[1,768,256]{2,1,0:T(8,128)(2,1)}, u32[]{:S(2)}, u32[]{:S(2)}) collective-permute-start(bf16[1,768,256]{2,1,0:T(8,128)(2,1)} %bitcast.12), channel_id=1, source_target_pairs={{0,64},{64,0},{1,65},{65,1},{2,66},{66,2},{3,67},{67,3},{4,68},{68... | collective-permute-start | bytes 1179656 | tf_op jit(solution)/shard_map/ppermute | solution.py:196
  133.2 0.9 copy.18.refs_20_
  134.1 0.7 collective-permute-done.18.refs_11_
  134.9 0.3 copy-done.6
  135.2 11.4 %shard_map.68 = f32[8,768]{1,0:T(8,128)} custom-call(s32[3]{0:T(128)} %pad_add_fusion.where, bf16[768,256]{1,0:T(8,128)(2,1)} %bitcast.32, bf16[768,256]{1,0:T(8,128)(2,1)} %copy-done.7, bf16[768,256]{1,0:T(8,128)(2,1)} %collective-permute-done.1.refs_2_, bf16[768,256]{1,0:T(8,128)(2,1)} %collective-permute-done.2.refs_3_, bf16[768,256]{1,0:T(8,128)(2,1)} %copy-done.8, ...), custom_call_target="tpu_custom_call" | custom-call | flops 6442450944 | bytes 14680064 | tf_op jit(solution)/shard_map/pallas_call | solution.py:151
  146.6 0.7 slice.21
  147.3 0.1 reshape.109
  147.4 0.1 broadcast_in_dim.60
  147.6 0.1 all_to_all.14
  147.7 22.9 %all_to_all.21 = f32[64,1,384]{2,1,0:T(1,128)S(1)} all-to-all(f32[64,1,384]{2,1,0:T(1,128)S(1)} %all_to_all.14), channel_id=1, replica_groups=mesh['x'=4,'c'=2,'z'=16,'y'=4] {'z','y'}, dimensions={0} | all-to-all | bytes 196608 | tf_op jit(solution)/shard_map/all_to_all | solution.py:77
  170.6 0.2 reduce.3
  170.8 0.1 reshape.110
  170.9 0.2 slice_reduce_fusion.1
  171.2 0.1 reshape.111
  171.2 0.1 select_reduce_fusion
  171.4 0.5 select_reduce_fusion.3
  171.9 0.1 pad_maximum_fusion.2
  172.0 17.7 %all_to_all.22 = f32[32,1,128]{2,1,0:T(1,128)S(1)} all-to-all(f32[32,1,128]{2,1,0:T(1,128)S(1)} %broadcast_in_dim.63), channel_id=1, replica_groups=mesh['x'=4,'c'=2,'z'=16,'y'=4] {'x','c','y'}, dimensions={0} | all-to-all | bytes 32768 | tf_op jit(solution)/shard_map/all_to_all | solution.py:25
  189.8 0.6 maximum_divide_fusion
  (52 shorter events, 0.3 us)
Async XLA Ops:
  13.4 47.9 %copy-start.1 = (bf16[256,768]{0,1:T(8,128)(2,1)}, bf16[256,768]{0,1:T(8,128)(2,1)S(1)}, u32[]{:S(2)}) copy-start(bf16[256,768]{0,1:T(8,128)(2,1)S(1)} %copy.17) | copy-start | bytes 1179652
  13.4 22.2 %collective-permute-start.6 = (bf16[768,256]{1,0:T(8,128)(2,1)S(1)}, bf16[768,256]{1,0:T(8,128)(2,1)S(1)}, u32[]{:S(2)}, u32[]{:S(2)}) collective-permute-start(bf16[768,256]{1,0:T(8,128)(2,1)S(1)} %bitcast.30), channel_id=1, source_target_pairs={{0,64},{64,0},{1,65},{65,1},{2,66},{66,2},{3,67},{67,3},{4,68},{68... | collective-permute-start | bytes 1179656 | tf_op jit(solution)/shard_map/ppermute | solution.py:179
  20.9 39.1 %collective-permute-start.19 = (bf16[512,1024]{1,0:T(8,128)(2,1)}, bf16[512,1024]{1,0:T(8,128)(2,1)S(1)}, u32[]{:S(2)}, u32[]{:S(2)}) collective-permute-start(bf16[512,1024]{1,0:T(8,128)(2,1)} %refs_12_.1), channel_id=1, source_target_pairs={{0,384},{128,0},{256,128},{384,256},{64,448},{192,64},{320,192},{4... | collective-permute-start | bytes 3145736 | tf_op jit(solution)/shard_map/ppermute | solution.py:37
  22.9 37.2 %collective-permute-start.20 = (bf16[512,1024]{1,0:T(8,128)(2,1)}, bf16[512,1024]{1,0:T(8,128)(2,1)}, u32[]{:S(2)}, u32[]{:S(2)}) collective-permute-start(bf16[512,1024]{1,0:T(8,128)(2,1)} %refs_12_.1), channel_id=1, source_target_pairs={{0,128},{128,256},{256,384},{384,0},{64,192},{192,320},{320,448},{... | collective-permute-start | bytes 3145736 | tf_op jit(solution)/shard_map/ppermute | solution.py:37
  26.2 14.1 %collective-permute-start = (bf16[768,256]{1,0:T(8,128)(2,1)S(1)}, bf16[768,256]{1,0:T(8,128)(2,1)S(1)}, u32[]{:S(2)}, u32[]{:S(2)}) collective-permute-start(bf16[768,256]{1,0:T(8,128)(2,1)S(1)} %bitcast.31), channel_id=1, source_target_pairs={{0,4},{4,8},{8,12},{12,16},{16,20},{20,24},{24,28},{28,32},{32,36}... | collective-permute-start | bytes 1179656 | tf_op jit(solution)/shard_map/ppermute | solution.py:35
  35.6 10.1 %collective-permute-start.7 = (bf16[768,256]{1,0:T(8,128)(2,1)S(1)}, bf16[768,256]{1,0:T(8,128)(2,1)S(1)}, u32[]{:S(2)}, u32[]{:S(2)}) collective-permute-start(bf16[768,256]{1,0:T(8,128)(2,1)S(1)} %collective-permute-done.6), channel_id=1, source_target_pairs={{0,4},{4,8},{8,12},{12,16},{16,20},{20,24},{24,28},{28,32},{32,36}... | collective-permute-start | bytes 1179656 | tf_op jit(solution)/shard_map/ppermute | solution.py:35
  40.3 21.0 %copy-start.7 = (bf16[768,256]{1,0:T(8,128)(2,1)}, bf16[768,256]{1,0:T(8,128)(2,1)S(1)}, u32[]{:S(2)}) copy-start(bf16[768,256]{1,0:T(8,128)(2,1)S(1)} %collective-permute-done.refs_1_) | copy-start | bytes 1179652
  40.3 11.7 %collective-permute-start.1 = (bf16[768,256]{1,0:T(8,128)(2,1)S(1)}, bf16[768,256]{1,0:T(8,128)(2,1)}, u32[]{:S(2)}, u32[]{:S(2)}) collective-permute-start(bf16[768,256]{1,0:T(8,128)(2,1)S(1)} %collective-permute-done.refs_1_), channel_id=1, source_target_pairs={{0,4},{4,8},{8,12},{12,16},{16,20},{20,24},{24,28},{28,32},{32,36}... | collective-permute-start | bytes 1179656 | tf_op jit(solution)/shard_map/ppermute | solution.py:35
  45.8 10.1 %collective-permute-start.8 = (bf16[768,256]{1,0:T(8,128)(2,1)S(1)}, bf16[768,256]{1,0:T(8,128)(2,1)S(1)}, u32[]{:S(2)}, u32[]{:S(2)}) collective-permute-start(bf16[768,256]{1,0:T(8,128)(2,1)S(1)} %collective-permute-done.7), channel_id=1, source_target_pairs={{0,4},{4,8},{8,12},{12,16},{16,20},{20,24},{24,28},{28,32},{32,36}... | collective-permute-start | bytes 1179656 | tf_op jit(solution)/shard_map/ppermute | solution.py:35
  50.0 37.9 %collective-permute-start.22 = (bf16[512,1024]{1,0:T(8,128)(2,1)}, bf16[512,1024]{1,0:T(8,128)(2,1)}, u32[]{:S(2)}, u32[]{:S(2)}) collective-permute-start(bf16[512,1024]{1,0:T(8,128)(2,1)} %refs_12_.1), channel_id=1, source_target_pairs={{0,64},{64,0},{1,65},{65,1},{2,66},{66,2},{3,67},{67,3},{4,68},{68... | collective-permute-start | bytes 3145736 | tf_op jit(solution)/shard_map/ppermute | solution.py:51
  51.9 15.4 %copy-start.2 = (s32[768]{0:T(1024)S(1)}, s32[768]{0:T(1024)}, u32[]{:S(2)}) copy-start(s32[768]{0:T(1024)} %param.8) | copy-start | bytes 9220
  52.0 21.4 %copy-start.3 = (s32[768]{0:T(1024)S(1)}, s32[768]{0:T(1024)}, u32[]{:S(2)}) copy-start(s32[768]{0:T(1024)} %param.7) | copy-start | bytes 9220
  52.0 33.6 %copy-start.4 = (s32[6]{0:T(128)S(1)}, s32[6]{0:T(128)}, u32[]{:S(2)}) copy-start(s32[6]{0:T(128)} %param.9) | copy-start | bytes 76
  52.0 15.7 %collective-permute-start.2 = (bf16[768,256]{1,0:T(8,128)(2,1)}, bf16[768,256]{1,0:T(8,128)(2,1)}, u32[]{:S(2)}, u32[]{:S(2)}) collective-permute-start(bf16[768,256]{1,0:T(8,128)(2,1)} %collective-permute-done.1.refs_2_), channel_id=1, source_target_pairs={{0,4},{4,8},{8,12},{12,16},{16,20},{20,24},{24,28},{28,32},{32,36}... | collective-permute-start | bytes 1179656 | tf_op jit(solution)/shard_map/ppermute | solution.py:35
  55.9 15.6 %collective-permute-start.9 = (bf16[768,256]{1,0:T(8,128)(2,1)S(1)}, bf16[768,256]{1,0:T(8,128)(2,1)S(1)}, u32[]{:S(2)}, u32[]{:S(2)}) collective-permute-start(bf16[768,256]{1,0:T(8,128)(2,1)S(1)} %collective-permute-done.8), channel_id=1, source_target_pairs={{0,4},{4,8},{8,12},{12,16},{16,20},{20,24},{24,28},{28,32},{32,36}... | collective-permute-start | bytes 1179656 | tf_op jit(solution)/shard_map/ppermute | solution.py:35
  60.1 5.3 %copy-start = (bf16[512,1024]{1,0:T(8,128)(2,1)}, bf16[512,1024]{1,0:T(8,128)(2,1)S(1)}, u32[]{:S(2)}) copy-start(bf16[512,1024]{1,0:T(8,128)(2,1)S(1)} %collective-permute-done.19.refs_13_) | copy-start | bytes 3145732
  61.4 45.2 %collective-permute-start.21 = (bf16[512,1024]{1,0:T(8,128)(2,1)}, bf16[512,1024]{1,0:T(8,128)(2,1)}, u32[]{:S(2)}, u32[]{:S(2)}) collective-permute-start(bf16[512,1024]{1,0:T(8,128)(2,1)} %broadcast_select_fusion), channel_id=1, source_target_pairs={{0,128},{128,256},{256,384},{384,0},{64,448},{192,64},{320,192},{4... | collective-permute-start | bytes 3145736 | tf_op jit(solution)/shard_map/ppermute | solution.py:37
  65.4 43.8 %collective-permute-start.23 = (bf16[512,1024]{1,0:T(8,128)(2,1)S(1)}, bf16[512,1024]{1,0:T(8,128)(2,1)}, u32[]{:S(2)}, u32[]{:S(2)}) collective-permute-start(bf16[512,1024]{1,0:T(8,128)(2,1)S(1)} %collective-permute-done.19.refs_13_), channel_id=1, source_target_pairs={{0,64},{64,0},{1,65},{65,1},{2,66},{66,2},{3,67},{67,3},{4,68},{68... | collective-permute-start | bytes 3145736 | tf_op jit(solution)/shard_map/ppermute | solution.py:51
  67.7 18.0 %collective-permute-start.3 = (bf16[768,256]{1,0:T(8,128)(2,1)}, bf16[768,256]{1,0:T(8,128)(2,1)S(1)}, u32[]{:S(2)}, u32[]{:S(2)}) collective-permute-start(bf16[768,256]{1,0:T(8,128)(2,1)} %collective-permute-done.2.refs_3_), channel_id=1, source_target_pairs={{0,4},{4,8},{8,12},{12,16},{16,20},{20,24},{24,28},{28,32},{32,36}... | collective-permute-start | bytes 1179656 | tf_op jit(solution)/shard_map/ppermute | solution.py:35
  71.4 9.5 %collective-permute-start.11 = (bf16[768,256]{1,0:T(8,128)(2,1)S(1)}, bf16[768,256]{1,0:T(8,128)(2,1)S(1)}, u32[]{:S(2)}, u32[]{:S(2)}) collective-permute-start(bf16[768,256]{1,0:T(8,128)(2,1)S(1)} %collective-permute-done.9), channel_id=1, source_target_pairs={{0,4},{4,8},{8,12},{12,16},{16,20},{20,24},{24,28},{28,32},{32,36}... | collective-permute-start | bytes 1179656 | tf_op jit(solution)/shard_map/ppermute | solution.py:35
  80.9 11.6 %collective-permute-start.12 = (bf16[768,256]{1,0:T(8,128)(2,1)S(1)}, bf16[768,256]{1,0:T(8,128)(2,1)S(1)}, u32[]{:S(2)}, u32[]{:S(2)}) collective-permute-start(bf16[768,256]{1,0:T(8,128)(2,1)S(1)} %collective-permute-done.11), channel_id=1, source_target_pairs={{0,4},{4,8},{8,12},{12,16},{16,20},{20,24},{24,28},{28,32},{32,36}... | collective-permute-start | bytes 1179656 | tf_op jit(solution)/shard_map/ppermute | solution.py:35
  85.7 9.8 %copy-start.8 = (bf16[768,256]{1,0:T(8,128)(2,1)}, bf16[768,256]{1,0:T(8,128)(2,1)S(1)}, u32[]{:S(2)}) copy-start(bf16[768,256]{1,0:T(8,128)(2,1)S(1)} %collective-permute-done.3.refs_4_) | copy-start | bytes 1179652
  85.7 30.5 %collective-permute-start.25 = (bf16[512,1024]{1,0:T(8,128)(2,1)}, bf16[512,1024]{1,0:T(8,128)(2,1)S(1)}, u32[]{:S(2)}, u32[]{:S(2)}) collective-permute-start(bf16[512,1024]{1,0:T(8,128)(2,1)} %collective-permute-done.20.refs_15_), channel_id=1, source_target_pairs={{0,64},{64,0},{1,65},{65,1},{2,66},{66,2},{3,67},{67,3},{4,68},{68... | collective-permute-start | bytes 3145736 | tf_op jit(solution)/shard_map/ppermute | solution.py:51
  87.8 9.4 %collective-permute-start.4 = (bf16[768,256]{1,0:T(8,128)(2,1)S(1)}, bf16[768,256]{1,0:T(8,128)(2,1)S(1)}, u32[]{:S(2)}, u32[]{:S(2)}) collective-permute-start(bf16[768,256]{1,0:T(8,128)(2,1)S(1)} %collective-permute-done.3.refs_4_), channel_id=1, source_target_pairs={{0,4},{4,8},{8,12},{12,16},{16,20},{20,24},{24,28},{28,32},{32,36}... | collective-permute-start | bytes 1179656 | tf_op jit(solution)/shard_map/ppermute | solution.py:35
  92.5 8.9 %collective-permute-start.13 = (bf16[768,256]{1,0:T(8,128)(2,1)S(1)}, bf16[768,256]{1,0:T(8,128)(2,1)S(1)}, u32[]{:S(2)}, u32[]{:S(2)}) collective-permute-start(bf16[768,256]{1,0:T(8,128)(2,1)S(1)} %collective-permute-done.12), channel_id=1, source_target_pairs={{0,4},{4,8},{8,12},{12,16},{16,20},{20,24},{24,28},{28,32},{32,36}... | collective-permute-start | bytes 1179656 | tf_op jit(solution)/shard_map/ppermute | solution.py:35
  97.2 9.4 %copy-start.9 = (bf16[768,256]{1,0:T(8,128)(2,1)}, bf16[768,256]{1,0:T(8,128)(2,1)S(1)}, u32[]{:S(2)}) copy-start(bf16[768,256]{1,0:T(8,128)(2,1)S(1)} %collective-permute-done.4.refs_5_) | copy-start | bytes 1179652
  97.2 36.9 %collective-permute-start.10 = (bf16[3,768,256]{2,1,0:T(8,128)(2,1)S(1)}, bf16[3,768,256]{2,1,0:T(8,128)(2,1)}, u32[]{:S(2)}, u32[]{:S(2)}) collective-permute-start(bf16[3,768,256]{2,1,0:T(8,128)(2,1)S(1)} %pad_maximum_fusion), channel_id=1, source_target_pairs={{0,64},{64,0},{1,65},{65,1},{2,66},{66,2},{3,67},{67,3},{4,68},{68... | collective-permute-start | bytes 3538952 | tf_op jit(solution)/shard_map/ppermute | solution.py:196
  101.4 9.7 %collective-permute-start.5 = (bf16[768,256]{1,0:T(8,128)(2,1)S(1)}, bf16[768,256]{1,0:T(8,128)(2,1)S(1)}, u32[]{:S(2)}, u32[]{:S(2)}) collective-permute-start(bf16[768,256]{1,0:T(8,128)(2,1)S(1)} %collective-permute-done.4.refs_5_), channel_id=1, source_target_pairs={{0,4},{4,8},{8,12},{12,16},{16,20},{20,24},{24,28},{28,32},{32,36}... | collective-permute-start | bytes 1179656 | tf_op jit(solution)/shard_map/ppermute | solution.py:35
  106.6 28.3 %collective-permute-start.14 = (bf16[3,768,256]{2,1,0:T(8,128)(2,1)S(1)}, bf16[3,768,256]{2,1,0:T(8,128)(2,1)}, u32[]{:S(2)}, u32[]{:S(2)}) collective-permute-start(bf16[3,768,256]{2,1,0:T(8,128)(2,1)S(1)} %pad_maximum_fusion.1), channel_id=1, source_target_pairs={{0,64},{64,0},{1,65},{65,1},{2,66},{66,2},{3,67},{67,3},{4,68},{68... | collective-permute-start | bytes 3538952 | tf_op jit(solution)/shard_map/ppermute | solution.py:196
  109.2 24.9 %collective-permute-start.24 = (bf16[512,1024]{1,0:T(8,128)(2,1)}, bf16[512,1024]{1,0:T(8,128)(2,1)S(1)}, u32[]{:S(2)}, u32[]{:S(2)}) collective-permute-start(bf16[512,1024]{1,0:T(8,128)(2,1)} %collective-permute-done.21.refs_14_), channel_id=1, source_target_pairs={{0,64},{64,0},{1,65},{65,1},{2,66},{66,2},{3,67},{67,3},{4,68},{68... | collective-permute-start | bytes 3145736 | tf_op jit(solution)/shard_map/ppermute | solution.py:51
  111.2 14.9 %copy-start.10 = (bf16[768,256]{1,0:T(8,128)(2,1)}, bf16[768,256]{1,0:T(8,128)(2,1)S(1)}, u32[]{:S(2)}) copy-start(bf16[768,256]{1,0:T(8,128)(2,1)S(1)} %collective-permute-done.5.refs_6_) | copy-start | bytes 1179652
  111.2 9.7 %collective-permute-start.15 = (bf16[768,256]{1,0:T(8,128)(2,1)S(1)}, bf16[768,256]{1,0:T(8,128)(2,1)}, u32[]{:S(2)}, u32[]{:S(2)}) collective-permute-start(bf16[768,256]{1,0:T(8,128)(2,1)S(1)} %collective-permute-done.5.refs_6_), channel_id=1, source_target_pairs={{0,4},{4,8},{8,12},{12,16},{16,20},{20,24},{24,28},{28,32},{32,36}... | collective-permute-start | bytes 1179656 | tf_op jit(solution)/shard_map/ppermute | solution.py:35
  116.2 9.8 %copy-start.5 = (bf16[512,1024]{1,0:T(8,128)(2,1)}, bf16[512,1024]{1,0:T(8,128)(2,1)S(1)}, u32[]{:S(2)}) copy-start(bf16[512,1024]{1,0:T(8,128)(2,1)S(1)} %collective-permute-done.25.refs_19_) | copy-start | bytes 3145732
  116.2 9.8 %collective-permute-start.17 = (bf16[768,256]{1,0:T(8,128)(2,1)S(1)}, bf16[768,256]{1,0:T(8,128)(2,1)}, u32[]{:S(2)}, u32[]{:S(2)}) collective-permute-start(bf16[768,256]{1,0:T(8,128)(2,1)S(1)} %collective-permute-done.13), channel_id=1, source_target_pairs={{0,4},{4,8},{8,12},{12,16},{16,20},{20,24},{24,28},{28,32},{32,36}... | collective-permute-start | bytes 1179656 | tf_op jit(solution)/shard_map/ppermute | solution.py:35
  120.9 13.3 %collective-permute-start.16 = (bf16[768,256]{1,0:T(8,128)(2,1)}, bf16[768,256]{1,0:T(8,128)(2,1)}, u32[]{:S(2)}, u32[]{:S(2)}) collective-permute-start(bf16[768,256]{1,0:T(8,128)(2,1)} %collective-permute-done.15.refs_9_), channel_id=1, source_target_pairs={{0,4},{4,8},{8,12},{12,16},{16,20},{20,24},{24,28},{28,32},{32,36}... | collective-permute-start | bytes 1179656 | tf_op jit(solution)/shard_map/ppermute | solution.py:35
  126.0 8.8 %collective-permute-start.18 = (bf16[1,768,256]{2,1,0:T(8,128)(2,1)}, bf16[1,768,256]{2,1,0:T(8,128)(2,1)}, u32[]{:S(2)}, u32[]{:S(2)}) collective-permute-start(bf16[1,768,256]{2,1,0:T(8,128)(2,1)} %bitcast.12), channel_id=1, source_target_pairs={{0,64},{64,0},{1,65},{65,1},{2,66},{66,2},{3,67},{67,3},{4,68},{68... | collective-permute-start | bytes 1179656 | tf_op jit(solution)/shard_map/ppermute | solution.py:196
  134.1 1.0 copy-start.6

commit v9 on v7

--- a/solution.py
+++ b/solution.py
@@ -18,7 +18,7 @@
 LIMIT = 60 << 20
 ROUNDS = 8
 BATCHES = ((1, 2, 3), (4, 5, 6), (7,))
-DEPTHS = (0, 2, 6, 11, 16)
+DEPTHS = (0, 1, 3, 7, 11, 16)
 
 
 def to_all(array, axis, copies):
@@ -94,18 +94,23 @@
         def fetch_block(k):
             return pltpu.make_async_copy(blocks[k], lefts.at[k], sems.at[1, k])
 
-        for k, far in enumerate(away):
-            source = lax.rem(z + far * (2 * core - 1) + 16, 16)
-            fetch_block(k).start()
-            mine = lax.rem(source // 2, 2) == core
-            pl.when(mine)(fetch(k, own, source).start)
-            pl.when(jnp.logical_not(mine))(fetch(k, theirs, source).start)
+        def begin_fetch(step):
+            for k in range(DEPTHS[step], DEPTHS[step + 1]):
+                source = lax.rem(z + away[k] * (2 * core - 1) + 16, 16)
+                fetch_block(k).start()
+                mine = lax.rem(source // 2, 2) == core
+                pl.when(mine)(fetch(k, own, source).start)
+                pl.when(jnp.logical_not(mine))(fetch(k, theirs, source).start)
 
+        begin_fetch(0)
+        begin_fetch(1)
         tokens, columns = acc.shape
-        for first, end in zip(DEPTHS, DEPTHS[1:]):
+        for step, (first, end) in enumerate(zip(DEPTHS, DEPTHS[1:])):
             for k in range(first, end):
                 fetch_block(k).wait()
                 fetch(k, own, 0).wait()
+            if step + 3 < len(DEPTHS):
+                begin_fetch(step + 2)
             deep = slice(first * BLOCK, end * BLOCK)
             for at in range(0, tokens, TILE):
                 part = slice(at, at + TILE)
@@ -124,7 +129,7 @@
                 picked = jnp.sum(picked, axis=1, keepdims=True)
                 lse = jnp.log(total) + top
                 lane = lax.broadcasted_iota(jnp.int32, (TILE, 128), 1)
-                out[:, part] = jnp.where(lane == 0, lse, picked).T[:8]
+                out[:, part] = jnp.where(lane == 0, lse, picked).T[:2]
 
     return kernel
 
@@ -138,7 +143,7 @@
         product_kernel(kinds, away),
         in_specs=[pl.BlockSpec(memory_space=pltpu.SMEM)] + [hbm] * (len(blocks) + 2) + [vmem],
         out_specs=vmem,
-        out_shape=jax.ShapeDtypeStruct((8, tokens), jnp.float32),
+        out_shape=jax.ShapeDtypeStruct((2, tokens), jnp.float32),
         scratch_shapes=[
             pltpu.VMEM((tokens, columns), jnp.float32),
             pltpu.VMEM((count * BLOCK, columns), jnp.bfloat16),
@@ -181,7 +186,7 @@
     away = [*range(7), *(-r for some in BATCHES[:2] for r in some), 7, 8, *(-r for r in BATCHES[2])]
     blocks = [*own[:7], *swapped[:2], own[7], own[8], swapped[2]]
     stats = product(where, away, blocks, weights, wanted)
-    return tail(stats[:2], *ready)
+    return tail(stats, *ready)
 
 
 def solution(mesh):

time: 224 us -> 224 us (level)
  no operation moved by 1% of the time
where the time goes in v9:
time: 224 us; the launch traced here: 223 us
  starting transfers between devices  104 us (46%)
  blocking collectives  51 us (23%)
  waiting for transfers between devices  45 us (20%)
  Pallas kernels  11.7 us (5%)
  local copies, waits for them, and re-layouts  6.25 us (3%)
  other arithmetic  4.12 us (2%)
    ppermute x15, starting transfers between devices, along_z(): return lax.ppermute(array, ('c', 'z'), pairs)  71.1 us
    all_to_all x1, waiting for transfers between devices, to_all(): lax.all_to_all(jnp.broadcast_to(array[None], (copies, *array.shape)), axi...  37.3 us
    all_to_all x2, blocking collectives, to_all(): lax.all_to_all(jnp.broadcast_to(array[None], (copies, *array.shape)), axi...  26.4 us
    all_to_all x1, blocking collectives, tail(): got = lax.all_to_all(send.reshape(zs * ys, -1), VOCAB, 0, 0, tiled=True)  24.7 us
    ppermute x3, starting transfers between devices, loss(): swapped.append(lax.ppermute(jnp.stack([other[r] for r in some]), 'c', SWAP))  12.8 us
    pallas_call x1, Pallas kernels, product(): pl.pallas_call(product_kernel(kinds, away), in_specs=[pl.BlockSpec(memory...  11.7 us
    ppermute x1, starting transfers between devices, gathered_weight(): return (own, lax.ppermute(own, 'c', SWAP))  7.55 us
    ppermute x1, starting transfers between devices, loss(): theirs = lax.ppermute(mine, 'c', SWAP)  7.33 us
  transfers between devices with their start and end apart: 21, of which 9 were waited for; matrix products, arithmetic and copies ran while one was open for 1% of the time, Pallas kernels for 0%

profile of v9, /device:TPU:1, one launch (start us, length us, event | category | flops | bytes accessed | tf_op | source)
XLA Modules:
  0.0 223.2 jit_solution(16369661658334639969)
XLA Ops:
  0.6 0.6 pad_add_fusion.where
  1.2 0.9 broadcast_in_dim.40
  2.1 11.0 %all_to_all.25 = bf16[4,64,768]{2,1,0:T(8,128)(2,1)S(1)} all-to-all(bf16[4,64,768]{2,1,0:T(8,128)(2,1)S(1)} %broadcast_in_dim.40), channel_id=1, replica_groups=mesh['x'=4,'c'=2,'z'=16,'y'=4] {'y'}, dimensions={0} | all-to-all | bytes 786432 | tf_op jit(solution)/shard_map/all_to_all | solution.py:25
  13.2 2.5 %broadcast_in_dim.66 = bf16[4,512,1024]{2,1,0:T(8,128)(2,1)} broadcast(bf16[512,1024]{1,0:T(8,128)(2,1)S(1)} %copy-done), dimensions={1,2} | broadcast | bytes 5242880 | tf_op jit(solution)/shard_map/broadcast_in_dim | solution.py:26
  15.7 5.1 %all-to-all-start.1 = ((bf16[4,512,1024]{2,1,0:T(8,128)(2,1)}), bf16[4,512,1024]{2,1,0:T(8,128)(2,1)}, u32[]{:S(2)}, u32[]{:S(2)}) async-start(bf16[4,512,1024]{2,1,0:T(8,128)(2,1)} %broadcast_in_dim.66), calls=%async_computation.1 | async-start | bytes 8388608 | tf_op jit(solution)/shard_map/all_to_all | solution.py:25
  20.9 0.2 copy.17
  21.0 7.3 %collective-permute-start.6 = (bf16[768,256]{1,0:T(8,128)(2,1)S(1)}, bf16[768,256]{1,0:T(8,128)(2,1)S(1)}, u32[]{:S(2)}, u32[]{:S(2)}) collective-permute-start(bf16[768,256]{1,0:T(8,128)(2,1)S(1)} %bitcast.29), channel_id=1, source_target_pairs={{0,64},{64,0},{1,65},{65,1},{2,66},{66,2},{3,67},{67,3},{4,68},{68... | collective-permute-start | bytes 1179656 | tf_op jit(solution)/shard_map/ppermute | solution.py:168
  28.4 37.3 %all-to-all-done.1.refs_12_ = bf16[4,512,1024]{2,1,0:T(8,128)(2,1)} async-done(((bf16[4,512,1024]{2,1,0:T(8,128)(2,1)}), bf16[4,512,1024]{2,1,0:T(8,128)(2,1)}, u32[]{:S(2)}, u32[]{:S(2)}) %all-to-all-start.1) | async-done | bytes 4194336 | tf_op jit(solution)/shard_map/all_to_all | solution.py:25
  65.6 7.5 %collective-permute-start.19 = (bf16[4,512,1024]{2,1,0:T(8,128)(2,1)}, bf16[4,512,1024]{2,1,0:T(8,128)(2,1)}, u32[]{:S(2)}, u32[]{:S(2)}) collective-permute-start(bf16[4,512,1024]{2,1,0:T(8,128)(2,1)} %all-to-all-done.1.refs_12_), channel_id=1, source_target_pairs={{0,64},{64,0},{1,65},{65,1},{2,66},{66,2},{3,67},{67,3},{4,68},{68... | collective-permute-start | bytes 12582920 | tf_op jit(solution)/shard_map/ppermute | solution.py:38
  73.2 0.0 collective-permute-done.6
  73.2 11.3 %collective-permute-start.7 = (bf16[768,256]{1,0:T(8,128)(2,1)S(1)}, bf16[768,256]{1,0:T(8,128)(2,1)S(1)}, u32[]{:S(2)}, u32[]{:S(2)}) collective-permute-start(bf16[768,256]{1,0:T(8,128)(2,1)S(1)} %collective-permute-done.6), channel_id=1, source_target_pairs={{0,4},{4,8},{8,12},{12,16},{16,20},{20,24},{24,28},{28,32},{32,36}... | collective-permute-start | bytes 1179656 | tf_op jit(solution)/shard_map/ppermute | solution.py:33
  84.5 2.6 %collective-permute-start = (bf16[768,256]{1,0:T(8,128)(2,1)S(1)}, bf16[768,256]{1,0:T(8,128)(2,1)S(1)}, u32[]{:S(2)}, u32[]{:S(2)}) collective-permute-start(bf16[768,256]{1,0:T(8,128)(2,1)S(1)} %bitcast.30), channel_id=1, source_target_pairs={{0,4},{4,8},{8,12},{12,16},{16,20},{20,24},{24,28},{28,32},{32,36}... | collective-permute-start | bytes 1179656 | tf_op jit(solution)/shard_map/ppermute | solution.py:33
  87.2 2.1 collective-permute-done.7
  89.2 5.0 %collective-permute-start.8 = (bf16[768,256]{1,0:T(8,128)(2,1)S(1)}, bf16[768,256]{1,0:T(8,128)(2,1)S(1)}, u32[]{:S(2)}, u32[]{:S(2)}) collective-permute-start(bf16[768,256]{1,0:T(8,128)(2,1)S(1)} %collective-permute-done.7), channel_id=1, source_target_pairs={{0,4},{4,8},{8,12},{12,16},{16,20},{20,24},{24,28},{28,32},{32,36}... | collective-permute-start | bytes 1179656 | tf_op jit(solution)/shard_map/ppermute | solution.py:33
  94.3 0.0 collective-permute-done.refs_1_
  94.3 4.2 %collective-permute-start.1 = (bf16[768,256]{1,0:T(8,128)(2,1)S(1)}, bf16[768,256]{1,0:T(8,128)(2,1)S(1)}, u32[]{:S(2)}, u32[]{:S(2)}) collective-permute-start(bf16[768,256]{1,0:T(8,128)(2,1)S(1)} %collective-permute-done.refs_1_), channel_id=1, source_target_pairs={{0,4},{4,8},{8,12},{12,16},{16,20},{20,24},{24,28},{28,32},{32,36}... | collective-permute-start | bytes 1179656 | tf_op jit(solution)/shard_map/ppermute | solution.py:33
  98.5 0.5 collective-permute-done.8
  99.0 5.0 %collective-permute-start.9 = (bf16[768,256]{1,0:T(8,128)(2,1)S(1)}, bf16[768,256]{1,0:T(8,128)(2,1)S(1)}, u32[]{:S(2)}, u32[]{:S(2)}) collective-permute-start(bf16[768,256]{1,0:T(8,128)(2,1)S(1)} %collective-permute-done.8), channel_id=1, source_target_pairs={{0,4},{4,8},{8,12},{12,16},{16,20},{20,24},{24,28},{28,32},{32,36}... | collective-permute-start | bytes 1179656 | tf_op jit(solution)/shard_map/ppermute | solution.py:33
  104.1 4.1 %collective-permute-start.2 = (bf16[768,256]{1,0:T(8,128)(2,1)S(1)}, bf16[768,256]{1,0:T(8,128)(2,1)S(1)}, u32[]{:S(2)}, u32[]{:S(2)}) collective-permute-start(bf16[768,256]{1,0:T(8,128)(2,1)S(1)} %collective-permute-done.1.refs_2_), channel_id=1, source_target_pairs={{0,4},{4,8},{8,12},{12,16},{16,20},{20,24},{24,28},{28,32},{32,36}... | collective-permute-start | bytes 1179656 | tf_op jit(solution)/shard_map/ppermute | solution.py:33
  108.2 0.1 reshape.109
  108.3 0.1 select_reduce_fusion.4
  108.4 0.3 collective-permute-done.9
  108.7 5.0 %collective-permute-start.11 = (bf16[768,256]{1,0:T(8,128)(2,1)S(1)}, bf16[768,256]{1,0:T(8,128)(2,1)S(1)}, u32[]{:S(2)}, u32[]{:S(2)}) collective-permute-start(bf16[768,256]{1,0:T(8,128)(2,1)S(1)} %collective-permute-done.9), channel_id=1, source_target_pairs={{0,4},{4,8},{8,12},{12,16},{16,20},{20,24},{24,28},{28,32},{32,36}... | collective-permute-start | bytes 1179656 | tf_op jit(solution)/shard_map/ppermute | solution.py:33
  113.8 4.1 %collective-permute-start.3 = (bf16[768,256]{1,0:T(8,128)(2,1)S(1)}, bf16[768,256]{1,0:T(8,128)(2,1)}, u32[]{:S(2)}, u32[]{:S(2)}) collective-permute-start(bf16[768,256]{1,0:T(8,128)(2,1)S(1)} %collective-permute-done.2.refs_3_), channel_id=1, source_target_pairs={{0,4},{4,8},{8,12},{12,16},{16,20},{20,24},{24,28},{28,32},{32,36}... | collective-permute-start | bytes 1179656 | tf_op jit(solution)/shard_map/ppermute | solution.py:33
  117.9 0.5 collective-permute-done.11
  118.4 5.0 %collective-permute-start.12 = (bf16[768,256]{1,0:T(8,128)(2,1)S(1)}, bf16[768,256]{1,0:T(8,128)(2,1)S(1)}, u32[]{:S(2)}, u32[]{:S(2)}) collective-permute-start(bf16[768,256]{1,0:T(8,128)(2,1)S(1)} %collective-permute-done.11), channel_id=1, source_target_pairs={{0,4},{4,8},{8,12},{12,16},{16,20},{20,24},{24,28},{28,32},{32,36}... | collective-permute-start | bytes 1179656 | tf_op jit(solution)/shard_map/ppermute | solution.py:33
  123.4 0.1 select_reduce_fusion.2
  123.5 0.1 eq.39
  123.6 0.6 select_reduce_fusion.1
  124.2 0.6 fusion.2
  124.9 0.1 iota.37
  125.0 2.9 %collective-permute-start.4 = (bf16[768,256]{1,0:T(8,128)(2,1)}, bf16[768,256]{1,0:T(8,128)(2,1)S(1)}, u32[]{:S(2)}, u32[]{:S(2)}) collective-permute-start(bf16[768,256]{1,0:T(8,128)(2,1)} %collective-permute-done.3.refs_4_), channel_id=1, source_target_pairs={{0,4},{4,8},{8,12},{12,16},{16,20},{20,24},{24,28},{28,32},{32,36}... | collective-permute-start | bytes 1179656 | tf_op jit(solution)/shard_map/ppermute | solution.py:33
  127.8 0.3 collective-permute-done.12
  128.1 5.0 %collective-permute-start.13 = (bf16[768,256]{1,0:T(8,128)(2,1)S(1)}, bf16[768,256]{1,0:T(8,128)(2,1)S(1)}, u32[]{:S(2)}, u32[]{:S(2)}) collective-permute-start(bf16[768,256]{1,0:T(8,128)(2,1)S(1)} %collective-permute-done.12), channel_id=1, source_target_pairs={{0,4},{4,8},{8,12},{12,16},{16,20},{20,24},{24,28},{28,32},{32,36}... | collective-permute-start | bytes 1179656 | tf_op jit(solution)/shard_map/ppermute | solution.py:33
  133.2 0.1 pad_maximum_fusion
  133.3 4.7 %collective-permute-start.10 = (bf16[3,768,256]{2,1,0:T(8,128)(2,1)S(1)}, bf16[3,768,256]{2,1,0:T(8,128)(2,1)}, u32[]{:S(2)}, u32[]{:S(2)}) collective-permute-start(bf16[3,768,256]{2,1,0:T(8,128)(2,1)S(1)} %pad_maximum_fusion), channel_id=1, source_target_pairs={{0,64},{64,0},{1,65},{65,1},{2,66},{66,2},{3,67},{67,3},{4,68},{68... | collective-permute-start | bytes 3538952 | tf_op jit(solution)/shard_map/ppermute | solution.py:185
  138.1 4.9 %collective-permute-start.5 = (bf16[768,256]{1,0:T(8,128)(2,1)S(1)}, bf16[768,256]{1,0:T(8,128)(2,1)S(1)}, u32[]{:S(2)}, u32[]{:S(2)}) collective-permute-start(bf16[768,256]{1,0:T(8,128)(2,1)S(1)} %collective-permute-done.4.refs_5_), channel_id=1, source_target_pairs={{0,4},{4,8},{8,12},{12,16},{16,20},{20,24},{24,28},{28,32},{32,36}... | collective-permute-start | bytes 1179656 | tf_op jit(solution)/shard_map/ppermute | solution.py:33
  143.0 0.1 pad_maximum_fusion.1
  143.1 3.9 %collective-permute-start.14 = (bf16[3,768,256]{2,1,0:T(8,128)(2,1)S(1)}, bf16[3,768,256]{2,1,0:T(8,128)(2,1)}, u32[]{:S(2)}, u32[]{:S(2)}) collective-permute-start(bf16[3,768,256]{2,1,0:T(8,128)(2,1)S(1)} %pad_maximum_fusion.1), channel_id=1, source_target_pairs={{0,64},{64,0},{1,65},{65,1},{2,66},{66,2},{3,67},{67,3},{4,68},{68... | collective-permute-start | bytes 3538952 | tf_op jit(solution)/shard_map/ppermute | solution.py:185
  147.0 0.7 collective-permute-done.5.refs_6_
  147.6 5.0 %collective-permute-start.15 = (bf16[768,256]{1,0:T(8,128)(2,1)S(1)}, bf16[768,256]{1,0:T(8,128)(2,1)S(1)}, u32[]{:S(2)}, u32[]{:S(2)}) collective-permute-start(bf16[768,256]{1,0:T(8,128)(2,1)S(1)} %collective-permute-done.5.refs_6_), channel_id=1, source_target_pairs={{0,4},{4,8},{8,12},{12,16},{16,20},{20,24},{24,28},{28,32},{32,36}... | collective-permute-start | bytes 1179656 | tf_op jit(solution)/shard_map/ppermute | solution.py:33
  152.7 1.9 collective-permute-start.17
  154.6 2.8 %collective-permute-done.15.refs_9_ = bf16[768,256]{1,0:T(8,128)(2,1)S(1)} collective-permute-done((bf16[768,256]{1,0:T(8,128)(2,1)S(1)}, bf16[768,256]{1,0:T(8,128)(2,1)S(1)}, u32[]{:S(2)}, u32[]{:S(2)}) %collective-permute-start.15) | collective-permute-done | bytes 393248 | tf_op jit(solution)/shard_map/ppermute | solution.py:33
  157.4 5.0 %collective-permute-start.16 = (bf16[768,256]{1,0:T(8,128)(2,1)S(1)}, bf16[768,256]{1,0:T(8,128)(2,1)S(1)}, u32[]{:S(2)}, u32[]{:S(2)}) collective-permute-start(bf16[768,256]{1,0:T(8,128)(2,1)S(1)} %collective-permute-done.15.refs_9_), channel_id=1, source_target_pairs={{0,4},{4,8},{8,12},{12,16},{16,20},{20,24},{24,28},{28,32},{32,36}... | collective-permute-start | bytes 1179656 | tf_op jit(solution)/shard_map/ppermute | solution.py:33
  162.4 4.2 %collective-permute-start.18 = (bf16[1,768,256]{2,1,0:T(8,128)(2,1)}, bf16[1,768,256]{2,1,0:T(8,128)(2,1)}, u32[]{:S(2)}, u32[]{:S(2)}) collective-permute-start(bf16[1,768,256]{2,1,0:T(8,128)(2,1)} %bitcast.11), channel_id=1, source_target_pairs={{0,64},{64,0},{1,65},{65,1},{2,66},{66,2},{3,67},{67,3},{4,68},{68... | collective-permute-start | bytes 1179656 | tf_op jit(solution)/shard_map/ppermute | solution.py:185
  166.6 1.0 copy.18.refs_14_
  167.6 0.7 collective-permute-done.18.refs_11_
  168.3 0.0 copy-done.13
  168.4 11.7 %shard_map.68 = f32[2,768]{1,0:T(2,128)} custom-call(s32[2]{0:T(128)} %pad_add_fusion.where, bf16[768,256]{1,0:T(8,128)(2,1)} %bitcast.31, bf16[768,256]{1,0:T(8,128)(2,1)} %copy-done.7, bf16[768,256]{1,0:T(8,128)(2,1)} %copy-done.8, bf16[768,256]{1,0:T(8,128)(2,1)} %copy-done.9, bf16[768,256]{1,0:T(8,128)(2,1)} %collective-permute-done.3.refs_4_, ...), custom_call_target="tpu_custom_call" | custom-call | flops 6442450944 | bytes 14680064 | tf_op jit(solution)/shard_map/pallas_call | solution.py:142
  180.0 0.0 copy-start.6
  180.0 0.8 reshape.110
  180.9 0.1 broadcast_in_dim.67
  181.0 0.1 all_to_all.18
  181.2 24.7 %all_to_all.26 = f32[64,1,384]{2,1,0:T(1,128)S(1)} all-to-all(f32[64,1,384]{2,1,0:T(1,128)S(1)} %all_to_all.18), channel_id=1, replica_groups=mesh['x'=4,'c'=2,'z'=16,'y'=4] {'z','y'}, dimensions={0} | all-to-all | bytes 196608 | tf_op jit(solution)/shard_map/all_to_all | solution.py:63
  205.8 0.2 reduce.3
  206.1 0.1 reshape.111
  206.2 0.2 slice_reduce_fusion.1
  206.4 0.1 reshape.112
  206.5 0.0 copy-done.2
  206.5 0.1 select_reduce_fusion
  206.7 0.1 pad_maximum_fusion.2
  206.7 0.5 select_reduce_fusion.3
  207.3 15.3 %all_to_all.27 = f32[32,1,128]{2,1,0:T(1,128)S(1)} all-to-all(f32[32,1,128]{2,1,0:T(1,128)S(1)} %broadcast_in_dim.70), channel_id=1, replica_groups=mesh['x'=4,'c'=2,'z'=16,'y'=4] {'x','c','y'}, dimensions={0} | all-to-all | bytes 32768 | tf_op jit(solution)/shard_map/all_to_all | solution.py:25
  222.6 0.6 maximum_divide_fusion
  (47 shorter events, 0.2 us)
Async XLA Ops:
  0.6 12.6 %copy-start = (bf16[512,1024]{1,0:T(8,128)(2,1)S(1)}, bf16[512,1024]{1,0:T(8,128)(2,1)}, u32[]{:S(2)}) copy-start(bf16[512,1024]{1,0:T(8,128)(2,1)} %param.6) | copy-start | bytes 3145732
  15.7 92.5 %copy-start.3 = (s32[768]{0:T(1024)S(1)}, s32[768]{0:T(1024)}, u32[]{:S(2)}) copy-start(s32[768]{0:T(1024)} %param.8) | copy-start | bytes 9220
  15.7 92.6 %copy-start.5 = (s32[6]{0:T(128)S(1)}, s32[6]{0:T(128)}, u32[]{:S(2)}) copy-start(s32[6]{0:T(128)} %param.9) | copy-start | bytes 76
  15.7 98.0 %copy-start.4 = (s32[768]{0:T(1024)S(1)}, s32[768]{0:T(1024)}, u32[]{:S(2)}) copy-start(s32[768]{0:T(1024)} %param.7) | copy-start | bytes 9220
  15.7 49.9 %all-to-all-start.1 = ((bf16[4,512,1024]{2,1,0:T(8,128)(2,1)}), bf16[4,512,1024]{2,1,0:T(8,128)(2,1)}, u32[]{:S(2)}, u32[]{:S(2)}) async-start(bf16[4,512,1024]{2,1,0:T(8,128)(2,1)} %broadcast_in_dim.66), calls=%async_computation.1 | async-start | bytes 8388608 | tf_op jit(solution)/shard_map/all_to_all | solution.py:25
  21.0 112.3 %copy-start.1 = (bf16[256,768]{0,1:T(8,128)(2,1)}, bf16[256,768]{0,1:T(8,128)(2,1)S(1)}, u32[]{:S(2)}) copy-start(bf16[256,768]{0,1:T(8,128)(2,1)S(1)} %copy.17) | copy-start | bytes 1179652
  21.0 52.2 %collective-permute-start.6 = (bf16[768,256]{1,0:T(8,128)(2,1)S(1)}, bf16[768,256]{1,0:T(8,128)(2,1)S(1)}, u32[]{:S(2)}, u32[]{:S(2)}) collective-permute-start(bf16[768,256]{1,0:T(8,128)(2,1)S(1)} %bitcast.29), channel_id=1, source_target_pairs={{0,64},{64,0},{1,65},{65,1},{2,66},{66,2},{3,67},{67,3},{4,68},{68... | collective-permute-start | bytes 1179656 | tf_op jit(solution)/shard_map/ppermute | solution.py:168
  65.6 102.7 %collective-permute-start.19 = (bf16[4,512,1024]{2,1,0:T(8,128)(2,1)}, bf16[4,512,1024]{2,1,0:T(8,128)(2,1)}, u32[]{:S(2)}, u32[]{:S(2)}) collective-permute-start(bf16[4,512,1024]{2,1,0:T(8,128)(2,1)} %all-to-all-done.1.refs_12_), channel_id=1, source_target_pairs={{0,64},{64,0},{1,65},{65,1},{2,66},{66,2},{3,67},{67,3},{4,68},{68... | collective-permute-start | bytes 12582920 | tf_op jit(solution)/shard_map/ppermute | solution.py:38
  73.2 16.0 %collective-permute-start.7 = (bf16[768,256]{1,0:T(8,128)(2,1)S(1)}, bf16[768,256]{1,0:T(8,128)(2,1)S(1)}, u32[]{:S(2)}, u32[]{:S(2)}) collective-permute-start(bf16[768,256]{1,0:T(8,128)(2,1)S(1)} %collective-permute-done.6), channel_id=1, source_target_pairs={{0,4},{4,8},{8,12},{12,16},{16,20},{20,24},{24,28},{28,32},{32,36}... | collective-permute-start | bytes 1179656 | tf_op jit(solution)/shard_map/ppermute | solution.py:33
  84.5 9.7 %collective-permute-start = (bf16[768,256]{1,0:T(8,128)(2,1)S(1)}, bf16[768,256]{1,0:T(8,128)(2,1)S(1)}, u32[]{:S(2)}, u32[]{:S(2)}) collective-permute-start(bf16[768,256]{1,0:T(8,128)(2,1)S(1)} %bitcast.30), channel_id=1, source_target_pairs={{0,4},{4,8},{8,12},{12,16},{16,20},{20,24},{24,28},{28,32},{32,36}... | collective-permute-start | bytes 1179656 | tf_op jit(solution)/shard_map/ppermute | solution.py:33
  89.2 9.7 %collective-permute-start.8 = (bf16[768,256]{1,0:T(8,128)(2,1)S(1)}, bf16[768,256]{1,0:T(8,128)(2,1)S(1)}, u32[]{:S(2)}, u32[]{:S(2)}) collective-permute-start(bf16[768,256]{1,0:T(8,128)(2,1)S(1)} %collective-permute-done.7), channel_id=1, source_target_pairs={{0,4},{4,8},{8,12},{12,16},{16,20},{20,24},{24,28},{28,32},{32,36}... | collective-permute-start | bytes 1179656 | tf_op jit(solution)/shard_map/ppermute | solution.py:33
  94.3 14.1 %copy-start.7 = (bf16[768,256]{1,0:T(8,128)(2,1)}, bf16[768,256]{1,0:T(8,128)(2,1)S(1)}, u32[]{:S(2)}) copy-start(bf16[768,256]{1,0:T(8,128)(2,1)S(1)} %collective-permute-done.refs_1_) | copy-start | bytes 1179652
  94.3 9.8 %collective-permute-start.1 = (bf16[768,256]{1,0:T(8,128)(2,1)S(1)}, bf16[768,256]{1,0:T(8,128)(2,1)S(1)}, u32[]{:S(2)}, u32[]{:S(2)}) collective-permute-start(bf16[768,256]{1,0:T(8,128)(2,1)S(1)} %collective-permute-done.refs_1_), channel_id=1, source_target_pairs={{0,4},{4,8},{8,12},{12,16},{16,20},{20,24},{24,28},{28,32},{32,36}... | collective-permute-start | bytes 1179656 | tf_op jit(solution)/shard_map/ppermute | solution.py:33
  99.0 9.7 %collective-permute-start.9 = (bf16[768,256]{1,0:T(8,128)(2,1)S(1)}, bf16[768,256]{1,0:T(8,128)(2,1)S(1)}, u32[]{:S(2)}, u32[]{:S(2)}) collective-permute-start(bf16[768,256]{1,0:T(8,128)(2,1)S(1)} %collective-permute-done.8), channel_id=1, source_target_pairs={{0,4},{4,8},{8,12},{12,16},{16,20},{20,24},{24,28},{28,32},{32,36}... | collective-permute-start | bytes 1179656 | tf_op jit(solution)/shard_map/ppermute | solution.py:33
  104.0 29.1 %copy-start.8 = (bf16[768,256]{1,0:T(8,128)(2,1)}, bf16[768,256]{1,0:T(8,128)(2,1)S(1)}, u32[]{:S(2)}) copy-start(bf16[768,256]{1,0:T(8,128)(2,1)S(1)} %collective-permute-done.1.refs_2_) | copy-start | bytes 1179652
  104.1 9.7 %collective-permute-start.2 = (bf16[768,256]{1,0:T(8,128)(2,1)S(1)}, bf16[768,256]{1,0:T(8,128)(2,1)S(1)}, u32[]{:S(2)}, u32[]{:S(2)}) collective-permute-start(bf16[768,256]{1,0:T(8,128)(2,1)S(1)} %collective-permute-done.1.refs_2_), channel_id=1, source_target_pairs={{0,4},{4,8},{8,12},{12,16},{16,20},{20,24},{24,28},{28,32},{32,36}... | collective-permute-start | bytes 1179656 | tf_op jit(solution)/shard_map/ppermute | solution.py:33
  108.7 9.7 %collective-permute-start.11 = (bf16[768,256]{1,0:T(8,128)(2,1)S(1)}, bf16[768,256]{1,0:T(8,128)(2,1)S(1)}, u32[]{:S(2)}, u32[]{:S(2)}) collective-permute-start(bf16[768,256]{1,0:T(8,128)(2,1)S(1)} %collective-permute-done.9), channel_id=1, source_target_pairs={{0,4},{4,8},{8,12},{12,16},{16,20},{20,24},{24,28},{28,32},{32,36}... | collective-permute-start | bytes 1179656 | tf_op jit(solution)/shard_map/ppermute | solution.py:33
  113.8 19.4 %copy-start.9 = (bf16[768,256]{1,0:T(8,128)(2,1)}, bf16[768,256]{1,0:T(8,128)(2,1)S(1)}, u32[]{:S(2)}) copy-start(bf16[768,256]{1,0:T(8,128)(2,1)S(1)} %collective-permute-done.2.refs_3_) | copy-start | bytes 1179652
  113.8 11.1 %collective-permute-start.3 = (bf16[768,256]{1,0:T(8,128)(2,1)S(1)}, bf16[768,256]{1,0:T(8,128)(2,1)}, u32[]{:S(2)}, u32[]{:S(2)}) collective-permute-start(bf16[768,256]{1,0:T(8,128)(2,1)S(1)} %collective-permute-done.2.refs_3_), channel_id=1, source_target_pairs={{0,4},{4,8},{8,12},{12,16},{16,20},{20,24},{24,28},{28,32},{32,36}... | collective-permute-start | bytes 1179656 | tf_op jit(solution)/shard_map/ppermute | solution.py:33
  118.4 9.7 %collective-permute-start.12 = (bf16[768,256]{1,0:T(8,128)(2,1)S(1)}, bf16[768,256]{1,0:T(8,128)(2,1)S(1)}, u32[]{:S(2)}, u32[]{:S(2)}) collective-permute-start(bf16[768,256]{1,0:T(8,128)(2,1)S(1)} %collective-permute-done.11), channel_id=1, source_target_pairs={{0,4},{4,8},{8,12},{12,16},{16,20},{20,24},{24,28},{28,32},{32,36}... | collective-permute-start | bytes 1179656 | tf_op jit(solution)/shard_map/ppermute | solution.py:33
  125.0 13.1 %collective-permute-start.4 = (bf16[768,256]{1,0:T(8,128)(2,1)}, bf16[768,256]{1,0:T(8,128)(2,1)S(1)}, u32[]{:S(2)}, u32[]{:S(2)}) collective-permute-start(bf16[768,256]{1,0:T(8,128)(2,1)} %collective-permute-done.3.refs_4_), channel_id=1, source_target_pairs={{0,4},{4,8},{8,12},{12,16},{16,20},{20,24},{24,28},{28,32},{32,36}... | collective-permute-start | bytes 1179656 | tf_op jit(solution)/shard_map/ppermute | solution.py:33
  128.1 14.8 %collective-permute-start.13 = (bf16[768,256]{1,0:T(8,128)(2,1)S(1)}, bf16[768,256]{1,0:T(8,128)(2,1)S(1)}, u32[]{:S(2)}, u32[]{:S(2)}) collective-permute-start(bf16[768,256]{1,0:T(8,128)(2,1)S(1)} %collective-permute-done.12), channel_id=1, source_target_pairs={{0,4},{4,8},{8,12},{12,16},{16,20},{20,24},{24,28},{28,32},{32,36}... | collective-permute-start | bytes 1179656 | tf_op jit(solution)/shard_map/ppermute | solution.py:33
  133.3 34.3 %collective-permute-start.10 = (bf16[3,768,256]{2,1,0:T(8,128)(2,1)S(1)}, bf16[3,768,256]{2,1,0:T(8,128)(2,1)}, u32[]{:S(2)}, u32[]{:S(2)}) collective-permute-start(bf16[3,768,256]{2,1,0:T(8,128)(2,1)S(1)} %pad_maximum_fusion), channel_id=1, source_target_pairs={{0,64},{64,0},{1,65},{65,1},{2,66},{66,2},{3,67},{67,3},{4,68},{68... | collective-permute-start | bytes 3538952 | tf_op jit(solution)/shard_map/ppermute | solution.py:185
  138.1 5.0 %copy-start.10 = (bf16[768,256]{1,0:T(8,128)(2,1)}, bf16[768,256]{1,0:T(8,128)(2,1)S(1)}, u32[]{:S(2)}) copy-start(bf16[768,256]{1,0:T(8,128)(2,1)S(1)} %collective-permute-done.4.refs_5_) | copy-start | bytes 1179652
  138.1 9.6 %collective-permute-start.5 = (bf16[768,256]{1,0:T(8,128)(2,1)S(1)}, bf16[768,256]{1,0:T(8,128)(2,1)S(1)}, u32[]{:S(2)}, u32[]{:S(2)}) collective-permute-start(bf16[768,256]{1,0:T(8,128)(2,1)S(1)} %collective-permute-done.4.refs_5_), channel_id=1, source_target_pairs={{0,4},{4,8},{8,12},{12,16},{16,20},{20,24},{24,28},{28,32},{32,36}... | collective-permute-start | bytes 1179656 | tf_op jit(solution)/shard_map/ppermute | solution.py:33
  143.1 25.2 %collective-permute-start.14 = (bf16[3,768,256]{2,1,0:T(8,128)(2,1)S(1)}, bf16[3,768,256]{2,1,0:T(8,128)(2,1)}, u32[]{:S(2)}, u32[]{:S(2)}) collective-permute-start(bf16[3,768,256]{2,1,0:T(8,128)(2,1)S(1)} %pad_maximum_fusion.1), channel_id=1, source_target_pairs={{0,64},{64,0},{1,65},{65,1},{2,66},{66,2},{3,67},{67,3},{4,68},{68... | collective-permute-start | bytes 3538952 | tf_op jit(solution)/shard_map/ppermute | solution.py:185
  147.6 20.7 %copy-start.11 = (bf16[768,256]{1,0:T(8,128)(2,1)}, bf16[768,256]{1,0:T(8,128)(2,1)S(1)}, u32[]{:S(2)}) copy-start(bf16[768,256]{1,0:T(8,128)(2,1)S(1)} %collective-permute-done.5.refs_6_) | copy-start | bytes 1179652
  147.6 9.7 %collective-permute-start.15 = (bf16[768,256]{1,0:T(8,128)(2,1)S(1)}, bf16[768,256]{1,0:T(8,128)(2,1)S(1)}, u32[]{:S(2)}, u32[]{:S(2)}) collective-permute-start(bf16[768,256]{1,0:T(8,128)(2,1)S(1)} %collective-permute-done.5.refs_6_), channel_id=1, source_target_pairs={{0,4},{4,8},{8,12},{12,16},{16,20},{20,24},{24,28},{28,32},{32,36}... | collective-permute-start | bytes 1179656 | tf_op jit(solution)/shard_map/ppermute | solution.py:33
  152.7 9.7 %collective-permute-start.17 = (bf16[768,256]{1,0:T(8,128)(2,1)S(1)}, bf16[768,256]{1,0:T(8,128)(2,1)}, u32[]{:S(2)}, u32[]{:S(2)}) collective-permute-start(bf16[768,256]{1,0:T(8,128)(2,1)S(1)} %collective-permute-done.13), channel_id=1, source_target_pairs={{0,4},{4,8},{8,12},{12,16},{16,20},{20,24},{24,28},{28,32},{32,36}... | collective-permute-start | bytes 1179656 | tf_op jit(solution)/shard_map/ppermute | solution.py:33
  157.4 11.0 %copy-start.12 = (bf16[768,256]{1,0:T(8,128)(2,1)}, bf16[768,256]{1,0:T(8,128)(2,1)S(1)}, u32[]{:S(2)}) copy-start(bf16[768,256]{1,0:T(8,128)(2,1)S(1)} %collective-permute-done.15.refs_9_) | copy-start | bytes 1179652
  157.4 10.2 %collective-permute-start.16 = (bf16[768,256]{1,0:T(8,128)(2,1)S(1)}, bf16[768,256]{1,0:T(8,128)(2,1)S(1)}, u32[]{:S(2)}, u32[]{:S(2)}) collective-permute-start(bf16[768,256]{1,0:T(8,128)(2,1)S(1)} %collective-permute-done.15.refs_9_), channel_id=1, source_target_pairs={{0,4},{4,8},{8,12},{12,16},{16,20},{20,24},{24,28},{28,32},{32,36}... | collective-permute-start | bytes 1179656 | tf_op jit(solution)/shard_map/ppermute | solution.py:33
  162.4 5.9 %collective-permute-start.18 = (bf16[1,768,256]{2,1,0:T(8,128)(2,1)}, bf16[1,768,256]{2,1,0:T(8,128)(2,1)}, u32[]{:S(2)}, u32[]{:S(2)}) collective-permute-start(bf16[1,768,256]{2,1,0:T(8,128)(2,1)} %bitcast.11), channel_id=1, source_target_pairs={{0,64},{64,0},{1,65},{65,1},{2,66},{66,2},{3,67},{67,3},{4,68},{68... | collective-permute-start | bytes 1179656 | tf_op jit(solution)/shard_map/ppermute | solution.py:185
  167.6 0.8 copy-start.13
  180.0 26.5 %copy-start.2 = (f32[64,192]{1,0:T(8,128)S(1)}, f32[64,192]{1,0:T(8,128)}, u32[]{:S(2)}) copy-start(f32[64,192]{1,0:T(8,128)} %fusion.2) | copy-start | bytes 147460
  180.0 26.6 %copy-start.6 = (f32[64]{0:T(128)S(1)}, f32[64]{0:T(128)}, u32[]{:S(2)}) copy-start(f32[64]{0:T(128)} %select_reduce_fusion.1) | copy-start | bytes 772

commit v10 on v9

--- a/solution.py
+++ b/solution.py
@@ -67,7 +67,7 @@
     loss = (jnp.log(total) + top - jnp.sum(got[:, 1], axis=0)) * mask
     sums = jnp.sum(jnp.where(here > 0, loss[None], 0.0), axis=1)
     token_loss = jnp.sum(jnp.where(outputs > 0, loss.reshape(zs, own), 0.0), axis=0)
-    part, token_loss = lax.optimization_barrier((jnp.concatenate([sums, counts]), token_loss))
+    part = jnp.concatenate([sums, counts])
     axes = ("x", "c", "y")
     whole = jnp.sum(to_all(part, axes, lax.axis_size(axes)), axis=0)
     mean = whole[:DOMAINS] / jnp.maximum(whole[DOMAINS:], 1.0)
@@ -163,7 +163,7 @@
     ys = lax.axis_size("y")
     core, z, y = (lax.axis_index(name) for name in ("c", "z", "y"))
     low = lax.axis_index(VOCAB) * weight.shape[1]
-    hidden, where, z, y, low = lax.optimization_barrier((hidden, jnp.stack([core, z]), z, y, low))
+    hidden, core, z, y, low = lax.optimization_barrier((hidden, core, z, y, low))
     mine = to_all(hidden.T, "y", ys).reshape(BLOCK, -1).T
     theirs = lax.ppermute(mine, "c", SWAP)
     weights = gathered_weight(weight)
@@ -176,8 +176,11 @@
             )
             ready = before_tail(targets.shape[0], z, y, domains, seq_len)
             wanted = (targets - low)[:, None]
+            where = jnp.where(lax.iota(jnp.int32, 2) == 0, core, z)
         if r == 4:
-            own[4], ready, wanted = lax.optimization_barrier((own[4], ready, wanted))
+            own[4], ready, wanted, where = lax.optimization_barrier(
+                (own[4], ready, wanted, where)
+            )
         if r < ROUNDS:
             other.append(along_z(other[-1]))
     swapped = []

time: 224 us -> 224 us (level)
  blocking collectives: 51 us -> 35.7 us
  starting transfers between devices: 104 us -> 112 us
  waiting for transfers between devices: 45 us -> 51.4 us
    all_to_all x2 -> x1, blocking collectives: 26.4 us -> 11 us  [to_all(): lax.all_to_all(jnp.broadcast_to(array[None], (copies, *array.shape)), axi...]
    all_to_all x1 -> x2, starting transfers between devices: 5.13 us -> 13.7 us  [to_all(): lax.all_to_all(jnp.broadcast_to(array[None], (copies, *array.shape)), axi...]
    all_to_all x1 -> x2, waiting for transfers between devices: 37.3 us -> 43.7 us  [to_all(): lax.all_to_all(jnp.broadcast_to(array[None], (copies, *array.shape)), axi...]
  transfers between devices with their start and end apart: 21 -> 22, of which waited for: 9 -> 10; matrix products, arithmetic and copies ran while one was open for 1% -> 2% of each run, Pallas kernels for 0% -> 0%
where the time goes in v10:
time: 224 us; the launch traced here: 223 us
  starting transfers between devices  112 us (50%)
  waiting for transfers between devices  51.4 us (23%)
  blocking collectives  35.7 us (16%)
  Pallas kernels  11.7 us (5%)
  local copies, waits for them, and re-layouts  6.96 us (3%)
  other arithmetic  4.06 us (2%)
    ppermute x15, starting transfers between devices, along_z(): return lax.ppermute(array, ('c', 'z'), pairs)  70.7 us
    all_to_all x2, waiting for transfers between devices, to_all(): lax.all_to_all(jnp.broadcast_to(array[None], (copies, *array.shape)), axi...  43.7 us
    all_to_all x1, blocking collectives, tail(): got = lax.all_to_all(send.reshape(zs * ys, -1), VOCAB, 0, 0, tiled=True)  24.7 us
    all_to_all x2, starting transfers between devices, to_all(): lax.all_to_all(jnp.broadcast_to(array[None], (copies, *array.shape)), axi...  13.7 us
    ppermute x3, starting transfers between devices, loss(): swapped.append(lax.ppermute(jnp.stack([other[r] for r in some]), 'c', SWAP))  12.8 us
    pallas_call x1, Pallas kernels, product(): pl.pallas_call(product_kernel(kinds, away), in_specs=[pl.BlockSpec(memory...  11.7 us
    all_to_all x1, blocking collectives, to_all(): lax.all_to_all(jnp.broadcast_to(array[None], (copies, *array.shape)), axi...  11 us
    ppermute x1, starting transfers between devices, gathered_weight(): return (own, lax.ppermute(own, 'c', SWAP))  7.55 us
  transfers between devices with their start and end apart: 22, of which 10 were waited for; matrix products, arithmetic and copies ran while one was open for 2% of the time, Pallas kernels for 0%

profile of v10, /device:TPU:1, one launch (start us, length us, event | category | flops | bytes accessed | tf_op | source)
XLA Modules:
  0.0 223.0 jit_solution(260225263228852690)
XLA Ops:
  0.6 1.0 broadcast_in_dim.69
  1.7 11.0 %all_to_all.25 = bf16[4,64,768]{2,1,0:T(8,128)(2,1)S(1)} all-to-all(bf16[4,64,768]{2,1,0:T(8,128)(2,1)S(1)} %broadcast_in_dim.69), channel_id=1, replica_groups=mesh['x'=4,'c'=2,'z'=16,'y'=4] {'y'}, dimensions={0} | all-to-all | bytes 786432 | tf_op jit(solution)/shard_map/all_to_all | solution.py:25
  12.7 2.5 %broadcast_in_dim.76 = bf16[4,512,1024]{2,1,0:T(8,128)(2,1)} broadcast(bf16[512,1024]{1,0:T(8,128)(2,1)S(1)} %copy-done), dimensions={1,2} | broadcast | bytes 5242880 | tf_op jit(solution)/shard_map/broadcast_in_dim | solution.py:26
  15.2 5.1 %all-to-all-start.1 = ((bf16[4,512,1024]{2,1,0:T(8,128)(2,1)}), bf16[4,512,1024]{2,1,0:T(8,128)(2,1)}, u32[]{:S(2)}, u32[]{:S(2)}) async-start(bf16[4,512,1024]{2,1,0:T(8,128)(2,1)} %broadcast_in_dim.76), calls=%async_computation.1 | async-start | bytes 8388608 | tf_op jit(solution)/shard_map/all_to_all | solution.py:25
  20.4 0.2 copy.17
  20.5 7.3 %collective-permute-start.6 = (bf16[768,256]{1,0:T(8,128)(2,1)S(1)}, bf16[768,256]{1,0:T(8,128)(2,1)S(1)}, u32[]{:S(2)}, u32[]{:S(2)}) collective-permute-start(bf16[768,256]{1,0:T(8,128)(2,1)S(1)} %bitcast.27), channel_id=1, source_target_pairs={{0,64},{64,0},{1,65},{65,1},{2,66},{66,2},{3,67},{67,3},{4,68},{68... | collective-permute-start | bytes 1179656 | tf_op jit(solution)/shard_map/ppermute | solution.py:168
  27.9 37.3 %all-to-all-done.1.refs_12_ = bf16[4,512,1024]{2,1,0:T(8,128)(2,1)} async-done(((bf16[4,512,1024]{2,1,0:T(8,128)(2,1)}), bf16[4,512,1024]{2,1,0:T(8,128)(2,1)}, u32[]{:S(2)}, u32[]{:S(2)}) %all-to-all-start.1) | async-done | bytes 4194336 | tf_op jit(solution)/shard_map/all_to_all | solution.py:25
  65.1 7.5 %collective-permute-start.19 = (bf16[4,512,1024]{2,1,0:T(8,128)(2,1)}, bf16[4,512,1024]{2,1,0:T(8,128)(2,1)}, u32[]{:S(2)}, u32[]{:S(2)}) collective-permute-start(bf16[4,512,1024]{2,1,0:T(8,128)(2,1)} %all-to-all-done.1.refs_12_), channel_id=1, source_target_pairs={{0,64},{64,0},{1,65},{65,1},{2,66},{66,2},{3,67},{67,3},{4,68},{68... | collective-permute-start | bytes 12582920 | tf_op jit(solution)/shard_map/ppermute | solution.py:38
  72.7 11.3 %collective-permute-start.7 = (bf16[768,256]{1,0:T(8,128)(2,1)S(1)}, bf16[768,256]{1,0:T(8,128)(2,1)S(1)}, u32[]{:S(2)}, u32[]{:S(2)}) collective-permute-start(bf16[768,256]{1,0:T(8,128)(2,1)S(1)} %collective-permute-done.6), channel_id=1, source_target_pairs={{0,4},{4,8},{8,12},{12,16},{16,20},{20,24},{24,28},{28,32},{32,36}... | collective-permute-start | bytes 1179656 | tf_op jit(solution)/shard_map/ppermute | solution.py:33
  84.0 2.6 %collective-permute-start = (bf16[768,256]{1,0:T(8,128)(2,1)S(1)}, bf16[768,256]{1,0:T(8,128)(2,1)S(1)}, u32[]{:S(2)}, u32[]{:S(2)}) collective-permute-start(bf16[768,256]{1,0:T(8,128)(2,1)S(1)} %bitcast.28), channel_id=1, source_target_pairs={{0,4},{4,8},{8,12},{12,16},{16,20},{20,24},{24,28},{28,32},{32,36}... | collective-permute-start | bytes 1179656 | tf_op jit(solution)/shard_map/ppermute | solution.py:33
  86.7 2.1 collective-permute-done.7
  88.7 5.0 %collective-permute-start.8 = (bf16[768,256]{1,0:T(8,128)(2,1)S(1)}, bf16[768,256]{1,0:T(8,128)(2,1)S(1)}, u32[]{:S(2)}, u32[]{:S(2)}) collective-permute-start(bf16[768,256]{1,0:T(8,128)(2,1)S(1)} %collective-permute-done.7), channel_id=1, source_target_pairs={{0,4},{4,8},{8,12},{12,16},{16,20},{20,24},{24,28},{28,32},{32,36}... | collective-permute-start | bytes 1179656 | tf_op jit(solution)/shard_map/ppermute | solution.py:33
  93.8 4.2 %collective-permute-start.1 = (bf16[768,256]{1,0:T(8,128)(2,1)S(1)}, bf16[768,256]{1,0:T(8,128)(2,1)S(1)}, u32[]{:S(2)}, u32[]{:S(2)}) collective-permute-start(bf16[768,256]{1,0:T(8,128)(2,1)S(1)} %collective-permute-done.refs_1_), channel_id=1, source_target_pairs={{0,4},{4,8},{8,12},{12,16},{16,20},{20,24},{24,28},{28,32},{32,36}... | collective-permute-start | bytes 1179656 | tf_op jit(solution)/shard_map/ppermute | solution.py:33
  98.0 0.5 collective-permute-done.8
  98.5 5.0 %collective-permute-start.9 = (bf16[768,256]{1,0:T(8,128)(2,1)S(1)}, bf16[768,256]{1,0:T(8,128)(2,1)S(1)}, u32[]{:S(2)}, u32[]{:S(2)}) collective-permute-start(bf16[768,256]{1,0:T(8,128)(2,1)S(1)} %collective-permute-done.8), channel_id=1, source_target_pairs={{0,4},{4,8},{8,12},{12,16},{16,20},{20,24},{24,28},{28,32},{32,36}... | collective-permute-start | bytes 1179656 | tf_op jit(solution)/shard_map/ppermute | solution.py:33
  103.5 0.5 compare_select_fusion.where
  104.0 3.6 %collective-permute-start.2 = (bf16[768,256]{1,0:T(8,128)(2,1)S(1)}, bf16[768,256]{1,0:T(8,128)(2,1)S(1)}, u32[]{:S(2)}, u32[]{:S(2)}) collective-permute-start(bf16[768,256]{1,0:T(8,128)(2,1)S(1)} %collective-permute-done.1.refs_2_), channel_id=1, source_target_pairs={{0,4},{4,8},{8,12},{12,16},{16,20},{20,24},{24,28},{28,32},{32,36}... | collective-permute-start | bytes 1179656 | tf_op jit(solution)/shard_map/ppermute | solution.py:33
  107.7 0.1 reshape.109
  107.8 0.1 select_reduce_fusion.4
  107.9 0.3 collective-permute-done.9
  108.2 5.0 %collective-permute-start.11 = (bf16[768,256]{1,0:T(8,128)(2,1)S(1)}, bf16[768,256]{1,0:T(8,128)(2,1)S(1)}, u32[]{:S(2)}, u32[]{:S(2)}) collective-permute-start(bf16[768,256]{1,0:T(8,128)(2,1)S(1)} %collective-permute-done.9), channel_id=1, source_target_pairs={{0,4},{4,8},{8,12},{12,16},{16,20},{20,24},{24,28},{28,32},{32,36}... | collective-permute-start | bytes 1179656 | tf_op jit(solution)/shard_map/ppermute | solution.py:33
  113.3 4.1 %collective-permute-start.3 = (bf16[768,256]{1,0:T(8,128)(2,1)S(1)}, bf16[768,256]{1,0:T(8,128)(2,1)}, u32[]{:S(2)}, u32[]{:S(2)}) collective-permute-start(bf16[768,256]{1,0:T(8,128)(2,1)S(1)} %collective-permute-done.2.refs_3_), channel_id=1, source_target_pairs={{0,4},{4,8},{8,12},{12,16},{16,20},{20,24},{24,28},{28,32},{32,36}... | collective-permute-start | bytes 1179656 | tf_op jit(solution)/shard_map/ppermute | solution.py:33
  117.4 0.5 collective-permute-done.11
  117.9 5.0 %collective-permute-start.12 = (bf16[768,256]{1,0:T(8,128)(2,1)S(1)}, bf16[768,256]{1,0:T(8,128)(2,1)S(1)}, u32[]{:S(2)}, u32[]{:S(2)}) collective-permute-start(bf16[768,256]{1,0:T(8,128)(2,1)S(1)} %collective-permute-done.11), channel_id=1, source_target_pairs={{0,4},{4,8},{8,12},{12,16},{16,20},{20,24},{24,28},{28,32},{32,36}... | collective-permute-start | bytes 1179656 | tf_op jit(solution)/shard_map/ppermute | solution.py:33
  122.9 0.1 select_reduce_fusion.2
  123.0 0.1 eq.42
  123.1 0.6 select_reduce_fusion.1
  123.7 0.6 fusion.2
  124.4 0.1 iota.40
  124.5 2.9 %collective-permute-start.4 = (bf16[768,256]{1,0:T(8,128)(2,1)}, bf16[768,256]{1,0:T(8,128)(2,1)S(1)}, u32[]{:S(2)}, u32[]{:S(2)}) collective-permute-start(bf16[768,256]{1,0:T(8,128)(2,1)} %collective-permute-done.3.refs_4_), channel_id=1, source_target_pairs={{0,4},{4,8},{8,12},{12,16},{16,20},{20,24},{24,28},{28,32},{32,36}... | collective-permute-start | bytes 1179656 | tf_op jit(solution)/shard_map/ppermute | solution.py:33
  127.3 0.3 collective-permute-done.12
  127.6 5.0 %collective-permute-start.13 = (bf16[768,256]{1,0:T(8,128)(2,1)S(1)}, bf16[768,256]{1,0:T(8,128)(2,1)S(1)}, u32[]{:S(2)}, u32[]{:S(2)}) collective-permute-start(bf16[768,256]{1,0:T(8,128)(2,1)S(1)} %collective-permute-done.12), channel_id=1, source_target_pairs={{0,4},{4,8},{8,12},{12,16},{16,20},{20,24},{24,28},{28,32},{32,36}... | collective-permute-start | bytes 1179656 | tf_op jit(solution)/shard_map/ppermute | solution.py:33
  132.7 0.1 pad_maximum_fusion
  132.8 4.7 %collective-permute-start.10 = (bf16[3,768,256]{2,1,0:T(8,128)(2,1)S(1)}, bf16[3,768,256]{2,1,0:T(8,128)(2,1)}, u32[]{:S(2)}, u32[]{:S(2)}) collective-permute-start(bf16[3,768,256]{2,1,0:T(8,128)(2,1)S(1)} %pad_maximum_fusion), channel_id=1, source_target_pairs={{0,64},{64,0},{1,65},{65,1},{2,66},{66,2},{3,67},{67,3},{4,68},{68... | collective-permute-start | bytes 3538952 | tf_op jit(solution)/shard_map/ppermute | solution.py:188
  137.6 4.9 %collective-permute-start.5 = (bf16[768,256]{1,0:T(8,128)(2,1)S(1)}, bf16[768,256]{1,0:T(8,128)(2,1)S(1)}, u32[]{:S(2)}, u32[]{:S(2)}) collective-permute-start(bf16[768,256]{1,0:T(8,128)(2,1)S(1)} %collective-permute-done.4.refs_5_), channel_id=1, source_target_pairs={{0,4},{4,8},{8,12},{12,16},{16,20},{20,24},{24,28},{28,32},{32,36}... | collective-permute-start | bytes 1179656 | tf_op jit(solution)/shard_map/ppermute | solution.py:33
  142.4 0.1 pad_maximum_fusion.1
  142.6 3.9 %collective-permute-start.14 = (bf16[3,768,256]{2,1,0:T(8,128)(2,1)S(1)}, bf16[3,768,256]{2,1,0:T(8,128)(2,1)}, u32[]{:S(2)}, u32[]{:S(2)}) collective-permute-start(bf16[3,768,256]{2,1,0:T(8,128)(2,1)S(1)} %pad_maximum_fusion.1), channel_id=1, source_target_pairs={{0,64},{64,0},{1,65},{65,1},{2,66},{66,2},{3,67},{67,3},{4,68},{68... | collective-permute-start | bytes 3538952 | tf_op jit(solution)/shard_map/ppermute | solution.py:188
  146.5 0.7 collective-permute-done.5.refs_6_
  147.1 5.0 %collective-permute-start.15 = (bf16[768,256]{1,0:T(8,128)(2,1)S(1)}, bf16[768,256]{1,0:T(8,128)(2,1)S(1)}, u32[]{:S(2)}, u32[]{:S(2)}) collective-permute-start(bf16[768,256]{1,0:T(8,128)(2,1)S(1)} %collective-permute-done.5.refs_6_), channel_id=1, source_target_pairs={{0,4},{4,8},{8,12},{12,16},{16,20},{20,24},{24,28},{28,32},{32,36}... | collective-permute-start | bytes 1179656 | tf_op jit(solution)/shard_map/ppermute | solution.py:33
  152.2 1.9 collective-permute-start.17
  154.1 2.8 %collective-permute-done.15.refs_9_ = bf16[768,256]{1,0:T(8,128)(2,1)S(1)} collective-permute-done((bf16[768,256]{1,0:T(8,128)(2,1)S(1)}, bf16[768,256]{1,0:T(8,128)(2,1)S(1)}, u32[]{:S(2)}, u32[]{:S(2)}) %collective-permute-start.15) | collective-permute-done | bytes 393248 | tf_op jit(solution)/shard_map/ppermute | solution.py:33
  156.9 5.0 %collective-permute-start.16 = (bf16[768,256]{1,0:T(8,128)(2,1)S(1)}, bf16[768,256]{1,0:T(8,128)(2,1)S(1)}, u32[]{:S(2)}, u32[]{:S(2)}) collective-permute-start(bf16[768,256]{1,0:T(8,128)(2,1)S(1)} %collective-permute-done.15.refs_9_), channel_id=1, source_target_pairs={{0,4},{4,8},{8,12},{12,16},{16,20},{20,24},{24,28},{28,32},{32,36}... | collective-permute-start | bytes 1179656 | tf_op jit(solution)/shard_map/ppermute | solution.py:33
  161.9 4.2 %collective-permute-start.18 = (bf16[1,768,256]{2,1,0:T(8,128)(2,1)}, bf16[1,768,256]{2,1,0:T(8,128)(2,1)}, u32[]{:S(2)}, u32[]{:S(2)}) collective-permute-start(bf16[1,768,256]{2,1,0:T(8,128)(2,1)} %bitcast.9), channel_id=1, source_target_pairs={{0,64},{64,0},{1,65},{65,1},{2,66},{66,2},{3,67},{67,3},{4,68},{68... | collective-permute-start | bytes 1179656 | tf_op jit(solution)/shard_map/ppermute | solution.py:188
  166.1 1.0 copy.18.refs_14_
  167.1 0.7 collective-permute-done.18.refs_11_
  167.8 0.1 copy-done.13
  167.9 11.7 %shard_map.68 = f32[2,768]{1,0:T(2,128)} custom-call(s32[2]{0:T(128)} %compare_select_fusion.where, bf16[768,256]{1,0:T(8,128)(2,1)} %bitcast.29, bf16[768,256]{1,0:T(8,128)(2,1)} %copy-done.7, bf16[768,256]{1,0:T(8,128)(2,1)} %copy-done.8, bf16[768,256]{1,0:T(8,128)(2,1)} %copy-done.9, bf16[768,256]{1,0:T(8,128)(2,1)} %collective-permute-done.3.refs_4_, ...), custom_call_target="tpu_custom_call" | custom-call | flops 6442450944 | bytes 14680064 | tf_op jit(solution)/shard_map/pallas_call | solution.py:142
  179.5 0.0 copy-start.6
  179.6 0.8 reshape.110
  180.4 0.1 broadcast_in_dim.77
  180.6 0.1 all_to_all.18
  180.7 24.7 %all_to_all.26 = f32[64,1,384]{2,1,0:T(1,128)S(1)} all-to-all(f32[64,1,384]{2,1,0:T(1,128)S(1)} %all_to_all.18), channel_id=1, replica_groups=mesh['x'=4,'c'=2,'z'=16,'y'=4] {'z','y'}, dimensions={0} | all-to-all | bytes 196608 | tf_op jit(solution)/shard_map/all_to_all | solution.py:63
  205.3 0.2 reduce.3
  205.6 0.1 reshape.111
  205.7 0.2 slice_reduce_fusion.1
  205.9 0.1 reshape.112
  206.0 0.0 copy-done.2
  206.0 0.1 select_reduce_fusion
  206.2 0.1 pad_maximum_fusion.2
  206.2 0.6 broadcast_in_dim.80
  206.8 8.6 %all-to-all-start.3 = ((f32[32,1,128]{2,1,0:T(1,128)}), f32[32,1,128]{2,1,0:T(1,128)S(1)}, u32[]{:S(2)}, u32[]{:S(2)}) async-start(f32[32,1,128]{2,1,0:T(1,128)} %broadcast_in_dim.80), calls=%async_computation.3 | async-start | bytes 32768 | tf_op jit(solution)/shard_map/all_to_all | solution.py:25
  215.4 0.5 select_reduce_fusion.3
  216.0 6.4 %all-to-all-done.3 = f32[32,1,128]{2,1,0:T(1,128)S(1)} async-done(((f32[32,1,128]{2,1,0:T(1,128)}), f32[32,1,128]{2,1,0:T(1,128)S(1)}, u32[]{:S(2)}, u32[]{:S(2)}) %all-to-all-start.3) | async-done | bytes 16416 | tf_op jit(solution)/shard_map/all_to_all | solution.py:25
  222.4 0.6 maximum_divide_fusion
  (48 shorter events, 0.2 us)
Async XLA Ops:
  0.6 12.1 %copy-start = (bf16[512,1024]{1,0:T(8,128)(2,1)S(1)}, bf16[512,1024]{1,0:T(8,128)(2,1)}, u32[]{:S(2)}) copy-start(bf16[512,1024]{1,0:T(8,128)(2,1)} %param.6) | copy-start | bytes 3145732
  15.2 92.5 %copy-start.3 = (s32[768]{0:T(1024)S(1)}, s32[768]{0:T(1024)}, u32[]{:S(2)}) copy-start(s32[768]{0:T(1024)} %param.8) | copy-start | bytes 9220
  15.2 92.6 %copy-start.5 = (s32[6]{0:T(128)S(1)}, s32[6]{0:T(128)}, u32[]{:S(2)}) copy-start(s32[6]{0:T(128)} %param.9) | copy-start | bytes 76
  15.2 98.0 %copy-start.4 = (s32[768]{0:T(1024)S(1)}, s32[768]{0:T(1024)}, u32[]{:S(2)}) copy-start(s32[768]{0:T(1024)} %param.7) | copy-start | bytes 9220
  15.2 49.9 %all-to-all-start.1 = ((bf16[4,512,1024]{2,1,0:T(8,128)(2,1)}), bf16[4,512,1024]{2,1,0:T(8,128)(2,1)}, u32[]{:S(2)}, u32[]{:S(2)}) async-start(bf16[4,512,1024]{2,1,0:T(8,128)(2,1)} %broadcast_in_dim.76), calls=%async_computation.1 | async-start | bytes 8388608 | tf_op jit(solution)/shard_map/all_to_all | solution.py:25
  20.5 112.3 %copy-start.1 = (bf16[256,768]{0,1:T(8,128)(2,1)}, bf16[256,768]{0,1:T(8,128)(2,1)S(1)}, u32[]{:S(2)}) copy-start(bf16[256,768]{0,1:T(8,128)(2,1)S(1)} %copy.17) | copy-start | bytes 1179652
  20.5 52.2 %collective-permute-start.6 = (bf16[768,256]{1,0:T(8,128)(2,1)S(1)}, bf16[768,256]{1,0:T(8,128)(2,1)S(1)}, u32[]{:S(2)}, u32[]{:S(2)}) collective-permute-start(bf16[768,256]{1,0:T(8,128)(2,1)S(1)} %bitcast.27), channel_id=1, source_target_pairs={{0,64},{64,0},{1,65},{65,1},{2,66},{66,2},{3,67},{67,3},{4,68},{68... | collective-permute-start | bytes 1179656 | tf_op jit(solution)/shard_map/ppermute | solution.py:168
  65.1 102.7 %collective-permute-start.19 = (bf16[4,512,1024]{2,1,0:T(8,128)(2,1)}, bf16[4,512,1024]{2,1,0:T(8,128)(2,1)}, u32[]{:S(2)}, u32[]{:S(2)}) collective-permute-start(bf16[4,512,1024]{2,1,0:T(8,128)(2,1)} %all-to-all-done.1.refs_12_), channel_id=1, source_target_pairs={{0,64},{64,0},{1,65},{65,1},{2,66},{66,2},{3,67},{67,3},{4,68},{68... | collective-permute-start | bytes 12582920 | tf_op jit(solution)/shard_map/ppermute | solution.py:38
  72.7 16.0 %collective-permute-start.7 = (bf16[768,256]{1,0:T(8,128)(2,1)S(1)}, bf16[768,256]{1,0:T(8,128)(2,1)S(1)}, u32[]{:S(2)}, u32[]{:S(2)}) collective-permute-start(bf16[768,256]{1,0:T(8,128)(2,1)S(1)} %collective-permute-done.6), channel_id=1, source_target_pairs={{0,4},{4,8},{8,12},{12,16},{16,20},{20,24},{24,28},{28,32},{32,36}... | collective-permute-start | bytes 1179656 | tf_op jit(solution)/shard_map/ppermute | solution.py:33
  84.0 9.7 %collective-permute-start = (bf16[768,256]{1,0:T(8,128)(2,1)S(1)}, bf16[768,256]{1,0:T(8,128)(2,1)S(1)}, u32[]{:S(2)}, u32[]{:S(2)}) collective-permute-start(bf16[768,256]{1,0:T(8,128)(2,1)S(1)} %bitcast.28), channel_id=1, source_target_pairs={{0,4},{4,8},{8,12},{12,16},{16,20},{20,24},{24,28},{28,32},{32,36}... | collective-permute-start | bytes 1179656 | tf_op jit(solution)/shard_map/ppermute | solution.py:33
  88.7 9.7 %collective-permute-start.8 = (bf16[768,256]{1,0:T(8,128)(2,1)S(1)}, bf16[768,256]{1,0:T(8,128)(2,1)S(1)}, u32[]{:S(2)}, u32[]{:S(2)}) collective-permute-start(bf16[768,256]{1,0:T(8,128)(2,1)S(1)} %collective-permute-done.7), channel_id=1, source_target_pairs={{0,4},{4,8},{8,12},{12,16},{16,20},{20,24},{24,28},{28,32},{32,36}... | collective-permute-start | bytes 1179656 | tf_op jit(solution)/shard_map/ppermute | solution.py:33
  93.8 14.1 %copy-start.7 = (bf16[768,256]{1,0:T(8,128)(2,1)}, bf16[768,256]{1,0:T(8,128)(2,1)S(1)}, u32[]{:S(2)}) copy-start(bf16[768,256]{1,0:T(8,128)(2,1)S(1)} %collective-permute-done.refs_1_) | copy-start | bytes 1179652
  93.8 10.3 %collective-permute-start.1 = (bf16[768,256]{1,0:T(8,128)(2,1)S(1)}, bf16[768,256]{1,0:T(8,128)(2,1)S(1)}, u32[]{:S(2)}, u32[]{:S(2)}) collective-permute-start(bf16[768,256]{1,0:T(8,128)(2,1)S(1)} %collective-permute-done.refs_1_), channel_id=1, source_target_pairs={{0,4},{4,8},{8,12},{12,16},{16,20},{20,24},{24,28},{28,32},{32,36}... | collective-permute-start | bytes 1179656 | tf_op jit(solution)/shard_map/ppermute | solution.py:33
  98.5 9.7 %collective-permute-start.9 = (bf16[768,256]{1,0:T(8,128)(2,1)S(1)}, bf16[768,256]{1,0:T(8,128)(2,1)S(1)}, u32[]{:S(2)}, u32[]{:S(2)}) collective-permute-start(bf16[768,256]{1,0:T(8,128)(2,1)S(1)} %collective-permute-done.8), channel_id=1, source_target_pairs={{0,4},{4,8},{8,12},{12,16},{16,20},{20,24},{24,28},{28,32},{32,36}... | collective-permute-start | bytes 1179656 | tf_op jit(solution)/shard_map/ppermute | solution.py:33
  104.0 28.6 %copy-start.8 = (bf16[768,256]{1,0:T(8,128)(2,1)}, bf16[768,256]{1,0:T(8,128)(2,1)S(1)}, u32[]{:S(2)}) copy-start(bf16[768,256]{1,0:T(8,128)(2,1)S(1)} %collective-permute-done.1.refs_2_) | copy-start | bytes 1179652
  104.0 9.2 %collective-permute-start.2 = (bf16[768,256]{1,0:T(8,128)(2,1)S(1)}, bf16[768,256]{1,0:T(8,128)(2,1)S(1)}, u32[]{:S(2)}, u32[]{:S(2)}) collective-permute-start(bf16[768,256]{1,0:T(8,128)(2,1)S(1)} %collective-permute-done.1.refs_2_), channel_id=1, source_target_pairs={{0,4},{4,8},{8,12},{12,16},{16,20},{20,24},{24,28},{28,32},{32,36}... | collective-permute-start | bytes 1179656 | tf_op jit(solution)/shard_map/ppermute | solution.py:33
  108.2 9.7 %collective-permute-start.11 = (bf16[768,256]{1,0:T(8,128)(2,1)S(1)}, bf16[768,256]{1,0:T(8,128)(2,1)S(1)}, u32[]{:S(2)}, u32[]{:S(2)}) collective-permute-start(bf16[768,256]{1,0:T(8,128)(2,1)S(1)} %collective-permute-done.9), channel_id=1, source_target_pairs={{0,4},{4,8},{8,12},{12,16},{16,20},{20,24},{24,28},{28,32},{32,36}... | collective-permute-start | bytes 1179656 | tf_op jit(solution)/shard_map/ppermute | solution.py:33
  113.3 19.4 %copy-start.9 = (bf16[768,256]{1,0:T(8,128)(2,1)}, bf16[768,256]{1,0:T(8,128)(2,1)S(1)}, u32[]{:S(2)}) copy-start(bf16[768,256]{1,0:T(8,128)(2,1)S(1)} %collective-permute-done.2.refs_3_) | copy-start | bytes 1179652
  113.3 11.1 %collective-permute-start.3 = (bf16[768,256]{1,0:T(8,128)(2,1)S(1)}, bf16[768,256]{1,0:T(8,128)(2,1)}, u32[]{:S(2)}, u32[]{:S(2)}) collective-permute-start(bf16[768,256]{1,0:T(8,128)(2,1)S(1)} %collective-permute-done.2.refs_3_), channel_id=1, source_target_pairs={{0,4},{4,8},{8,12},{12,16},{16,20},{20,24},{24,28},{28,32},{32,36}... | collective-permute-start | bytes 1179656 | tf_op jit(solution)/shard_map/ppermute | solution.py:33
  117.9 9.7 %collective-permute-start.12 = (bf16[768,256]{1,0:T(8,128)(2,1)S(1)}, bf16[768,256]{1,0:T(8,128)(2,1)S(1)}, u32[]{:S(2)}, u32[]{:S(2)}) collective-permute-start(bf16[768,256]{1,0:T(8,128)(2,1)S(1)} %collective-permute-done.11), channel_id=1, source_target_pairs={{0,4},{4,8},{8,12},{12,16},{16,20},{20,24},{24,28},{28,32},{32,36}... | collective-permute-start | bytes 1179656 | tf_op jit(solution)/shard_map/ppermute | solution.py:33
  124.5 13.1 %collective-permute-start.4 = (bf16[768,256]{1,0:T(8,128)(2,1)}, bf16[768,256]{1,0:T(8,128)(2,1)S(1)}, u32[]{:S(2)}, u32[]{:S(2)}) collective-permute-start(bf16[768,256]{1,0:T(8,128)(2,1)} %collective-permute-done.3.refs_4_), channel_id=1, source_target_pairs={{0,4},{4,8},{8,12},{12,16},{16,20},{20,24},{24,28},{28,32},{32,36}... | collective-permute-start | bytes 1179656 | tf_op jit(solution)/shard_map/ppermute | solution.py:33
  127.6 14.8 %collective-permute-start.13 = (bf16[768,256]{1,0:T(8,128)(2,1)S(1)}, bf16[768,256]{1,0:T(8,128)(2,1)S(1)}, u32[]{:S(2)}, u32[]{:S(2)}) collective-permute-start(bf16[768,256]{1,0:T(8,128)(2,1)S(1)} %collective-permute-done.12), channel_id=1, source_target_pairs={{0,4},{4,8},{8,12},{12,16},{16,20},{20,24},{24,28},{28,32},{32,36}... | collective-permute-start | bytes 1179656 | tf_op jit(solution)/shard_map/ppermute | solution.py:33
  132.8 34.3 %collective-permute-start.10 = (bf16[3,768,256]{2,1,0:T(8,128)(2,1)S(1)}, bf16[3,768,256]{2,1,0:T(8,128)(2,1)}, u32[]{:S(2)}, u32[]{:S(2)}) collective-permute-start(bf16[3,768,256]{2,1,0:T(8,128)(2,1)S(1)} %pad_maximum_fusion), channel_id=1, source_target_pairs={{0,64},{64,0},{1,65},{65,1},{2,66},{66,2},{3,67},{67,3},{4,68},{68... | collective-permute-start | bytes 3538952 | tf_op jit(solution)/shard_map/ppermute | solution.py:188
  137.6 5.0 %copy-start.10 = (bf16[768,256]{1,0:T(8,128)(2,1)}, bf16[768,256]{1,0:T(8,128)(2,1)S(1)}, u32[]{:S(2)}) copy-start(bf16[768,256]{1,0:T(8,128)(2,1)S(1)} %collective-permute-done.4.refs_5_) | copy-start | bytes 1179652
  137.6 9.6 %collective-permute-start.5 = (bf16[768,256]{1,0:T(8,128)(2,1)S(1)}, bf16[768,256]{1,0:T(8,128)(2,1)S(1)}, u32[]{:S(2)}, u32[]{:S(2)}) collective-permute-start(bf16[768,256]{1,0:T(8,128)(2,1)S(1)} %collective-permute-done.4.refs_5_), channel_id=1, source_target_pairs={{0,4},{4,8},{8,12},{12,16},{16,20},{20,24},{24,28},{28,32},{32,36}... | collective-permute-start | bytes 1179656 | tf_op jit(solution)/shard_map/ppermute | solution.py:33
  142.6 25.2 %collective-permute-start.14 = (bf16[3,768,256]{2,1,0:T(8,128)(2,1)S(1)}, bf16[3,768,256]{2,1,0:T(8,128)(2,1)}, u32[]{:S(2)}, u32[]{:S(2)}) collective-permute-start(bf16[3,768,256]{2,1,0:T(8,128)(2,1)S(1)} %pad_maximum_fusion.1), channel_id=1, source_target_pairs={{0,64},{64,0},{1,65},{65,1},{2,66},{66,2},{3,67},{67,3},{4,68},{68... | collective-permute-start | bytes 3538952 | tf_op jit(solution)/shard_map/ppermute | solution.py:188
  147.1 20.7 %copy-start.11 = (bf16[768,256]{1,0:T(8,128)(2,1)}, bf16[768,256]{1,0:T(8,128)(2,1)S(1)}, u32[]{:S(2)}) copy-start(bf16[768,256]{1,0:T(8,128)(2,1)S(1)} %collective-permute-done.5.refs_6_) | copy-start | bytes 1179652
  147.1 9.7 %collective-permute-start.15 = (bf16[768,256]{1,0:T(8,128)(2,1)S(1)}, bf16[768,256]{1,0:T(8,128)(2,1)S(1)}, u32[]{:S(2)}, u32[]{:S(2)}) collective-permute-start(bf16[768,256]{1,0:T(8,128)(2,1)S(1)} %collective-permute-done.5.refs_6_), channel_id=1, source_target_pairs={{0,4},{4,8},{8,12},{12,16},{16,20},{20,24},{24,28},{28,32},{32,36}... | collective-permute-start | bytes 1179656 | tf_op jit(solution)/shard_map/ppermute | solution.py:33
  152.2 9.7 %collective-permute-start.17 = (bf16[768,256]{1,0:T(8,128)(2,1)S(1)}, bf16[768,256]{1,0:T(8,128)(2,1)}, u32[]{:S(2)}, u32[]{:S(2)}) collective-permute-start(bf16[768,256]{1,0:T(8,128)(2,1)S(1)} %collective-permute-done.13), channel_id=1, source_target_pairs={{0,4},{4,8},{8,12},{12,16},{16,20},{20,24},{24,28},{28,32},{32,36}... | collective-permute-start | bytes 1179656 | tf_op jit(solution)/shard_map/ppermute | solution.py:33
  156.9 11.0 %copy-start.12 = (bf16[768,256]{1,0:T(8,128)(2,1)}, bf16[768,256]{1,0:T(8,128)(2,1)S(1)}, u32[]{:S(2)}) copy-start(bf16[768,256]{1,0:T(8,128)(2,1)S(1)} %collective-permute-done.15.refs_9_) | copy-start | bytes 1179652
  156.9 10.2 %collective-permute-start.16 = (bf16[768,256]{1,0:T(8,128)(2,1)S(1)}, bf16[768,256]{1,0:T(8,128)(2,1)S(1)}, u32[]{:S(2)}, u32[]{:S(2)}) collective-permute-start(bf16[768,256]{1,0:T(8,128)(2,1)S(1)} %collective-permute-done.15.refs_9_), channel_id=1, source_target_pairs={{0,4},{4,8},{8,12},{12,16},{16,20},{20,24},{24,28},{28,32},{32,36}... | collective-permute-start | bytes 1179656 | tf_op jit(solution)/shard_map/ppermute | solution.py:33
  161.9 5.9 %collective-permute-start.18 = (bf16[1,768,256]{2,1,0:T(8,128)(2,1)}, bf16[1,768,256]{2,1,0:T(8,128)(2,1)}, u32[]{:S(2)}, u32[]{:S(2)}) collective-permute-start(bf16[1,768,256]{2,1,0:T(8,128)(2,1)} %bitcast.9), channel_id=1, source_target_pairs={{0,64},{64,0},{1,65},{65,1},{2,66},{66,2},{3,67},{67,3},{4,68},{68... | collective-permute-start | bytes 1179656 | tf_op jit(solution)/shard_map/ppermute | solution.py:188
  167.1 0.8 copy-start.13
  179.5 26.5 %copy-start.2 = (f32[64,192]{1,0:T(8,128)S(1)}, f32[64,192]{1,0:T(8,128)}, u32[]{:S(2)}) copy-start(f32[64,192]{1,0:T(8,128)} %fusion.2) | copy-start | bytes 147460
  179.5 26.6 %copy-start.6 = (f32[64]{0:T(128)S(1)}, f32[64]{0:T(128)}, u32[]{:S(2)}) copy-start(f32[64]{0:T(128)} %select_reduce_fusion.1) | copy-start | bytes 772
  206.8 15.5 %all-to-all-start.3 = ((f32[32,1,128]{2,1,0:T(1,128)}), f32[32,1,128]{2,1,0:T(1,128)S(1)}, u32[]{:S(2)}, u32[]{:S(2)}) async-start(f32[32,1,128]{2,1,0:T(1,128)} %broadcast_in_dim.80), calls=%async_computation.3 | async-start | bytes 32768 | tf_op jit(solution)/shard_map/all_to_all | solution.py:25
